TPU v7x, 32 devices: a whole 2x2x4 slice. The times are simulated.
32 devices in a mesh: section: 2 (over x), dp: 4 (over z), expert: 4 (over y, core).
Axes of the slice: x: 2, y: 2, z: 4, core: 2. Of those that a mesh axis runs over, the one named last changes fastest.
Arguments:
- boundary: bfloat16 [2, 1, 2048, 2048], P('section', None, ('dp', 'expert')), may hold values from -6 to 6
- lengths: int32 [1, 4, 4, 3], P(None, 'dp'), may hold values from 1 to 64, 128 in all within a row
- routes: int32 [2, 1, 2048, 6], P('section', None, ('dp', 'expert')), may hold values from 0 to 15, all different within a row; in each aligned block of 128 rows (0 to 127, 128 to 255, ..., all dimensions but the last counted through in order) at most 64 rows name the same one
- attn_gain: float32 [2, 2048], P('section'), may hold values from 0.5 to 1.5
- query_weight: bfloat16 [2, 2048, 3072], P('section', None, 'expert'), may hold values from -0.125 to 0.125
- compress_weight: bfloat16 [2, 2048, 576], P('section'), may hold values from -0.125 to 0.125
- latent_gain: float32 [2, 512], P('section'), may hold values from 0.5 to 1.5
- expand_weight: bfloat16 [2, 512, 4096], P('section', None, 'expert'), may hold values from -0.25 to 0.25
- output_weight: bfloat16 [2, 2048, 2048], P('section', 'expert'), may hold values from -1 to 1
- ffn_gain: float32 [2, 2048], P('section'), may hold values from 0.5 to 1.5
- router_weight: bfloat16 [2, 2048, 16], P('section'), may hold values from -0.375 to 0.375
- shared_in: bfloat16 [2, 2048, 2, 2816], P('section', None, None, 'expert'), may hold values from -0.125 to 0.125
- shared_out: bfloat16 [2, 2816, 2048], P('section', 'expert'), may hold values from -0.109375 to 0.109375
- expert_in: bfloat16 [2, 16, 2048, 2, 768], P('section', ('dp', 'expert')), may hold values from -0.125 to 0.125
- expert_out: bfloat16 [2, 16, 768, 2048], P('section', ('dp', 'expert')), may hold values from -0.875 to 0.875
Outputs:
- ends: float32 [2, 1, 2048, 2048], P('section', None, ('dp', 'expert'))
- attn_gain_grad: float32 [2, 2048], P('section')
- query_grad: float32 [2, 2048, 3072], P('section', None, 'expert')
- compress_grad: float32 [2, 2048, 576], P('section')
- latent_gain_grad: float32 [2, 512], P('section')
- expand_grad: float32 [2, 512, 4096], P('section', None, 'expert')
- output_grad: float32 [2, 2048, 2048], P('section', 'expert')
- ffn_gain_grad: float32 [2, 2048], P('section')
- router_grad: float32 [2, 2048, 16], P('section')
- shared_in_grad: float32 [2, 2048, 2, 2816], P('section', None, None, 'expert')
- shared_out_grad: float32 [2, 2816, 2048], P('section', 'expert')
- expert_in_grad: float32 [2, 16, 2048, 2, 768], P('section', ('dp', 'expert'))
- expert_out_grad: float32 [2, 16, 768, 2048], P('section', ('dp', 'expert'))
Inputs may be any that keep to these rules, and one draw needn't show every extreme that they name: The lengths of each row of 3 sum to 128, and the largest of each row is exactly 64. `routes`: each row names 6 different experts. In the rows of one device (aligned blocks of 128 rows, section, micro-batch and rows taken together) no expert is named by more than 64 rows, and in every draw some block has an expert named by exactly 64.
All inputs are finite; a program needn't handle non-finite values.
Results may differ from a plain program's by a relative error of at most 0.034.
Values may be sent and summed in bfloat16 or wider, within the bound.
A program may use at most 448 MiB of HBM per device.

v0:
```python
import jax
import jax.numpy as jnp
from jax import lax
from jax.sharding import PartitionSpec as P

NOPE = 128
ROPE = 64
VD = 128
LAT = 512
FE = 768
TOP = 6
TOK_DEV = 128


epsilon = 1e-06
rope_base = 10000.0
masked_score = -1e30
block_limit = 512


def from_behind(value, axis, steps):
    count = lax.axis_size(axis)
    initial, last = (max(0, -steps), min(count, count - steps))
    return lax.ppermute(value, axis, [(source, source + steps) for source in range(initial, last)])


def contract(form, left, right):
    return jnp.einsum(form, left, right, preferred_element_type=jnp.float32)


def rms_forward(inputs, gain_vec):
    norm_scale = lax.rsqrt(jnp.mean(inputs * inputs, axis=-1, keepdims=True) + epsilon)
    return (inputs * norm_scale * gain_vec, norm_scale)


def rms_backward(inputs, norm_scale, gain_vec, upstream):
    weighted = upstream * gain_vec
    grad_gain = jnp.sum(upstream * inputs * norm_scale, axis=0)
    cubed = norm_scale * norm_scale * norm_scale
    grad_inputs = norm_scale * weighted - inputs * cubed * jnp.mean(
        weighted * inputs, axis=-1, keepdims=True
    )
    return (grad_inputs, grad_gain)


def rope_tables(position, half_width):
    freqs = rope_base ** (-jnp.arange(half_width, dtype=jnp.float32) / half_width)
    angles = position.astype(jnp.float32)[:, None] * freqs[None, :]
    return (jnp.cos(angles), jnp.sin(angles))


def rotate(inputs, cosine, sine_table):
    half_width = cosine.shape[-1]
    former = inputs[..., :half_width]
    latter = inputs[..., half_width:]
    return jnp.concatenate(
        [former * cosine - latter * sine_table, latter * cosine + former * sine_table], axis=-1
    )


def pack_layout(pack_lengths, pack_rows):
    starts = jnp.cumsum(pack_lengths) - pack_lengths
    row_index = jnp.arange(pack_rows, dtype=jnp.int32)
    begun = row_index[:, None] >= starts[None, :]
    segment = jnp.sum(begun.astype(jnp.int32), axis=1)
    opening = jnp.max(jnp.where(begun, starts[None, :], 0), axis=1)
    return (segment, row_index - opening)


def group_layout(group_lengths, group_rows):
    segment, position = jax.vmap(lambda one: pack_layout(one, group_rows))(group_lengths)
    seq_count = group_lengths.shape[1]
    offsets = jnp.arange(group_lengths.shape[0], dtype=jnp.int32)[:, None] * seq_count
    return ((segment + offsets).reshape(-1), position.reshape(-1))


def block_size(row_count):
    return min(row_count, TOK_DEV * max(1, block_limit // TOK_DEV))


def visible(segment, offset, block_rows):
    seg_block = segment[offset : offset + block_rows]
    row_index = jnp.arange(block_rows, dtype=jnp.int32)
    same_seq = seg_block[:, None] == seg_block[None, :]
    return same_seq & (row_index[None, :] <= row_index[:, None])


def silu_parts(pre_gate):
    sigmoid_part = jax.nn.sigmoid(pre_gate)
    activated = pre_gate * sigmoid_part
    slope = sigmoid_part * (1.0 + pre_gate * (1.0 - sigmoid_part))
    return (activated, slope)


def slot_count(row_count, expert_count):
    return 4 * row_count * TOP // (3 * expert_count)


def gather_rows(local_rows):
    return lax.all_gather(local_rows, "expert", axis=0, tiled=True)


def sum_rows(partial_rows):
    return lax.psum_scatter(partial_rows, "expert", scatter_dimension=0, tiled=True)


def trade_slots(slot_rows):
    return lax.all_to_all(slot_rows, ("dp", "expert"), split_axis=0, concat_axis=0, tiled=True)


def project_heads(row_block, key_block, query_weight, expand_weight, cosine, sine_table):
    row_count = row_block.shape[0]
    head_count = query_weight.shape[1] // (NOPE + ROPE)
    query_raw = jnp.dot(row_block, query_weight, preferred_element_type=jnp.float32).reshape(
        row_count, head_count, NOPE + ROPE
    )
    query_heads = jnp.concatenate(
        [
            query_raw[..., :NOPE],
            rotate(query_raw[..., NOPE:], cosine[:, None, :], sine_table[:, None, :]),
        ],
        axis=-1,
    ).astype(jnp.bfloat16)
    latent = (
        jnp.dot(key_block[:, :LAT], expand_weight, preferred_element_type=jnp.float32)
        .reshape(row_count, head_count, NOPE + VD)
        .astype(jnp.bfloat16)
    )
    shared_key = jnp.broadcast_to(key_block[:, None, LAT:], (row_count, head_count, ROPE))
    key_heads = jnp.concatenate([latent[..., :NOPE], shared_key], axis=-1)
    return (query_heads, key_heads, latent[..., NOPE:])


def attention_forward(query_heads, key_heads, value_heads, segment):
    row_count = query_heads.shape[0]
    block_rows = block_size(row_count)
    factor = (NOPE + ROPE) ** (-0.5)
    out_blocks = []
    log_blocks = []
    for offset in range(0, row_count, block_rows):
        allowed = visible(segment, offset, block_rows)
        scores = (
            contract(
                "bhc,khc->hbk",
                query_heads[offset : offset + block_rows],
                key_heads[offset : offset + block_rows],
            )
            * factor
        )
        scores = jnp.where(allowed[None], scores, masked_score)
        row_max = jnp.max(scores, axis=-1, keepdims=True)
        log_total = row_max + jnp.log(jnp.sum(jnp.exp(scores - row_max), axis=-1, keepdims=True))
        weights = jnp.exp(scores - log_total).astype(jnp.bfloat16)
        out_blocks.append(
            contract("hbk,khv->bhv", weights, value_heads[offset : offset + block_rows]).astype(
                jnp.bfloat16
            )
        )
        log_blocks.append(log_total[..., 0])
    attended = jnp.concatenate(out_blocks, axis=0)
    return (attended.reshape(row_count, -1), jnp.concatenate(log_blocks, axis=1))


def attention_backward(query_heads, key_heads, value_heads, segment, log_totals, grad_attended):
    row_count, head_count, qk_width = query_heads.shape
    block_rows = block_size(row_count)
    factor = (NOPE + ROPE) ** (-0.5)
    grad_out = grad_attended.reshape(row_count, head_count, VD)
    key_blocks = []
    value_blocks = []
    query_blocks = []
    for offset in range(0, row_count, block_rows):
        allowed = visible(segment, offset, block_rows)
        query_part = query_heads[offset : offset + block_rows]
        key_part = key_heads[offset : offset + block_rows]
        value_part = value_heads[offset : offset + block_rows]
        scores = contract("bhc,khc->hbk", query_part, key_part) * factor
        scores = jnp.where(allowed[None], scores, masked_score)
        weights = jnp.exp(scores - log_totals[:, offset : offset + block_rows, None])
        grad_part = grad_out[offset : offset + block_rows]
        value_blocks.append(contract("hbk,bhv->khv", weights.astype(jnp.bfloat16), grad_part))
        grad_weights = contract("bhv,khv->hbk", grad_part, value_part)
        centre = jnp.sum(weights * grad_weights, axis=-1, keepdims=True)
        grad_scores = (weights * (grad_weights - centre) * factor).astype(jnp.bfloat16)
        query_blocks.append(contract("hbk,khc->bhc", grad_scores, key_part))
        key_blocks.append(contract("hbk,bhc->khc", grad_scores, query_part))
    return (
        jnp.concatenate(query_blocks, axis=0),
        jnp.concatenate(key_blocks, axis=0),
        jnp.concatenate(value_blocks, axis=0),
    )


def project_backward(
    row_block,
    key_block,
    query_weight,
    expand_weight,
    cosine,
    sine_table,
    grad_query,
    grad_keys,
    grad_values,
):
    row_count, head_count, qk_width = grad_query.shape
    grad_q = jnp.concatenate(
        [
            grad_query[..., :NOPE],
            rotate(grad_query[..., NOPE:], cosine[:, None, :], -sine_table[:, None, :]),
        ],
        axis=-1,
    )
    grad_q = grad_q.reshape(row_count, head_count * qk_width).astype(jnp.bfloat16)
    grad_latent = (
        jnp.concatenate([grad_keys[..., :NOPE], grad_values], axis=-1)
        .reshape(row_count, -1)
        .astype(jnp.bfloat16)
    )
    grad_shared = jnp.sum(grad_keys[..., NOPE:], axis=1)
    query_part = jnp.dot(row_block.T, grad_q, preferred_element_type=jnp.float32)
    expand_part = jnp.dot(key_block[:, :LAT].T, grad_latent, preferred_element_type=jnp.float32)
    grad_rows = jnp.dot(grad_q, query_weight.T, preferred_element_type=jnp.float32)
    grad_keyed = jnp.concatenate(
        [jnp.dot(grad_latent, expand_weight.T, preferred_element_type=jnp.float32), grad_shared],
        axis=1,
    )
    return (query_part, expand_part, grad_rows, grad_keyed)


def slot_plan(route_rows, expert_count, capacity):
    flat_routes = route_rows.reshape(-1)
    pair_count = flat_routes.shape[0]
    onehot = (flat_routes[:, None] == jnp.arange(expert_count, dtype=jnp.int32)[None, :]).astype(
        jnp.int32
    )
    earlier = jnp.cumsum(onehot, axis=0) - onehot
    slot_id = flat_routes * capacity + jnp.sum(earlier * onehot, axis=1)
    matches = slot_id[None, :] == jnp.arange(expert_count * capacity, dtype=jnp.int32)[:, None]
    filled = jnp.any(matches, axis=1)
    source = jnp.sum(
        jnp.where(matches, jnp.arange(pair_count, dtype=jnp.int32)[None, :], 0), axis=1
    )
    return (slot_id, filled, source)


def layer_forward(hidden, group_lengths, route_rows, params, expert_index):
    (
        attn_gain,
        query_weight,
        compress_weight,
        latent_gain,
        expand_weight,
        output_weight,
        ffn_gain,
        router_weight,
        shared_in,
        shared_out,
        expert_in,
        expert_out,
    ) = params
    row_count, model_width = hidden.shape
    pack_rows = row_count * lax.axis_size("expert")
    segment, position = group_layout(group_lengths, row_count)
    cosine, sine_table = rope_tables(position, ROPE // 2)
    own_cos = lax.dynamic_slice_in_dim(cosine, expert_index * row_count, row_count, 0)
    own_sin = lax.dynamic_slice_in_dim(sine_table, expert_index * row_count, row_count, 0)
    normed32, scale_attn = rms_forward(hidden, attn_gain)
    normed = normed32.astype(jnp.bfloat16)
    compressed = jnp.dot(normed, compress_weight, preferred_element_type=jnp.float32)
    latent32, scale_latent = rms_forward(compressed[:, :LAT], latent_gain)
    keyed_rows = jnp.concatenate(
        [latent32, rotate(compressed[:, LAT:], own_cos, own_sin)], axis=1
    ).astype(jnp.bfloat16)
    rows_all, keys_all = (
        lax.all_gather(normed, "expert", axis=0, tiled=True),
        lax.all_gather(keyed_rows, "expert", axis=0, tiled=True),
    )
    query_heads, key_heads, value_heads = project_heads(
        rows_all, keys_all, query_weight, expand_weight, cosine, sine_table
    )
    attended, log_totals = attention_forward(query_heads, key_heads, value_heads, segment)
    mixed_rows = hidden + sum_rows(
        jnp.dot(attended, output_weight, preferred_element_type=jnp.float32)
    )
    ffn32, scale_ffn = rms_forward(mixed_rows, ffn_gain)
    ffn_in = ffn32.astype(jnp.bfloat16)
    expert_count = router_weight.shape[1]
    router_prob = jax.nn.softmax(
        jnp.dot(ffn_in, router_weight, preferred_element_type=jnp.float32), axis=-1
    )
    choose = (route_rows[..., None] == jnp.arange(expert_count, dtype=jnp.int32)).astype(
        jnp.float32
    )
    gate_values = jnp.sum(router_prob[:, None, :] * choose, axis=-1)
    ffn_all = gather_rows(ffn_in)
    shared_pre = jnp.dot(
        ffn_all, shared_in.reshape(model_width, -1), preferred_element_type=jnp.float32
    ).reshape(pack_rows, 2, -1)
    shared_act, shared_slope = silu_parts(shared_pre[:, 0])
    shared_hid = (shared_act * shared_pre[:, 1]).astype(jnp.bfloat16)
    shared_sum = sum_rows(jnp.dot(shared_hid, shared_out, preferred_element_type=jnp.float32))
    capacity = slot_count(row_count, expert_count)
    slot_id, filled, source = slot_plan(route_rows, expert_count, capacity)
    outgoing = jnp.where(filled[:, None], ffn_in[source // TOP], jnp.zeros_like(ffn_in[:1]))
    arrived = trade_slots(outgoing.reshape(expert_count, capacity, model_width)).reshape(
        expert_count * capacity, model_width
    )
    expert_pre = jnp.dot(
        arrived, expert_in.reshape(model_width, -1), preferred_element_type=jnp.float32
    ).reshape(-1, 2, FE)
    expert_act, expert_slope = silu_parts(expert_pre[:, 0])
    expert_hid = (expert_act * expert_pre[:, 1]).astype(jnp.bfloat16)
    produced = jnp.dot(expert_hid, expert_out, preferred_element_type=jnp.float32).astype(
        jnp.bfloat16
    )
    returned = trade_slots(produced.reshape(expert_count, capacity, model_width)).reshape(
        expert_count * capacity, model_width
    )
    picked = returned[slot_id].reshape(row_count, TOP, model_width)
    routed = jnp.sum(gate_values[..., None] * picked.astype(jnp.float32), axis=1)
    result = mixed_rows + shared_sum + routed
    stored = {
        "segment": segment,
        "cosine": cosine,
        "sine_table": sine_table,
        "own_cos": own_cos,
        "own_sin": own_sin,
        "normed": normed,
        "compressed": compressed,
        "scale_attn": scale_attn,
        "scale_latent": scale_latent,
        "rows_all": rows_all,
        "keys_all": keys_all,
        "query_heads": query_heads,
        "key_heads": key_heads,
        "value_heads": value_heads,
        "attended": attended,
        "log_totals": log_totals,
        "mixed_rows": mixed_rows,
        "scale_ffn": scale_ffn,
        "ffn_in": ffn_in,
        "ffn_all": ffn_all,
        "router_prob": router_prob,
        "choose": choose,
        "gate_values": gate_values,
        "shared_pre": shared_pre,
        "shared_hid": shared_hid,
        "slot_id": slot_id,
        "filled": filled,
        "source": source,
        "arrived": arrived,
        "expert_pre": expert_pre,
        "expert_hid": expert_hid,
        "picked": picked,
    }
    return (result, stored)


def layer_backward(hidden, params, stored, upstream):
    (
        attn_gain,
        query_weight,
        compress_weight,
        latent_gain,
        expand_weight,
        output_weight,
        ffn_gain,
        router_weight,
        shared_in,
        shared_out,
        expert_in,
        expert_out,
    ) = params
    row_count, model_width = hidden.shape
    expert_count = router_weight.shape[1]
    capacity = slot_count(row_count, expert_count)
    source = stored["source"]
    grad_gates = jnp.sum(upstream[:, None, :] * stored["picked"].astype(jnp.float32), axis=-1)
    flat_gates = stored["gate_values"].reshape(-1)
    back_rows = (flat_gates[source][:, None] * upstream[source // TOP]).astype(jnp.bfloat16)
    back_rows = jnp.where(stored["filled"][:, None], back_rows, jnp.zeros_like(back_rows[:1]))
    grad_produced = trade_slots(back_rows.reshape(expert_count, capacity, model_width)).reshape(
        expert_count * capacity, model_width
    )
    grad_hidden_units = jnp.dot(grad_produced, expert_out.T, preferred_element_type=jnp.float32)
    grad_expert_out = jnp.dot(
        stored["expert_hid"].T, grad_produced, preferred_element_type=jnp.float32
    )
    expert_pre = stored["expert_pre"]
    expert_act, expert_slope = silu_parts(expert_pre[:, 0])
    grad_pre = (
        jnp.stack(
            [grad_hidden_units * expert_pre[:, 1] * expert_slope, grad_hidden_units * expert_act],
            axis=1,
        )
        .reshape(expert_pre.shape[0], -1)
        .astype(jnp.bfloat16)
    )
    flat_in = expert_in.reshape(model_width, -1)
    grad_expert_in = jnp.dot(
        stored["arrived"].T, grad_pre, preferred_element_type=jnp.float32
    ).reshape(model_width, 2, FE)
    grad_arrived = jnp.dot(grad_pre, flat_in.T, preferred_element_type=jnp.float32).astype(
        jnp.bfloat16
    )
    grad_sent = trade_slots(grad_arrived.reshape(expert_count, capacity, model_width)).reshape(
        expert_count * capacity, model_width
    )
    grad_ffn = jnp.sum(
        grad_sent[stored["slot_id"]].reshape(row_count, TOP, model_width).astype(jnp.float32),
        axis=1,
    )
    grad_prob = jnp.sum(grad_gates[..., None] * stored["choose"], axis=1)
    router_prob = stored["router_prob"]
    grad_logits = (
        router_prob * (grad_prob - jnp.sum(router_prob * grad_prob, axis=-1, keepdims=True))
    ).astype(jnp.bfloat16)
    grad_router = jnp.dot(stored["ffn_in"].T, grad_logits, preferred_element_type=jnp.float32)
    grad_ffn = grad_ffn + jnp.dot(grad_logits, router_weight.T, preferred_element_type=jnp.float32)
    upstream_all = gather_rows(upstream.astype(jnp.bfloat16))
    grad_shared_hid = jnp.dot(upstream_all, shared_out.T, preferred_element_type=jnp.float32)
    grad_shared_out = jnp.dot(
        stored["shared_hid"].T, upstream_all, preferred_element_type=jnp.float32
    )
    shared_pre = stored["shared_pre"]
    shared_act, shared_slope = silu_parts(shared_pre[:, 0])
    grad_shared_pre = (
        jnp.stack(
            [grad_shared_hid * shared_pre[:, 1] * shared_slope, grad_shared_hid * shared_act],
            axis=1,
        )
        .reshape(shared_pre.shape[0], -1)
        .astype(jnp.bfloat16)
    )
    grad_shared_in = jnp.dot(
        stored["ffn_all"].T, grad_shared_pre, preferred_element_type=jnp.float32
    ).reshape(model_width, 2, -1)
    grad_ffn = grad_ffn + sum_rows(
        jnp.dot(
            grad_shared_pre,
            shared_in.reshape(model_width, -1).T,
            preferred_element_type=jnp.float32,
        )
    )
    grad_mixed_norm, grad_ffn_gain = rms_backward(
        stored["mixed_rows"], stored["scale_ffn"], ffn_gain, grad_ffn
    )
    grad_mixed = upstream + grad_mixed_norm
    grad_mixed_all = gather_rows(grad_mixed.astype(jnp.bfloat16))
    grad_attended = jnp.dot(
        grad_mixed_all, output_weight.T, preferred_element_type=jnp.float32
    ).astype(jnp.bfloat16)
    grad_output = jnp.dot(stored["attended"].T, grad_mixed_all, preferred_element_type=jnp.float32)
    grad_query, grad_keys, grad_values = attention_backward(
        stored["query_heads"],
        stored["key_heads"],
        stored["value_heads"],
        stored["segment"],
        stored["log_totals"],
        grad_attended,
    )
    grad_query_w, grad_expand_w, grad_rows, grad_keyed = project_backward(
        stored["rows_all"],
        stored["keys_all"],
        query_weight,
        expand_weight,
        stored["cosine"],
        stored["sine_table"],
        grad_query,
        grad_keys,
        grad_values,
    )
    own_rows, own_keyed = (
        lax.psum_scatter(grad_rows, "expert", scatter_dimension=0, tiled=True),
        lax.psum_scatter(grad_keyed, "expert", scatter_dimension=0, tiled=True),
    )
    grad_latent, grad_latent_gain = rms_backward(
        stored["compressed"][:, :LAT], stored["scale_latent"], latent_gain, own_keyed[:, :LAT]
    )
    grad_compressed = jnp.concatenate(
        [grad_latent, rotate(own_keyed[:, LAT:], stored["own_cos"], -stored["own_sin"])], axis=1
    ).astype(jnp.bfloat16)
    grad_compress = jnp.dot(stored["normed"].T, grad_compressed, preferred_element_type=jnp.float32)
    grad_normed = own_rows + jnp.dot(
        grad_compressed, compress_weight.T, preferred_element_type=jnp.float32
    )
    grad_hidden_norm, grad_attn_gain = rms_backward(
        hidden, stored["scale_attn"], attn_gain, grad_normed
    )
    grads = (
        grad_attn_gain,
        grad_query_w,
        grad_compress,
        grad_latent_gain,
        grad_expand_w,
        grad_output,
        grad_ffn_gain,
        grad_router,
        grad_shared_in,
        grad_shared_out,
        grad_expert_in,
        grad_expert_out,
    )
    return (grad_mixed + grad_hidden_norm, grads)


def body(
    boundary,
    lengths,
    routes,
    attn_gain,
    query_weight,
    compress_weight,
    latent_gain,
    expand_weight,
    output_weight,
    ffn_gain,
    router_weight,
    shared_in,
    shared_out,
    expert_in,
    expert_out,
):
    params = (
        attn_gain[0],
        query_weight[0],
        compress_weight[0],
        latent_gain[0],
        expand_weight[0],
        output_weight[0],
        ffn_gain[0],
        router_weight[0],
        shared_in[0],
        shared_out[0],
        expert_in[0, 0],
        expert_out[0, 0],
    )
    micro_count = boundary.shape[1]
    section_id = lax.axis_index("section")
    is_first = section_id == 0
    expert_index = lax.axis_index("expert")
    inbound = jnp.zeros(boundary.shape[2:], jnp.bfloat16)
    stored_list = []
    results = []
    for tick_id in range(micro_count + 1):
        batch_id = jnp.clip(tick_id - section_id, 0, micro_count - 1)
        fresh_rows = lax.dynamic_index_in_dim(boundary[0], batch_id, 0, keepdims=False)
        hidden = jnp.where(is_first, fresh_rows, inbound).astype(jnp.float32)
        group_lengths = lax.dynamic_index_in_dim(lengths[:, 0], batch_id, 0, keepdims=False)
        route_rows = lax.dynamic_index_in_dim(routes[0], batch_id, 0, keepdims=False)
        result, stored = layer_forward(hidden, group_lengths, route_rows, params, expert_index)
        stored_list.append((hidden, stored))
        results.append(result)
        if tick_id < micro_count:
            inbound = from_behind(result.astype(jnp.bfloat16), "section", 1)
    totals = None
    downbound = jnp.zeros(boundary.shape[2:], jnp.float32)
    input_grads = []
    for turn_id in range(micro_count + 1):
        hidden, stored = stored_list[micro_count - turn_id]
        batch_id = micro_count - turn_id - section_id
        is_live = (batch_id >= 0) & (batch_id < micro_count)
        target = lax.dynamic_index_in_dim(
            boundary[0], jnp.clip(batch_id, 0, micro_count - 1), 0, keepdims=False
        ).astype(jnp.float32)
        upstream = jnp.where(
            is_first, downbound, jnp.where(is_live, target, jnp.zeros_like(target))
        )
        grad_hidden, grads = layer_backward(hidden, params, stored, upstream)
        if totals is None:
            totals = grads
        else:
            totals = tuple((left_term + right_term for left_term, right_term in zip(totals, grads)))
        input_grads.append(grad_hidden)
        if turn_id < micro_count:
            downbound = from_behind(grad_hidden, "section", -1)
    ends = jnp.stack([jnp.where(is_first, input_grads[micro_count], results[1])])[None]
    (
        grad_attn_gain,
        grad_query_w,
        grad_compress,
        grad_latent_gain,
        grad_expand_w,
        grad_output,
        grad_ffn_gain,
        grad_router,
        grad_shared_in,
        grad_shared_out,
        grad_expert_in,
        grad_expert_out,
    ) = totals
    grad_query_w, grad_expand_w, grad_output, grad_shared_in, grad_shared_out = lax.psum(
        (grad_query_w, grad_expand_w, grad_output, grad_shared_in, grad_shared_out), "dp"
    )
    grad_attn_gain, grad_compress, grad_latent_gain, grad_ffn_gain, grad_router = lax.psum(
        (grad_attn_gain, grad_compress, grad_latent_gain, grad_ffn_gain, grad_router),
        ("dp", "expert"),
    )
    return (
        ends,
        grad_attn_gain[None],
        grad_query_w[None],
        grad_compress[None],
        grad_latent_gain[None],
        grad_expand_w[None],
        grad_output[None],
        grad_ffn_gain[None],
        grad_router[None],
        grad_shared_in[None],
        grad_shared_out[None],
        grad_expert_in[None, None],
        grad_expert_out[None, None],
    )


def solution(mesh):
    return jax.shard_map(
        body,
        mesh=mesh,
        in_specs=(
            P("section", None, ("dp", "expert"), None),
            P(None, "dp", None, None),
            P("section", None, ("dp", "expert"), None),
            P("section", None),
            P("section", None, "expert"),
            P("section", None, None),
            P("section", None),
            P("section", None, "expert"),
            P("section", "expert", None),
            P("section", None),
            P("section", None, None),
            P("section", None, None, "expert"),
            P("section", "expert", None),
            P("section", ("dp", "expert"), None, None, None),
            P("section", ("dp", "expert"), None, None),
        ),
        out_specs=(
            P("section", None, ("dp", "expert"), None),
            P("section", None),
            P("section", None, "expert"),
            P("section", None, None),
            P("section", None),
            P("section", None, "expert"),
            P("section", "expert", None),
            P("section", None),
            P("section", None, None),
            P("section", None, None, "expert"),
            P("section", "expert", None),
            P("section", ("dp", "expert"), None, None, None),
            P("section", ("dp", "expert"), None, None),
        ),
        check_vma=False,
    )
```

profile of v0, /device:TPU:3, one launch (start us, length us, event | category | flops | bytes accessed | tf_op | source)
XLA Modules:
  0.0 2632.7 jit_solution(5928563475551697312)
XLA Ops:
  62.6 35.2 %reduce-scatter.11.cloned.1.call-done = f32[128,2048]{1,0:T(8,128)} async-done(((f32[512,2048]{1,0:T(8,128)}), f32[128,2048]{1,0:T(8,128)}) %reduce-scatter.11.cloned.1.call-update) | async-done | bytes 1048592 | tf_op jit(solution)/shard_map/reduce_scatter | solution.py:104
  138.8 29.3 %all-gather.11.cloned.1.call-done = bf16[512,2048]{1,0:T(8,128)(2,1)} async-done(((bf16[128,2048]{1,0:T(8,128)(2,1)}), bf16[512,2048]{1,0:T(8,128)(2,1)}) %all-gather.11.cloned.1.call-update) | async-done | bytes 2097168 | tf_op jit(solution)/shard_map/all_gather | solution.py:100
  179.7 20.8 all-to-all-done
  218.2 19.6 all-to-all-start.1
  250.1 65.7 %all-to-all-done.1 = bf16[16,64,2048]{2,1,0:T(8,128)(2,1)} async-done(((bf16[16,64,2048]{2,1,0:T(8,128)(2,1)}), bf16[16,64,2048]{2,1,0:T(8,128)(2,1)}, u32[]{:S(2)}, u32[]{:S(2)}) %all-to-all-start.1) | async-done | bytes 4194336 | tf_op jit(solution)/shard_map/all_to_all | solution.py:108
  382.0 16.1 all-gather.13.cloned.1.call-done
  422.2 34.6 %reduce-scatter.15.cloned.1.call-done = f32[128,2048]{1,0:T(8,128)} async-done(((f32[512,2048]{1,0:T(8,128)}), f32[128,2048]{1,0:T(8,128)}) %reduce-scatter.15.cloned.1.call-update) | async-done | bytes 1048592 | tf_op jit(solution)/shard_map/reduce_scatter | solution.py:104
  485.2 98.0 %all_to_all.40 = bf16[16,64,2048]{2,1,0:T(8,128)(2,1)} all-to-all(bf16[16,64,2048]{2,1,0:T(8,128)(2,1)S(1)} %get-tuple-element.134), channel_id=1, replica_groups=mesh['section'=2,'dp'=4,'expert'=4] {'dp','expert'}, dimensions={0} | all-to-all | bytes 8388608 | tf_op jit(solution)/shard_map/all_to_all | solution.py:108
  608.4 57.7 %all-to-all-done.2 = bf16[16,64,2048]{2,1,0:T(8,128)(2,1)} async-done(((bf16[16,64,2048]{2,1,0:T(8,128)(2,1)}), bf16[16,64,2048]{2,1,0:T(8,128)(2,1)}, u32[]{:S(2)}, u32[]{:S(2)}) %all-to-all-start.2) | async-done | bytes 4194336 | tf_op jit(solution)/shard_map/all_to_all | solution.py:108
  666.2 19.1 all-to-all-start.5
  729.3 34.2 %all-to-all-done.5 = bf16[16,64,2048]{2,1,0:T(8,128)(2,1)} async-done(((bf16[16,64,2048]{2,1,0:T(8,128)(2,1)}), bf16[16,64,2048]{2,1,0:T(8,128)(2,1)}, u32[]{:S(2)}, u32[]{:S(2)}) %all-to-all-start.5) | async-done | bytes 4194336 | tf_op jit(solution)/shard_map/all_to_all | solution.py:108
  763.5 19.2 all-to-all-start.4
  807.7 53.2 %all-to-all-done.4 = bf16[16,64,2048]{2,1,0:T(8,128)(2,1)} async-done(((bf16[16,64,2048]{2,1,0:T(8,128)(2,1)}), bf16[16,64,2048]{2,1,0:T(8,128)(2,1)}, u32[]{:S(2)}, u32[]{:S(2)}) %all-to-all-start.4) | async-done | bytes 4194336 | tf_op jit(solution)/shard_map/all_to_all | solution.py:108
  889.5 36.7 %all-gather.19.cloned.1.call-done = bf16[512,2048]{1,0:T(8,128)(2,1)} async-done(((bf16[128,2048]{1,0:T(8,128)(2,1)}), bf16[512,2048]{1,0:T(8,128)(2,1)}) %all-gather.19.cloned.1.call-update) | async-done | bytes 2097168 | tf_op jit(solution)/shard_map/all_gather | solution.py:100
  980.9 43.3 %reduce-scatter.19.cloned.1.call-done = f32[128,2048]{1,0:T(8,128)} async-done(((f32[512,2048]{1,0:T(8,128)}), f32[128,2048]{1,0:T(8,128)}) %reduce-scatter.19.cloned.1.call-update) | async-done | bytes 1048592 | tf_op jit(solution)/shard_map/reduce_scatter | solution.py:474
  1037.3 16.3 collective-permute-done.1
  1078.5 44.8 %all-gather.21.cloned.1.call-done = bf16[512,2048]{1,0:T(8,128)(2,1)} async-done(((bf16[128,2048]{1,0:T(8,128)(2,1)}), bf16[512,2048]{1,0:T(8,128)(2,1)}) %all-gather.21.cloned.1.call-update) | async-done | bytes 2097168 | tf_op jit(solution)/shard_map/all_gather | solution.py:100
  1137.5 18.2 all-to-all-done.6
  1176.7 18.8 all-to-all-start.7
  1200.6 73.0 %all-to-all-done.7 = bf16[16,64,2048]{2,1,0:T(8,128)(2,1)} async-done(((bf16[16,64,2048]{2,1,0:T(8,128)(2,1)}), bf16[16,64,2048]{2,1,0:T(8,128)(2,1)}, u32[]{:S(2)}, u32[]{:S(2)}) %all-to-all-start.7) | async-done | bytes 4194336 | tf_op jit(solution)/shard_map/all_to_all | solution.py:108
  1301.6 37.8 %all-gather.23.cloned.1.call-done = bf16[512,2048]{1,0:T(8,128)(2,1)} async-done(((bf16[128,2048]{1,0:T(8,128)(2,1)}), bf16[512,2048]{1,0:T(8,128)(2,1)}) %all-gather.23.cloned.1.call-update) | async-done | bytes 2097168 | tf_op jit(solution)/shard_map/all_gather | solution.py:100
  1488.0 38.4 %copy.146 = f32[1,1,2048,2,768]{4,3,2,1,0:T(2,128)} copy(f32[1,1,2048,2,768]{4,2,3,1,0:T(8,128)S(1)} %add_bitcast_fusion) | data formatting | bytes 25165824
  1538.0 56.0 %all-reduce = (f32[1,2048]{1,0:T(1,128)}, f32[1,512]{1,0:T(1,128)}, f32[1,2048]{1,0:T(1,128)}) all-reduce(f32[1,2048]{1,0:T(1,128)S(1)} %bitcast.581, f32[1,512]{1,0:T(1,128)S(1)} %bitcast.586, f32[1,2048]{1,0:T(1,128)S(1)} %bitcast.580), channel_id=1, replica_groups=mesh['section'=2,'dp'=4,'expert'=4] {'dp','expert'}, use_global_device_ids=true, to_apply=%region_56.57 | all-reduce | flops 4608 | bytes 36864 | tf_op jit(solution)/shard_map/psum | solution.py:595
  1608.7 988.5 %all-reduce.8.cloned.1.call-done = (f32[1,2048,768]{2,1,0:T(8,128)}, f32[1,512,1024]{2,1,0:T(8,128)}, f32[1,512,2048]{2,1,0:T(8,128)}, f32[1,2048,2,704]{1,3,2,0:T(8,128)}, f32[1,704,2048]{2,1,0:T(8,128)}) async-done(((f32[1,2048,768]{2,1,0:T(8,128)}, f32[1,512,1024]{2,1,0:T(8,128)}, f32[1,512,2048]{2,1,0:T(8,128)}, f32[1,2048,2,704]{1,3,2,0:T(8,128)}, f32[1,704,2048]{2,1,0:T(8,128)}), ...) | async-done | bytes 29884432 | tf_op jit(solution)/shard_map/psum | solution.py:592
  (643 shorter events, 741.3 us)
Async XLA Ops:
  11.4 86.5 %reduce-scatter.11.cloned.1.call-start = ((), (), s32[]{:S(2)}) async-start(), calls=%async_computation.19 | async-start | bytes 5242880 | tf_op jit(solution)/shard_map/reduce_scatter | solution.py:104
  116.9 83.6 %all-to-all-start = ((bf16[16,64,2048]{2,1,0:T(8,128)(2,1)}), bf16[16,64,2048]{2,1,0:T(8,128)(2,1)}, u32[]{:S(2)}, u32[]{:S(2)}) async-start(bf16[16,64,2048]{2,1,0:T(8,128)(2,1)} %broadcast_select_fusion.1), calls=%async_computation.2 | async-start | bytes 8388608 | tf_op jit(solution)/shard_map/all_to_all | solution.py:108
  123.1 216.8 %reduce-scatter.13.cloned.1.call-start = ((), (), s32[]{:S(2)}) async-start(), calls=%async_computation.21 | async-start | bytes 5242880 | tf_op jit(solution)/shard_map/reduce_scatter | solution.py:104
  218.2 97.7 %all-to-all-start.1 = ((bf16[16,64,2048]{2,1,0:T(8,128)(2,1)}), bf16[16,64,2048]{2,1,0:T(8,128)(2,1)}, u32[]{:S(2)}, u32[]{:S(2)}) async-start(bf16[16,64,2048]{2,1,0:T(8,128)(2,1)} %bitcast.531), calls=%async_computation.3 | async-start | bytes 8388608 | tf_op jit(solution)/shard_map/all_to_all | solution.py:108
  237.7 160.4 %all-gather.13.cloned.1.call-start = ((), (), s32[]{:S(2)}) async-start(), calls=%async_computation.22 | async-start | bytes 2621440 | tf_op jit(solution)/shard_map/all_gather | solution.py:275
  361.0 95.9 %reduce-scatter.15.cloned.1.call-start = ((), (), s32[]{:S(2)}) async-start(), calls=%async_computation.23 | async-start | bytes 5242880 | tf_op jit(solution)/shard_map/reduce_scatter | solution.py:104
  583.2 83.0 %all-to-all-start.2 = ((bf16[16,64,2048]{2,1,0:T(8,128)(2,1)}), bf16[16,64,2048]{2,1,0:T(8,128)(2,1)}, u32[]{:S(2)}, u32[]{:S(2)}) async-start(bf16[16,64,2048]{2,1,0:T(8,128)(2,1)} %get-tuple-element.135), calls=%async_computation.5 | async-start | bytes 8388608 | tf_op jit(solution)/shard_map/all_to_all | solution.py:108
  588.0 97.4 %all-gather.17.cloned.1.call-start = ((), (), s32[]{:S(2)}) async-start(), calls=%async_computation.25 | async-start | bytes 2621440 | tf_op jit(solution)/shard_map/all_gather | solution.py:100
  588.7 104.8 %all-gather.15.cloned.1.call-start = ((), (), s32[]{:S(2)}) async-start(), calls=%async_computation.24 | async-start | bytes 2621440 | tf_op jit(solution)/shard_map/all_gather | solution.py:100
  666.2 97.4 %all-to-all-start.5 = ((bf16[16,64,2048]{2,1,0:T(8,128)(2,1)}), bf16[16,64,2048]{2,1,0:T(8,128)(2,1)}, u32[]{:S(2)}, u32[]{:S(2)}) async-start(bf16[16,64,2048]{2,1,0:T(8,128)(2,1)} %bitcast.530), calls=%async_computation.8 | async-start | bytes 8388608 | tf_op jit(solution)/shard_map/all_to_all | solution.py:108
  685.3 199.2 %reduce-scatter.17.cloned.1.call-start = ((), (), s32[]{:S(2)}) async-start(), calls=%async_computation.26 | async-start | bytes 5242880 | tf_op jit(solution)/shard_map/reduce_scatter | solution.py:104
  763.5 97.3 %all-to-all-start.4 = ((bf16[16,64,2048]{2,1,0:T(8,128)(2,1)}), bf16[16,64,2048]{2,1,0:T(8,128)(2,1)}, u32[]{:S(2)}, u32[]{:S(2)}) async-start(bf16[16,64,2048]{2,1,0:T(8,128)(2,1)} %bitcast.532), calls=%async_computation.7 | async-start | bytes 8388608 | tf_op jit(solution)/shard_map/all_to_all | solution.py:108
  782.7 143.5 %all-gather.19.cloned.1.call-start = ((), (), s32[]{:S(2)}) async-start(), calls=%async_computation.27 | async-start | bytes 2621440 | tf_op jit(solution)/shard_map/all_gather | solution.py:100
  889.3 87.4 %reduce-scatter.21.cloned.1.call-start = ((), (), s32[]{:S(2)}) async-start(), calls=%async_computation.29 | async-start | bytes 1474560 | tf_op jit(solution)/shard_map/reduce_scatter | solution.py:475
  951.5 72.7 %reduce-scatter.19.cloned.1.call-start = ((), (), s32[]{:S(2)}) async-start(), calls=%async_computation.28 | async-start | bytes 5242880 | tf_op jit(solution)/shard_map/reduce_scatter | solution.py:474
  1071.3 84.4 %all-to-all-start.6 = ((bf16[16,64,2048]{2,1,0:T(8,128)(2,1)}), bf16[16,64,2048]{2,1,0:T(8,128)(2,1)}, u32[]{:S(2)}, u32[]{:S(2)}) async-start(bf16[16,64,2048]{2,1,0:T(8,128)(2,1)} %fusion.7), calls=%async_computation.12 | async-start | bytes 8388608 | tf_op jit(solution)/shard_map/all_to_all | solution.py:108
  1078.3 218.7 %reduce-scatter.23.cloned.1.call-start = ((), (), s32[]{:S(2)}) async-start(), calls=%async_computation.31 | async-start | bytes 5242880 | tf_op jit(solution)/shard_map/reduce_scatter | solution.py:104
  1176.7 97.0 %all-to-all-start.7 = ((bf16[16,64,2048]{2,1,0:T(8,128)(2,1)}), bf16[16,64,2048]{2,1,0:T(8,128)(2,1)}, u32[]{:S(2)}, u32[]{:S(2)}) async-start(bf16[16,64,2048]{2,1,0:T(8,128)(2,1)} %bitcast.533), calls=%async_computation.13 | async-start | bytes 8388608 | tf_op jit(solution)/shard_map/all_to_all | solution.py:108
  1195.5 143.9 %all-gather.23.cloned.1.call-start = ((), (), s32[]{:S(2)}) async-start(), calls=%async_computation.32 | async-start | bytes 2621440 | tf_op jit(solution)/shard_map/all_gather | solution.py:100
  1301.2 116.0 %reduce-scatter.27.cloned.1.call-start = ((), (), s32[]{:S(2)}) async-start(), calls=%async_computation.34 | async-start | bytes 1474560 | tf_op jit(solution)/shard_map/reduce_scatter | solution.py:475
  1364.7 169.5 %reduce-scatter.25.cloned.1.call-start = ((), (), s32[]{:S(2)}) async-start(), calls=%async_computation.33 | async-start | bytes 5242880 | tf_op jit(solution)/shard_map/reduce_scatter | solution.py:474
  1382.5 211.6 %reduce-scatter.29.cloned.1.call-start = ((), (), s32[]{:S(2)}) async-start(), calls=%async_computation.35 | async-start | bytes 5242880 | tf_op jit(solution)/shard_map/reduce_scatter | solution.py:104
  1389.3 219.3 %all-reduce.6.cloned.1.call-start = ((), (), s32[]{:S(2)}) async-start(), calls=%async_computation.36 | async-start | bytes 9699328 | tf_op jit(solution)/shard_map/psum | solution.py:595
  1426.4 1170.7 %all-reduce.8.cloned.1.call-start = ((), (), s32[]{:S(2)}) async-start(), calls=%async_computation.37 | async-start | bytes 59768832 | tf_op jit(solution)/shard_map/psum | solution.py:592
  (182 other events, 3334.2 us)
Sparse Core Ops, SparseCore 0:
  11.5 27.3 all-gather.8
  52.7 45.1 reduce-scatter.10
  124.7 43.4 all-gather.10
  179.8 44.8 reduce-scatter.12
  361.1 37.0 all-gather.12
  411.6 45.2 reduce-scatter.14
  590.3 43.3 all-gather.16
  635.9 32.2 all-gather.14
  708.1 60.1 reduce-scatter.16
  889.4 36.7 all-gather.18
  951.6 25.0 reduce-scatter.20
  979.6 44.5 reduce-scatter.18
  1080.5 42.8 all-gather.20
  1137.6 43.9 reduce-scatter.22
  1301.3 38.1 all-gather.22
  1364.8 25.0 reduce-scatter.26
  1392.2 44.5 reduce-scatter.24
  1439.8 44.5 reduce-scatter.28
  1488.8 119.8 all-reduce.5
  1612.8 984.3 all-reduce.7
where the time goes:
time: 2650 us; the launch traced here: 2630 us
  waiting for transfers between devices  1640 us (62%)
  matrix products  330 us (12%)
  local copies, waits for them, and re-layouts  251 us (9%)
  blocking collectives  178 us (7%)
  other arithmetic  115 us (4%)
  starting transfers between devices  101 us (4%)
    psum x1, waiting for transfers between devices, body(): lax.psum((grad_query_w, grad_expand_w, grad_output, grad_shared_in, grad_...  988 us
    all_to_all x7, waiting for transfers between devices, trade_slots(): lax.all_to_all(slot_rows, ('dp', 'expert'), split_axis=0, concat_axis=0,...  323 us
    all_gather x6, waiting for transfers between devices, gather_rows(): return lax.all_gather(local_rows, 'expert', axis=0, tiled=True)  149 us
    unnamed x367, local copies, waits for them, and re-layouts  107 us
    all_to_all x1, blocking collectives, trade_slots(): lax.all_to_all(slot_rows, ('dp', 'expert'), split_axis=0, concat_axis=0,...  98 us
    all_to_all x7, starting transfers between devices, trade_slots(): lax.all_to_all(slot_rows, ('dp', 'expert'), split_axis=0, concat_axis=0,...  93.2 us
    reduce_scatter x6, waiting for transfers between devices, sum_rows(): lax.psum_scatter(partial_rows, 'expert', scatter_dimension=0, tiled=True)  69.9 us
    psum x1, blocking collectives, body(): lax.psum((grad_attn_gain, grad_compress, grad_latent_gain, grad_ffn_gain,...  56 us
  transfers between devices with their start and end apart: 29, of which 20 were waited for; matrix products, arithmetic and copies ran while one was open for 18% of the time, Pallas kernels for 0%

commit v1 on v0

v1 whole, which is shorter than its diff:
```python
import functools

import jax
import jax.numpy as jnp
from jax import lax
from jax.experimental import pallas as pl
from jax.experimental.pallas import tpu as pltpu
from jax.sharding import PartitionSpec as P

NOPE = 128
ROPE = 64
VD = 128
LAT = 512

QK = NOPE + ROPE
KV = NOPE + VD
HALF = ROPE // 2
epsilon = 1e-06
rope_base = 10000.0
masked_score = -1e30
BOTH = ("dp", "expert")


def dot(left, right):
    return jnp.dot(left, right, preferred_element_type=jnp.float32)


def dot_t(left, right):
    return lax.dot_general(
        left, right, (((1,), (1,)), ((), ())), preferred_element_type=jnp.float32
    )


def t_dot(left, right):
    return lax.dot_general(
        left, right, (((0,), (0,)), ((), ())), preferred_element_type=jnp.float32
    )


def bf16(value):
    return value.astype(jnp.bfloat16)


def gather_all(rows):
    return lax.all_gather(rows, BOTH, axis=0, tiled=True)


def gather_pack(rows):
    return lax.all_gather(rows, "expert", axis=0, tiled=True)


def scatter_all(partial_rows):
    return lax.psum_scatter(partial_rows, BOTH, scatter_dimension=0, tiled=True)


def scatter_pack(partial_rows):
    return lax.psum_scatter(partial_rows, "expert", scatter_dimension=0, tiled=True)


def rms_forward(inputs, gain_vec):
    norm_scale = lax.rsqrt(jnp.mean(inputs * inputs, axis=-1, keepdims=True) + epsilon)
    return (inputs * norm_scale * gain_vec, norm_scale)


def rms_backward(inputs, norm_scale, gain_vec, upstream):
    weighted = upstream * gain_vec
    grad_gain = jnp.sum(upstream * inputs * norm_scale, axis=0)
    cubed = norm_scale * norm_scale * norm_scale
    grad_inputs = norm_scale * weighted - inputs * cubed * jnp.mean(
        weighted * inputs, axis=-1, keepdims=True
    )
    return (grad_inputs, grad_gain)


def rotate(inputs, cosine, sine):
    half = cosine.shape[-1]
    former = inputs[..., :half]
    latter = inputs[..., half:]
    return jnp.concatenate(
        [former * cosine - latter * sine, latter * cosine + former * sine], axis=-1
    )


def silu_parts(pre_gate):
    sigmoid = jax.nn.sigmoid(pre_gate)
    return (pre_gate * sigmoid, sigmoid * (1.0 + pre_gate * (1.0 - sigmoid)))


def block_layout(block_lengths, rows):
    starts = jnp.cumsum(block_lengths, axis=1) - block_lengths
    index = jnp.arange(rows, dtype=jnp.int32)
    begun = index[None, :, None] >= starts[:, None, :]
    segment = jnp.sum(begun.astype(jnp.int32), axis=2)
    opening = jnp.max(jnp.where(begun, starts[:, None, :], 0), axis=2)
    return segment, index[None, :] - opening


def allowed_pairs(seg_col, seg_row):
    rows = seg_col.shape[0]
    later = lax.broadcasted_iota(jnp.int32, (rows, rows), 0)
    earlier = lax.broadcasted_iota(jnp.int32, (rows, rows), 1)
    return (seg_col == seg_row) & (earlier <= later)


def attend_kernel(heads, q_ref, lat_ref, key_ref, cos_ref, sin_ref, col_ref, row_ref, out_ref, rot_ref):
    factor = QK**-0.5
    allowed = allowed_pairs(col_ref[...], row_ref[0])
    cosine, sine = cos_ref[...], sin_ref[...]
    shared = key_ref[:, LAT:]
    for head in range(heads):
        raw = q_ref[:, head * QK : (head + 1) * QK]
        query = bf16(
            jnp.concatenate([raw[:, :NOPE], rotate(raw[:, NOPE:], cosine, sine)], axis=1)
        )
        rot_ref[:, head * QK : (head + 1) * QK] = query
        key = jnp.concatenate([lat_ref[:, head * KV : head * KV + NOPE], shared], axis=1)
        value = lat_ref[:, head * KV + NOPE : (head + 1) * KV]
        scores = jnp.where(allowed, dot_t(query, key) * factor, masked_score)
        top = jnp.max(scores, axis=1, keepdims=True)
        powers = jnp.exp(scores - top)
        probs = powers / jnp.sum(powers, axis=1, keepdims=True)
        out_ref[:, head * VD : (head + 1) * VD] = bf16(dot(bf16(probs), value))


def attend(query_raw, latent, keyed, tables):
    cosine, sine, seg_col, seg_row = tables
    count, _, rows = seg_row.shape
    heads = query_raw.shape[1] // QK
    block = lambda width: pl.BlockSpec((rows, width), lambda i: (i, 0))
    return pl.pallas_call(
        functools.partial(attend_kernel, heads),
        grid=(count,),
        in_specs=[
            block(heads * QK),
            block(heads * KV),
            block(LAT + ROPE),
            block(HALF),
            block(HALF),
            block(1),
            pl.BlockSpec((1, 1, rows), lambda i: (i, 0, 0)),
        ],
        out_specs=[block(heads * VD), block(heads * QK)],
        out_shape=[
            jax.ShapeDtypeStruct((count * rows, heads * VD), jnp.bfloat16),
            jax.ShapeDtypeStruct((count * rows, heads * QK), jnp.bfloat16),
        ],
        name="attend",
        cost_estimate=pl.CostEstimate(
            flops=2 * count * heads * rows * rows * (QK + VD),
            bytes_accessed=count * rows * heads * (QK * 6 + KV * 2 + VD * 2),
            transcendentals=count * heads * rows * rows,
        ),
    )(query_raw, latent, keyed, cosine, sine, seg_col, seg_row)


def attend_back_kernel(
    heads, q_ref, lat_ref, key_ref, grad_ref, cos_ref, sin_ref, col_ref, row_ref, dq_ref, dlat_ref, dkey_ref
):
    factor = QK**-0.5
    allowed = allowed_pairs(col_ref[...], row_ref[0])
    cosine, sine = cos_ref[...], sin_ref[...]
    shared = key_ref[:, LAT:]
    total = None
    for head in range(heads):
        query = q_ref[:, head * QK : (head + 1) * QK]
        key = jnp.concatenate([lat_ref[:, head * KV : head * KV + NOPE], shared], axis=1)
        value = lat_ref[:, head * KV + NOPE : (head + 1) * KV]
        grad = grad_ref[:, head * VD : (head + 1) * VD]
        scores = jnp.where(allowed, dot_t(query, key) * factor, masked_score)
        top = jnp.max(scores, axis=1, keepdims=True)
        powers = jnp.exp(scores - top)
        probs = powers / jnp.sum(powers, axis=1, keepdims=True)
        grad_value = t_dot(bf16(probs), grad)
        grad_probs = dot_t(grad, value)
        centre = jnp.sum(probs * grad_probs, axis=1, keepdims=True)
        grad_scores = bf16(probs * (grad_probs - centre) * factor)
        grad_query = dot(grad_scores, key)
        grad_key = t_dot(grad_scores, query)
        dq_ref[:, head * QK : (head + 1) * QK] = bf16(
            jnp.concatenate(
                [grad_query[:, :NOPE], rotate(grad_query[:, NOPE:], cosine, -sine)], axis=1
            )
        )
        dlat_ref[:, head * KV : head * KV + NOPE] = bf16(grad_key[:, :NOPE])
        dlat_ref[:, head * KV + NOPE : (head + 1) * KV] = bf16(grad_value)
        part = grad_key[:, NOPE:]
        total = part if total is None else total + part
    dkey_ref[...] = total


def attend_back(query, latent, keyed, grad, tables):
    cosine, sine, seg_col, seg_row = tables
    count, _, rows = seg_row.shape
    heads = query.shape[1] // QK
    block = lambda width: pl.BlockSpec((rows, width), lambda i: (i, 0))
    return pl.pallas_call(
        functools.partial(attend_back_kernel, heads),
        grid=(count,),
        in_specs=[
            block(heads * QK),
            block(heads * KV),
            block(LAT + ROPE),
            block(heads * VD),
            block(HALF),
            block(HALF),
            block(1),
            pl.BlockSpec((1, 1, rows), lambda i: (i, 0, 0)),
        ],
        out_specs=[block(heads * QK), block(heads * KV), block(ROPE)],
        out_shape=[
            jax.ShapeDtypeStruct((count * rows, heads * QK), jnp.bfloat16),
            jax.ShapeDtypeStruct((count * rows, heads * KV), jnp.bfloat16),
            jax.ShapeDtypeStruct((count * rows, ROPE), jnp.float32),
        ],
        name="attend_back",
        cost_estimate=pl.CostEstimate(
            flops=2 * count * heads * rows * rows * (3 * QK + 2 * VD),
            bytes_accessed=count * rows * heads * (QK * 4 + KV * 4 + VD * 2),
            transcendentals=count * heads * rows * rows,
        ),
    )(query, latent, keyed, grad, cosine, sine, seg_col, seg_row)


def split_in(flat):
    half = flat.shape[1] // 2
    return flat[:, :half], flat[:, half:]


def gated_hidden(pre):
    gate, up = split_in(pre)
    return silu_parts(gate)[0] * up


def gated_back(pre, grad_hidden):
    gate, up = split_in(pre)
    act, slope = silu_parts(gate)
    return bf16(jnp.concatenate([grad_hidden * up * slope, grad_hidden * act], axis=1))


def body(
    boundary,
    lengths,
    routes,
    attn_gain,
    query_weight,
    compress_weight,
    latent_gain,
    expand_weight,
    output_weight,
    ffn_gain,
    router_weight,
    shared_in,
    shared_out,
    expert_in,
    expert_out,
):
    attn_gain, latent_gain, ffn_gain = attn_gain[0], latent_gain[0], ffn_gain[0]
    query_weight, compress_weight = query_weight[0], compress_weight[0]
    expand_weight, output_weight = expand_weight[0], output_weight[0]
    router_weight, shared_out, expert_out = router_weight[0], shared_out[0], expert_out[0, 0]
    width = boundary.shape[3]
    rows = boundary.shape[2]
    shared_in_shape, expert_in_shape = shared_in.shape, expert_in.shape
    shared_in = shared_in.reshape(width, -1)
    expert_in = expert_in.reshape(width, -1)

    packs, members = lax.axis_size("dp"), lax.axis_size("expert")
    count = packs * members
    pack, member = lax.axis_index("dp"), lax.axis_index("expert")
    me = pack * members + member
    is_first = lax.axis_index("section") == 0
    pack_rows = members * rows
    top = routes.shape[3]
    experts = router_weight.shape[1]

    def own_pack(value, per_block=None):
        size = value.shape[0] // packs
        return lax.dynamic_slice_in_dim(value, pack * size, size, 0)

    own_lengths = lax.dynamic_index_in_dim(lengths[0, 0], member, 0, keepdims=True)
    whole = gather_all(jnp.concatenate([routes.reshape(1, rows * top), own_lengths], axis=1))
    routes_all = whole[:, : rows * top].reshape(count * rows, top)
    routed = jnp.any(routes_all == me, axis=1, keepdims=True).astype(jnp.float32)
    segment, position = block_layout(whole[:, rows * top :], rows)
    freqs = rope_base ** (-jnp.arange(HALF, dtype=jnp.float32) / HALF)
    angles = position.reshape(-1).astype(jnp.float32)[:, None] * freqs[None, :]
    tables_all = (
        jnp.cos(angles),
        jnp.sin(angles),
        segment.reshape(count * rows, 1),
        segment.reshape(count, 1, rows),
    )
    tables_pack = tuple(own_pack(table) for table in tables_all)
    own_cos, own_sin = (
        lax.dynamic_slice_in_dim(table, me * rows, rows, 0) for table in tables_all[:2]
    )
    own_column = (lax.broadcasted_iota(jnp.int32, (1, experts), 1) == me).astype(jnp.float32)

    def forward(hidden, keep):
        normed32, scale_attn = rms_forward(hidden, attn_gain)
        normed = bf16(normed32)
        compressed = dot(normed, compress_weight)
        latent32, scale_latent = rms_forward(compressed[:, :LAT], latent_gain)
        keyed = bf16(
            jnp.concatenate([latent32, rotate(compressed[:, LAT:], own_cos, own_sin)], axis=1)
        )
        if keep:
            normed_all, keyed_all = gather_all(normed), gather_all(keyed)
            normed_pack, keyed_pack = own_pack(normed_all), own_pack(keyed_all)
        else:
            normed_pack, keyed_pack = gather_pack(normed), gather_pack(keyed)
        query_raw = dot(normed_pack, query_weight)
        latent = bf16(dot(keyed_pack[:, :LAT], expand_weight))
        attended, query = attend(query_raw, latent, keyed_pack, tables_pack)
        mixed = hidden + scatter_pack(bf16(dot(attended, output_weight))).astype(jnp.float32)
        ffn32, scale_ffn = rms_forward(mixed, ffn_gain)
        ffn = bf16(ffn32)
        ffn_all = gather_all(ffn)
        prob_all = jax.nn.softmax(dot(ffn_all, router_weight), axis=-1)
        own_prob = jnp.sum(prob_all * own_column, axis=1, keepdims=True)
        gate = own_prob * routed
        expert_pre = dot(ffn_all, expert_in)
        expert_hid = gated_hidden(expert_pre)
        gated = bf16(gate * expert_hid)
        ffn_pack = own_pack(ffn_all)
        shared_pre = dot(ffn_pack, shared_in)
        shared_hid = bf16(gated_hidden(shared_pre))
        partial = dot(gated, expert_out)
        shared_part = dot(shared_hid, shared_out)
        partial = bf16(
            lax.dynamic_update_slice_in_dim(
                partial, own_pack(partial) + shared_part, pack * pack_rows, 0
            )
        )
        result = mixed + scatter_all(partial).astype(jnp.float32)
        if not keep:
            return result, None
        stored = dict(
            normed=normed,
            compressed=compressed,
            scale_attn=scale_attn,
            scale_latent=scale_latent,
            normed_all=normed_all,
            keyed_all=keyed_all,
            keyed_pack=keyed_pack,
            latent=latent,
            query=query,
            mixed=mixed,
            scale_ffn=scale_ffn,
            ffn_all=ffn_all,
            prob_all=prob_all,
            own_prob=own_prob,
            gate=gate,
            expert_pre=expert_pre,
            gated=gated,
            shared_pre=shared_pre,
        )
        return result, stored

    def backward(hidden, stored, upstream, weights):
        upstream_all = gather_all(bf16(upstream))
        grad_units = dot_t(upstream_all, expert_out)
        expert_pre = stored["expert_pre"]
        grad_pre = gated_back(expert_pre, stored["gate"] * grad_units)
        grad_gate = jnp.sum(grad_units * gated_hidden(expert_pre), axis=1, keepdims=True)
        moved = stored["own_prob"] * grad_gate * routed
        grad_logits = bf16(moved * (own_column - stored["prob_all"]))
        upstream_pack = own_pack(upstream_all)
        grad_shared = gated_back(stored["shared_pre"], dot_t(upstream_pack, shared_out))
        shared_part = dot_t(grad_shared, shared_in)
        partial = dot_t(grad_pre, expert_in) + dot_t(grad_logits, router_weight)
        partial = bf16(
            lax.dynamic_update_slice_in_dim(
                partial, own_pack(partial) + shared_part, pack * pack_rows, 0
            )
        )
        grad_ffn = scatter_all(partial).astype(jnp.float32)
        grad_mixed_norm, grad_ffn_gain = rms_backward(
            stored["mixed"], stored["scale_ffn"], ffn_gain, grad_ffn
        )
        grad_mixed = upstream + grad_mixed_norm
        if weights:
            grad_mixed_all = gather_all(bf16(grad_mixed))
            query_all_raw = dot(stored["normed_all"], query_weight)
            latent_all = bf16(dot(stored["keyed_all"][:, :LAT], expand_weight))
            attended_all, query_all = attend(
                query_all_raw, latent_all, stored["keyed_all"], tables_all
            )
            grad_attended = bf16(dot_t(grad_mixed_all, output_weight))
            grad_query_all, grad_latent_all, grad_shared_key = attend_back(
                query_all, latent_all, stored["keyed_all"], grad_attended, tables_all
            )
            grad_query, grad_latent_heads, grad_shared_key = (
                own_pack(value) for value in (grad_query_all, grad_latent_all, grad_shared_key)
            )
        else:
            grad_mixed_pack = gather_pack(bf16(grad_mixed))
            grad_attended = bf16(dot_t(grad_mixed_pack, output_weight))
            grad_query, grad_latent_heads, grad_shared_key = attend_back(
                stored["query"], stored["latent"], stored["keyed_pack"], grad_attended, tables_pack
            )
        own = scatter_pack(
            bf16(
                jnp.concatenate(
                    [
                        dot_t(grad_query, query_weight),
                        dot_t(grad_latent_heads, expand_weight),
                        grad_shared_key,
                    ],
                    axis=1,
                )
            )
        ).astype(jnp.float32)
        grad_latent, grad_latent_gain = rms_backward(
            stored["compressed"][:, :LAT],
            stored["scale_latent"],
            latent_gain,
            own[:, width : width + LAT],
        )
        grad_compressed = bf16(
            jnp.concatenate([grad_latent, rotate(own[:, width + LAT :], own_cos, -own_sin)], axis=1)
        )
        grad_normed = own[:, :width] + dot_t(grad_compressed, compress_weight)
        grad_hidden_norm, grad_attn_gain = rms_backward(
            hidden, stored["scale_attn"], attn_gain, grad_normed
        )
        grad_hidden = grad_mixed + grad_hidden_norm
        if not weights:
            return grad_hidden, None
        shared_pre = dot(stored["ffn_all"], shared_in)
        shared_hid = bf16(gated_hidden(shared_pre))
        grad_shared_all = gated_back(shared_pre, dot_t(upstream_all, shared_out))
        grads = dict(
            query=t_dot(stored["normed_all"], grad_query_all),
            expand=t_dot(stored["keyed_all"][:, :LAT], grad_latent_all),
            output=t_dot(attended_all, grad_mixed_all),
            shared_in=t_dot(stored["ffn_all"], grad_shared_all),
            shared_out=t_dot(shared_hid, upstream_all),
            expert_in=t_dot(stored["ffn_all"], grad_pre),
            expert_out=t_dot(stored["gated"], upstream_all),
            compress=t_dot(stored["normed_all"], gather_all(grad_compressed)),
        )
        small = jnp.concatenate([grad_attn_gain, grad_latent_gain, grad_ffn_gain])
        small = jnp.sum(gather_all(small[None]), axis=0)
        router = lax.psum(t_dot(stored["ffn_all"], grad_logits), BOTH)
        grads["attn_gain"] = small[:width]
        grads["latent_gain"] = small[width : width + LAT]
        grads["ffn_gain"] = small[width + LAT :]
        grads["router"] = router
        return grad_hidden, grads

    fresh = boundary[0, 0].astype(jnp.float32)
    first_result, _ = forward(fresh, False)
    inbound = lax.ppermute(bf16(first_result), "section", [(0, 1)])
    hidden = jnp.where(is_first, fresh, inbound.astype(jnp.float32))
    result, stored = forward(hidden, True)
    grad_first, _ = backward(hidden, stored, fresh, False)
    downbound = lax.ppermute(grad_first, "section", [(1, 0)])
    upstream = jnp.where(is_first, downbound, fresh)
    grad_hidden, grads = backward(hidden, stored, upstream, True)
    ends = jnp.where(is_first, grad_hidden, result)
    return (
        ends[None, None],
        grads["attn_gain"][None],
        grads["query"][None],
        grads["compress"][None],
        grads["latent_gain"][None],
        grads["expand"][None],
        grads["output"][None],
        grads["ffn_gain"][None],
        grads["router"][None],
        grads["shared_in"].reshape(shared_in_shape),
        grads["shared_out"][None],
        grads["expert_in"].reshape(expert_in_shape),
        grads["expert_out"][None, None],
    )


def solution(mesh):
    return jax.shard_map(
        body,
        mesh=mesh,
        in_specs=(
            P("section", None, BOTH, None),
            P(None, "dp", None, None),
            P("section", None, BOTH, None),
            P("section", None),
            P("section", None, "expert"),
            P("section", None, None),
            P("section", None),
            P("section", None, "expert"),
            P("section", "expert", None),
            P("section", None),
            P("section", None, None),
            P("section", None, None, "expert"),
            P("section", "expert", None),
            P("section", BOTH, None, None, None),
            P("section", BOTH, None, None),
        ),
        out_specs=(
            P("section", None, BOTH, None),
            P("section", None),
            P("section", None, "expert"),
            P("section", None, None),
            P("section", None),
            P("section", None, "expert"),
            P("section", "expert", None),
            P("section", None),
            P("section", None, None),
            P("section", None, None, "expert"),
            P("section", "expert", None),
            P("section", BOTH, None, None, None),
            P("section", BOTH, None, None),
        ),
        check_vma=False,
    )
```

time: 2650 us -> 1650 us (0.62)
  waiting for transfers between devices: 1640 us -> 932 us
  local copies, waits for them, and re-layouts: 251 us -> 41.9 us
  blocking collectives: 178 us -> 52.5 us
  Pallas kernels: 0 us -> 94.4 us
  starting transfers between devices: 101 us -> 16.1 us
  matrix products: 330 us -> 410 us
  other arithmetic: 115 us -> 71.2 us
    psum x2 -> x1, waiting for transfers between devices: 999 us -> 56.8 us  [backward(): router = lax.psum(t_dot(stored['ffn_all'], grad_logits), BOTH)]
    all_to_all x7 -> x0, waiting for transfers between devices: 323 us -> none  [trade_slots(): lax.all_to_all(slot_rows, ('dp', 'expert'), split_axis=0, concat_axis=0,...]
    reduce_scatter x10 -> x8, waiting for transfers between devices: 120 us -> 414 us  [the longest x4 304 us: scatter_all(): return lax.psum_scatter(partial_rows, BOTH, scatter_dimension=0, tiled=True)]
    all_gather x8 -> x10, waiting for transfers between devices: 165 us -> 426 us  [the longest x8 403 us: gather_all(): return lax.all_gather(rows, BOTH, axis=0, tiled=True)]
    all_to_all x1 -> x0, blocking collectives: 98 us -> none  [trade_slots(): lax.all_to_all(slot_rows, ('dp', 'expert'), split_axis=0, concat_axis=0,...]
    pallas_call x0 -> x5, Pallas kernels: none -> 94.4 us  [the longest x2 50.7 us: attend_back(): pl.pallas_call(functools.partial(attend_back_kernel, heads), grid=(count,...]
    all_to_all x7 -> x0, starting transfers between devices: 93.2 us -> none  [trade_slots(): lax.all_to_all(slot_rows, ('dp', 'expert'), split_axis=0, concat_axis=0,...]
    gather x10 -> x0, local copies, waits for them, and re-layouts: 88.8 us -> none  [the longest x2 20.2 us: layer_backward(): upstream[source // TOP]]
  transfers between devices with their start and end apart: 29 -> 21, of which waited for: 20 -> 18; matrix products, arithmetic and copies ran while one was open for 18% -> 15% of each run, Pallas kernels for 0% -> 2%
where the time goes in v1:
time: 1650 us; the launch traced here: 1630 us
  waiting for transfers between devices  932 us (56%)
  matrix products  410 us (25%)
  Pallas kernels  94.4 us (6%)
  other arithmetic  71.2 us (4%)
  blocking collectives  52.5 us (3%)
  local copies, waits for them, and re-layouts  41.9 us (3%)
    all_gather x8, waiting for transfers between devices, gather_all(): return lax.all_gather(rows, BOTH, axis=0, tiled=True)  403 us
    reduce_scatter x4, waiting for transfers between devices, scatter_all(): return lax.psum_scatter(partial_rows, BOTH, scatter_dimension=0, tiled=True)  304 us
    dot_general x19, matrix products, dot_t(): lax.dot_general(left, right, (((1,), (1,)), ((), ())), preferred_element_...  162 us
    dot_general x21, matrix products, dot(): return jnp.dot(left, right, preferred_element_type=jnp.float32)  150 us
    reduce_scatter x4, waiting for transfers between devices, scatter_pack(): lax.psum_scatter(partial_rows, 'expert', scatter_dimension=0, tiled=True)  110 us
    dot_general x9, matrix products, t_dot(): lax.dot_general(left, right, (((0,), (0,)), ((), ())), preferred_element_...  97.4 us
    psum x1, waiting for transfers between devices, backward(): router = lax.psum(t_dot(stored['ffn_all'], grad_logits), BOTH)  56.8 us
    pallas_call x2, Pallas kernels, attend_back(): pl.pallas_call(functools.partial(attend_back_kernel, heads), grid=(count,...  50.7 us
  transfers between devices with their start and end apart: 21, of which 18 were waited for; matrix products, arithmetic and copies ran while one was open for 15% of the time, Pallas kernels for 2%

profile of v1, /device:TPU:3, one launch (start us, length us, event | category | flops | bytes accessed | tf_op | source)
XLA Modules:
  0.0 1633.8 jit_solution(3382822696078005431)
XLA Ops:
  12.6 22.5 %all-gather.2 = s32[16,1,771]{2,1,0:T(1,128)S(1)} all-gather(s32[1,1,771]{2,1,0:T(1,128)S(1)} %add_bitcast_fusion), channel_id=1, replica_groups=mesh['section'=2,'dp'=4,'expert'=4] {'dp','expert'}, dimensions={0}, use_global_device_ids=true | all-gather | bytes 52428 | tf_op jit(solution)/shard_map/all_gather | solution.py:45
  75.8 27.8 %reduce-scatter.9.cloned.1.call-done = bf16[128,2048]{1,0:T(8,128)(2,1)} async-done(((bf16[512,2048]{1,0:T(8,128)(2,1)}), bf16[128,2048]{1,0:T(8,128)(2,1)}) %reduce-scatter.9.cloned.1.call-update) | async-done | bytes 524304 | tf_op jit(solution)/shard_map/reduce_scatter | solution.py:57
  127.2 55.1 %all-gather.17.cloned.1.call-done = bf16[2048,2048]{1,0:T(8,128)(2,1)} async-done(((bf16[128,2048]{1,0:T(8,128)(2,1)}), bf16[2048,2048]{1,0:T(8,128)(2,1)}) %all-gather.17.cloned.1.call-update) | async-done | bytes 8388624 | tf_op jit(solution)/shard_map/all_gather | solution.py:45
  229.1 101.3 %reduce-scatter.11.cloned.1.call-done = bf16[128,2048]{1,0:T(8,128)(2,1)} async-done(((bf16[2048,2048]{1,0:T(8,128)(2,1)}), bf16[128,2048]{1,0:T(8,128)(2,1)}) %reduce-scatter.11.cloned.1.call-update) | async-done | bytes 524304 | tf_op jit(solution)/shard_map/reduce_scatter | solution.py:53
  357.7 44.5 %all-gather.21.cloned.1.call-done.key_ref = bf16[2048,576]{1,0:T(8,128)(2,1)} async-done(((bf16[128,576]{1,0:T(8,128)(2,1)}), bf16[2048,576]{1,0:T(8,128)(2,1)}) %all-gather.21.cloned.1.call-update) | async-done | bytes 2359312 | tf_op jit(solution)/shard_map/all_gather | solution.py:45
  407.3 70.7 %all-gather.19.cloned.1.call-done = bf16[2048,2048]{1,0:T(8,128)(2,1)} async-done(((bf16[128,2048]{1,0:T(8,128)(2,1)}), bf16[2048,2048]{1,0:T(8,128)(2,1)}) %all-gather.19.cloned.1.call-update) | async-done | bytes 8388624 | tf_op jit(solution)/shard_map/all_gather | solution.py:45
  496.1 29.3 %reduce-scatter.13.cloned.1.call-done = bf16[128,2048]{1,0:T(8,128)(2,1)} async-done(((bf16[512,2048]{1,0:T(8,128)(2,1)}), bf16[128,2048]{1,0:T(8,128)(2,1)}) %reduce-scatter.13.cloned.1.call-update) | async-done | bytes 524304 | tf_op jit(solution)/shard_map/reduce_scatter | solution.py:57
  530.3 74.3 %all-gather.23.cloned.1.call-done = bf16[2048,2048]{1,0:T(8,128)(2,1)} async-done(((bf16[128,2048]{1,0:T(8,128)(2,1)}), bf16[2048,2048]{1,0:T(8,128)(2,1)}) %all-gather.23.cloned.1.call-update) | async-done | bytes 8388624 | tf_op jit(solution)/shard_map/all_gather | solution.py:45
  627.9 51.7 %all-gather.33.cloned.1.call-done = bf16[1,1,2048,2048]{3,2,1,0:T(8,128)(2,1)} async-done(((bf16[1,1,128,2048]{3,2,1,0:T(8,128)(2,1)}), bf16[1,1,2048,2048]{3,2,1,0:T(8,128)(2,1)}) %all-gather.33.cloned.1.call-update) | async-done | bytes 8388624 | tf_op jit(solution)/shard_map/all_gather | solution.py:45
  694.2 19.5 %fusion.4 = f32[2048,2048]{1,0:T(8,128)} fusion(bf16[2048,1536]{1,0:T(8,128)(2,1)} %bitcast.263, bf16[2048,768]{1,0:T(8,128)(2,1)S(1)} %get-tuple-element.126, bf16[2048,768]{1,0:T(8,128)(2,1)S(1)} %get-tuple-element.125), kind=kOutput, calls=%fused_computation.7 | convolution fusion | flops 12897484800 | bytes 29360128 | tf_op jit(solution)/shard_map/dot_general | solution.py:29
  743.7 101.3 %reduce-scatter.15.cloned.1.call-done = bf16[128,2048]{1,0:T(8,128)(2,1)} async-done(((bf16[2048,2048]{1,0:T(8,128)(2,1)}), bf16[128,2048]{1,0:T(8,128)(2,1)}) %reduce-scatter.15.cloned.1.call-update) | async-done | bytes 524304 | tf_op jit(solution)/shard_map/reduce_scatter | solution.py:53
  850.1 23.1 %all-gather.25.cloned.1.call-done = bf16[512,2048]{1,0:T(8,128)(2,1)} async-done(((bf16[128,2048]{1,0:T(8,128)(2,1)}), bf16[512,2048]{1,0:T(8,128)(2,1)}) %all-gather.25.cloned.1.call-update) | async-done | bytes 2097168 | tf_op jit(solution)/shard_map/all_gather | solution.py:49
  897.8 34.9 %reduce-scatter.17.cloned.1.call-done = bf16[128,2624]{1,0:T(8,128)(2,1)} async-done(((bf16[512,2624]{1,0:T(8,128)(2,1)}), bf16[128,2624]{1,0:T(8,128)(2,1)}) %reduce-scatter.17.cloned.1.call-update) | async-done | bytes 671760 | tf_op jit(solution)/shard_map/reduce_scatter | solution.py:57
  943.0 21.6 %collective-permute-done.1 = f32[128,2048]{1,0:T(8,128)S(1)} collective-permute-done((f32[128,2048]{1,0:T(8,128)S(1)}, f32[128,2048]{1,0:T(8,128)S(1)}, u32[]{:S(2)}, u32[]{:S(2)}) %collective-permute-start.1) | collective-permute-done | bytes 1048608 | tf_op jit(solution)/shard_map/ppermute | solution.py:458
  966.5 76.9 %all-gather.27.cloned.1.call-done = bf16[2048,2048]{1,0:T(8,128)(2,1)} async-done(((bf16[128,2048]{1,0:T(8,128)(2,1)}), bf16[2048,2048]{1,0:T(8,128)(2,1)}) %all-gather.27.cloned.1.call-update) | async-done | bytes 8388624 | tf_op jit(solution)/shard_map/all_gather | solution.py:45
  1043.4 21.0 %multiply_convert_fusion.2 = (bf16[2048,768]{1,0:T(8,128)(2,1)}, bf16[2048,768]{1,0:T(8,128)(2,1)}, f32[2048]{0:T(1024)S(1)}) fusion(f32[2048,1536]{1,0:T(8,128)} %fusion.167, f32[2048]{0:T(1024)S(1)} %copy-done.59, f32[2048,768]{1,0:T(8,128)} %get-tuple-element.128, bf16[2048,2048]{1,0:T(8,128)(2,1)} %all-gather.27.cloned.1.call-done, ...), kind=kOutput, calls=%fused_computation.15 | convolution fusion | flops 6467614720 | bytes 36716544 | tf_op jit(solution)/shard_map/dot_general | solution.py:29
  1064.4 19.7 %fusion.15 = f32[2048,2048]{1,0:T(8,128)} fusion(bf16[2048,1536]{1,0:T(8,128)(2,1)} %bitcast.264, bf16[2048,768]{1,0:T(8,128)(2,1)} %get-tuple-element.124, bf16[2048,768]{1,0:T(8,128)(2,1)} %get-tuple-element.123), kind=kOutput, calls=%fused_computation.37 | convolution fusion | flops 12897484800 | bytes 29360128 | tf_op jit(solution)/shard_map/dot_general | solution.py:29
  1108.0 101.3 %reduce-scatter.19.cloned.1.call-done = bf16[128,2048]{1,0:T(8,128)(2,1)} async-done(((bf16[2048,2048]{1,0:T(8,128)(2,1)}), bf16[128,2048]{1,0:T(8,128)(2,1)}) %reduce-scatter.19.cloned.1.call-update) | async-done | bytes 524304 | tf_op jit(solution)/shard_map/reduce_scatter | solution.py:53
  1232.8 27.3 %attend.5 = (bf16[2048,512]{1,0:T(8,128)(2,1)}, bf16[2048,768]{1,0:T(8,128)(2,1)}) custom-call(f32[2048,768]{1,0:T(8,128)} %fusion.26.q_ref, bf16[2048,1024]{1,0:T(8,128)(2,1)} %convolution_convert_fusion.lat_ref, bf16[2048,576]{1,0:T(8,128)(2,1)} %all-gather.21.cloned.1.call-done.key_ref, f32[2048,32]{1,0:T(8,128)} %copy-done.9, f32[2048,32]{1,0:T(8,128)} %copy-done.10, ...), custom_call_target="tpu_custom_call" | custom-call | flops 671088640 | bytes 15728640 | tf_op jit(solution)/shard_map/attend/pallas_call | solution.py:130
  1260.1 29.7 %all-gather.29.cloned.1.call-done = bf16[2048,2048]{1,0:T(8,128)(2,1)} async-done(((bf16[128,2048]{1,0:T(8,128)(2,1)}), bf16[2048,2048]{1,0:T(8,128)(2,1)}) %all-gather.29.cloned.1.call-update) | async-done | bytes 8388624 | tf_op jit(solution)/shard_map/all_gather | solution.py:45
  1299.7 39.5 %attend_back.3 = (bf16[2048,768]{1,0:T(8,128)(2,1)}, bf16[2048,1024]{1,0:T(8,128)(2,1)}, f32[2048,64]{1,0:T(8,128)}) custom-call(bf16[2048,768]{1,0:T(8,128)(2,1)} %get-tuple-element.30.q_ref, bf16[2048,1024]{1,0:T(8,128)(2,1)} %convolution_convert_fusion.lat_ref, bf16[2048,576]{1,0:T(8,128)(2,1)} %all-gather.21.cloned.1.call-done.key_ref, ...), custom_call_target="tpu_custom_call" | custom-call | flops 1744830464 | bytes 16777216 | tf_op jit(solution)/shard_map/attend_back/pallas_call | solution.py:196
  1422.1 19.3 %copy.164 = f32[1,1,2048,2,768]{4,3,2,1,0:T(2,128)} copy(f32[1,1,2048,2,768]{2,4,3,1,0:T(8,128)} %bitcast.259) | data formatting | bytes 25165824
  1531.5 22.0 %all-gather.3 = f32[16,1,4608]{2,1,0:T(1,128)S(1)} all-gather(f32[1,1,4608]{2,1,0:T(1,128)S(1)} %reshape.234), channel_id=3, replica_groups=mesh['section'=2,'dp'=4,'expert'=4] {'dp','expert'}, dimensions={0}, use_global_device_ids=true | all-gather | bytes 313344 | tf_op jit(solution)/shard_map/all_gather | solution.py:45
  1568.8 56.8 %all-reduce.2.cloned.1.call-done = f32[1,2048,16]{1,2,0:T(8,128)} async-done(((f32[1,2048,16]{1,2,0:T(8,128)}), f32[1,2048,16]{1,2,0:T(8,128)}) %all-reduce.2.cloned.1.call-update) | async-done | bytes 131088 | tf_op jit(solution)/shard_map/psum | solution.py:445
  (359 shorter events, 527.3 us)
Async XLA Ops:
  7.2 50.5 %all-gather.15.cloned.1.call-start = ((), (), s32[]{:S(2)}) async-start(), calls=%async_computation.8 | async-start | bytes 2621440 | tf_op jit(solution)/shard_map/all_gather | solution.py:49
  10.7 92.9 %reduce-scatter.9.cloned.1.call-start = ((), (), s32[]{:S(2)}) async-start(), calls=%async_computation.9 | async-start | bytes 2621440 | tf_op jit(solution)/shard_map/reduce_scatter | solution.py:57
  75.8 106.6 %all-gather.17.cloned.1.call-start = ((), (), s32[]{:S(2)}) async-start(), calls=%async_computation.10 | async-start | bytes 8912896 | tf_op jit(solution)/shard_map/all_gather | solution.py:45
  107.3 223.1 %reduce-scatter.11.cloned.1.call-start = ((), (), s32[]{:S(2)}) async-start(), calls=%async_computation.11 | async-start | bytes 8912896 | tf_op jit(solution)/shard_map/reduce_scatter | solution.py:53
  127.2 567.0 %copy-start.40 = (pred[2048]{0:T(1024)(128)(4,1)}, pred[2048]{0:T(1024)(128)(4,1)S(1)}, u32[]{:S(2)}) copy-start(pred[2048]{0:T(1024)(128)(4,1)S(1)} %reduce_or.9) | copy-start | bytes 6148
  127.2 586.5 %copy-start.43 = (f32[16]{0:T(128)}, f32[16]{0:T(128)S(1)}, u32[]{:S(2)}) copy-start(f32[16]{0:T(128)S(1)} %compare_convert_fusion) | copy-start | bytes 196
  229.1 173.1 %all-gather.21.cloned.1.call-start = ((), (), s32[]{:S(2)}) async-start(), calls=%async_computation.13 | async-start | bytes 2785280 | tf_op jit(solution)/shard_map/all_gather | solution.py:45
  332.8 14.6 collective-permute-start
  357.1 120.9 %all-gather.19.cloned.1.call-start = ((), (), s32[]{:S(2)}) async-start(), calls=%async_computation.12 | async-start | bytes 8912896 | tf_op jit(solution)/shard_map/all_gather | solution.py:45
  357.7 167.7 %reduce-scatter.13.cloned.1.call-start = ((), (), s32[]{:S(2)}) async-start(), calls=%async_computation.14 | async-start | bytes 2621440 | tf_op jit(solution)/shard_map/reduce_scatter | solution.py:57
  496.0 108.5 %all-gather.23.cloned.1.call-start = ((), (), s32[]{:S(2)}) async-start(), calls=%async_computation.15 | async-start | bytes 8912896 | tf_op jit(solution)/shard_map/all_gather | solution.py:45
  529.5 150.1 %all-gather.33.cloned.1.call-start = ((), (), s32[]{:S(2)}) async-start(), calls=%async_computation.26 | async-start | bytes 8912896 | tf_op jit(solution)/shard_map/all_gather | solution.py:45
  530.3 314.8 %reduce-scatter.15.cloned.1.call-start = ((), (), s32[]{:S(2)}) async-start(), calls=%async_computation.16 | async-start | bytes 8912896 | tf_op jit(solution)/shard_map/reduce_scatter | solution.py:53
  610.4 473.7 %copy-start.26 = (f32[2048]{0:T(1024)}, f32[2048]{0:T(1024)S(1)}, u32[]{:S(2)}) copy-start(f32[2048]{0:T(1024)S(1)} %get-tuple-element.156) | copy-start | bytes 24580
  743.7 129.5 %all-gather.25.cloned.1.call-start = ((), (), s32[]{:S(2)}) async-start(), calls=%async_computation.17 | async-start | bytes 2621440 | tf_op jit(solution)/shard_map/all_gather | solution.py:49
  850.0 82.6 %reduce-scatter.17.cloned.1.call-start = ((), (), s32[]{:S(2)}) async-start(), calls=%async_computation.18 | async-start | bytes 3440640 | tf_op jit(solution)/shard_map/reduce_scatter | solution.py:57
  897.7 145.6 %all-gather.27.cloned.1.call-start = ((), (), s32[]{:S(2)}) async-start(), calls=%async_computation.19 | async-start | bytes 8912896 | tf_op jit(solution)/shard_map/all_gather | solution.py:45
  940.7 23.8 %collective-permute-start.1 = (f32[128,2048]{1,0:T(8,128)S(1)}, f32[128,2048]{1,0:T(8,128)S(1)}, u32[]{:S(2)}, u32[]{:S(2)}) collective-permute-start(f32[128,2048]{1,0:T(8,128)S(1)} %subtract_add_fusion), channel_id=1, source_target_pairs={{16,0},{17,1},{18,2},{19,3},{20,4},{21,5},{22,6},{23,7},{24,8},{25... | collective-permute-start | bytes 3145736 | tf_op jit(solution)/shard_map/ppermute | solution.py:458
  966.5 242.9 %reduce-scatter.19.cloned.1.call-start = ((), (), s32[]{:S(2)}) async-start(), calls=%async_computation.20 | async-start | bytes 8912896 | tf_op jit(solution)/shard_map/reduce_scatter | solution.py:53
  1108.0 181.8 %all-gather.29.cloned.1.call-start = ((), (), s32[]{:S(2)}) async-start(), calls=%async_computation.21 | async-start | bytes 8912896 | tf_op jit(solution)/shard_map/all_gather | solution.py:45
  1214.9 166.7 %reduce-scatter.21.cloned.1.call-start = ((), (), s32[]{:S(2)}) async-start(), calls=%async_computation.22 | async-start | bytes 3440640 | tf_op jit(solution)/shard_map/reduce_scatter | solution.py:57
  1348.2 206.7 %reduce-scatter.23.cloned.1.call-start = ((), (), s32[]{:S(2)}) async-start(), calls=%async_computation.23 | async-start | bytes 8912896 | tf_op jit(solution)/shard_map/reduce_scatter | solution.py:53
  1363.8 195.2 %all-gather.31.cloned.1.call-start = ((), (), s32[]{:S(2)}) async-start(), calls=%async_computation.24 | async-start | bytes 2785280 | tf_op jit(solution)/shard_map/all_gather | solution.py:45
  1385.6 239.9 %all-reduce.2.cloned.1.call-start = ((), (), s32[]{:S(2)}) async-start(), calls=%async_computation.25 | async-start | bytes 262144 | tf_op jit(solution)/shard_map/psum | solution.py:445
  (83 other events, 2867.4 us)
Sparse Core Ops, SparseCore 0:
  10.8 24.4 all-gather.14
  75.9 27.6 reduce-scatter.8
  107.4 74.8 all-gather.16
  229.2 101.1 reduce-scatter.10
  357.2 44.9 all-gather.20
  404.8 73.1 all-gather.18
  496.1 29.1 reduce-scatter.12
  529.6 74.8 all-gather.22
  606.7 72.8 all-gather.32
  743.8 101.2 reduce-scatter.14
  850.1 22.9 all-gather.24
  897.9 34.7 reduce-scatter.16
  966.6 76.7 all-gather.26
  1108.1 101.1 reduce-scatter.18
  1215.1 74.7 all-gather.28
  1348.3 33.3 reduce-scatter.20
  1385.6 103.2 reduce-scatter.22
  1491.0 43.4 all-gather.30
  1538.5 86.9 all-reduce.1

commit v2 on v1

v2 whole, which is shorter than its diff:
```python
import functools

import jax
import jax.numpy as jnp
from jax import lax
from jax.experimental import pallas as pl
from jax.experimental.pallas import tpu as pltpu
from jax.sharding import PartitionSpec as P

NOPE = 128
ROPE = 64
VD = 128
LAT = 512

QK = NOPE + ROPE
KV = NOPE + VD
HALF = ROPE // 2
epsilon = 1e-06
rope_base = 10000.0
masked_score = -1e30
BOTH = ("dp", "expert")
MESH = pl.DeviceIdType.MESH
IDS = {
    name: index
    for index, name in enumerate(
        (
            "gather_target",
            "gather_inputs_first",
            "gather_ffn_first",
            "gather_inputs_second",
            "gather_ffn_second",
            "gather_mixed",
            "gather_upstream",
            "gather_keyed_first",
            "gather_keyed_second",
            "scatter_attended_first",
            "scatter_ffn_first",
            "scatter_attended_second",
            "scatter_result",
            "scatter_ffn_back_second",
            "scatter_heads_second",
            "scatter_ffn_back_first",
        )
    )
}


def dot(left, right):
    return jnp.dot(left, right, preferred_element_type=jnp.float32)


def dot_t(left, right):
    return lax.dot_general(
        left, right, (((1,), (1,)), ((), ())), preferred_element_type=jnp.float32
    )


def t_dot(left, right):
    return lax.dot_general(
        left, right, (((0,), (0,)), ((), ())), preferred_element_type=jnp.float32
    )


def bf16(value):
    return value.astype(jnp.bfloat16)


def rms_forward(inputs, gain_vec):
    norm_scale = lax.rsqrt(jnp.mean(inputs * inputs, axis=-1, keepdims=True) + epsilon)
    return (inputs * norm_scale * gain_vec, norm_scale)


def rms_backward(inputs, norm_scale, gain_vec, upstream):
    weighted = upstream * gain_vec
    grad_gain = jnp.sum(upstream * inputs * norm_scale, axis=0)
    cubed = norm_scale * norm_scale * norm_scale
    grad_inputs = norm_scale * weighted - inputs * cubed * jnp.mean(
        weighted * inputs, axis=-1, keepdims=True
    )
    return (grad_inputs, grad_gain)


def rotate(inputs, cosine, sine):
    half = cosine.shape[-1]
    former = inputs[..., :half]
    latter = inputs[..., half:]
    return jnp.concatenate(
        [former * cosine - latter * sine, latter * cosine + former * sine], axis=-1
    )


def silu_parts(pre_gate):
    sigmoid = jax.nn.sigmoid(pre_gate)
    return (pre_gate * sigmoid, sigmoid * (1.0 + pre_gate * (1.0 - sigmoid)))


def block_layout(block_lengths, rows):
    starts = jnp.cumsum(block_lengths, axis=1) - block_lengths
    index = jnp.arange(rows, dtype=jnp.int32)
    begun = index[None, :, None] >= starts[:, None, :]
    segment = jnp.sum(begun.astype(jnp.int32), axis=2)
    opening = jnp.max(jnp.where(begun, starts[:, None, :], 0), axis=2)
    return segment, index[None, :] - opening


def places(spots):
    member = lax.axis_index("expert")
    spot = lax.axis_index("dp") if spots > 1 else 0
    return spot, member // 2, lax.rem(member, 2)


def to_partner(chip, core):
    return {"expert": chip * 2 + 1 - core}


def to_other(chip, core):
    return {"expert": (1 - chip) * 2 + core}


def when(condition, action):
    if condition is True:
        action()
    else:
        pl.when(condition)(action)


def greet(spots, spot, chip, core):
    barrier = pltpu.get_barrier_semaphore()

    def signal(target):
        pl.semaphore_signal(barrier, inc=1, device_id=target, device_id_type=MESH)

    signal(to_partner(chip, core))
    signal(to_other(chip, core))
    if spots > 1:
        pl.when(spot > 0)(lambda: signal({"dp": spot - 1}))
        pl.when(spot < spots - 1)(lambda: signal({"dp": spot + 1}))
        ends = jnp.where(spot > 0, 1, 0) + jnp.where(spot < spots - 1, 1, 0)
        pl.semaphore_wait(barrier, 2 + ends)
    else:
        pl.semaphore_wait(barrier, 2)


def remote(source, target_ref, target, out_sem, in_sem):
    return pltpu.make_async_remote_copy(
        src_ref=source,
        dst_ref=target_ref,
        send_sem=out_sem,
        recv_sem=in_sem,
        device_id=target,
        device_id_type=MESH,
    )


def slot(spot, chip, core):
    return spot * 4 + chip * 2 + core


def gather_kernel(spots, cuts, active, *refs):
    arrays = len(cuts)
    x_refs, o_refs, sems = refs[:arrays], refs[-9 - arrays : -9], refs[-9:]
    own_sem, up_out, up_in, down_out, down_in, over_out, over_in, pair_out, pair_in = sems
    units = [
        (a, pl.ds(part * (x_refs[a].shape[0] // parts), x_refs[a].shape[0] // parts))
        for a, parts in enumerate(cuts)
        for part in range(parts)
    ]

    def run():
        spot, chip, core = places(spots)
        greet(spots, spot, chip, core)

        def piece(unit, index):
            array, cut = units[unit]
            return o_refs[array].at[index, cut]

        def first(unit):
            array, cut = units[unit]
            return x_refs[array].at[cut]

        def up(source, at, unit, reach):
            return remote(
                source, piece(unit, slot(at, chip, core)), {"dp": spot + 1}, up_out.at[reach, unit], up_in.at[reach, unit]
            )

        def down(source, at, unit, reach):
            return remote(
                source,
                piece(unit, slot(at, chip, core)),
                {"dp": spot - 1},
                down_out.at[reach, unit],
                down_in.at[reach, unit],
            )

        def over(source, at, unit):
            return remote(
                source, piece(unit, slot(at, chip, core)), to_other(chip, core), over_out.at[at, unit], over_in.at[at, unit]
            )

        def pair(source, at, c, unit):
            return remote(
                source,
                piece(unit, slot(at, c, core)),
                to_partner(chip, core),
                pair_out.at[c, at, unit],
                pair_in.at[c, at, unit],
            )

        mine = slot(spot, chip, core)
        for unit in range(len(units)):
            source = first(unit)
            over(source, spot, unit).start()
            if spots > 1:
                pl.when(spot < spots - 1)(lambda: up(source, spot, unit, 0).start())
                pl.when(spot > 0)(lambda: down(source, spot, unit, 0).start())
            pair(source, spot, chip, unit).start()
        own = [pltpu.make_async_copy(x_refs[a], o_refs[a].at[mine], own_sem.at[a]) for a in range(arrays)]
        for copy in own:
            copy.start()
        for reach in range(1, spots):
            for unit in range(len(units)):

                def below(reach=reach, unit=unit):
                    at = spot - reach
                    source = piece(unit, slot(at, chip, core))
                    up(source, at, unit, reach - 1).wait_recv()
                    pl.when(spot < spots - 1)(lambda: up(source, at, unit, reach).start())
                    over(source, at, unit).start()
                    pair(source, at, chip, unit).start()

                def above(reach=reach, unit=unit):
                    at = spot + reach
                    source = piece(unit, slot(at, chip, core))
                    down(source, at, unit, reach - 1).wait_recv()
                    pl.when(spot > 0)(lambda: down(source, at, unit, reach).start())
                    over(source, at, unit).start()
                    pair(source, at, chip, unit).start()

                pl.when(spot >= reach)(below)
                pl.when(spot + reach < spots)(above)
        for reach in range(spots):
            sides = [(True, spot)]
            if reach > 0:
                sides = [(spot >= reach, spot - reach), (spot + reach < spots, spot + reach)]
            for unit in range(len(units)):
                for there, at in sides:

                    def hand_on(at=at, unit=unit):
                        source = piece(unit, slot(at, 1 - chip, core))
                        over(source, at, unit).wait_recv()
                        pair(source, at, 1 - chip, unit).start()

                    when(there, hand_on)
        for copy in own:
            copy.wait()
        for unit in range(len(units)):
            source = piece(unit, mine)
            for at in range(spots):
                over(source, at, unit).wait_send()
                for c in range(2):
                    pair(source, at, c, unit).wait()
            for reach in range(spots - 1):
                pl.when((spot >= reach) & (spot < spots - 1))(lambda: up(source, spot, unit, reach).wait_send())
                pl.when((spot + reach < spots) & (spot > 0))(lambda: down(source, spot, unit, reach).wait_send())

    if active is None:
        run()
    else:
        pl.when(lax.axis_index("section") == active)(run)


def gather_blocks(values, across, name, active=None, into=None, parts=4):
    axes = BOTH if across else "expert"
    if lax.axis_size("expert") != 4:
        found = [lax.all_gather(value, axes, axis=0, tiled=True) for value in values]
        if into is None:
            return found
        chosen = lax.axis_index("section") == active
        return [jnp.where(chosen, new, old) for new, old in zip(found, into)]
    spots = lax.axis_size("dp") if across else 1
    cuts = [parts if value.shape[0] % (16 * parts) == 0 else 1 for value in values]
    units = sum(cuts)
    dma = pltpu.SemaphoreType.DMA
    hops = max(spots - 1, 1)
    shapes = [jax.ShapeDtypeStruct((spots * 4, *value.shape), value.dtype) for value in values]
    held = [] if into is None else [old.reshape(shape.shape) for old, shape in zip(into, shapes)]
    outs = pl.pallas_call(
        functools.partial(gather_kernel, spots, cuts, active),
        out_shape=shapes,
        in_specs=[pl.BlockSpec(memory_space=pltpu.VMEM)] * len(values)
        + [pl.BlockSpec(memory_space=pl.ANY)] * len(held),
        out_specs=[pl.BlockSpec(memory_space=pl.ANY)] * len(values),
        input_output_aliases={len(values) + index: index for index in range(len(held))},
        scratch_shapes=[
            dma((len(values),)),
            dma((hops, units)),
            dma((hops, units)),
            dma((hops, units)),
            dma((hops, units)),
            dma((spots, units)),
            dma((spots, units)),
            dma((2, spots, units)),
            dma((2, spots, units)),
        ],
        compiler_params=pltpu.CompilerParams(collective_id=IDS[name], has_side_effects=True),
        name=name,
    )(*values, *held)
    return [out.reshape(-1, out.shape[2]) for out in outs]


def add_into(target, sources, rows, step=16):
    def some(index, carry):
        at = pl.ds(pl.multiple_of(index * step, step), step)
        total = sources[0][at, :].astype(jnp.float32)
        for source in sources[1:]:
            total = total + source[at, :].astype(jnp.float32)
        target[at, :] = total.astype(target.dtype)
        return carry

    lax.fori_loop(0, rows // step, some, 0)


def scatter_kernel(
    spots,
    parts,
    active,
    x_ref,
    o_ref,
    pair_buf,
    over_src,
    over_buf,
    line_src,
    up_buf,
    down_buf,
    pair_out,
    pair_in,
    over_out,
    over_in,
    line_out,
    up_in,
    down_in,
):
    rows = x_ref.shape[1] // parts
    cut = lambda part: pl.ds(part * rows, rows)

    def run():
        spot, chip, core = places(spots)
        greet(spots, spot, chip, core)

        def order(step):
            if step == spots - 1:
                return spot
            fall = spots - 1 - step
            fall = jnp.where(fall <= spot, fall - 1, fall)
            rise = jnp.where(step >= spot, step + 1, step)
            return jnp.where(2 * spot < spots - 1, fall, rise)

        def pair(at, c, part):
            return remote(
                x_ref.at[slot(at, c, 1 - core), cut(part)],
                pair_buf.at[at, c, cut(part)],
                to_partner(chip, core),
                pair_out.at[at, c, part],
                pair_in.at[at, c, part],
            )

        def over(at, part):
            return remote(
                over_src.at[at, cut(part)],
                over_buf.at[at, cut(part)],
                to_other(chip, core),
                over_out.at[at, part],
                over_in.at[at, part],
            )

        def up(at, part):
            return remote(
                line_src.at[at, cut(part)],
                up_buf.at[at, cut(part)],
                {"dp": spot + 1},
                line_out.at[at, part],
                up_in.at[at, part],
            )

        def down(at, part):
            return remote(
                line_src.at[at, cut(part)],
                down_buf.at[at, cut(part)],
                {"dp": spot - 1},
                line_out.at[at, part],
                down_in.at[at, part],
            )

        for c in (1 - chip, chip):
            for step in range(spots):
                for part in range(parts):
                    pair(order(step), c, part).start()
        for step in range(spots):
            at = order(step)
            for part in range(parts):
                pair(at, 1 - chip, part).wait_recv()
                add_into(
                    over_src.at[at, cut(part)],
                    [x_ref.at[slot(at, 1 - chip, core), cut(part)], pair_buf.at[at, 1 - chip, cut(part)]],
                    rows,
                )
                over(at, part).start()
        for step in range(spots):
            at = order(step)
            for part in range(parts):
                pair(at, chip, part).wait_recv()
                over(at, part).wait_recv()
                base = [
                    x_ref.at[slot(at, chip, core), cut(part)],
                    pair_buf.at[at, chip, cut(part)],
                    over_buf.at[at, cut(part)],
                ]
                ups, downs = up_buf.at[at, cut(part)], down_buf.at[at, cut(part)]
                if step < spots - 1:
                    target = line_src.at[at, cut(part)]

                    def rising(first):
                        if not first:
                            up(at, part).wait_recv()
                        add_into(target, base if first else base + [ups], rows)
                        up(at, part).start()

                    def falling(first):
                        if not first:
                            down(at, part).wait_recv()
                        add_into(target, base if first else base + [downs], rows)
                        down(at, part).start()

                    pl.when((at > spot) & (spot == 0))(lambda: rising(True))
                    pl.when((at > spot) & (spot > 0))(lambda: rising(False))
                    pl.when((at < spot) & (spot == spots - 1))(lambda: falling(True))
                    pl.when((at < spot) & (spot < spots - 1))(lambda: falling(False))
                elif spots == 1:
                    add_into(o_ref.at[cut(part)], base, rows)
                else:

                    def finish(ends):
                        if ends < 1:
                            up(at, part).wait_recv()
                        if ends > -1:
                            down(at, part).wait_recv()
                        extra = ([ups] if ends < 1 else []) + ([downs] if ends > -1 else [])
                        add_into(o_ref.at[cut(part)], base + extra, rows)

                    pl.when(spot == 0)(lambda: finish(1))
                    pl.when(spot == spots - 1)(lambda: finish(-1))
                    pl.when((spot > 0) & (spot < spots - 1))(lambda: finish(0))
        for part in range(parts):
            for step in range(spots):
                at = order(step)
                pair(at, 0, part).wait_send()
                pair(at, 1, part).wait_send()
                over(at, part).wait_send()
                if step < spots - 1:
                    up(at, part).wait_send()

    if active is None:
        run()
    else:
        pl.when(lax.axis_index("section") == active)(run)


def scatter_blocks(partial, across, name, active=None, parts=4):
    if lax.axis_size("expert") != 4:
        axes = BOTH if across else "expert"
        return lax.psum_scatter(partial, axes, scatter_dimension=0, tiled=True).astype(jnp.float32)
    spots = lax.axis_size("dp") if across else 1
    rows, width = partial.shape[0] // (spots * 4), partial.shape[1]
    dma = pltpu.SemaphoreType.DMA
    hold = lambda *lead: pltpu.VMEM((*lead, rows, width), partial.dtype)
    return pl.pallas_call(
        functools.partial(scatter_kernel, spots, parts, active),
        out_shape=jax.ShapeDtypeStruct((rows, width), jnp.float32),
        in_specs=[pl.BlockSpec(memory_space=pltpu.VMEM)],
        out_specs=pl.BlockSpec(memory_space=pltpu.VMEM),
        scratch_shapes=[
            hold(spots, 2),
            hold(spots),
            hold(spots),
            hold(spots),
            hold(spots),
            hold(spots),
            dma((spots, 2, parts)),
            dma((spots, 2, parts)),
            dma((spots, parts)),
            dma((spots, parts)),
            dma((spots, parts)),
            dma((spots, parts)),
            dma((spots, parts)),
        ],
        compiler_params=pltpu.CompilerParams(collective_id=IDS[name], has_side_effects=True),
        name=name,
    )(partial.reshape(spots * 4, rows, width))


def allowed_pairs(seg_col, seg_row):
    rows = seg_col.shape[0]
    later = lax.broadcasted_iota(jnp.int32, (rows, rows), 0)
    earlier = lax.broadcasted_iota(jnp.int32, (rows, rows), 1)
    return (seg_col == seg_row) & (earlier <= later)


def attend_kernel(heads, q_ref, lat_ref, key_ref, cos_ref, sin_ref, col_ref, row_ref, out_ref, rot_ref):
    factor = QK**-0.5
    allowed = allowed_pairs(col_ref[...], row_ref[0])
    cosine, sine = cos_ref[...], sin_ref[...]
    shared = key_ref[:, LAT:]
    for head in range(heads):
        raw = q_ref[:, head * QK : (head + 1) * QK]
        query = bf16(
            jnp.concatenate([raw[:, :NOPE], rotate(raw[:, NOPE:], cosine, sine)], axis=1)
        )
        rot_ref[:, head * QK : (head + 1) * QK] = query
        key = jnp.concatenate([lat_ref[:, head * KV : head * KV + NOPE], shared], axis=1)
        value = lat_ref[:, head * KV + NOPE : (head + 1) * KV]
        scores = jnp.where(allowed, dot_t(query, key) * factor, masked_score)
        top = jnp.max(scores, axis=1, keepdims=True)
        powers = jnp.exp(scores - top)
        probs = powers / jnp.sum(powers, axis=1, keepdims=True)
        out_ref[:, head * VD : (head + 1) * VD] = bf16(dot(bf16(probs), value))


def attend(query_raw, latent, keyed, tables):
    cosine, sine, seg_col, seg_row = tables
    count, _, rows = seg_row.shape
    heads = query_raw.shape[1] // QK
    block = lambda width: pl.BlockSpec((rows, width), lambda i: (i, 0))
    return pl.pallas_call(
        functools.partial(attend_kernel, heads),
        grid=(count,),
        in_specs=[
            block(heads * QK),
            block(heads * KV),
            block(LAT + ROPE),
            block(HALF),
            block(HALF),
            block(1),
            pl.BlockSpec((1, 1, rows), lambda i: (i, 0, 0)),
        ],
        out_specs=[block(heads * VD), block(heads * QK)],
        out_shape=[
            jax.ShapeDtypeStruct((count * rows, heads * VD), jnp.bfloat16),
            jax.ShapeDtypeStruct((count * rows, heads * QK), jnp.bfloat16),
        ],
        name="attend",
        cost_estimate=pl.CostEstimate(
            flops=2 * count * heads * rows * rows * (QK + VD),
            bytes_accessed=count * rows * heads * (QK * 6 + KV * 2 + VD * 2),
            transcendentals=count * heads * rows * rows,
        ),
    )(query_raw, latent, keyed, cosine, sine, seg_col, seg_row)


def attend_back_kernel(
    heads, q_ref, lat_ref, key_ref, grad_ref, cos_ref, sin_ref, col_ref, row_ref, dq_ref, dlat_ref, dkey_ref
):
    factor = QK**-0.5
    allowed = allowed_pairs(col_ref[...], row_ref[0])
    cosine, sine = cos_ref[...], sin_ref[...]
    shared = key_ref[:, LAT:]
    total = None
    for head in range(heads):
        query = q_ref[:, head * QK : (head + 1) * QK]
        key = jnp.concatenate([lat_ref[:, head * KV : head * KV + NOPE], shared], axis=1)
        value = lat_ref[:, head * KV + NOPE : (head + 1) * KV]
        grad = grad_ref[:, head * VD : (head + 1) * VD]
        scores = jnp.where(allowed, dot_t(query, key) * factor, masked_score)
        top = jnp.max(scores, axis=1, keepdims=True)
        powers = jnp.exp(scores - top)
        probs = powers / jnp.sum(powers, axis=1, keepdims=True)
        grad_value = t_dot(bf16(probs), grad)
        grad_probs = dot_t(grad, value)
        centre = jnp.sum(probs * grad_probs, axis=1, keepdims=True)
        grad_scores = bf16(probs * (grad_probs - centre) * factor)
        grad_query = dot(grad_scores, key)
        grad_key = t_dot(grad_scores, query)
        dq_ref[:, head * QK : (head + 1) * QK] = bf16(
            jnp.concatenate(
                [grad_query[:, :NOPE], rotate(grad_query[:, NOPE:], cosine, -sine)], axis=1
            )
        )
        dlat_ref[:, head * KV : head * KV + NOPE] = bf16(grad_key[:, :NOPE])
        dlat_ref[:, head * KV + NOPE : (head + 1) * KV] = bf16(grad_value)
        part = grad_key[:, NOPE:]
        total = part if total is None else total + part
    dkey_ref[...] = total


def attend_back(query, latent, keyed, grad, tables):
    cosine, sine, seg_col, seg_row = tables
    count, _, rows = seg_row.shape
    heads = query.shape[1] // QK
    block = lambda width: pl.BlockSpec((rows, width), lambda i: (i, 0))
    return pl.pallas_call(
        functools.partial(attend_back_kernel, heads),
        grid=(count,),
        in_specs=[
            block(heads * QK),
            block(heads * KV),
            block(LAT + ROPE),
            block(heads * VD),
            block(HALF),
            block(HALF),
            block(1),
            pl.BlockSpec((1, 1, rows), lambda i: (i, 0, 0)),
        ],
        out_specs=[block(heads * QK), block(heads * KV), block(ROPE)],
        out_shape=[
            jax.ShapeDtypeStruct((count * rows, heads * QK), jnp.bfloat16),
            jax.ShapeDtypeStruct((count * rows, heads * KV), jnp.bfloat16),
            jax.ShapeDtypeStruct((count * rows, ROPE), jnp.float32),
        ],
        name="attend_back",
        cost_estimate=pl.CostEstimate(
            flops=2 * count * heads * rows * rows * (3 * QK + 2 * VD),
            bytes_accessed=count * rows * heads * (QK * 4 + KV * 4 + VD * 2),
            transcendentals=count * heads * rows * rows,
        ),
    )(query, latent, keyed, grad, cosine, sine, seg_col, seg_row)


def gated_hidden(gate, up):
    return silu_parts(gate)[0] * up


def gated_back(gate, up, grad_hidden):
    act, slope = silu_parts(gate)
    return bf16(grad_hidden * up * slope), bf16(grad_hidden * act)


def experts_kernel(
    full,
    here_ref,
    x_ref,
    routed_ref,
    own_ref,
    in_ref,
    out_w_ref,
    router_ref,
    shared_in_ref,
    shared_out_ref,
    pre_ref,
    gated_ref,
    prob_ref,
    shared_pre_ref,
    *partial_ref,
):
    units = gated_ref.shape[1]
    x = x_ref[...]
    logits = dot(x, router_ref[...])
    powers = jnp.exp(logits - jnp.max(logits, axis=1, keepdims=True))
    prob = powers / jnp.sum(powers, axis=1, keepdims=True)
    prob_ref[...] = prob
    gate = jnp.sum(prob * own_ref[...], axis=1, keepdims=True) * routed_ref[...]
    pre = dot(x, in_ref[...])
    pre_ref[...] = bf16(pre)
    gated = bf16(gate * gated_hidden(pre[:, :units], pre[:, units:]))
    gated_ref[...] = gated
    tile = pl.program_id(0)
    inside = (tile >= here_ref[0]) & (tile < here_ref[1])
    half = shared_out_ref.shape[0]

    def shared():
        left = dot_t(x, shared_in_ref[:half])
        right = dot_t(x, shared_in_ref[half:])
        shared_pre_ref[0] = bf16(left)
        shared_pre_ref[1] = bf16(right)
        return left, right

    if full:

        def with_shared():
            hidden = bf16(gated_hidden(*shared()))
            partial_ref[0][...] = bf16(dot(gated, out_w_ref[...]) + dot(hidden, shared_out_ref[...]))

        def without():
            partial_ref[0][...] = bf16(dot(gated, out_w_ref[...]))

        pl.when(inside)(with_shared)
        pl.when(jnp.logical_not(inside))(without)
    else:
        pl.when(inside)(lambda: shared() and None)


def tile_rows(pack_rows):
    return min(256, pack_rows)


def tile_here(pack, pack_rows):
    tiles = pack_rows // tile_rows(pack_rows)
    return jnp.stack([pack * tiles, (pack + 1) * tiles]).astype(jnp.int32)


def specs_of(rows, tile):
    block = lambda width: pl.BlockSpec((tile, width), lambda i, here: (i, 0))
    whole = lambda array: pl.BlockSpec(
        array.shape, lambda i, here: (0,) * array.ndim, pipeline_mode=pl.Buffered(1)
    )
    inner = lambda i, here: jnp.clip(i - here[0], 0, here[1] - here[0] - 1)
    return block, whole, inner


def experts(x, routed, own_column, weights, here, pack_rows, full):
    expert_in, expert_out, router, shared_in, shared_out = weights
    rows, width = x.shape
    tile = tile_rows(pack_rows)
    units, half = expert_out.shape[0], shared_out.shape[0]
    block, whole, inner = specs_of(rows, tile)
    shape = jax.ShapeDtypeStruct
    out_shape = [
        shape((rows, 2 * units), jnp.bfloat16),
        shape((rows, units), jnp.bfloat16),
        shape((rows, router.shape[1]), jnp.float32),
        shape((2, pack_rows, half), jnp.bfloat16),
    ]
    out_specs = [
        block(2 * units),
        block(units),
        block(router.shape[1]),
        pl.BlockSpec((2, tile, half), lambda i, here: (0, inner(i, here), 0)),
    ]
    if full:
        out_shape.append(shape((rows, width), jnp.bfloat16))
        out_specs.append(block(width))
    return pl.pallas_call(
        functools.partial(experts_kernel, full),
        grid_spec=pltpu.PrefetchScalarGridSpec(
            num_scalar_prefetch=1,
            grid=(rows // tile,),
            in_specs=[
                block(width),
                block(1),
                whole(own_column),
                whole(expert_in),
                whole(expert_out),
                whole(router),
                whole(shared_in),
                whole(shared_out),
            ],
            out_specs=out_specs,
        ),
        out_shape=out_shape,
        name="experts_full" if full else "experts_inner",
        cost_estimate=pl.CostEstimate(
            flops=2 * rows * width * units * 3, bytes_accessed=rows * width * 4, transcendentals=rows * units
        ),
    )(here, x, routed, own_column, expert_in, expert_out, router, shared_in, shared_out)


def experts_back_kernel(
    here_ref,
    grad_ref,
    pre_ref,
    prob_ref,
    routed_ref,
    own_ref,
    in_ref,
    out_w_ref,
    router_ref,
    shared_pre_ref,
    shared_in_ref,
    shared_out_ref,
    grad_pre_ref,
    moved_ref,
    partial_ref,
):
    units = out_w_ref.shape[0]
    grad = grad_ref[...]
    prob = prob_ref[...]
    own_prob = jnp.sum(prob * own_ref[...], axis=1, keepdims=True) * routed_ref[...]
    gate, up = pre_ref[:, :units].astype(jnp.float32), pre_ref[:, units:].astype(jnp.float32)
    grad_units = dot_t(grad, out_w_ref[...])
    act, slope = silu_parts(gate)
    grad_gate = jnp.sum(grad_units * act * up, axis=1, keepdims=True)
    moved = own_prob * grad_gate
    moved_ref[...] = moved
    grad_logits = bf16(moved * (own_ref[...] - prob))
    scaled = own_prob * grad_units
    grad_pre_ref[:, :units] = bf16(scaled * up * slope)
    grad_pre_ref[:, units:] = bf16(scaled * act)
    base = dot_t(grad_pre_ref[...], in_ref[...]) + dot_t(grad_logits, router_ref[...])
    tile = pl.program_id(0)
    inside = (tile >= here_ref[0]) & (tile < here_ref[1])
    half = shared_out_ref.shape[0]

    def with_shared():
        left, right = gated_back(
            shared_pre_ref[0].astype(jnp.float32),
            shared_pre_ref[1].astype(jnp.float32),
            dot_t(grad, shared_out_ref[...]),
        )
        partial_ref[...] = bf16(base + dot(left, shared_in_ref[:half]) + dot(right, shared_in_ref[half:]))

    def without():
        partial_ref[...] = bf16(base)

    pl.when(inside)(with_shared)
    pl.when(jnp.logical_not(inside))(without)


def experts_back(grad, stored, routed, own_column, weights, here, pack_rows):
    expert_in, expert_out, router, shared_in, shared_out = weights
    rows, width = grad.shape
    tile = tile_rows(pack_rows)
    units, half = expert_out.shape[0], shared_out.shape[0]
    block, whole, inner = specs_of(rows, tile)
    shape = jax.ShapeDtypeStruct
    return pl.pallas_call(
        experts_back_kernel,
        grid_spec=pltpu.PrefetchScalarGridSpec(
            num_scalar_prefetch=1,
            grid=(rows // tile,),
            in_specs=[
                block(width),
                block(2 * units),
                block(router.shape[1]),
                block(1),
                whole(own_column),
                whole(expert_in),
                whole(expert_out),
                whole(router),
                pl.BlockSpec((2, tile, half), lambda i, here: (0, inner(i, here), 0)),
                whole(shared_in),
                whole(shared_out),
            ],
            out_specs=[block(2 * units), block(1), block(width)],
        ),
        out_shape=[
            shape((rows, 2 * units), jnp.bfloat16),
            shape((rows, 1), jnp.float32),
            shape((rows, width), jnp.bfloat16),
        ],
        name="experts_back",
        cost_estimate=pl.CostEstimate(
            flops=2 * rows * width * units * 3, bytes_accessed=rows * width * 4, transcendentals=rows * units
        ),
    )(
        here,
        grad,
        stored["pre"],
        stored["prob"],
        routed,
        own_column,
        expert_in,
        expert_out,
        router,
        stored["shared_pre"],
        shared_in,
        shared_out,
    )


def pair_grad_kernel(x_ref, grad_ref, out_ref):
    units = out_ref.shape[2]
    x = x_ref[...]
    out_ref[:, 0, :] = t_dot(x, grad_ref[:, :units])
    out_ref[:, 1, :] = t_dot(x, grad_ref[:, units:])


def pair_grad(x, grad):
    rows, width = x.shape
    units = grad.shape[1] // 2
    if rows > 4096:
        return t_dot(x, grad).reshape(width, 2, units)
    tile = 256
    return pl.pallas_call(
        pair_grad_kernel,
        grid=(width // tile,),
        in_specs=[
            pl.BlockSpec((rows, tile), lambda i: (0, i)),
            pl.BlockSpec((rows, 2 * units), lambda i: (0, 0), pipeline_mode=pl.Buffered(1)),
        ],
        out_specs=pl.BlockSpec((tile, 2, units), lambda i: (i, 0, 0)),
        out_shape=jax.ShapeDtypeStruct((width, 2, units), jnp.float32),
        name="pair_grad",
        cost_estimate=pl.CostEstimate(
            flops=4 * rows * width * units, bytes_accessed=rows * (width + 2 * units) * 2 + width * units * 8, transcendentals=0
        ),
    )(x, grad)


def blank(shape, dtype):
    return pl.pallas_call(
        lambda out_ref: None,
        out_shape=jax.ShapeDtypeStruct(shape, dtype),
        out_specs=pl.BlockSpec(memory_space=pl.ANY),
        name="blank",
    )()


def body(
    boundary,
    lengths,
    routes,
    attn_gain,
    query_weight,
    compress_weight,
    latent_gain,
    expand_weight,
    output_weight,
    ffn_gain,
    router_weight,
    shared_in,
    shared_out,
    expert_in,
    expert_out,
):
    attn_gain, latent_gain, ffn_gain = attn_gain[0], latent_gain[0], ffn_gain[0]
    query_weight, compress_weight = query_weight[0], compress_weight[0]
    expand_weight, output_weight = expand_weight[0], output_weight[0]
    router_weight, shared_out, expert_out = router_weight[0], shared_out[0], expert_out[0, 0]
    width = boundary.shape[3]
    rows = boundary.shape[2]
    shared_half = shared_out.shape[0]
    units = expert_out.shape[0]
    shared_in_t = jnp.transpose(shared_in[0], (1, 2, 0)).reshape(2 * shared_half, width)
    expert_in = expert_in.reshape(width, 2 * units)
    weights = (expert_in, expert_out, router_weight, shared_in_t, shared_out)

    packs, members = lax.axis_size("dp"), lax.axis_size("expert")
    count = packs * members
    pack, member = lax.axis_index("dp"), lax.axis_index("expert")
    me = pack * members + member
    is_first = lax.axis_index("section") == 0
    pack_rows = members * rows
    top = routes.shape[3]
    experts_count = router_weight.shape[1]
    here = tile_here(pack, pack_rows)

    def own_pack(value):
        size = value.shape[0] // packs
        return lax.dynamic_slice_in_dim(value, pack * size, size, 0)

    def tables_of(block_lengths):
        segment, position = block_layout(block_lengths, rows)
        blocks = segment.shape[0]
        freqs = rope_base ** (-jnp.arange(HALF, dtype=jnp.float32) / HALF)
        angles = position.reshape(-1).astype(jnp.float32)[:, None] * freqs[None, :]
        return (
            jnp.cos(angles),
            jnp.sin(angles),
            segment.reshape(blocks * rows, 1),
            segment.reshape(blocks, 1, rows),
        )

    own_lengths = lax.dynamic_index_in_dim(lengths[0, 0], member, 0, keepdims=False)
    layout = jnp.concatenate([routes.reshape(rows * top), own_lengths])
    layout = jnp.pad(layout, (0, -layout.shape[0] % 1024)).reshape(8, -1)

    def routed_of(layout_all):
        routes_all = layout_all.reshape(count, -1)[:, : rows * top].reshape(count * rows, top)
        return jnp.any(routes_all == me, axis=1, keepdims=True).astype(jnp.float32)

    tables_pack = tables_of(lengths[0, 0])
    own_cos, own_sin = (
        lax.dynamic_slice_in_dim(table, member * rows, rows, 0) for table in tables_pack[:2]
    )
    own_column = (lax.broadcasted_iota(jnp.int32, (1, experts_count), 1) == me).astype(jnp.float32)

    def inputs_of(hidden):
        normed32, scale_attn = rms_forward(hidden, attn_gain)
        normed = bf16(normed32)
        compressed = dot(normed, compress_weight)
        latent32, scale_latent = rms_forward(compressed[:, :LAT], latent_gain)
        keyed = bf16(
            jnp.concatenate([latent32, rotate(compressed[:, LAT:], own_cos, own_sin)], axis=1)
        )
        return normed, keyed, (compressed, scale_attn, scale_latent)

    def heads_of(normed, keyed, tables):
        query_raw = dot(normed, query_weight)
        latent = bf16(dot(keyed[:, :LAT], expand_weight))
        attended, query = attend(query_raw, latent, keyed, tables)
        return attended, query, latent

    fresh = boundary[0, 0].astype(jnp.float32)

    normed, keyed, _ = inputs_of(fresh)
    pack_inputs = gather_blocks([normed, keyed], False, "gather_inputs_first", 0)
    attended, _, _ = heads_of(*pack_inputs, tables_pack)
    mixed_first = fresh + scatter_blocks(
        bf16(dot(attended, output_weight)), False, "scatter_attended_first", 0
    )
    ffn_all, layout_all = gather_blocks(
        [bf16(rms_forward(mixed_first, ffn_gain)[0]), layout], True, "gather_ffn_first", 0
    )
    *_, partial = experts(ffn_all, routed_of(layout_all), own_column, weights, here, pack_rows, True)
    result_first = mixed_first + scatter_blocks(partial, True, "scatter_ffn_first", 0)
    target_all, layout_all = gather_blocks(
        [boundary[0, 0], layout], True, "gather_target", 1, [blank(ffn_all.shape, jnp.bfloat16), layout_all]
    )
    sent, target_all, layout_all = lax.optimization_barrier((bf16(result_first), target_all, layout_all))
    inbound = lax.ppermute(sent, "section", [(0, 1)])
    routed = routed_of(layout_all)
    tables_all = tables_of(layout_all.reshape(count, -1)[:, rows * top : rows * top + lengths.shape[3]])

    hidden = jnp.where(is_first, fresh, inbound.astype(jnp.float32))
    normed, keyed, (compressed, scale_attn, scale_latent) = inputs_of(hidden)
    normed_pack, keyed_pack = gather_blocks([normed, keyed], False, "gather_inputs_second", 1, pack_inputs)
    attended, query, latent = heads_of(normed_pack, keyed_pack, tables_pack)
    mixed = hidden + scatter_blocks(bf16(dot(attended, output_weight)), False, "scatter_attended_second", 1)
    mixed = jnp.where(is_first, mixed_first, mixed)
    ffn32, scale_ffn = rms_forward(mixed, ffn_gain)
    (ffn_all,) = gather_blocks([bf16(ffn32)], True, "gather_ffn_second", 1, [ffn_all])
    pre, gated, prob, shared_pre = experts(ffn_all, routed, own_column, weights, here, pack_rows, False)
    stored = dict(pre=pre, prob=prob, shared_pre=shared_pre)

    def latent_back(own):
        grad_latent, grad_latent_gain = rms_backward(
            compressed[:, :LAT], scale_latent, latent_gain, own[:, width : width + LAT]
        )
        grad_compressed = bf16(
            jnp.concatenate([grad_latent, rotate(own[:, width + LAT :], own_cos, -own_sin)], axis=1)
        )
        grad_normed = own[:, :width] + dot_t(grad_compressed, compress_weight)
        grad_hidden_norm, grad_attn_gain = rms_backward(hidden, scale_attn, attn_gain, grad_normed)
        return grad_compressed, grad_hidden_norm, grad_attn_gain, grad_latent_gain

    def heads_back(grad_query, grad_latent_heads, grad_shared_key):
        return bf16(
            jnp.concatenate(
                [
                    dot_t(grad_query, query_weight),
                    dot_t(grad_latent_heads, expand_weight),
                    grad_shared_key,
                ],
                axis=1,
            )
        )

    def prepare(normed_all, keyed_all):
        attended_all, query_all, latent_all = heads_of(normed_all, keyed_all, tables_all)
        left = dot_t(ffn_all, shared_in_t[:shared_half])
        right = dot_t(ffn_all, shared_in_t[shared_half:])
        return attended_all, query_all, latent_all, bf16(left), bf16(right), bf16(gated_hidden(left, right))

    grad_pre_second, moved_second, partial = experts_back(
        target_all, stored, routed, own_column, weights, here, pack_rows
    )
    grad_ffn_second = scatter_blocks(partial, True, "scatter_ffn_back_second", 1)
    grad_mixed = fresh + rms_backward(mixed, scale_ffn, ffn_gain, grad_ffn_second)[0]
    (grad_mixed_pack,) = gather_blocks([bf16(grad_mixed)], False, "gather_mixed", 1)
    own_second = scatter_blocks(
        heads_back(
            *attend_back(query, latent, keyed_pack, bf16(dot_t(grad_mixed_pack, output_weight)), tables_pack)
        ),
        False,
        "scatter_heads_second",
        1,
    )
    grad_second = grad_mixed + latent_back(own_second)[1]

    all_inputs = gather_blocks([normed, keyed], True, "gather_keyed_first", 0)
    prepared = lax.cond(
        is_first,
        prepare,
        lambda *_: tuple(blank(like.shape, like.dtype) for like in jax.eval_shape(prepare, *all_inputs)),
        *all_inputs,
    )
    grad_second, prepared, all_inputs = lax.optimization_barrier((grad_second, prepared, all_inputs))
    downbound = lax.ppermute(grad_second, "section", [(1, 0)])

    normed_late, keyed_late, gated_late, _ = lax.optimization_barrier((normed, keyed, gated, grad_second))
    normed_all, keyed_all = gather_blocks([normed_late, keyed_late], True, "gather_keyed_second", 1, all_inputs)
    attended_all, query_all, latent_all, shared_gate, shared_up, shared_hid = lax.cond(
        is_first, lambda *values: values[2:], lambda *values: prepare(*values[:2]), normed_all, keyed_all, *prepared
    )

    def finish(gated_late, shared_hid):
        partial = bf16(dot(gated_late, expert_out))
        addend = dot(own_pack(shared_hid), shared_out)
        return lax.dynamic_update_slice_in_dim(
            partial, bf16(own_pack(partial).astype(jnp.float32) + addend), pack * pack_rows, 0
        )

    partial = lax.cond(
        is_first, lambda *_: blank((count * rows, width), jnp.bfloat16), finish, gated_late, shared_hid
    )
    result = mixed + scatter_blocks(partial, True, "scatter_result", 1)

    upstream = jnp.where(is_first, downbound, fresh)
    (upstream_all,) = gather_blocks([bf16(upstream)], True, "gather_upstream", 0, [target_all])
    grad_pre, moved, partial = lax.cond(
        is_first,
        lambda upstream_all, *_: tuple(
            experts_back(upstream_all, stored, routed, own_column, weights, here, pack_rows)
        ),
        lambda _, *old: (*old, blank((count * rows, width), jnp.bfloat16)),
        upstream_all,
        grad_pre_second,
        moved_second,
    )
    grad_ffn = jnp.where(is_first, scatter_blocks(partial, True, "scatter_ffn_back_first", 0), grad_ffn_second)
    grad_mixed_norm, grad_ffn_gain = rms_backward(mixed, scale_ffn, ffn_gain, grad_ffn)
    grad_mixed = upstream + grad_mixed_norm
    grad_mixed_all = lax.all_gather(bf16(grad_mixed), BOTH, axis=0, tiled=True)
    grad_attended = bf16(dot_t(grad_mixed_all, output_weight))
    grad_query, grad_latent_heads, grad_shared_key = attend_back(
        query_all, latent_all, keyed_all, grad_attended, tables_all
    )
    own = lax.psum_scatter(
        heads_back(own_pack(grad_query), own_pack(grad_latent_heads), own_pack(grad_shared_key)),
        "expert",
        scatter_dimension=0,
        tiled=True,
    ).astype(jnp.float32)
    grad_compressed, grad_hidden_norm, grad_attn_gain, grad_latent_gain = latent_back(own)
    grad_hidden = grad_mixed + grad_hidden_norm

    small = jnp.concatenate([grad_attn_gain, grad_latent_gain, grad_ffn_gain, moved[:, 0]])
    small = jnp.pad(small, (0, -small.shape[0] % 1024)).reshape(8, -1)
    grad_compressed_all = lax.all_gather(grad_compressed, BOTH, axis=0, tiled=True)
    small_all = lax.all_gather(small, BOTH, axis=0, tiled=True).reshape(count, -1)
    gains = jnp.sum(small_all[:, : 2 * width + LAT], axis=0)
    moved_all = small_all[:, 2 * width + LAT : 2 * width + LAT + count * rows].T
    grad_logits = bf16(moved_all - prob * jnp.sum(moved_all, axis=1, keepdims=True))
    left, right = gated_back(
        shared_gate.astype(jnp.float32), shared_up.astype(jnp.float32), dot_t(upstream_all, shared_out)
    )
    grad_shared_in = jnp.stack([t_dot(ffn_all, left), t_dot(ffn_all, right)], axis=1)
    ends = jnp.where(is_first, grad_hidden, result)
    return (
        ends[None, None],
        gains[:width][None],
        t_dot(normed_all, grad_query)[None],
        t_dot(normed_all, grad_compressed_all)[None],
        gains[width : width + LAT][None],
        t_dot(keyed_all[:, :LAT], grad_latent_heads)[None],
        t_dot(attended_all, grad_mixed_all)[None],
        gains[width + LAT :][None],
        t_dot(ffn_all, grad_logits)[None],
        grad_shared_in[None],
        t_dot(shared_hid, upstream_all)[None],
        pair_grad(ffn_all, grad_pre)[None, None],
        t_dot(gated, upstream_all)[None, None],
    )


def solution(mesh):
    return jax.shard_map(
        body,
        mesh=mesh,
        in_specs=(
            P("section", None, BOTH, None),
            P(None, "dp", None, None),
            P("section", None, BOTH, None),
            P("section", None),
            P("section", None, "expert"),
            P("section", None, None),
            P("section", None),
            P("section", None, "expert"),
            P("section", "expert", None),
            P("section", None),
            P("section", None, None),
            P("section", None, None, "expert"),
            P("section", "expert", None),
            P("section", BOTH, None, None, None),
            P("section", BOTH, None, None),
        ),
        out_specs=(
            P("section", None, BOTH, None),
            P("section", None),
            P("section", None, "expert"),
            P("section", None, None),
            P("section", None),
            P("section", None, "expert"),
            P("section", "expert", None),
            P("section", None),
            P("section", None, None),
            P("section", None, None, "expert"),
            P("section", "expert", None),
            P("section", BOTH, None, None, None),
            P("section", BOTH, None, None),
        ),
        check_vma=False,
    )
```

time: 1650 us -> 1150 us (0.70)
  waiting for transfers between devices: 932 us -> 108 us
  Pallas kernels: 94.4 us -> 660 us
  matrix products: 410 us -> 212 us
  blocking collectives: 52.5 us -> 24.3 us
    pallas_call x0 -> x28, Pallas kernels: none -> 565 us  [the longest x9 223 us: gather_blocks(): pl.pallas_call(functools.partial(gather_kernel, spots, cuts, active), out...]
    all_gather x10 -> x2, waiting for transfers between devices: 426 us -> 0.02 us  [the longest x1 0.02 us: body(): grad_mixed_all = lax.all_gather(bf16(grad_mixed), BOTH, axis=0, tiled=True)]
    reduce_scatter x8 -> x1, waiting for transfers between devices: 414 us -> 6.15 us  [body(): lax.psum_scatter(heads_back(own_pack(grad_query), own_pack(grad_latent_he...]
    dot_general x19 -> x11, matrix products: 162 us -> 63.5 us  [dot_t(): lax.dot_general(left, right, (((1,), (1,)), ((), ())), preferred_element_...]
    dot_general x21 -> x12, matrix products: 150 us -> 59.7 us  [dot(): return jnp.dot(left, right, preferred_element_type=jnp.float32)]
    ppermute x2, waiting for transfers between devices: 34.9 us -> 102 us  [the longest x1 84.3 us: body(): inbound = lax.ppermute(sent, 'section', [(0, 1)])]
    psum x1 -> x0, waiting for transfers between devices: 56.8 us -> none  [backward(): router = lax.psum(t_dot(stored['ffn_all'], grad_logits), BOTH)]
    all_gather x3 -> x1, blocking collectives: 52.5 us -> 24.3 us  [body(): lax.all_gather(small, BOTH, axis=0, tiled=True).reshape(count, -1)]
  transfers between devices with their start and end apart: 21 -> 5, of which waited for: 18 -> 3; matrix products, arithmetic and copies ran while one was open for 15% -> 16% of each run, Pallas kernels for 2% -> 18%
where the time goes in v2:
time: 1150 us; the launch traced here: 1140 us
  Pallas kernels  660 us (57%)
  matrix products  212 us (18%)
  waiting for transfers between devices  108 us (9%)
  other arithmetic  60.6 us (5%)
  local copies, waits for them, and re-layouts  51 us (4%)
  blocking collectives  24.3 us (2%)
  between operations  15.2 us (1%)
    pallas_call x9, Pallas kernels, gather_blocks(): pl.pallas_call(functools.partial(gather_kernel, spots, cuts, active), out...  223 us
    pallas_call x7, Pallas kernels, scatter_blocks(): pl.pallas_call(functools.partial(scatter_kernel, spots, parts, active), o...  197 us
    dot_general x9, matrix products, t_dot(): lax.dot_general(left, right, (((0,), (0,)), ((), ())), preferred_element_...  89.1 us
    ppermute x1, waiting for transfers between devices, body(): inbound = lax.ppermute(sent, 'section', [(0, 1)])  84.3 us
    pallas_call x2, Pallas kernels, experts(): pl.pallas_call(functools.partial(experts_kernel, full), grid_spec=pltpu.P...  68.6 us
    dot_general x11, matrix products, dot_t(): lax.dot_general(left, right, (((1,), (1,)), ((), ())), preferred_element_...  63.5 us
    dot_general x12, matrix products, dot(): return jnp.dot(left, right, preferred_element_type=jnp.float32)  59.7 us
    pallas_call x1, Pallas kernels, experts_back(): pl.pallas_call(experts_back_kernel, grid_spec=pltpu.PrefetchScalarGridSpe...  57 us
  transfers between devices with their start and end apart: 5, of which 3 were waited for; matrix products, arithmetic and copies ran while one was open for 16% of the time, Pallas kernels for 18%

profile of v2, /device:TPU:3, one launch (start us, length us, event | category | flops | bytes accessed | tf_op | source)
XLA Modules:
  0.0 1139.5 jit_solution(7615897260494955824)
XLA Ops:
  58.8 39.1 %experts_full.1 = (bf16[2048,1536]{1,0:T(8,128)(2,1)}, bf16[2048,768]{1,0:T(8,128)(2,1)}, f32[2048,16]{1,0:T(8,128)}, bf16[2,512,704]{2,1,0:T(8,128)(2,1)}, bf16[2048,2048]{1,0:T(8,128)(2,1)}) custom-call(s32[2]{0:T(128)S(1)} %pad_add_fusion.1.here_ref, bf16[2048,2048]{1,0:T(8,128)(2,1)} %bitcast.220, f32[2048,1]{1,0:T(8,128)} %copy.139.routed_ref, ...), custom_call_target="tpu_custom_call" | custom-call | flops 19327352832 | bytes 16777216 | tf_op jit(solution)/shard_map/experts_full/pallas_call | solution.py:730
  106.0 53.9 %gather_target.1 = (bf16[16,128,2048]{2,1,0:T(8,128)(2,1)}, s32[16,8,128]{2,1,0:T(8,128)}) custom-call(bf16[128,2048]{1,0:T(8,128)(2,1)} %bitcast.209, s32[8,128]{1,0:T(8,128)} %pad_bitcast_fusion.refs_1_, bf16[16,128,2048]{2,1,0:T(8,128)(2,1)} %bitcast.210, s32[16,8,128]{2,1,0:T(8,128)} %get-tuple-element.290.refs_3_), custom_call_target="tpu_custom_call", output_to_operand_aliasing={{0}: (2, {}), {1}: (3, {})} | custom-call | tf_op jit(solution)/shard_map/gather_target/pallas_call | solution.py:287
  172.6 84.3 %collective-permute-done = bf16[128,2048]{1,0:T(8,128)(2,1)S(1)} collective-permute-done((bf16[128,2048]{1,0:T(8,128)(2,1)}, bf16[128,2048]{1,0:T(8,128)(2,1)S(1)}, u32[]{:S(2)}, u32[]{:S(2)}) %collective-permute-start) | collective-permute-done | bytes 524320 | tf_op jit(solution)/shard_map/ppermute | solution.py:998
  261.1 21.4 %gather_inputs_second.1 = (bf16[4,128,2048]{2,1,0:T(8,128)(2,1)}, bf16[4,128,576]{2,1,0:T(8,128)(2,1)}) custom-call(bf16[128,2048]{1,0:T(8,128)(2,1)} %copy-done.13, bf16[128,576]{1,0:T(8,128)(2,1)} %pad_maximum_fusion.3.refs_1_, bf16[4,128,2048]{2,1,0:T(8,128)(2,1)} %get-tuple-element.286.refs_2_, ...), custom_call_target="tpu_custom_call", output_to_operand_aliasing={{0}: (2, {}), {1}: (3, {})} | custom-call | tf_op jit(solution)/shard_map/gather_inputs_second/pallas_call | solution.py:287
  306.0 18.0 %scatter_attended_second.1 = f32[128,2048]{1,0:T(8,128)} custom-call(bf16[4,128,2048]{2,1,0:T(8,128)(2,1)} %bitcast.255), custom_call_target="tpu_custom_call" | custom-call | tf_op jit(solution)/shard_map/scatter_attended_second/pallas_call | solution.py:476
  327.9 52.4 %gather_ffn_second.1 = bf16[16,128,2048]{2,1,0:T(8,128)(2,1)} custom-call(bf16[128,2048]{1,0:T(8,128)(2,1)} %multiply_convert_fusion.6.refs_0_, bf16[16,128,2048]{2,1,0:T(8,128)(2,1)} %get-tuple-element.289.refs_1_), custom_call_target="tpu_custom_call", output_to_operand_aliasing={{}: (1, {})} | custom-call | tf_op jit(solution)/shard_map/gather_ffn_second/pallas_call | solution.py:287
  380.3 29.5 %experts_inner.1 = (bf16[2048,1536]{1,0:T(8,128)(2,1)}, bf16[2048,768]{1,0:T(8,128)(2,1)}, f32[2048,16]{1,0:T(8,128)}, bf16[2,512,704]{2,1,0:T(8,128)(2,1)}) custom-call(s32[2]{0:T(128)S(1)} %pad_add_fusion.1.here_ref, bf16[2048,2048]{1,0:T(8,128)(2,1)} %bitcast.221, f32[2048,1]{1,0:T(8,128)} %copy.144.routed_ref, f32[1,16]{1,0:T(1,128)S(1)} %compare_convert_fusion.own_ref, ...), custom_call_target="tpu_custom_call" | custom-call | flops 19327352832 | bytes 16777216 | tf_op jit(solution)/shard_map/experts_inner/pallas_call | solution.py:730
  409.9 57.0 %experts_back.3 = (bf16[2048,1536]{1,0:T(8,128)(2,1)}, f32[2048,1]{1,0:T(8,128)}, bf16[2048,2048]{1,0:T(8,128)(2,1)}) custom-call(s32[2]{0:T(128)S(1)} %pad_add_fusion.1.here_ref, bf16[2048,2048]{1,0:T(8,128)(2,1)} %bitcast.211, bf16[2048,1536]{1,0:T(8,128)(2,1)} %get-tuple-element.300.pre_ref, f32[2048,16]{1,0:T(8,128)} %get-tuple-element.301.prob_ref, ...), custom_call_target="tpu_custom_call" | custom-call | flops 19327352832 | bytes 16777216 | tf_op jit(solution)/shard_map/experts_back/pallas_call | solution.py:813
  466.8 54.7 %scatter_ffn_back_second.1 = f32[128,2048]{1,0:T(8,128)} custom-call(bf16[16,128,2048]{2,1,0:T(8,128)(2,1)} %bitcast.237), custom_call_target="tpu_custom_call" | custom-call | tf_op jit(solution)/shard_map/scatter_ffn_back_second/pallas_call | solution.py:476
  526.0 17.0 %gather_mixed.1 = bf16[4,128,2048]{2,1,0:T(8,128)(2,1)} custom-call(bf16[128,2048]{1,0:T(8,128)(2,1)} %fusion.76.refs_0_), custom_call_target="tpu_custom_call" | custom-call | tf_op jit(solution)/shard_map/gather_mixed/pallas_call | solution.py:287
  567.6 21.8 %scatter_heads_second.1 = f32[128,2624]{1,0:T(8,128)} custom-call(bf16[4,128,2624]{2,1,0:T(8,128)(2,1)} %pad_maximum_fusion.x_ref), custom_call_target="tpu_custom_call" | custom-call | tf_op jit(solution)/shard_map/scatter_heads_second/pallas_call | solution.py:476
  595.7 14.2 %conditional.4 = (bf16[2048,512]{1,0:T(8,128)(2,1)}, bf16[2048,768]{1,0:T(8,128)(2,1)}, bf16[2048,1024]{1,0:T(8,128)(2,1)}, bf16[2048,704]{0,1:T(8,128)(2,1)}, b...) conditional(s32[]{:T(128)} %convert_element_type.206, () %tuple.61, (bf16[2048,2048]{1,0:T(8,128)(2,1)}, ...), branch_computations={%region_17.18_spmd, %region_18.19_spmd} | conditional | flops 21085814784 | bytes 165429392 | solution.py:1059
  618.1 17.7 %collective-permute-done.1 = f32[128,2048]{1,0:T(8,128)S(1)} collective-permute-done((f32[128,2048]{1,0:T(8,128)S(1)}, f32[128,2048]{1,0:T(8,128)S(1)}, u32[]{:S(2)}, u32[]{:S(2)}) %collective-permute-start.1) | collective-permute-done | bytes 1048608 | tf_op jit(solution)/shard_map/ppermute | solution.py:1066
  652.3 67.5 %gather_keyed_second.1 = (bf16[16,128,2048]{2,1,0:T(8,128)(2,1)}, bf16[16,128,576]{2,1,0:T(8,128)(2,1)}) custom-call(bf16[128,2048]{1,0:T(8,128)(2,1)} %copy-done.13, bf16[128,576]{1,0:T(8,128)(2,1)} %pad_maximum_fusion.3.refs_1_, bf16[16,128,2048]{2,1,0:T(8,128)(2,1)} %get-tuple-element.308, ...), custom_call_target="tpu_custom_call", output_to_operand_aliasing={{0}: (2, {}), {1}: (3, {})} | custom-call | tf_op jit(solution)/shard_map/gather_keyed_second/pallas_call | solution.py:287
  719.8 68.9 %conditional.6 = (bf16[2048,512]{1,0:T(8,128)(2,1)}, bf16[2048,768]{1,0:T(8,128)(2,1)}, bf16[2048,1024]{1,0:T(8,128)(2,1)}, bf16[2048,704]{0,1:T(8,128)(2,1)}, f32[2048,704]{0,1:T(8,128)}, /*index=5*/f32[2048,704]{0,1:T(8,128)}) conditional(s32[]{:T(128)} %convert_element_type.206, (bf16[2048,2048]{1,0:T(8,128)(2,1)}, ...), branch_computations={%region_22.23_spmd.clone, %region_23.24_spmd.clone} | conditional | flops 21088698368 | bytes 171196560 | solution.py:1070
  736.8 13.7 %convert_convert_fusion = (f32[2048,704]{0,1:T(8,128)}, bf16[2048,704]{0,1:T(8,128)(2,1)}, f32[2048,704]{0,1:T(8,128)}) fusion(f32[2048,704]{0,1:T(8,128)} %fusion.10, bf16[2048,2048]{1,0:T(8,128)(2,1)S(1)} %copy-done.8, bf16[1408,2048]{1,0:T(8,128)(2,1)} %get-tuple-element.546), kind=kOutput, calls=%fused_computation.14 | convolution fusion | flops 5919997952 | bytes 31457280 | tf_op jit(solution)/shard_map/cond/branch_0_fun/dot_general | solution.py:53
  761.0 27.3 %attend.9 = (bf16[2048,512]{1,0:T(8,128)(2,1)}, bf16[2048,768]{1,0:T(8,128)(2,1)}) custom-call(f32[2048,768]{1,0:T(8,128)} %fusion.80.q_ref, bf16[2048,1024]{1,0:T(8,128)(2,1)} %convolution_convert_fusion.2.lat_ref, bf16[2048,576]{1,0:T(8,128)(2,1)} %get-tuple-element.540.key_ref, f32[2048,32]{1,0:T(8,128)} %get-tuple-element.542.cos_ref, ...), custom_call_target="tpu_custom_call" | custom-call | flops 671088640 | bytes 15728640 | tf_op jit(solution)/shard_map/cond/branch_0_fun/attend/pallas_call | solution.py:533
  788.7 21.1 %conditional.7 = (bf16[2048,2048]{1,0:T(8,128)(2,1)}) conditional(s32[]{:T(128)} %convert_element_type.206, (bf16[2048,768]{1,0:T(8,128)(2,1)}, bf16[768,2048]{1,0:T(8,128)(2,1)}, s32[]{:T(128)}, bf16[2048,704]{0,1:T(8,128)(2,1)}, bf16[704,2048]{1,0:T(8,128)(2,1)}) %tuple.168, () %tuple.70), branch_computations={%region_27.28_spmd, %region_28.29_spmd} | conditional | flops 7926185984 | bytes 39846992 | solution.py:1081
  809.8 87.7 %scatter_result.1 = f32[128,2048]{1,0:T(8,128)} custom-call(bf16[16,128,2048]{2,1,0:T(8,128)(2,1)} %bitcast.57.x_ref), custom_call_target="tpu_custom_call" | custom-call | tf_op jit(solution)/shard_map/scatter_result/pallas_call | solution.py:476
  909.4 12.4 %convolution_bitcast_fusion.2 = f32[2048,1,704]{0,2,1:T(8,128)S(1)} fusion(bf16[2048,2048]{1,0:T(8,128)(2,1)} %bitcast.224, f32[2048,704]{0,1:T(8,128)S(1)} %fusion.64, f32[2048,704]{0,1:T(8,128)} %get-tuple-element.534), kind=kOutput, calls=%fused_computation.28 | convolution fusion | flops 5914230784 | bytes 25690112 | tf_op jit(solution)/shard_map/dot_general | solution.py:59
  921.9 12.5 %convolution_bitcast_fusion.3 = f32[2048,1,704]{0,2,1:T(8,128)} fusion(bf16[2048,2048]{1,0:T(8,128)(2,1)S(1)} %bitcast.229, f32[2048,704]{0,1:T(8,128)} %get-tuple-element.534, f32[2048,704]{0,1:T(8,128)} %copy-done.67, f32[2048,704]{0,1:T(8,128)} %get-tuple-element.535), kind=kOutput, calls=%fused_computation.29 | convolution fusion | flops 5919997952 | bytes 31457280 | tf_op jit(solution)/shard_map/dot_general | solution.py:59
  943.1 20.2 %pair_grad.1 = f32[2048,2,768]{2,1,0:T(2,128)} custom-call(bf16[2048,2048]{1,0:T(8,128)(2,1)} %bitcast.225, bf16[2048,1536]{1,0:T(8,128)(2,1)} %get-tuple-element.344.grad_ref), custom_call_target="tpu_custom_call" | custom-call | flops 12884901888 | bytes 27262976 | tf_op jit(solution)/shard_map/pair_grad/pallas_call | solution.py:871
  973.2 39.3 %attend_back.3 = (bf16[2048,768]{1,0:T(8,128)(2,1)}, bf16[2048,1024]{1,0:T(8,128)(2,1)}, f32[2048,64]{1,0:T(8,128)}) custom-call(bf16[2048,768]{1,0:T(8,128)(2,1)} %get-tuple-element.530.q_ref, bf16[2048,1024]{1,0:T(8,128)(2,1)} %get-tuple-element.531.lat_ref, bf16[2048,576]{1,0:T(8,128)(2,1)} %bitcast.218, ...), custom_call_target="tpu_custom_call" | custom-call | flops 1744830464 | bytes 16777216 | tf_op jit(solution)/shard_map/attend_back/pallas_call | solution.py:599
  1082.2 24.3 %all_gather.10 = f32[128,896]{1,0:T(8,128)} all-gather(f32[8,896]{1,0:T(8,128)S(1)} %reshape.366), channel_id=1, replica_groups=mesh['section'=2,'dp'=4,'expert'=4] {'dp','expert'}, dimensions={0}, use_global_device_ids=true | all-gather | bytes 487424 | tf_op jit(solution)/shard_map/all_gather | solution.py:1118
  (305 shorter events, 351.6 us)
Async XLA Ops:
  7.2 956.1 %all-gather.3.cloned.1.call-start = ((), (), s32[]{:S(2)}) async-start(), calls=%async_computation.1 | async-start | bytes 8912896 | tf_op jit(solution)/shard_map/all_gather | solution.py:1101
  9.0 12.7 %copy-start.42 = (s32[4,128]{1,0:T(4,128)}, s32[4,128]{1,0:T(4,128)S(1)}, u32[]{:S(2)}) copy-start(s32[4,128]{1,0:T(4,128)S(1)} %get-tuple-element.574) | copy-start | bytes 6148
  159.9 97.0 %copy-start.2 = (bf16[1,1,128,2048]{3,2,1,0:T(8,128)(2,1)S(1)}, bf16[1,1,128,2048]{3,2,1,0:T(8,128)(2,1)}, u32[]{:S(2)}) copy-start(bf16[1,1,128,2048]{3,2,1,0:T(8,128)(2,1)} %param.23) | copy-start | bytes 1572868
  159.9 97.0 %collective-permute-start = (bf16[128,2048]{1,0:T(8,128)(2,1)}, bf16[128,2048]{1,0:T(8,128)(2,1)S(1)}, u32[]{:S(2)}, u32[]{:S(2)}) collective-permute-start(bf16[128,2048]{1,0:T(8,128)(2,1)} %add_convert_fusion.1), channel_id=1, source_target_pairs={{0,16},{1,17},{2,18},{3,19},{4,20},{5,21},{6,22},{7,23},{8,24},{9,... | collective-permute-start | bytes 1572872 | tf_op jit(solution)/shard_map/ppermute | solution.py:998
  256.9 353.0 %copy-start.10 = (bf16[128,2048]{1,0:T(8,128)(2,1)}, bf16[128,2048]{1,0:T(8,128)(2,1)S(1)}, u32[]{:S(2)}) copy-start(bf16[128,2048]{1,0:T(8,128)(2,1)S(1)} %collective-permute-done) | copy-start | bytes 1572868
  257.1 352.7 %copy-start.47 = (f32[128]{0:T(128)}, f32[128]{0:T(128)S(1)}, u32[]{:S(2)}) copy-start(f32[128]{0:T(128)S(1)} %get-tuple-element.603) | copy-start | bytes 1540
  257.1 352.7 %copy-start.56 = (f32[128]{0:T(128)}, f32[128]{0:T(128)S(1)}, u32[]{:S(2)}) copy-start(f32[128]{0:T(128)S(1)} %get-tuple-element.602) | copy-start | bytes 1540
  260.2 331.4 %copy-start.50 = (f32[128]{0:T(128)}, f32[128]{0:T(128)S(1)}, u32[]{:S(2)}) copy-start(f32[128]{0:T(128)S(1)} %get-tuple-element.605) | copy-start | bytes 1540
  260.2 331.4 %copy-start.58 = (f32[128]{0:T(128)}, f32[128]{0:T(128)S(1)}, u32[]{:S(2)}) copy-start(f32[128]{0:T(128)S(1)} %get-tuple-element.604) | copy-start | bytes 1540
  326.0 322.6 %copy-start.45 = (f32[128]{0:T(128)}, f32[128]{0:T(128)S(1)}, u32[]{:S(2)}) copy-start(f32[128]{0:T(128)S(1)} %get-tuple-element.607) | copy-start | bytes 1540
  326.0 322.6 %copy-start.52 = (f32[128]{0:T(128)}, f32[128]{0:T(128)S(1)}, u32[]{:S(2)}) copy-start(f32[128]{0:T(128)S(1)} %get-tuple-element.606) | copy-start | bytes 1540
  612.4 23.4 %collective-permute-start.1 = (f32[128,2048]{1,0:T(8,128)S(1)}, f32[128,2048]{1,0:T(8,128)S(1)}, u32[]{:S(2)}, u32[]{:S(2)}) collective-permute-start(f32[128,2048]{1,0:T(8,128)S(1)} %subtract_add_fusion.1), channel_id=1, source_target_pairs={{16,0},{17,1},{18,2},{19,3},{20,4},{21,5},{22,6},{23,7},{24,8},{25... | collective-permute-start | bytes 3145736 | tf_op jit(solution)/shard_map/ppermute | solution.py:1066
  648.6 71.2 %copy-start.60 = (f32[128]{0:T(128)}, f32[128]{0:T(128)S(1)}, u32[]{:S(2)}) copy-start(f32[128]{0:T(128)S(1)} %broadcast_multiply_fusion.3) | copy-start | bytes 1540
  650.9 408.8 %reduce-scatter.2.cloned.1.call-start = ((), (), s32[]{:S(2)}) async-start(), calls=%async_computation.2 | async-start | bytes 3440640 | tf_op jit(solution)/shard_map/reduce_scatter | solution.py:1106
  652.3 67.6 %copy-start.12 = (f32[2048,32]{1,0:T(8,128)S(1)}, f32[2048,32]{1,0:T(8,128)}, u32[]{:S(2)}) copy-start(f32[2048,32]{1,0:T(8,128)} %get-tuple-element.598.sin_ref) | copy-start | bytes 786436
  728.7 21.9 %slice-start.6 = ((s8[8388608]{0:T(1024)(128)(4,1)}), s8[4194304]{0:T(1024)(128)(4,1)S(1)}, s32[]{:S(2)}) async-start(s8[8388608]{0:T(1024)(128)(4,1)} %bitcast.246), calls=%async_computation.10 | async-start | bytes 8388608 | tf_op jit(solution)/shard_map/cond
  736.8 13.7 %slice-start.7 = ((s8[8388608]{0:T(1024)(128)(4,1)}), s8[4194304]{0:T(1024)(128)(4,1)S(1)}, s32[]{:S(2)}) async-start(s8[8388608]{0:T(1024)(128)(4,1)} %bitcast.246), calls=%async_computation.11 | async-start | bytes 8388608 | tf_op jit(solution)/shard_map/cond
  899.6 22.2 %slice-start = ((s8[8388608]{0:T(1024)(128)(4,1)}), s8[4194304]{0:T(1024)(128)(4,1)S(1)}, s32[]{:S(2)}) async-start(s8[8388608]{0:T(1024)(128)(4,1)} %bitcast.227), calls=%async_computation.4 | async-start | bytes 8388608
  1021.6 101.4 %all-gather.5.cloned.1.call-start = ((), (), s32[]{:S(2)}) async-start(), calls=%async_computation.3 | async-start | bytes 2785280 | tf_op jit(solution)/shard_map/all_gather | solution.py:1117
  1021.6 22.8 %slice-start.4 = ((s8[8388608]{0:T(1024)(128)(4,1)}), s8[4194304]{0:T(1024)(128)(4,1)S(1)}, s32[]{:S(2)}) async-start(s8[8388608]{0:T(1024)(128)(4,1)} %bitcast.243), calls=%async_computation.8 | async-start | bytes 8388608
  1044.5 17.5 %copy-start.15 = (f32[128,576]{1,0:T(8,128)S(1)}, f32[128,576]{1,0:T(8,128)}, u32[]{:S(2)}) copy-start(f32[128,576]{1,0:T(8,128)} %copy-done.14) | copy-start | bytes 884740
  1044.5 17.5 %copy-start.40 = (f32[1,512]{1,0:T(1,128)S(1)}, f32[1,512]{1,0:T(1,128)}, u32[]{:S(2)}) copy-start(f32[1,512]{1,0:T(1,128)} %param.29) | copy-start | bytes 6148
  1044.5 17.5 %copy-start.51 = (f32[128]{0:T(128)S(1)}, f32[128]{0:T(128)}, u32[]{:S(2)}) copy-start(f32[128]{0:T(128)} %copy-done.50) | copy-start | bytes 1540
  1044.5 17.7 %copy-start.59 = (f32[128]{0:T(128)S(1)}, f32[128]{0:T(128)}, u32[]{:S(2)}) copy-start(f32[128]{0:T(128)} %copy-done.58) | copy-start | bytes 1540
  (52 other events, 313.8 us)
Sparse Core Ops, SparseCore 0:
  651.0 255.9 all-gather.2
  1021.7 37.9 reduce-scatter.1
  1063.2 45.3 all-gather.4

commit v3 on v2

--- a/solution.py
+++ b/solution.py
@@ -18,33 +18,9 @@
 epsilon = 1e-06
 rope_base = 10000.0
 masked_score = -1e30
-BOTH = ("dp", "expert")
+SECTION, PACKS, MEMBERS = "section", "dp", "expert"
+BOTH = (PACKS, MEMBERS)
 MESH = pl.DeviceIdType.MESH
-IDS = {
-    name: index
-    for index, name in enumerate(
-        (
-            "gather_target",
-            "gather_inputs_first",
-            "gather_ffn_first",
-            "gather_inputs_second",
-            "gather_ffn_second",
-            "gather_mixed",
-            "gather_upstream",
-            "gather_keyed_first",
-            "gather_keyed_second",
-            "scatter_attended_first",
-            "scatter_ffn_first",
-            "scatter_attended_second",
-            "scatter_result",
-            "scatter_ffn_back_second",
-            "scatter_heads_second",
-            "scatter_ffn_back_first",
-        )
-    )
-}
-
-
 def dot(left, right):
     return jnp.dot(left, right, preferred_element_type=jnp.float32)
 
@@ -104,17 +80,17 @@
 
 
 def places(spots):
-    member = lax.axis_index("expert")
-    spot = lax.axis_index("dp") if spots > 1 else 0
+    member = lax.axis_index(MEMBERS)
+    spot = lax.axis_index(PACKS) if spots > 1 else 0
     return spot, member // 2, lax.rem(member, 2)
 
 
 def to_partner(chip, core):
-    return {"expert": chip * 2 + 1 - core}
+    return {MEMBERS: chip * 2 + 1 - core}
 
 
 def to_other(chip, core):
-    return {"expert": (1 - chip) * 2 + core}
+    return {MEMBERS: (1 - chip) * 2 + core}
 
 
 def when(condition, action):
@@ -133,8 +109,8 @@
     signal(to_partner(chip, core))
     signal(to_other(chip, core))
     if spots > 1:
-        pl.when(spot > 0)(lambda: signal({"dp": spot - 1}))
-        pl.when(spot < spots - 1)(lambda: signal({"dp": spot + 1}))
+        pl.when(spot > 0)(lambda: signal({PACKS: spot - 1}))
+        pl.when(spot < spots - 1)(lambda: signal({PACKS: spot + 1}))
         ends = jnp.where(spot > 0, 1, 0) + jnp.where(spot < spots - 1, 1, 0)
         pl.semaphore_wait(barrier, 2 + ends)
     else:
@@ -180,14 +156,14 @@
 
         def up(source, at, unit, reach):
             return remote(
-                source, piece(unit, slot(at, chip, core)), {"dp": spot + 1}, up_out.at[reach, unit], up_in.at[reach, unit]
+                source, piece(unit, slot(at, chip, core)), {PACKS: spot + 1}, up_out.at[reach, unit], up_in.at[reach, unit]
             )
 
         def down(source, at, unit, reach):
             return remote(
                 source,
                 piece(unit, slot(at, chip, core)),
-                {"dp": spot - 1},
+                {PACKS: spot - 1},
                 down_out.at[reach, unit],
                 down_in.at[reach, unit],
             )
@@ -266,18 +242,18 @@
     if active is None:
         run()
     else:
-        pl.when(lax.axis_index("section") == active)(run)
-
-
-def gather_blocks(values, across, name, active=None, into=None, parts=4):
-    axes = BOTH if across else "expert"
-    if lax.axis_size("expert") != 4:
+        pl.when(lax.axis_index(SECTION) == active)(run)
+
+
+def gather_blocks(values, across, number, active=None, into=None, parts=4):
+    axes = BOTH if across else MEMBERS
+    if lax.axis_size(MEMBERS) != 4:
         found = [lax.all_gather(value, axes, axis=0, tiled=True) for value in values]
         if into is None:
             return found
-        chosen = lax.axis_index("section") == active
+        chosen = lax.axis_index(SECTION) == active
         return [jnp.where(chosen, new, old) for new, old in zip(found, into)]
-    spots = lax.axis_size("dp") if across else 1
+    spots = lax.axis_size(PACKS) if across else 1
     cuts = [parts if value.shape[0] % (16 * parts) == 0 else 1 for value in values]
     units = sum(cuts)
     dma = pltpu.SemaphoreType.DMA
@@ -302,8 +278,7 @@
             dma((2, spots, units)),
             dma((2, spots, units)),
         ],
-        compiler_params=pltpu.CompilerParams(collective_id=IDS[name], has_side_effects=True),
-        name=name,
+        compiler_params=pltpu.CompilerParams(collective_id=number, has_side_effects=True),
     )(*values, *held)
     return [out.reshape(-1, out.shape[2]) for out in outs]
 
@@ -326,12 +301,14 @@
     active,
     x_ref,
     o_ref,
+    own_buf,
     pair_buf,
     over_src,
     over_buf,
     line_src,
     up_buf,
     down_buf,
+    own_in,
     pair_out,
     pair_in,
     over_out,
@@ -377,7 +354,7 @@
             return remote(
                 line_src.at[at, cut(part)],
                 up_buf.at[at, cut(part)],
-                {"dp": spot + 1},
+                {PACKS: spot + 1},
                 line_out.at[at, part],
                 up_in.at[at, part],
             )
@@ -386,32 +363,38 @@
             return remote(
                 line_src.at[at, cut(part)],
                 down_buf.at[at, cut(part)],
-                {"dp": spot - 1},
+                {PACKS: spot - 1},
                 line_out.at[at, part],
                 down_in.at[at, part],
             )
 
+        def own(at, c):
+            return pltpu.make_async_copy(x_ref.at[slot(at, c, core)], own_buf.at[at, c], own_in.at[at, c])
+
         for c in (1 - chip, chip):
             for step in range(spots):
+                own(order(step), c).start()
                 for part in range(parts):
                     pair(order(step), c, part).start()
         for step in range(spots):
             at = order(step)
+            own(at, 1 - chip).wait()
             for part in range(parts):
                 pair(at, 1 - chip, part).wait_recv()
                 add_into(
                     over_src.at[at, cut(part)],
-                    [x_ref.at[slot(at, 1 - chip, core), cut(part)], pair_buf.at[at, 1 - chip, cut(part)]],
+                    [own_buf.at[at, 1 - chip, cut(part)], pair_buf.at[at, 1 - chip, cut(part)]],
                     rows,
                 )
                 over(at, part).start()
         for step in range(spots):
             at = order(step)
+            own(at, chip).wait()
             for part in range(parts):
                 pair(at, chip, part).wait_recv()
                 over(at, part).wait_recv()
                 base = [
-                    x_ref.at[slot(at, chip, core), cut(part)],
+                    own_buf.at[at, chip, cut(part)],
                     pair_buf.at[at, chip, cut(part)],
                     over_buf.at[at, cut(part)],
                 ]
@@ -462,29 +445,31 @@
     if active is None:
         run()
     else:
-        pl.when(lax.axis_index("section") == active)(run)
-
-
-def scatter_blocks(partial, across, name, active=None, parts=4):
-    if lax.axis_size("expert") != 4:
-        axes = BOTH if across else "expert"
+        pl.when(lax.axis_index(SECTION) == active)(run)
+
+
+def scatter_blocks(partial, across, number, active=None, parts=4):
+    if lax.axis_size(MEMBERS) != 4:
+        axes = BOTH if across else MEMBERS
         return lax.psum_scatter(partial, axes, scatter_dimension=0, tiled=True).astype(jnp.float32)
-    spots = lax.axis_size("dp") if across else 1
+    spots = lax.axis_size(PACKS) if across else 1
     rows, width = partial.shape[0] // (spots * 4), partial.shape[1]
     dma = pltpu.SemaphoreType.DMA
     hold = lambda *lead: pltpu.VMEM((*lead, rows, width), partial.dtype)
     return pl.pallas_call(
         functools.partial(scatter_kernel, spots, parts, active),
         out_shape=jax.ShapeDtypeStruct((rows, width), jnp.float32),
-        in_specs=[pl.BlockSpec(memory_space=pltpu.VMEM)],
+        in_specs=[pl.BlockSpec(memory_space=pl.ANY)],
         out_specs=pl.BlockSpec(memory_space=pltpu.VMEM),
         scratch_shapes=[
+            hold(spots, 2),
             hold(spots, 2),
             hold(spots),
             hold(spots),
             hold(spots),
             hold(spots),
             hold(spots),
+            dma((spots, 2)),
             dma((spots, 2, parts)),
             dma((spots, 2, parts)),
             dma((spots, parts)),
@@ -493,8 +478,7 @@
             dma((spots, parts)),
             dma((spots, parts)),
         ],
-        compiler_params=pltpu.CompilerParams(collective_id=IDS[name], has_side_effects=True),
-        name=name,
+        compiler_params=pltpu.CompilerParams(collective_id=number, has_side_effects=True),
     )(partial.reshape(spots * 4, rows, width))
 
 
@@ -641,7 +625,6 @@
     own_ref,
     in_ref,
     out_w_ref,
-    router_ref,
     shared_in_ref,
     shared_out_ref,
     pre_ref,
@@ -652,14 +635,14 @@
 ):
     units = gated_ref.shape[1]
     x = x_ref[...]
-    logits = dot(x, router_ref[...])
+    pre = dot(x, in_ref[...])
+    logits = pre[:, 2 * units : 2 * units + own_ref.shape[1]]
     powers = jnp.exp(logits - jnp.max(logits, axis=1, keepdims=True))
     prob = powers / jnp.sum(powers, axis=1, keepdims=True)
     prob_ref[...] = prob
     gate = jnp.sum(prob * own_ref[...], axis=1, keepdims=True) * routed_ref[...]
-    pre = dot(x, in_ref[...])
-    pre_ref[...] = bf16(pre)
-    gated = bf16(gate * gated_hidden(pre[:, :units], pre[:, units:]))
+    pre_ref[...] = bf16(pre[:, : 2 * units])
+    gated = bf16(gate * gated_hidden(pre[:, :units], pre[:, units : 2 * units]))
     gated_ref[...] = gated
     tile = pl.program_id(0)
     inside = (tile >= here_ref[0]) & (tile < here_ref[1])
@@ -706,7 +689,8 @@
 
 
 def experts(x, routed, own_column, weights, here, pack_rows, full):
-    expert_in, expert_out, router, shared_in, shared_out = weights
+    expert_in, expert_out, shared_in, shared_out = weights
+    routes_width = own_column.shape[1]
     rows, width = x.shape
     tile = tile_rows(pack_rows)
     units, half = expert_out.shape[0], shared_out.shape[0]
@@ -715,13 +699,13 @@
     out_shape = [
         shape((rows, 2 * units), jnp.bfloat16),
         shape((rows, units), jnp.bfloat16),
-        shape((rows, router.shape[1]), jnp.float32),
+        shape((rows, routes_width), jnp.float32),
         shape((2, pack_rows, half), jnp.bfloat16),
     ]
     out_specs = [
         block(2 * units),
         block(units),
-        block(router.shape[1]),
+        block(routes_width),
         pl.BlockSpec((2, tile, half), lambda i, here: (0, inner(i, here), 0)),
     ]
     if full:
@@ -738,7 +722,6 @@
                 whole(own_column),
                 whole(expert_in),
                 whole(expert_out),
-                whole(router),
                 whole(shared_in),
                 whole(shared_out),
             ],
@@ -749,7 +732,7 @@
         cost_estimate=pl.CostEstimate(
             flops=2 * rows * width * units * 3, bytes_accessed=rows * width * 4, transcendentals=rows * units
         ),
-    )(here, x, routed, own_column, expert_in, expert_out, router, shared_in, shared_out)
+    )(here, x, routed, own_column, expert_in, expert_out, shared_in, shared_out)
 
 
 def experts_back_kernel(
@@ -761,13 +744,13 @@
     own_ref,
     in_ref,
     out_w_ref,
-    router_ref,
     shared_pre_ref,
     shared_in_ref,
     shared_out_ref,
     grad_pre_ref,
     moved_ref,
     partial_ref,
+    joined_ref,
 ):
     units = out_w_ref.shape[0]
     grad = grad_ref[...]
@@ -781,9 +764,12 @@
     moved_ref[...] = moved
     grad_logits = bf16(moved * (own_ref[...] - prob))
     scaled = own_prob * grad_units
-    grad_pre_ref[:, :units] = bf16(scaled * up * slope)
-    grad_pre_ref[:, units:] = bf16(scaled * act)
-    base = dot_t(grad_pre_ref[...], in_ref[...]) + dot_t(grad_logits, router_ref[...])
+    joined_ref[:, :units] = bf16(scaled * up * slope)
+    joined_ref[:, units : 2 * units] = bf16(scaled * act)
+    joined_ref[:, 2 * units :] = jnp.zeros_like(joined_ref[:, 2 * units :])
+    joined_ref[:, 2 * units : 2 * units + own_ref.shape[1]] = grad_logits
+    grad_pre_ref[...] = joined_ref[:, : 2 * units]
+    base = dot_t(joined_ref[...], in_ref[...])
     tile = pl.program_id(0)
     inside = (tile >= here_ref[0]) & (tile < here_ref[1])
     half = shared_out_ref.shape[0]
@@ -804,7 +790,8 @@
 
 
 def experts_back(grad, stored, routed, own_column, weights, here, pack_rows):
-    expert_in, expert_out, router, shared_in, shared_out = weights
+    expert_in, expert_out, shared_in, shared_out = weights
+    routes_width = own_column.shape[1]
     rows, width = grad.shape
     tile = tile_rows(pack_rows)
     units, half = expert_out.shape[0], shared_out.shape[0]
@@ -818,17 +805,17 @@
             in_specs=[
                 block(width),
                 block(2 * units),
-                block(router.shape[1]),
+                block(routes_width),
                 block(1),
                 whole(own_column),
                 whole(expert_in),
                 whole(expert_out),
-                whole(router),
                 pl.BlockSpec((2, tile, half), lambda i, here: (0, inner(i, here), 0)),
                 whole(shared_in),
                 whole(shared_out),
             ],
             out_specs=[block(2 * units), block(1), block(width)],
+            scratch_shapes=[pltpu.VMEM((tile, expert_in.shape[1]), jnp.bfloat16)],
         ),
         out_shape=[
             shape((rows, 2 * units), jnp.bfloat16),
@@ -848,7 +835,6 @@
         own_column,
         expert_in,
         expert_out,
-        router,
         stored["shared_pre"],
         shared_in,
         shared_out,
@@ -889,6 +875,7 @@
         lambda out_ref: None,
         out_shape=jax.ShapeDtypeStruct(shape, dtype),
         out_specs=pl.BlockSpec(memory_space=pl.ANY),
+        compiler_params=pltpu.CompilerParams(has_side_effects=True),
         name="blank",
     )()
 
@@ -919,17 +906,24 @@
     shared_half = shared_out.shape[0]
     units = expert_out.shape[0]
     shared_in_t = jnp.transpose(shared_in[0], (1, 2, 0)).reshape(2 * shared_half, width)
-    expert_in = expert_in.reshape(width, 2 * units)
-    weights = (expert_in, expert_out, router_weight, shared_in_t, shared_out)
-
-    packs, members = lax.axis_size("dp"), lax.axis_size("expert")
+    experts_count = router_weight.shape[1]
+    joined_in = jnp.concatenate(
+        [
+            expert_in.reshape(width, 2 * units),
+            router_weight,
+            jnp.zeros((width, -experts_count % 128), jnp.bfloat16),
+        ],
+        axis=1,
+    )
+    weights = (joined_in, expert_out, shared_in_t, shared_out)
+
+    packs, members = lax.axis_size(PACKS), lax.axis_size(MEMBERS)
     count = packs * members
-    pack, member = lax.axis_index("dp"), lax.axis_index("expert")
+    pack, member = lax.axis_index(PACKS), lax.axis_index(MEMBERS)
     me = pack * members + member
-    is_first = lax.axis_index("section") == 0
+    is_first = lax.axis_index(SECTION) == 0
     pack_rows = members * rows
     top = routes.shape[3]
-    experts_count = router_weight.shape[1]
     here = tile_here(pack, pack_rows)
 
     def own_pack(value):
@@ -981,32 +975,32 @@
     fresh = boundary[0, 0].astype(jnp.float32)
 
     normed, keyed, _ = inputs_of(fresh)
-    pack_inputs = gather_blocks([normed, keyed], False, "gather_inputs_first", 0)
+    pack_inputs = gather_blocks([normed, keyed], False, 1, 0)
     attended, _, _ = heads_of(*pack_inputs, tables_pack)
     mixed_first = fresh + scatter_blocks(
-        bf16(dot(attended, output_weight)), False, "scatter_attended_first", 0
+        bf16(dot(attended, output_weight)), False, 9, 0
     )
     ffn_all, layout_all = gather_blocks(
-        [bf16(rms_forward(mixed_first, ffn_gain)[0]), layout], True, "gather_ffn_first", 0
+        [bf16(rms_forward(mixed_first, ffn_gain)[0]), layout], True, 2, 0
     )
     *_, partial = experts(ffn_all, routed_of(layout_all), own_column, weights, here, pack_rows, True)
-    result_first = mixed_first + scatter_blocks(partial, True, "scatter_ffn_first", 0)
+    result_first = mixed_first + scatter_blocks(partial, True, 10, 0)
     target_all, layout_all = gather_blocks(
-        [boundary[0, 0], layout], True, "gather_target", 1, [blank(ffn_all.shape, jnp.bfloat16), layout_all]
+        [boundary[0, 0], layout], True, 0, 1, [blank(ffn_all.shape, jnp.bfloat16), layout_all]
     )
     sent, target_all, layout_all = lax.optimization_barrier((bf16(result_first), target_all, layout_all))
-    inbound = lax.ppermute(sent, "section", [(0, 1)])
+    inbound = lax.ppermute(sent, SECTION, [(0, 1)])
     routed = routed_of(layout_all)
     tables_all = tables_of(layout_all.reshape(count, -1)[:, rows * top : rows * top + lengths.shape[3]])
 
     hidden = jnp.where(is_first, fresh, inbound.astype(jnp.float32))
     normed, keyed, (compressed, scale_attn, scale_latent) = inputs_of(hidden)
-    normed_pack, keyed_pack = gather_blocks([normed, keyed], False, "gather_inputs_second", 1, pack_inputs)
+    normed_pack, keyed_pack = gather_blocks([normed, keyed], False, 3, 1, pack_inputs)
     attended, query, latent = heads_of(normed_pack, keyed_pack, tables_pack)
-    mixed = hidden + scatter_blocks(bf16(dot(attended, output_weight)), False, "scatter_attended_second", 1)
+    mixed = hidden + scatter_blocks(bf16(dot(attended, output_weight)), False, 11, 1)
     mixed = jnp.where(is_first, mixed_first, mixed)
     ffn32, scale_ffn = rms_forward(mixed, ffn_gain)
-    (ffn_all,) = gather_blocks([bf16(ffn32)], True, "gather_ffn_second", 1, [ffn_all])
+    (ffn_all,) = gather_blocks([bf16(ffn32)], True, 4, 1, [ffn_all])
     pre, gated, prob, shared_pre = experts(ffn_all, routed, own_column, weights, here, pack_rows, False)
     stored = dict(pre=pre, prob=prob, shared_pre=shared_pre)
 
@@ -1042,20 +1036,20 @@
     grad_pre_second, moved_second, partial = experts_back(
         target_all, stored, routed, own_column, weights, here, pack_rows
     )
-    grad_ffn_second = scatter_blocks(partial, True, "scatter_ffn_back_second", 1)
+    grad_ffn_second = scatter_blocks(partial, True, 13, 1)
     grad_mixed = fresh + rms_backward(mixed, scale_ffn, ffn_gain, grad_ffn_second)[0]
-    (grad_mixed_pack,) = gather_blocks([bf16(grad_mixed)], False, "gather_mixed", 1)
+    (grad_mixed_pack,) = gather_blocks([bf16(grad_mixed)], False, 5, 1)
     own_second = scatter_blocks(
         heads_back(
             *attend_back(query, latent, keyed_pack, bf16(dot_t(grad_mixed_pack, output_weight)), tables_pack)
         ),
         False,
-        "scatter_heads_second",
+        14,
         1,
     )
     grad_second = grad_mixed + latent_back(own_second)[1]
 
-    all_inputs = gather_blocks([normed, keyed], True, "gather_keyed_first", 0)
+    all_inputs = gather_blocks([normed, keyed], True, 7, 0)
     prepared = lax.cond(
         is_first,
         prepare,
@@ -1063,10 +1057,10 @@
         *all_inputs,
     )
     grad_second, prepared, all_inputs = lax.optimization_barrier((grad_second, prepared, all_inputs))
-    downbound = lax.ppermute(grad_second, "section", [(1, 0)])
+    downbound = lax.ppermute(bf16(grad_second), SECTION, [(1, 0)]).astype(jnp.float32)
 
     normed_late, keyed_late, gated_late, _ = lax.optimization_barrier((normed, keyed, gated, grad_second))
-    normed_all, keyed_all = gather_blocks([normed_late, keyed_late], True, "gather_keyed_second", 1, all_inputs)
+    normed_all, keyed_all = gather_blocks([normed_late, keyed_late], True, 8, 1, all_inputs)
     attended_all, query_all, latent_all, shared_gate, shared_up, shared_hid = lax.cond(
         is_first, lambda *values: values[2:], lambda *values: prepare(*values[:2]), normed_all, keyed_all, *prepared
     )
@@ -1081,10 +1075,10 @@
     partial = lax.cond(
         is_first, lambda *_: blank((count * rows, width), jnp.bfloat16), finish, gated_late, shared_hid
     )
-    result = mixed + scatter_blocks(partial, True, "scatter_result", 1)
+    result = mixed + scatter_blocks(partial, True, 12, 1)
 
     upstream = jnp.where(is_first, downbound, fresh)
-    (upstream_all,) = gather_blocks([bf16(upstream)], True, "gather_upstream", 0, [target_all])
+    (upstream_all,) = gather_blocks([bf16(upstream)], True, 6, 0, [target_all])
     grad_pre, moved, partial = lax.cond(
         is_first,
         lambda upstream_all, *_: tuple(
@@ -1095,7 +1089,7 @@
         grad_pre_second,
         moved_second,
     )
-    grad_ffn = jnp.where(is_first, scatter_blocks(partial, True, "scatter_ffn_back_first", 0), grad_ffn_second)
+    grad_ffn = jnp.where(is_first, scatter_blocks(partial, True, 15, 0), grad_ffn_second)
     grad_mixed_norm, grad_ffn_gain = rms_backward(mixed, scale_ffn, ffn_gain, grad_ffn)
     grad_mixed = upstream + grad_mixed_norm
     grad_mixed_all = lax.all_gather(bf16(grad_mixed), BOTH, axis=0, tiled=True)
@@ -1105,7 +1099,7 @@
     )
     own = lax.psum_scatter(
         heads_back(own_pack(grad_query), own_pack(grad_latent_heads), own_pack(grad_shared_key)),
-        "expert",
+        MEMBERS,
         scatter_dimension=0,
         tiled=True,
     ).astype(jnp.float32)
@@ -1114,15 +1108,17 @@
 
     small = jnp.concatenate([grad_attn_gain, grad_latent_gain, grad_ffn_gain, moved[:, 0]])
     small = jnp.pad(small, (0, -small.shape[0] % 1024)).reshape(8, -1)
-    grad_compressed_all = lax.all_gather(grad_compressed, BOTH, axis=0, tiled=True)
-    small_all = lax.all_gather(small, BOTH, axis=0, tiled=True).reshape(count, -1)
+    grad_compressed_all, small_all = gather_blocks([grad_compressed, small], True, 16)
+    small_all = small_all.reshape(count, -1)
     gains = jnp.sum(small_all[:, : 2 * width + LAT], axis=0)
     moved_all = small_all[:, 2 * width + LAT : 2 * width + LAT + count * rows].T
     grad_logits = bf16(moved_all - prob * jnp.sum(moved_all, axis=1, keepdims=True))
     left, right = gated_back(
         shared_gate.astype(jnp.float32), shared_up.astype(jnp.float32), dot_t(upstream_all, shared_out)
     )
-    grad_shared_in = jnp.stack([t_dot(ffn_all, left), t_dot(ffn_all, right)], axis=1)
+    grad_shared_in = lax.dot_general(
+        jnp.stack([left, right]), ffn_all, (((1,), (0,)), ((), ())), preferred_element_type=jnp.float32
+    )
     ends = jnp.where(is_first, grad_hidden, result)
     return (
         ends[None, None],
@@ -1134,7 +1130,7 @@
         t_dot(attended_all, grad_mixed_all)[None],
         gains[width + LAT :][None],
         t_dot(ffn_all, grad_logits)[None],
-        grad_shared_in[None],
+        jnp.transpose(grad_shared_in, (2, 0, 1))[None],
         t_dot(shared_hid, upstream_all)[None],
         pair_grad(ffn_all, grad_pre)[None, None],
         t_dot(gated, upstream_all)[None, None],
@@ -1146,36 +1142,36 @@
         body,
         mesh=mesh,
         in_specs=(
-            P("section", None, BOTH, None),
-            P(None, "dp", None, None),
-            P("section", None, BOTH, None),
-            P("section", None),
-            P("section", None, "expert"),
-            P("section", None, None),
-            P("section", None),
-            P("section", None, "expert"),
-            P("section", "expert", None),
-            P("section", None),
-            P("section", None, None),
-            P("section", None, None, "expert"),
-            P("section", "expert", None),
-            P("section", BOTH, None, None, None),
-            P("section", BOTH, None, None),
+            P(SECTION, None, BOTH, None),
+            P(None, PACKS, None, None),
+            P(SECTION, None, BOTH, None),
+            P(SECTION, None),
+            P(SECTION, None, MEMBERS),
+            P(SECTION, None, None),
+            P(SECTION, None),
+            P(SECTION, None, MEMBERS),
+            P(SECTION, MEMBERS, None),
+            P(SECTION, None),
+            P(SECTION, None, None),
+            P(SECTION, None, None, MEMBERS),
+            P(SECTION, MEMBERS, None),
+            P(SECTION, BOTH, None, None, None),
+            P(SECTION, BOTH, None, None),
         ),
         out_specs=(
-            P("section", None, BOTH, None),
-            P("section", None),
-            P("section", None, "expert"),
-            P("section", None, None),
-            P("section", None),
-            P("section", None, "expert"),
-            P("section", "expert", None),
-            P("section", None),
-            P("section", None, None),
-            P("section", None, None, "expert"),
-            P("section", "expert", None),
-            P("section", BOTH, None, None, None),
-            P("section", BOTH, None, None),
+            P(SECTION, None, BOTH, None),
+            P(SECTION, None),
+            P(SECTION, None, MEMBERS),
+            P(SECTION, None, None),
+            P(SECTION, None),
+            P(SECTION, None, MEMBERS),
+            P(SECTION, MEMBERS, None),
+            P(SECTION, None),
+            P(SECTION, None, None),
+            P(SECTION, None, None, MEMBERS),
+            P(SECTION, MEMBERS, None),
+            P(SECTION, BOTH, None, None, None),
+            P(SECTION, BOTH, None, None),
         ),
         check_vma=False,
     )

time: 1150 us -> 1100 us (0.957)
  blocking collectives: 24.3 us -> 0 us
  waiting for transfers between devices: 108 us -> 88.4 us
    pallas_call x9 -> x10, Pallas kernels: 223 us -> 256 us  [gather_blocks(): pl.pallas_call(functools.partial(gather_kernel, spots, cuts, active), out...]
    pallas_call x7, Pallas kernels: 197 us -> 166 us  [scatter_blocks(): pl.pallas_call(functools.partial(scatter_kernel, spots, parts, active), o...]
    dot_general x9 -> x7, matrix products: 89.1 us -> 63.3 us  [t_dot(): lax.dot_general(left, right, (((0,), (0,)), ((), ())), preferred_element_...]
    all_gather x1 -> x0, blocking collectives: 24.3 us -> none  [body(): lax.all_gather(small, BOTH, axis=0, tiled=True).reshape(count, -1)]
    dot_general x0 -> x1, matrix products: none -> 17.5 us  [body(): lax.dot_general(jnp.stack([left, right]), ffn_all, (((1,), (0,)), ((), ()...]
    ppermute x2, waiting for transfers between devices: 102 us -> 88.3 us  [the longest x1 84.5 us: body(): inbound = lax.ppermute(sent, SECTION, [(0, 1)])]
  transfers between devices with their start and end apart: 5 -> 4, of which waited for: 3 -> 2; matrix products, arithmetic and copies ran while one was open for 16% -> 14% of each run, Pallas kernels for 18% -> 17%
where the time goes in v3:
time: 1100 us; the launch traced here: 1090 us
  Pallas kernels  659 us (60%)
  matrix products  206 us (19%)
  waiting for transfers between devices  88.4 us (8%)
  local copies, waits for them, and re-layouts  61.8 us (6%)
  other arithmetic  51 us (5%)
  between operations  15.8 us (1%)
    pallas_call x10, Pallas kernels, gather_blocks(): pl.pallas_call(functools.partial(gather_kernel, spots, cuts, active), out...  256 us
    pallas_call x7, Pallas kernels, scatter_blocks(): pl.pallas_call(functools.partial(scatter_kernel, spots, parts, active), o...  166 us
    ppermute x1, waiting for transfers between devices, body(): inbound = lax.ppermute(sent, SECTION, [(0, 1)])  84.5 us
    pallas_call x2, Pallas kernels, experts(): pl.pallas_call(functools.partial(experts_kernel, full), grid_spec=pltpu.P...  73.9 us
    dot_general x11, matrix products, dot_t(): lax.dot_general(left, right, (((1,), (1,)), ((), ())), preferred_element_...  65.5 us
    dot_general x7, matrix products, t_dot(): lax.dot_general(left, right, (((0,), (0,)), ((), ())), preferred_element_...  63.3 us
    dot_general x12, matrix products, dot(): return jnp.dot(left, right, preferred_element_type=jnp.float32)  59.7 us
    pallas_call x2, Pallas kernels, attend_back(): pl.pallas_call(functools.partial(attend_back_kernel, heads), grid=(count,...  50.8 us
  transfers between devices with their start and end apart: 4, of which 2 were waited for; matrix products, arithmetic and copies ran while one was open for 14% of the time, Pallas kernels for 17%

profile of v3, /device:TPU:3, one launch (start us, length us, event | category | flops | bytes accessed | tf_op | source)
XLA Modules:
  0.0 1092.7 jit_solution(4536897774946582639)
XLA Ops:
  70.8 41.7 %experts_full.1 = (bf16[2048,1536]{1,0:T(8,128)(2,1)}, bf16[2048,768]{1,0:T(8,128)(2,1)}, f32[2048,16]{1,0:T(8,128)}, bf16[2,512,704]{2,1,0:T(8,128)(2,1)}, bf16[2048,2048]{1,0:T(8,128)(2,1)}) custom-call(s32[2]{0:T(128)S(1)} %pad_add_fusion.1.here_ref, bf16[2048,2048]{1,0:T(8,128)(2,1)} %bitcast.228, f32[2048,1]{1,0:T(8,128)} %copy.144.routed_ref, ...), custom_call_target="tpu_custom_call" | custom-call | flops 19327352832 | bytes 16777216 | tf_op jit(solution)/shard_map/experts_full/pallas_call | solution.py:714
  117.3 62.7 %shard_map.250 = (bf16[16,128,2048]{2,1,0:T(8,128)(2,1)}, s32[16,8,128]{2,1,0:T(8,128)}) custom-call(bf16[128,2048]{1,0:T(8,128)(2,1)} %bitcast.215, s32[8,128]{1,0:T(8,128)} %pad_bitcast_fusion.refs_1_, bf16[16,128,2048]{2,1,0:T(8,128)(2,1)} %bitcast.216, s32[16,8,128]{2,1,0:T(8,128)} %get-tuple-element.289.refs_3_), custom_call_target="tpu_custom_call", output_to_operand_aliasing={{0}: (2, {}), {1}: (3, {})} | custom-call | tf_op jit(solution)/shard_map/pallas_call | solution.py:263
  192.8 84.5 %collective-permute-done = bf16[128,2048]{1,0:T(8,128)(2,1)S(1)} collective-permute-done((bf16[128,2048]{1,0:T(8,128)(2,1)}, bf16[128,2048]{1,0:T(8,128)(2,1)S(1)}, u32[]{:S(2)}, u32[]{:S(2)}) %collective-permute-start) | collective-permute-done | bytes 524320 | tf_op jit(solution)/shard_map/ppermute | solution.py:992
  281.5 21.4 %shard_map.251 = (bf16[4,128,2048]{2,1,0:T(8,128)(2,1)}, bf16[4,128,576]{2,1,0:T(8,128)(2,1)}) custom-call(bf16[128,2048]{1,0:T(8,128)(2,1)} %copy-done.13, bf16[128,576]{1,0:T(8,128)(2,1)} %pad_maximum_fusion.3.refs_1_, bf16[4,128,2048]{2,1,0:T(8,128)(2,1)} %get-tuple-element.285.refs_2_, ...), custom_call_target="tpu_custom_call", output_to_operand_aliasing={{0}: (2, {}), {1}: (3, {})} | custom-call | tf_op jit(solution)/shard_map/pallas_call | solution.py:263
  326.4 16.6 %shard_map.252 = f32[128,2048]{1,0:T(8,128)} custom-call(bf16[4,128,2048]{2,1,0:T(8,128)(2,1)} %bitcast.259), custom_call_target="tpu_custom_call" | custom-call | tf_op jit(solution)/shard_map/pallas_call | solution.py:459
  346.9 52.4 %shard_map.253 = bf16[16,128,2048]{2,1,0:T(8,128)(2,1)} custom-call(bf16[128,2048]{1,0:T(8,128)(2,1)} %multiply_convert_fusion.4.refs_0_, bf16[16,128,2048]{2,1,0:T(8,128)(2,1)} %get-tuple-element.288.refs_1_), custom_call_target="tpu_custom_call", output_to_operand_aliasing={{}: (1, {})} | custom-call | tf_op jit(solution)/shard_map/pallas_call | solution.py:263
  399.3 32.2 %experts_inner.1 = (bf16[2048,1536]{1,0:T(8,128)(2,1)}, bf16[2048,768]{1,0:T(8,128)(2,1)}, f32[2048,16]{1,0:T(8,128)}, bf16[2,512,704]{2,1,0:T(8,128)(2,1)}) custom-call(s32[2]{0:T(128)S(1)} %pad_add_fusion.1.here_ref, bf16[2048,2048]{1,0:T(8,128)(2,1)} %bitcast.229, f32[2048,1]{1,0:T(8,128)} %copy.149.routed_ref, f32[1,16]{1,0:T(1,128)S(1)} %compare_convert_fusion.own_ref, ...), custom_call_target="tpu_custom_call" | custom-call | flops 19327352832 | bytes 16777216 | tf_op jit(solution)/shard_map/experts_inner/pallas_call | solution.py:714
  431.5 48.6 %experts_back.3 = (bf16[2048,1536]{1,0:T(8,128)(2,1)}, f32[2048,1]{1,0:T(8,128)}, bf16[2048,2048]{1,0:T(8,128)(2,1)}) custom-call(s32[2]{0:T(128)S(1)} %pad_add_fusion.1.here_ref, bf16[2048,2048]{1,0:T(8,128)(2,1)} %bitcast.217, bf16[2048,1536]{1,0:T(8,128)(2,1)} %get-tuple-element.299.pre_ref, f32[2048,16]{1,0:T(8,128)} %get-tuple-element.300.prob_ref, ...), custom_call_target="tpu_custom_call" | custom-call | flops 19327352832 | bytes 16777216 | tf_op jit(solution)/shard_map/experts_back/pallas_call | solution.py:800
  480.1 51.8 %shard_map.254 = f32[128,2048]{1,0:T(8,128)} custom-call(bf16[16,128,2048]{2,1,0:T(8,128)(2,1)} %bitcast.245), custom_call_target="tpu_custom_call" | custom-call | tf_op jit(solution)/shard_map/pallas_call | solution.py:459
  536.4 17.0 %shard_map.255 = bf16[4,128,2048]{2,1,0:T(8,128)(2,1)} custom-call(bf16[128,2048]{1,0:T(8,128)(2,1)} %fusion.84.refs_0_), custom_call_target="tpu_custom_call" | custom-call | tf_op jit(solution)/shard_map/pallas_call | solution.py:263
  576.4 20.3 %shard_map.256 = f32[128,2624]{1,0:T(8,128)} custom-call(bf16[4,128,2624]{2,1,0:T(8,128)(2,1)} %pad_maximum_fusion.x_ref), custom_call_target="tpu_custom_call" | custom-call | tf_op jit(solution)/shard_map/pallas_call | solution.py:459
  602.9 14.2 %conditional.4 = (bf16[2048,512]{1,0:T(8,128)(2,1)}, bf16[2048,768]{1,0:T(8,128)(2,1)}, bf16[2048,1024]{1,0:T(8,128)(2,1)}, bf16[2048,704]{0,1:T(8,128)(2,1)}, b...) conditional(s32[]{:T(128)} %convert_element_type.212, () %tuple.61, (bf16[2048,2048]{1,0:T(8,128)(2,1)}, ...), branch_computations={%region_17.18_spmd, %region_18.19_spmd} | conditional | flops 21085814784 | bytes 165429392 | solution.py:1053
  643.9 67.5 %shard_map.260 = (bf16[16,128,2048]{2,1,0:T(8,128)(2,1)}, bf16[16,128,576]{2,1,0:T(8,128)(2,1)}) custom-call(bf16[128,2048]{1,0:T(8,128)(2,1)} %copy-done.13, bf16[128,576]{1,0:T(8,128)(2,1)} %pad_maximum_fusion.3.refs_1_, bf16[16,128,2048]{2,1,0:T(8,128)(2,1)} %get-tuple-element.307, ...), custom_call_target="tpu_custom_call", output_to_operand_aliasing={{0}: (2, {}), {1}: (3, {})} | custom-call | tf_op jit(solution)/shard_map/pallas_call | solution.py:263
  711.4 68.8 %conditional.6 = (bf16[2048,512]{1,0:T(8,128)(2,1)}, bf16[2048,768]{1,0:T(8,128)(2,1)}, bf16[2048,1024]{1,0:T(8,128)(2,1)}, bf16[2048,704]{0,1:T(8,128)(2,1)}, f32[2048,704]{0,1:T(8,128)}, /*index=5*/f32[2048,704]{0,1:T(8,128)}) conditional(s32[]{:T(128)} %convert_element_type.212, (bf16[2048,2048]{1,0:T(8,128)(2,1)}, ...), branch_computations={%region_22.23_spmd.clone, %region_23.24_spmd.clone} | conditional | flops 21088698368 | bytes 171196560 | solution.py:1064
  728.6 13.7 %convert_convert_fusion = (f32[2048,704]{0,1:T(8,128)}, bf16[2048,704]{0,1:T(8,128)(2,1)}, f32[2048,704]{0,1:T(8,128)}) fusion(f32[2048,704]{0,1:T(8,128)} %fusion.10, bf16[2048,2048]{1,0:T(8,128)(2,1)S(1)} %copy-done.8, bf16[1408,2048]{1,0:T(8,128)(2,1)} %get-tuple-element.543), kind=kOutput, calls=%fused_computation.14 | convolution fusion | flops 5919997952 | bytes 31457280 | tf_op jit(solution)/shard_map/cond/branch_0_fun/dot_general | solution.py:29
  752.8 27.3 %attend.9 = (bf16[2048,512]{1,0:T(8,128)(2,1)}, bf16[2048,768]{1,0:T(8,128)(2,1)}) custom-call(f32[2048,768]{1,0:T(8,128)} %fusion.89.q_ref, bf16[2048,1024]{1,0:T(8,128)(2,1)} %convolution_convert_fusion.2.lat_ref, bf16[2048,576]{1,0:T(8,128)(2,1)} %get-tuple-element.537.key_ref, f32[2048,32]{1,0:T(8,128)} %get-tuple-element.539.cos_ref, ...), custom_call_target="tpu_custom_call" | custom-call | flops 671088640 | bytes 15728640 | tf_op jit(solution)/shard_map/cond/branch_0_fun/attend/pallas_call | solution.py:517
  780.3 21.1 %conditional.7 = (bf16[2048,2048]{1,0:T(8,128)(2,1)}) conditional(s32[]{:T(128)} %convert_element_type.212, (bf16[2048,768]{1,0:T(8,128)(2,1)}, bf16[768,2048]{1,0:T(8,128)(2,1)}, s32[]{:T(128)}, bf16[2048,704]{0,1:T(8,128)(2,1)}, bf16[704,2048]{1,0:T(8,128)(2,1)}) %tuple.165, () %tuple.70), branch_computations={%region_27.28_spmd, %region_28.29_spmd} | conditional | flops 7926185984 | bytes 39846992 | solution.py:1075
  801.4 71.7 %shard_map.261 = f32[128,2048]{1,0:T(8,128)} custom-call(bf16[16,128,2048]{2,1,0:T(8,128)(2,1)} %bitcast.57.x_ref), custom_call_target="tpu_custom_call" | custom-call | tf_op jit(solution)/shard_map/pallas_call | solution.py:459
  874.7 12.3 %convolution_bitcast_fusion = f32[1,1,768,2048]{3,2,1,0:T(8,128)} fusion(bf16[2048,768]{1,0:T(8,128)(2,1)} %get-tuple-element.337, bf16[2048,2048]{1,0:T(8,128)(2,1)} %bitcast.219), kind=kOutput, calls=%fused_computation.30 | convolution fusion | flops 6442450944 | bytes 17825792 | tf_op jit(solution)/shard_map/dot_general | solution.py:35
  897.3 13.6 %fusion.27 = (bf16[1,2048,704]{1,2,0:T(8,128)(2,1)}, bf16[1,2048,704]{1,2,0:T(8,128)(2,1)}) fusion(f32[2048,704]{0,1:T(8,128)} %get-tuple-element.531, f32[2048,704]{0,1:T(8,128)} %get-tuple-element.532, bf16[2048,2048]{1,0:T(8,128)(2,1)S(1)} %bitcast.223, bf16[1,704,2048]{2,1,0:T(8,128)(2,1)} %param.35), kind=kOutput, calls=%fused_computation.43 | convolution fusion | flops 5924323328 | bytes 28573696 | tf_op jit(solution)/shard_map/dot_general | solution.py:29
  910.9 17.5 %fusion.18 = f32[1,2048,2,704]{1,3,2,0:T(8,128)} fusion(bf16[2048,2048,1]{1,0,2:T(8,128)(2,1)S(1)} %bitcast.236, bf16[1,2048,704]{1,2,0:T(8,128)(2,1)} %get-tuple-element.584, bf16[1,2048,704]{1,2,0:T(8,128)(2,1)} %get-tuple-element.583), kind=kOutput, calls=%fused_computation.29 | convolution fusion | flops 11822694400 | bytes 25690112 | tf_op jit(solution)/shard_map/dot_general | solution.py:1119
  938.2 39.5 %attend_back.3 = (bf16[2048,768]{1,0:T(8,128)(2,1)}, bf16[2048,1024]{1,0:T(8,128)(2,1)}, f32[2048,64]{1,0:T(8,128)}) custom-call(bf16[2048,768]{1,0:T(8,128)(2,1)} %get-tuple-element.527.q_ref, bf16[2048,1024]{1,0:T(8,128)(2,1)} %get-tuple-element.528.lat_ref, bf16[2048,576]{1,0:T(8,128)(2,1)} %bitcast.226, ...), custom_call_target="tpu_custom_call" | custom-call | flops 1744830464 | bytes 16777216 | tf_op jit(solution)/shard_map/attend_back/pallas_call | solution.py:583
  985.9 20.0 %pair_grad.1 = f32[2048,2,768]{2,1,0:T(2,128)} custom-call(bf16[2048,2048]{1,0:T(8,128)(2,1)} %bitcast.232, bf16[2048,1536]{1,0:T(8,128)(2,1)} %get-tuple-element.345.grad_ref), custom_call_target="tpu_custom_call" | custom-call | flops 12884901888 | bytes 27262976 | tf_op jit(solution)/shard_map/pair_grad/pallas_call | solution.py:857
  1038.9 24.0 %shard_map.262 = (bf16[16,128,576]{2,1,0:T(8,128)(2,1)}, f32[16,8,896]{2,1,0:T(8,128)}) custom-call(bf16[128,576]{1,0:T(8,128)(2,1)} %copy-done.30, f32[8,896]{1,0:T(8,128)} %reshape.364.refs_1_), custom_call_target="tpu_custom_call" | custom-call | tf_op jit(solution)/shard_map/pallas_call | solution.py:263
  (305 shorter events, 320.0 us)
Async XLA Ops:
  7.2 921.2 %all-gather.2.cloned.1.call-start = ((), (), s32[]{:S(2)}) async-start(), calls=%async_computation.1 | async-start | bytes 8912896 | tf_op jit(solution)/shard_map/all_gather | solution.py:1095
  15.0 12.2 %copy-start.20 = (f32[512,32]{1,0:T(8,128)}, f32[512,32]{1,0:T(8,128)S(1)}, u32[]{:S(2)}) copy-start(f32[512,32]{1,0:T(8,128)S(1)} %get-tuple-element.599.cos_ref) | copy-start | bytes 196612
  15.0 12.2 %copy-start.21 = (f32[512,32]{1,0:T(8,128)}, f32[512,32]{1,0:T(8,128)S(1)}, u32[]{:S(2)}) copy-start(f32[512,32]{1,0:T(8,128)S(1)} %get-tuple-element.600.sin_ref) | copy-start | bytes 196612
  180.1 97.2 %copy-start.2 = (bf16[1,1,128,2048]{3,2,1,0:T(8,128)(2,1)S(1)}, bf16[1,1,128,2048]{3,2,1,0:T(8,128)(2,1)}, u32[]{:S(2)}) copy-start(bf16[1,1,128,2048]{3,2,1,0:T(8,128)(2,1)} %param.23) | copy-start | bytes 1572868
  180.1 97.2 %collective-permute-start = (bf16[128,2048]{1,0:T(8,128)(2,1)}, bf16[128,2048]{1,0:T(8,128)(2,1)S(1)}, u32[]{:S(2)}, u32[]{:S(2)}) collective-permute-start(bf16[128,2048]{1,0:T(8,128)(2,1)} %add_convert_fusion.1), channel_id=1, source_target_pairs={{0,16},{1,17},{2,18},{3,19},{4,20},{5,21},{6,22},{7,23},{8,24},{9,... | collective-permute-start | bytes 1572872 | tf_op jit(solution)/shard_map/ppermute | solution.py:992
  277.3 339.8 %copy-start.10 = (bf16[128,2048]{1,0:T(8,128)(2,1)}, bf16[128,2048]{1,0:T(8,128)(2,1)S(1)}, u32[]{:S(2)}) copy-start(bf16[128,2048]{1,0:T(8,128)(2,1)S(1)} %collective-permute-done) | copy-start | bytes 1572868
  277.6 339.6 %copy-start.44 = (f32[128]{0:T(128)}, f32[128]{0:T(128)S(1)}, u32[]{:S(2)}) copy-start(f32[128]{0:T(128)S(1)} %get-tuple-element.602) | copy-start | bytes 1540
  277.6 339.6 %copy-start.53 = (f32[128]{0:T(128)}, f32[128]{0:T(128)S(1)}, u32[]{:S(2)}) copy-start(f32[128]{0:T(128)S(1)} %get-tuple-element.601) | copy-start | bytes 1540
  280.7 318.2 %copy-start.49 = (f32[128]{0:T(128)}, f32[128]{0:T(128)S(1)}, u32[]{:S(2)}) copy-start(f32[128]{0:T(128)S(1)} %get-tuple-element.604) | copy-start | bytes 1540
  280.7 318.2 %copy-start.57 = (f32[128]{0:T(128)}, f32[128]{0:T(128)S(1)}, u32[]{:S(2)}) copy-start(f32[128]{0:T(128)S(1)} %get-tuple-element.603) | copy-start | bytes 1540
  345.0 295.2 %copy-start.42 = (f32[128]{0:T(128)}, f32[128]{0:T(128)S(1)}, u32[]{:S(2)}) copy-start(f32[128]{0:T(128)S(1)} %get-tuple-element.606) | copy-start | bytes 1540
  345.0 295.2 %copy-start.47 = (f32[128]{0:T(128)}, f32[128]{0:T(128)S(1)}, u32[]{:S(2)}) copy-start(f32[128]{0:T(128)S(1)} %get-tuple-element.605) | copy-start | bytes 1540
  619.7 12.2 %collective-permute-start.1 = (bf16[128,2048]{1,0:T(8,128)(2,1)S(1)}, bf16[128,2048]{1,0:T(8,128)(2,1)S(1)}, u32[]{:S(2)}, u32[]{:S(2)}) collective-permute-start(bf16[128,2048]{1,0:T(8,128)(2,1)S(1)} %subtract_add_fusion.1), channel_id=1, source_target_pairs={{16,0},{17,1},{18,2},{19,3},{20,4},{21,5},{22,6},{23,7},{24,8},{25... | collective-permute-start | bytes 1572872 | tf_op jit(solution)/shard_map/ppermute | solution.py:1060
  640.2 71.2 %copy-start.55 = (f32[128]{0:T(128)}, f32[128]{0:T(128)S(1)}, u32[]{:S(2)}) copy-start(f32[128]{0:T(128)S(1)} %broadcast_multiply_fusion.3) | copy-start | bytes 1540
  642.5 388.8 %reduce-scatter.2.cloned.1.call-start = ((), (), s32[]{:S(2)}) async-start(), calls=%async_computation.2 | async-start | bytes 3440640 | tf_op jit(solution)/shard_map/reduce_scatter | solution.py:1100
  643.9 67.5 %copy-start.12 = (f32[2048,32]{1,0:T(8,128)S(1)}, f32[2048,32]{1,0:T(8,128)}, u32[]{:S(2)}) copy-start(f32[2048,32]{1,0:T(8,128)} %get-tuple-element.597.sin_ref) | copy-start | bytes 786436
  720.5 21.9 %slice-start.8 = ((s8[8388608]{0:T(1024)(128)(4,1)}), s8[4194304]{0:T(1024)(128)(4,1)S(1)}, s32[]{:S(2)}) async-start(s8[8388608]{0:T(1024)(128)(4,1)} %bitcast.253), calls=%async_computation.11 | async-start | bytes 8388608 | tf_op jit(solution)/shard_map/cond
  728.6 13.7 %slice-start.9 = ((s8[8388608]{0:T(1024)(128)(4,1)}), s8[4194304]{0:T(1024)(128)(4,1)S(1)}, s32[]{:S(2)}) async-start(s8[8388608]{0:T(1024)(128)(4,1)} %bitcast.253), calls=%async_computation.12 | async-start | bytes 8388608 | tf_op jit(solution)/shard_map/cond
  874.6 12.3 %copy-start.15 = (bf16[2048,704]{0,1:T(8,128)(2,1)S(1)}, bf16[2048,704]{0,1:T(8,128)(2,1)}, u32[]{:S(2)}) copy-start(bf16[2048,704]{0,1:T(8,128)(2,1)} %get-tuple-element.529) | copy-start | bytes 8650756
  874.6 22.6 %slice-start = ((s8[8388608]{0:T(1024)(128)(4,1)}), s8[4194304]{0:T(1024)(128)(4,1)S(1)}, s32[]{:S(2)}) async-start(s8[8388608]{0:T(1024)(128)(4,1)} %bitcast.221), calls=%async_computation.3 | async-start | bytes 8388608
  886.9 23.9 %slice-start.2 = ((s8[8388608]{0:T(1024)(128)(4,1)}), s8[4194304]{0:T(1024)(128)(4,1)S(1)}, s32[]{:S(2)}) async-start(s8[8388608]{0:T(1024)(128)(4,1)} %bitcast.234), calls=%async_computation.5 | async-start | bytes 8388608
  897.3 13.6 %slice-start.3 = ((s8[8388608]{0:T(1024)(128)(4,1)}), s8[4194304]{0:T(1024)(128)(4,1)S(1)}, s32[]{:S(2)}) async-start(s8[8388608]{0:T(1024)(128)(4,1)} %bitcast.234), calls=%async_computation.6 | async-start | bytes 8388608
  1005.9 16.3 %slice-start.6 = ((s8[8388608]{0:T(1024)(128)(4,1)}), s8[4194304]{0:T(1024)(128)(4,1)S(1)}, s32[]{:S(2)}) async-start(s8[8388608]{0:T(1024)(128)(4,1)} %bitcast.250), calls=%async_computation.9 | async-start | bytes 8388608
  1022.3 12.4 %copy-start.58 = (f32[128]{0:T(128)S(1)}, f32[128]{0:T(128)}, u32[]{:S(2)}) copy-start(f32[128]{0:T(128)} %copy-done.57) | copy-start | bytes 1540
  (52 other events, 286.5 us)
Sparse Core Ops, SparseCore 0:
  642.6 250.0 all-gather.1
  986.0 35.4 reduce-scatter.1

commit v4 on v3

--- a/solution.py
+++ b/solution.py
@@ -279,6 +279,7 @@
             dma((2, spots, units)),
         ],
         compiler_params=pltpu.CompilerParams(collective_id=number, has_side_effects=True),
+        name=f"gather{number}",
     )(*values, *held)
     return [out.reshape(-1, out.shape[2]) for out in outs]
 
@@ -448,12 +449,13 @@
         pl.when(lax.axis_index(SECTION) == active)(run)
 
 
-def scatter_blocks(partial, across, number, active=None, parts=4):
+def scatter_blocks(partial, rows, across, number, active=None, parts=4):
     if lax.axis_size(MEMBERS) != 4:
         axes = BOTH if across else MEMBERS
-        return lax.psum_scatter(partial, axes, scatter_dimension=0, tiled=True).astype(jnp.float32)
+        taken = partial[: rows * lax.axis_size(axes)]
+        return lax.psum_scatter(taken, axes, scatter_dimension=0, tiled=True).astype(jnp.float32)
     spots = lax.axis_size(PACKS) if across else 1
-    rows, width = partial.shape[0] // (spots * 4), partial.shape[1]
+    width = partial.shape[1]
     dma = pltpu.SemaphoreType.DMA
     hold = lambda *lead: pltpu.VMEM((*lead, rows, width), partial.dtype)
     return pl.pallas_call(
@@ -479,7 +481,8 @@
             dma((spots, parts)),
         ],
         compiler_params=pltpu.CompilerParams(collective_id=number, has_side_effects=True),
-    )(partial.reshape(spots * 4, rows, width))
+        name=f"scatter{number}",
+    )(partial.reshape(-1, rows, width))
 
 
 def allowed_pairs(seg_col, seg_row):
@@ -509,22 +512,24 @@
         out_ref[:, head * VD : (head + 1) * VD] = bf16(dot(bf16(probs), value))
 
 
-def attend(query_raw, latent, keyed, tables):
+def attend(query_raw, latent, keyed, tables, groups=1):
     cosine, sine, seg_col, seg_row = tables
     count, _, rows = seg_row.shape
     heads = query_raw.shape[1] // QK
     block = lambda width: pl.BlockSpec((rows, width), lambda i: (i, 0))
+    same = lambda width: pl.BlockSpec((rows, width), lambda i: (0, 0) if groups > 1 else (i, 0))
+    count = count * groups
     return pl.pallas_call(
         functools.partial(attend_kernel, heads),
         grid=(count,),
         in_specs=[
             block(heads * QK),
             block(heads * KV),
-            block(LAT + ROPE),
-            block(HALF),
-            block(HALF),
-            block(1),
-            pl.BlockSpec((1, 1, rows), lambda i: (i, 0, 0)),
+            same(LAT + ROPE),
+            same(HALF),
+            same(HALF),
+            same(1),
+            pl.BlockSpec((1, 1, rows), lambda i: (0, 0, 0) if groups > 1 else (i, 0, 0)),
         ],
         out_specs=[block(heads * VD), block(heads * QK)],
         out_shape=[
@@ -575,23 +580,25 @@
     dkey_ref[...] = total
 
 
-def attend_back(query, latent, keyed, grad, tables):
+def attend_back(query, latent, keyed, grad, tables, groups=1):
     cosine, sine, seg_col, seg_row = tables
     count, _, rows = seg_row.shape
     heads = query.shape[1] // QK
     block = lambda width: pl.BlockSpec((rows, width), lambda i: (i, 0))
+    same = lambda width: pl.BlockSpec((rows, width), lambda i: (0, 0) if groups > 1 else (i, 0))
+    count = count * groups
     return pl.pallas_call(
         functools.partial(attend_back_kernel, heads),
         grid=(count,),
         in_specs=[
             block(heads * QK),
             block(heads * KV),
-            block(LAT + ROPE),
+            same(LAT + ROPE),
             block(heads * VD),
-            block(HALF),
-            block(HALF),
-            block(1),
-            pl.BlockSpec((1, 1, rows), lambda i: (i, 0, 0)),
+            same(HALF),
+            same(HALF),
+            same(1),
+            pl.BlockSpec((1, 1, rows), lambda i: (0, 0, 0) if groups > 1 else (i, 0, 0)),
         ],
         out_specs=[block(heads * QK), block(heads * KV), block(ROPE)],
         out_shape=[
@@ -617,22 +624,115 @@
     return bf16(grad_hidden * up * slope), bf16(grad_hidden * act)
 
 
-def experts_kernel(
-    full,
-    here_ref,
-    x_ref,
-    routed_ref,
-    own_ref,
-    in_ref,
-    out_w_ref,
-    shared_in_ref,
-    shared_out_ref,
-    pre_ref,
-    gated_ref,
-    prob_ref,
-    shared_pre_ref,
-    *partial_ref,
-):
+def load(sources, targets, sems):
+    copies = [
+        pltpu.make_async_copy(source, target, sems.at[index])
+        for index, (source, target) in enumerate(zip(sources, targets))
+    ]
+    for copy in copies:
+        copy.start()
+    for copy in copies:
+        copy.wait()
+
+
+class Tiles:
+    def __init__(self, rows, pack_rows, pack, active):
+        self.rows, self.pack_rows = rows, pack_rows
+        self.tile = min(256, pack_rows)
+        self.count = rows // self.tile
+        inner = pack_rows // self.tile
+        runs = (lax.axis_index(SECTION) == active).astype(jnp.int32)
+        self.control = jnp.stack([pack * inner, (pack + 1) * inner, runs]).astype(jnp.int32)
+
+    def source(self, width):
+        return pl.BlockSpec((self.tile, width), lambda i, control: (i * control[2], 0))
+
+    def small(self, array):
+        return pl.BlockSpec(array.shape, lambda i, control: (0,) * array.ndim)
+
+    def pack_source(self, width):
+        def index(i, control):
+            return (0, jnp.clip(i - control[0], 0, control[1] - control[0] - 1), 0)
+
+        return pl.BlockSpec((2, self.tile, width), index)
+
+    def result(self, width, dtype=jnp.bfloat16):
+        def index(i, control):
+            return (jnp.where(control[2] == 1, i, self.count), 0)
+
+        shape = jax.ShapeDtypeStruct((self.rows + self.tile, width), dtype)
+        return shape, pl.BlockSpec((self.tile, width), index)
+
+    def pair_result(self, width):
+        def index(i, control):
+            return (0, jnp.where(control[2] == 1, i, self.count), 0)
+
+        shape = jax.ShapeDtypeStruct((2, self.rows + self.tile, width), jnp.bfloat16)
+        return shape, pl.BlockSpec((2, self.tile, width), index)
+
+    def pack_result(self, width):
+        def index(i, control):
+            spot = jnp.clip(i - control[0], 0, control[1] - control[0] - 1)
+            return (0, jnp.where(control[2] == 1, spot, control[1] - control[0]), 0)
+
+        shape = jax.ShapeDtypeStruct((2, self.pack_rows + self.tile, width), jnp.bfloat16)
+        return shape, pl.BlockSpec((2, self.tile, width), index)
+
+    def call(self, kernel, name, sources, weights, results, into=(), scratch=(), flops=0):
+        arrays, specs = zip(*sources)
+        shapes, out_specs = zip(*results)
+        anywhere = pl.BlockSpec(memory_space=pl.ANY)
+        first = 1 + len(arrays) + len(weights)
+        return pl.pallas_call(
+            functools.partial(kernel, len(arrays), len(weights), len(into), len(results)),
+            grid_spec=pltpu.PrefetchScalarGridSpec(
+                num_scalar_prefetch=1,
+                grid=(self.count,),
+                in_specs=[*specs, *([anywhere] * (len(weights) + len(into)))],
+                out_specs=list(out_specs),
+                scratch_shapes=[
+                    *[pltpu.VMEM(weight.shape, weight.dtype) for weight in weights],
+                    pltpu.SemaphoreType.DMA((len(weights),)),
+                    *scratch,
+                ],
+            ),
+            out_shape=list(shapes),
+            input_output_aliases={first + index: index for index in range(len(into))},
+            name=name,
+            cost_estimate=pl.CostEstimate(flops=flops, bytes_accessed=self.rows * 16384, transcendentals=0),
+        )(self.control, *arrays, *weights, *into)
+
+
+def tiled(body):
+    def kernel(n_sources, n_weights, n_into, n_results, control, *refs):
+        sources, refs = refs[:n_sources], refs[n_sources:]
+        stored, refs = refs[:n_weights], refs[n_weights + n_into :]
+        results, refs = refs[:n_results], refs[n_results:]
+        weights, sems, scratch = refs[:n_weights], refs[n_weights], refs[n_weights + 1 :]
+
+        def run():
+            pl.when(pl.program_id(0) == 0)(lambda: load(stored, weights, sems))
+            body(control, sources, weights, results, scratch)
+
+        pl.when(control[2] == 1)(run)
+
+    return kernel
+
+
+def inside_pack(control):
+    tile = pl.program_id(0)
+    return (tile >= control[0]) & (tile < control[1])
+
+
+def shared_units(x, shared_in):
+    half = shared_in.shape[0] // 2
+    return dot_t(x, shared_in[:half]), dot_t(x, shared_in[half:])
+
+
+def experts_body(control, sources, weights, results, scratch):
+    x_ref, routed_ref, own_ref = sources
+    in_ref, shared_in_ref = weights[:2]
+    pre_ref, gated_ref, prob_ref, shared_pre_ref = results[:4]
     units = gated_ref.shape[1]
     x = x_ref[...]
     pre = dot(x, in_ref[...])
@@ -644,134 +744,67 @@
     pre_ref[...] = bf16(pre[:, : 2 * units])
     gated = bf16(gate * gated_hidden(pre[:, :units], pre[:, units : 2 * units]))
     gated_ref[...] = gated
-    tile = pl.program_id(0)
-    inside = (tile >= here_ref[0]) & (tile < here_ref[1])
-    half = shared_out_ref.shape[0]
 
     def shared():
-        left = dot_t(x, shared_in_ref[:half])
-        right = dot_t(x, shared_in_ref[half:])
+        left, right = shared_units(x, shared_in_ref)
         shared_pre_ref[0] = bf16(left)
         shared_pre_ref[1] = bf16(right)
         return left, right
 
-    if full:
-
-        def with_shared():
-            hidden = bf16(gated_hidden(*shared()))
-            partial_ref[0][...] = bf16(dot(gated, out_w_ref[...]) + dot(hidden, shared_out_ref[...]))
-
-        def without():
-            partial_ref[0][...] = bf16(dot(gated, out_w_ref[...]))
-
-        pl.when(inside)(with_shared)
-        pl.when(jnp.logical_not(inside))(without)
-    else:
-        pl.when(inside)(lambda: shared() and None)
-
-
-def tile_rows(pack_rows):
-    return min(256, pack_rows)
-
-
-def tile_here(pack, pack_rows):
-    tiles = pack_rows // tile_rows(pack_rows)
-    return jnp.stack([pack * tiles, (pack + 1) * tiles]).astype(jnp.int32)
-
-
-def specs_of(rows, tile):
-    block = lambda width: pl.BlockSpec((tile, width), lambda i, here: (i, 0))
-    whole = lambda array: pl.BlockSpec(
-        array.shape, lambda i, here: (0,) * array.ndim, pipeline_mode=pl.Buffered(1)
-    )
-    inner = lambda i, here: jnp.clip(i - here[0], 0, here[1] - here[0] - 1)
-    return block, whole, inner
-
-
-def experts(x, routed, own_column, weights, here, pack_rows, full):
-    expert_in, expert_out, shared_in, shared_out = weights
-    routes_width = own_column.shape[1]
-    rows, width = x.shape
-    tile = tile_rows(pack_rows)
-    units, half = expert_out.shape[0], shared_out.shape[0]
-    block, whole, inner = specs_of(rows, tile)
-    shape = jax.ShapeDtypeStruct
-    out_shape = [
-        shape((rows, 2 * units), jnp.bfloat16),
-        shape((rows, units), jnp.bfloat16),
-        shape((rows, routes_width), jnp.float32),
-        shape((2, pack_rows, half), jnp.bfloat16),
-    ]
-    out_specs = [
-        block(2 * units),
-        block(units),
-        block(routes_width),
-        pl.BlockSpec((2, tile, half), lambda i, here: (0, inner(i, here), 0)),
-    ]
-    if full:
-        out_shape.append(shape((rows, width), jnp.bfloat16))
-        out_specs.append(block(width))
-    return pl.pallas_call(
-        functools.partial(experts_kernel, full),
-        grid_spec=pltpu.PrefetchScalarGridSpec(
-            num_scalar_prefetch=1,
-            grid=(rows // tile,),
-            in_specs=[
-                block(width),
-                block(1),
-                whole(own_column),
-                whole(expert_in),
-                whole(expert_out),
-                whole(shared_in),
-                whole(shared_out),
-            ],
-            out_specs=out_specs,
-        ),
-        out_shape=out_shape,
-        name="experts_full" if full else "experts_inner",
-        cost_estimate=pl.CostEstimate(
-            flops=2 * rows * width * units * 3, bytes_accessed=rows * width * 4, transcendentals=rows * units
-        ),
-    )(here, x, routed, own_column, expert_in, expert_out, shared_in, shared_out)
-
-
-def experts_back_kernel(
-    here_ref,
-    grad_ref,
-    pre_ref,
-    prob_ref,
-    routed_ref,
-    own_ref,
-    in_ref,
-    out_w_ref,
-    shared_pre_ref,
-    shared_in_ref,
-    shared_out_ref,
-    grad_pre_ref,
-    moved_ref,
-    partial_ref,
-    joined_ref,
-):
-    units = out_w_ref.shape[0]
+    if len(weights) == 2:
+        pl.when(inside_pack(control))(lambda: shared() and None)
+        return
+    out_ref, shared_out_ref = weights[2:]
+    partial_ref = results[4]
+
+    def with_shared():
+        hidden = bf16(gated_hidden(*shared()))
+        partial_ref[...] = bf16(dot(gated, out_ref[...]) + dot(hidden, shared_out_ref[...]))
+
+    def without():
+        partial_ref[...] = bf16(dot(gated, out_ref[...]))
+
+    pl.when(inside_pack(control))(with_shared)
+    pl.when(jnp.logical_not(inside_pack(control)))(without)
+
+
+def finish_body(control, sources, weights, results, scratch):
+    gated_ref, shared_pre_ref = sources
+    out_ref, shared_out_ref = weights
+    (partial_ref,) = results
+
+    def with_shared():
+        hidden = bf16(gated_hidden(shared_pre_ref[0].astype(jnp.float32), shared_pre_ref[1].astype(jnp.float32)))
+        partial_ref[...] = bf16(dot(gated_ref[...], out_ref[...]) + dot(hidden, shared_out_ref[...]))
+
+    def without():
+        partial_ref[...] = bf16(dot(gated_ref[...], out_ref[...]))
+
+    pl.when(inside_pack(control))(with_shared)
+    pl.when(jnp.logical_not(inside_pack(control)))(without)
+
+
+def experts_back_body(control, sources, weights, results, scratch):
+    grad_ref, pre_ref, prob_ref, routed_ref, own_ref, shared_pre_ref = sources
+    in_ref, shared_in_ref, out_ref, shared_out_ref = weights
+    grad_pre_ref, moved_ref, partial_ref = results
+    (joined_ref,) = scratch
+    units = out_ref.shape[0]
     grad = grad_ref[...]
     prob = prob_ref[...]
     own_prob = jnp.sum(prob * own_ref[...], axis=1, keepdims=True) * routed_ref[...]
     gate, up = pre_ref[:, :units].astype(jnp.float32), pre_ref[:, units:].astype(jnp.float32)
-    grad_units = dot_t(grad, out_w_ref[...])
+    grad_units = dot_t(grad, out_ref[...])
     act, slope = silu_parts(gate)
-    grad_gate = jnp.sum(grad_units * act * up, axis=1, keepdims=True)
-    moved = own_prob * grad_gate
+    moved = own_prob * jnp.sum(grad_units * act * up, axis=1, keepdims=True)
     moved_ref[...] = moved
-    grad_logits = bf16(moved * (own_ref[...] - prob))
     scaled = own_prob * grad_units
     joined_ref[:, :units] = bf16(scaled * up * slope)
     joined_ref[:, units : 2 * units] = bf16(scaled * act)
     joined_ref[:, 2 * units :] = jnp.zeros_like(joined_ref[:, 2 * units :])
-    joined_ref[:, 2 * units : 2 * units + own_ref.shape[1]] = grad_logits
+    joined_ref[:, 2 * units : 2 * units + own_ref.shape[1]] = bf16(moved * (own_ref[...] - prob))
     grad_pre_ref[...] = joined_ref[:, : 2 * units]
     base = dot_t(joined_ref[...], in_ref[...])
-    tile = pl.program_id(0)
-    inside = (tile >= here_ref[0]) & (tile < here_ref[1])
     half = shared_out_ref.shape[0]
 
     def with_shared():
@@ -785,60 +818,40 @@
     def without():
         partial_ref[...] = bf16(base)
 
-    pl.when(inside)(with_shared)
-    pl.when(jnp.logical_not(inside))(without)
-
-
-def experts_back(grad, stored, routed, own_column, weights, here, pack_rows):
-    expert_in, expert_out, shared_in, shared_out = weights
-    routes_width = own_column.shape[1]
-    rows, width = grad.shape
-    tile = tile_rows(pack_rows)
-    units, half = expert_out.shape[0], shared_out.shape[0]
-    block, whole, inner = specs_of(rows, tile)
-    shape = jax.ShapeDtypeStruct
-    return pl.pallas_call(
-        experts_back_kernel,
-        grid_spec=pltpu.PrefetchScalarGridSpec(
-            num_scalar_prefetch=1,
-            grid=(rows // tile,),
-            in_specs=[
-                block(width),
-                block(2 * units),
-                block(routes_width),
-                block(1),
-                whole(own_column),
-                whole(expert_in),
-                whole(expert_out),
-                pl.BlockSpec((2, tile, half), lambda i, here: (0, inner(i, here), 0)),
-                whole(shared_in),
-                whole(shared_out),
-            ],
-            out_specs=[block(2 * units), block(1), block(width)],
-            scratch_shapes=[pltpu.VMEM((tile, expert_in.shape[1]), jnp.bfloat16)],
-        ),
-        out_shape=[
-            shape((rows, 2 * units), jnp.bfloat16),
-            shape((rows, 1), jnp.float32),
-            shape((rows, width), jnp.bfloat16),
-        ],
-        name="experts_back",
-        cost_estimate=pl.CostEstimate(
-            flops=2 * rows * width * units * 3, bytes_accessed=rows * width * 4, transcendentals=rows * units
-        ),
-    )(
-        here,
-        grad,
-        stored["pre"],
-        stored["prob"],
-        routed,
-        own_column,
-        expert_in,
-        expert_out,
-        stored["shared_pre"],
-        shared_in,
-        shared_out,
-    )
+    pl.when(inside_pack(control))(with_shared)
+    pl.when(jnp.logical_not(inside_pack(control)))(without)
+
+
+def shared_body(control, sources, weights, results, scratch):
+    pre_ref, hid_ref = results
+    left, right = shared_units(sources[0][...], weights[0])
+    pre_ref[0] = bf16(left)
+    pre_ref[1] = bf16(right)
+    hid_ref[...] = bf16(gated_hidden(left, right))
+
+
+def heads_body(block, control, sources, weights, results, scratch):
+    x_ref, key_ref, cos_ref, sin_ref, col_ref, row_ref = sources
+    query_w_ref, expand_ref = weights
+    out_ref, rot_ref, lat_ref = results
+    (q_ref,) = scratch
+    heads = q_ref.shape[1] // QK
+    q_ref[...] = dot(x_ref[...], query_w_ref[...])
+    lat_ref[...] = bf16(dot(key_ref[:, :LAT], expand_ref[...]))
+    for start in range(0, x_ref.shape[0], block):
+        at = pl.ds(start, block)
+        attend_kernel(
+            heads,
+            q_ref.at[at],
+            lat_ref.at[at],
+            key_ref.at[at],
+            cos_ref.at[at],
+            sin_ref.at[at],
+            col_ref.at[at],
+            row_ref.at[pl.ds(start // block, 1)],
+            out_ref.at[at],
+            rot_ref.at[at],
+        )
 
 
 def pair_grad_kernel(x_ref, grad_ref, out_ref):
@@ -852,7 +865,7 @@
     rows, width = x.shape
     units = grad.shape[1] // 2
     if rows > 4096:
-        return t_dot(x, grad).reshape(width, 2, units)
+        return t_dot(x, grad[:rows]).reshape(width, 2, units)
     tile = 256
     return pl.pallas_call(
         pair_grad_kernel,
@@ -903,10 +916,10 @@
     router_weight, shared_out, expert_out = router_weight[0], shared_out[0], expert_out[0, 0]
     width = boundary.shape[3]
     rows = boundary.shape[2]
-    shared_half = shared_out.shape[0]
+    half = shared_out.shape[0]
     units = expert_out.shape[0]
-    shared_in_t = jnp.transpose(shared_in[0], (1, 2, 0)).reshape(2 * shared_half, width)
     experts_count = router_weight.shape[1]
+    shared_in_t = jnp.transpose(shared_in[0], (1, 2, 0)).reshape(2 * half, width)
     joined_in = jnp.concatenate(
         [
             expert_in.reshape(width, 2 * units),
@@ -915,7 +928,6 @@
         ],
         axis=1,
     )
-    weights = (joined_in, expert_out, shared_in_t, shared_out)
 
     packs, members = lax.axis_size(PACKS), lax.axis_size(MEMBERS)
     count = packs * members
@@ -923,8 +935,10 @@
     me = pack * members + member
     is_first = lax.axis_index(SECTION) == 0
     pack_rows = members * rows
+    all_rows = count * rows
+    heads = output_weight.shape[0] // VD
     top = routes.shape[3]
-    here = tile_here(pack, pack_rows)
+    tiles = [Tiles(all_rows, pack_rows, pack, active) for active in range(2)]
 
     def own_pack(value):
         size = value.shape[0] // packs
@@ -947,13 +961,12 @@
     layout = jnp.pad(layout, (0, -layout.shape[0] % 1024)).reshape(8, -1)
 
     def routed_of(layout_all):
-        routes_all = layout_all.reshape(count, -1)[:, : rows * top].reshape(count * rows, top)
+        routes_all = layout_all.reshape(count, -1)[:, : rows * top].reshape(all_rows, top)
         return jnp.any(routes_all == me, axis=1, keepdims=True).astype(jnp.float32)
 
     tables_pack = tables_of(lengths[0, 0])
-    own_cos, own_sin = (
-        lax.dynamic_slice_in_dim(table, member * rows, rows, 0) for table in tables_pack[:2]
-    )
+    tables_own = tables_of(own_lengths[None])
+    own_cos, own_sin = tables_own[:2]
     own_column = (lax.broadcasted_iota(jnp.int32, (1, experts_count), 1) == me).astype(jnp.float32)
 
     def inputs_of(hidden):
@@ -966,43 +979,125 @@
         )
         return normed, keyed, (compressed, scale_attn, scale_latent)
 
-    def heads_of(normed, keyed, tables):
-        query_raw = dot(normed, query_weight)
-        latent = bf16(dot(keyed[:, :LAT], expand_weight))
-        attended, query = attend(query_raw, latent, keyed, tables)
-        return attended, query, latent
+    def run_experts(section, x, routed, into, full):
+        at = tiles[section]
+        results = [
+            at.result(2 * units),
+            at.result(units),
+            at.result(experts_count, jnp.float32),
+            at.pack_result(half),
+        ]
+        weights = [joined_in, shared_in_t]
+        if full:
+            results.append(at.result(width))
+            weights += [expert_out, shared_out]
+        return at.call(
+            tiled(experts_body),
+            "experts",
+            [(x, at.source(width)), (routed, at.source(1)), (own_column, at.small(own_column))],
+            weights,
+            results,
+            into,
+            flops=6 * all_rows * width * units,
+        )
+
+    def run_experts_back(section, grad, routed, stored, into):
+        at = tiles[section]
+        pre, _, prob, shared_pre = stored
+        return at.call(
+            tiled(experts_back_body),
+            "experts_back",
+            [
+                (grad, at.source(width)),
+                (pre, at.source(2 * units)),
+                (prob, at.source(experts_count)),
+                (routed, at.source(1)),
+                (own_column, at.small(own_column)),
+                (shared_pre, at.pack_source(half)),
+            ],
+            [joined_in, shared_in_t, expert_out, shared_out],
+            [at.result(2 * units), at.result(1, jnp.float32), at.result(width)],
+            into,
+            [pltpu.VMEM((at.tile, joined_in.shape[1]), jnp.bfloat16)],
+            flops=6 * all_rows * width * units,
+        )
+
+    def prepare(section, normed_all, keyed_all, ffn_all, tables, into):
+        at = tiles[section]
+        cosine, sine, seg_col, seg_row = tables
+        blocks = at.tile // rows
+        row_spec = pl.BlockSpec((blocks, 1, rows), lambda i, control: (i * control[2], 0, 0))
+        found = at.call(
+            tiled(functools.partial(heads_body, rows)),
+            "heads",
+            [
+                (normed_all, at.source(width)),
+                (keyed_all, at.source(LAT + ROPE)),
+                (cosine, at.source(HALF)),
+                (sine, at.source(HALF)),
+                (seg_col, at.source(1)),
+                (seg_row, row_spec),
+            ],
+            [query_weight, expand_weight],
+            [at.result(heads * VD), at.result(heads * QK), at.result(heads * KV)],
+            into[:3],
+            [pltpu.VMEM((at.tile, heads * QK), jnp.float32)],
+            flops=4 * all_rows * width * heads * QK,
+        )
+        shared = at.call(
+            tiled(shared_body),
+            "shared",
+            [(ffn_all, at.source(width))],
+            [shared_in_t],
+            [at.pair_result(half), at.result(half)],
+            into[3:],
+            flops=4 * all_rows * width * half,
+        )
+        return [*found, *shared]
 
     fresh = boundary[0, 0].astype(jnp.float32)
 
     normed, keyed, _ = inputs_of(fresh)
-    pack_inputs = gather_blocks([normed, keyed], False, 1, 0)
-    attended, _, _ = heads_of(*pack_inputs, tables_pack)
-    mixed_first = fresh + scatter_blocks(
-        bf16(dot(attended, output_weight)), False, 9, 0
-    )
+    normed_pack, keyed_pack = gather_blocks([normed, keyed], False, 0, 0)
+    attended, _ = attend(
+        dot(normed_pack, query_weight),
+        bf16(dot(keyed_pack[:, :LAT], expand_weight)),
+        keyed_pack,
+        tables_pack,
+    )
+    mixed_first = fresh + scatter_blocks(bf16(dot(attended, output_weight)), rows, False, 1, 0)
     ffn_all, layout_all = gather_blocks(
         [bf16(rms_forward(mixed_first, ffn_gain)[0]), layout], True, 2, 0
     )
-    *_, partial = experts(ffn_all, routed_of(layout_all), own_column, weights, here, pack_rows, True)
-    result_first = mixed_first + scatter_blocks(partial, True, 10, 0)
+    *stored, partial = run_experts(0, ffn_all, routed_of(layout_all), (), True)
+    result_first = mixed_first + scatter_blocks(partial, rows, True, 3, 0)
+    heads_weights = gather_blocks([query_weight, expand_weight, output_weight], False, 4, 1, parts=8)
     target_all, layout_all = gather_blocks(
-        [boundary[0, 0], layout], True, 0, 1, [blank(ffn_all.shape, jnp.bfloat16), layout_all]
-    )
-    sent, target_all, layout_all = lax.optimization_barrier((bf16(result_first), target_all, layout_all))
+        [boundary[0, 0], layout], True, 5, 1, [blank(ffn_all.shape, jnp.bfloat16), layout_all]
+    )
+    sent, target_all, layout_all, heads_weights = lax.optimization_barrier(
+        (bf16(result_first), target_all, layout_all, heads_weights)
+    )
     inbound = lax.ppermute(sent, SECTION, [(0, 1)])
     routed = routed_of(layout_all)
     tables_all = tables_of(layout_all.reshape(count, -1)[:, rows * top : rows * top + lengths.shape[3]])
+    query_heads, expand_heads, output_heads = (
+        value.reshape(members, -1, value.shape[1]) for value in heads_weights
+    )
 
     hidden = jnp.where(is_first, fresh, inbound.astype(jnp.float32))
     normed, keyed, (compressed, scale_attn, scale_latent) = inputs_of(hidden)
-    normed_pack, keyed_pack = gather_blocks([normed, keyed], False, 3, 1, pack_inputs)
-    attended, query, latent = heads_of(normed_pack, keyed_pack, tables_pack)
-    mixed = hidden + scatter_blocks(bf16(dot(attended, output_weight)), False, 11, 1)
+    latent = bf16(jnp.einsum("rd,mdc->mrc", keyed[:, :LAT], expand_heads, preferred_element_type=jnp.float32))
+    latent = latent.reshape(members * rows, -1)
+    query_raw = jnp.einsum("rd,mdc->mrc", normed, query_heads, preferred_element_type=jnp.float32)
+    attended, query = attend(query_raw.reshape(members * rows, -1), latent, keyed, tables_own, members)
+    mixed = hidden + jnp.einsum(
+        "mrc,mcd->rd", attended.reshape(members, rows, -1), output_heads, preferred_element_type=jnp.float32
+    )
     mixed = jnp.where(is_first, mixed_first, mixed)
     ffn32, scale_ffn = rms_forward(mixed, ffn_gain)
-    (ffn_all,) = gather_blocks([bf16(ffn32)], True, 4, 1, [ffn_all])
-    pre, gated, prob, shared_pre = experts(ffn_all, routed, own_column, weights, here, pack_rows, False)
-    stored = dict(pre=pre, prob=prob, shared_pre=shared_pre)
+    (ffn_all,) = gather_blocks([bf16(ffn32)], True, 6, 1, [ffn_all])
+    stored = run_experts(1, ffn_all, routed, stored, False)
 
     def latent_back(own):
         grad_latent, grad_latent_gain = rms_backward(
@@ -1015,81 +1110,60 @@
         grad_hidden_norm, grad_attn_gain = rms_backward(hidden, scale_attn, attn_gain, grad_normed)
         return grad_compressed, grad_hidden_norm, grad_attn_gain, grad_latent_gain
 
-    def heads_back(grad_query, grad_latent_heads, grad_shared_key):
-        return bf16(
-            jnp.concatenate(
-                [
-                    dot_t(grad_query, query_weight),
-                    dot_t(grad_latent_heads, expand_weight),
-                    grad_shared_key,
-                ],
-                axis=1,
-            )
-        )
-
-    def prepare(normed_all, keyed_all):
-        attended_all, query_all, latent_all = heads_of(normed_all, keyed_all, tables_all)
-        left = dot_t(ffn_all, shared_in_t[:shared_half])
-        right = dot_t(ffn_all, shared_in_t[shared_half:])
-        return attended_all, query_all, latent_all, bf16(left), bf16(right), bf16(gated_hidden(left, right))
-
-    grad_pre_second, moved_second, partial = experts_back(
-        target_all, stored, routed, own_column, weights, here, pack_rows
-    )
-    grad_ffn_second = scatter_blocks(partial, True, 13, 1)
+    *grad_units, partial = run_experts_back(1, target_all, routed, stored, ())
+    grad_ffn_second = scatter_blocks(partial, rows, True, 7, 1)
     grad_mixed = fresh + rms_backward(mixed, scale_ffn, ffn_gain, grad_ffn_second)[0]
-    (grad_mixed_pack,) = gather_blocks([bf16(grad_mixed)], False, 5, 1)
-    own_second = scatter_blocks(
-        heads_back(
-            *attend_back(query, latent, keyed_pack, bf16(dot_t(grad_mixed_pack, output_weight)), tables_pack)
-        ),
-        False,
-        14,
-        1,
-    )
-    grad_second = grad_mixed + latent_back(own_second)[1]
-
-    all_inputs = gather_blocks([normed, keyed], True, 7, 0)
-    prepared = lax.cond(
-        is_first,
-        prepare,
-        lambda *_: tuple(blank(like.shape, like.dtype) for like in jax.eval_shape(prepare, *all_inputs)),
-        *all_inputs,
-    )
+    grad_attended = jnp.einsum(
+        "rd,mcd->mrc", bf16(grad_mixed), output_heads, preferred_element_type=jnp.float32
+    )
+    grad_query, grad_latent_heads, grad_shared_key = attend_back(
+        query, latent, keyed, bf16(grad_attended).reshape(members * rows, -1), tables_own, members
+    )
+    own_second = jnp.concatenate(
+        [
+            jnp.einsum(
+                "mrc,mdc->rd",
+                grad_query.reshape(members, rows, -1),
+                query_heads,
+                preferred_element_type=jnp.float32,
+            ),
+            jnp.einsum(
+                "mrc,mdc->rd",
+                grad_latent_heads.reshape(members, rows, -1),
+                expand_heads,
+                preferred_element_type=jnp.float32,
+            ),
+            jnp.sum(grad_shared_key.reshape(members, rows, -1), axis=0),
+        ],
+        axis=1,
+    )
+    grad_second = bf16(grad_mixed + latent_back(own_second)[1])
+
+    all_inputs = gather_blocks([normed, keyed], True, 8, 0)
+    prepared = prepare(0, *all_inputs, ffn_all, tables_all, ())
     grad_second, prepared, all_inputs = lax.optimization_barrier((grad_second, prepared, all_inputs))
-    downbound = lax.ppermute(bf16(grad_second), SECTION, [(1, 0)]).astype(jnp.float32)
-
-    normed_late, keyed_late, gated_late, _ = lax.optimization_barrier((normed, keyed, gated, grad_second))
-    normed_all, keyed_all = gather_blocks([normed_late, keyed_late], True, 8, 1, all_inputs)
-    attended_all, query_all, latent_all, shared_gate, shared_up, shared_hid = lax.cond(
-        is_first, lambda *values: values[2:], lambda *values: prepare(*values[:2]), normed_all, keyed_all, *prepared
-    )
-
-    def finish(gated_late, shared_hid):
-        partial = bf16(dot(gated_late, expert_out))
-        addend = dot(own_pack(shared_hid), shared_out)
-        return lax.dynamic_update_slice_in_dim(
-            partial, bf16(own_pack(partial).astype(jnp.float32) + addend), pack * pack_rows, 0
-        )
-
-    partial = lax.cond(
-        is_first, lambda *_: blank((count * rows, width), jnp.bfloat16), finish, gated_late, shared_hid
-    )
-    result = mixed + scatter_blocks(partial, True, 12, 1)
+    downbound = lax.ppermute(grad_second, SECTION, [(1, 0)]).astype(jnp.float32)
+
+    normed_late, keyed_late, gated_late, _ = lax.optimization_barrier((normed, keyed, stored[1], grad_second))
+    normed_all, keyed_all = gather_blocks([normed_late, keyed_late], True, 9, 1, all_inputs)
+    prepared = prepare(1, normed_all, keyed_all, ffn_all, tables_all, prepared)
+    attended_all, query_all, latent_all, shared_pre, shared_hid = prepared
+    attended_all, shared_hid = attended_all[:all_rows], shared_hid[:all_rows]
+    at = tiles[1]
+    (partial,) = at.call(
+        tiled(finish_body),
+        "finish",
+        [(gated_late, at.source(units)), (stored[3], at.pack_source(half))],
+        [expert_out, shared_out],
+        [at.result(width)],
+        flops=2 * all_rows * width * units,
+    )
+    result = mixed + scatter_blocks(partial, rows, True, 10, 1)
 
     upstream = jnp.where(is_first, downbound, fresh)
-    (upstream_all,) = gather_blocks([bf16(upstream)], True, 6, 0, [target_all])
-    grad_pre, moved, partial = lax.cond(
-        is_first,
-        lambda upstream_all, *_: tuple(
-            experts_back(upstream_all, stored, routed, own_column, weights, here, pack_rows)
-        ),
-        lambda _, *old: (*old, blank((count * rows, width), jnp.bfloat16)),
-        upstream_all,
-        grad_pre_second,
-        moved_second,
-    )
-    grad_ffn = jnp.where(is_first, scatter_blocks(partial, True, 15, 0), grad_ffn_second)
+    (upstream_all,) = gather_blocks([bf16(upstream)], True, 11, 0, [target_all])
+    grad_pre, moved, partial = run_experts_back(0, upstream_all, routed, stored, grad_units)
+    grad_ffn = jnp.where(is_first, scatter_blocks(partial, rows, True, 12, 0), grad_ffn_second)
     grad_mixed_norm, grad_ffn_gain = rms_backward(mixed, scale_ffn, ffn_gain, grad_ffn)
     grad_mixed = upstream + grad_mixed_norm
     grad_mixed_all = lax.all_gather(bf16(grad_mixed), BOTH, axis=0, tiled=True)
@@ -1098,7 +1172,16 @@
         query_all, latent_all, keyed_all, grad_attended, tables_all
     )
     own = lax.psum_scatter(
-        heads_back(own_pack(grad_query), own_pack(grad_latent_heads), own_pack(grad_shared_key)),
+        bf16(
+            jnp.concatenate(
+                [
+                    dot_t(own_pack(grad_query), query_weight),
+                    dot_t(own_pack(grad_latent_heads), expand_weight),
+                    own_pack(grad_shared_key),
+                ],
+                axis=1,
+            )
+        ),
         MEMBERS,
         scatter_dimension=0,
         tiled=True,
@@ -1106,15 +1189,18 @@
     grad_compressed, grad_hidden_norm, grad_attn_gain, grad_latent_gain = latent_back(own)
     grad_hidden = grad_mixed + grad_hidden_norm
 
-    small = jnp.concatenate([grad_attn_gain, grad_latent_gain, grad_ffn_gain, moved[:, 0]])
+    small = jnp.concatenate([grad_attn_gain, grad_latent_gain, grad_ffn_gain, moved[:all_rows, 0]])
     small = jnp.pad(small, (0, -small.shape[0] % 1024)).reshape(8, -1)
-    grad_compressed_all, small_all = gather_blocks([grad_compressed, small], True, 16)
+    grad_compressed_all, small_all = gather_blocks([grad_compressed, small], True, 13)
     small_all = small_all.reshape(count, -1)
     gains = jnp.sum(small_all[:, : 2 * width + LAT], axis=0)
-    moved_all = small_all[:, 2 * width + LAT : 2 * width + LAT + count * rows].T
+    moved_all = small_all[:, 2 * width + LAT : 2 * width + LAT + all_rows].T
+    prob = stored[2][:all_rows]
     grad_logits = bf16(moved_all - prob * jnp.sum(moved_all, axis=1, keepdims=True))
     left, right = gated_back(
-        shared_gate.astype(jnp.float32), shared_up.astype(jnp.float32), dot_t(upstream_all, shared_out)
+        shared_pre[0, :all_rows].astype(jnp.float32),
+        shared_pre[1, :all_rows].astype(jnp.float32),
+        dot_t(upstream_all, shared_out),
     )
     grad_shared_in = lax.dot_general(
         jnp.stack([left, right]), ffn_all, (((1,), (0,)), ((), ())), preferred_element_type=jnp.float32
@@ -1133,7 +1219,7 @@
         jnp.transpose(grad_shared_in, (2, 0, 1))[None],
         t_dot(shared_hid, upstream_all)[None],
         pair_grad(ffn_all, grad_pre)[None, None],
-        t_dot(gated, upstream_all)[None, None],
+        t_dot(stored[1][:all_rows], upstream_all)[None, None],
     )
 
 

time: 1100 us -> 1000 us (0.909)
  waiting for transfers between devices: 88.4 us -> 10.9 us
  Pallas kernels: 659 us -> 715 us
  matrix products: 206 us -> 165 us
  local copies, waits for them, and re-layouts: 61.8 us -> 40.3 us
    pallas_call x10 -> x9, Pallas kernels: 256 us -> 352 us  [gather_blocks(): pl.pallas_call(functools.partial(gather_kernel, spots, cuts, active), out...]
    ppermute x1, waiting for transfers between devices: 84.5 us -> 0.01 us  [body(): inbound = lax.ppermute(sent, SECTION, [(0, 1)])]
    pallas_call x7 -> x5, Pallas kernels: 166 us -> 113 us  [scatter_blocks(): pl.pallas_call(functools.partial(scatter_kernel, spots, parts, active), o...]
    dot_general x12 -> x5, matrix products: 59.7 us -> 13.5 us  [dot(): return jnp.dot(left, right, preferred_element_type=jnp.float32)]
    pallas_call x3 -> x9, Pallas kernels: 123 us -> 164 us  [call(): pl.pallas_call(functools.partial(kernel, len(arrays), len(weights), len(i...]
    dot_general x0 -> x6, matrix products: none -> 36.5 us  [the longest x1 9.87 us: body(): jnp.einsum('mrc,mdc->rd', grad_query.reshape(members, rows, -1), query_he...]
    dot_general x11 -> x6, matrix products: 65.5 us -> 32.4 us  [dot_t(): lax.dot_general(left, right, (((1,), (1,)), ((), ())), preferred_element_...]
    pallas_call x3 -> x2, Pallas kernels: 43.7 us -> 16.4 us  [attend(): pl.pallas_call(functools.partial(attend_kernel, heads), grid=(count,), in...]
  transfers between devices with their start and end apart: 4 -> 4, of which waited for: 2 -> 1; matrix products, arithmetic and copies ran while one was open for 14% -> 10% of each run, Pallas kernels for 17% -> 21%
where the time goes in v4:
time: 1000 us; the launch traced here: 994 us
  Pallas kernels  715 us (72%)
  matrix products  165 us (16%)
  other arithmetic  44.7 us (4%)
  local copies, waits for them, and re-layouts  40.3 us (4%)
  between operations  15.6 us (2%)
  waiting for transfers between devices  10.9 us (1%)
    pallas_call x9, Pallas kernels, gather_blocks(): pl.pallas_call(functools.partial(gather_kernel, spots, cuts, active), out...  352 us
    pallas_call x9, Pallas kernels, call(): pl.pallas_call(functools.partial(kernel, len(arrays), len(weights), len(i...  164 us
    pallas_call x5, Pallas kernels, scatter_blocks(): pl.pallas_call(functools.partial(scatter_kernel, spots, parts, active), o...  113 us
    dot_general x7, matrix products, t_dot(): lax.dot_general(left, right, (((0,), (0,)), ((), ())), preferred_element_...  63.7 us
    pallas_call x2, Pallas kernels, attend_back(): pl.pallas_call(functools.partial(attend_back_kernel, heads), grid=(count,...  50.9 us
    dot_general x6, matrix products, dot_t(): lax.dot_general(left, right, (((1,), (1,)), ((), ())), preferred_element_...  32.4 us
    pallas_call x1, Pallas kernels, pair_grad(): pl.pallas_call(pair_grad_kernel, grid=(width // tile,), in_specs=[pl.Bloc...  20 us
  transfers between devices with their start and end apart: 4, of which 1 were waited for; matrix products, arithmetic and copies ran while one was open for 10% of the time, Pallas kernels for 21%

profile of v4, /device:TPU:3, one launch (start us, length us, event | category | flops | bytes accessed | tf_op | source)
XLA Modules:
  0.0 994.4 jit_solution(11565269602358137803)
XLA Ops:
  59.3 11.0 %concatenate.31.refs_3_.refs_6_ = bf16[2048,1664]{1,0:T(8,128)(2,1)} concatenate(bf16[2048,1536]{1,0:T(8,128)(2,1)} %bitcast.256, bf16[2048,16]{1,0:T(8,128)(2,1)S(1)} %bitcast.277, bf16[2048,112]{1,0:T(8,128)(2,1)} %broadcast_in_dim.60), dimensions={1} | concatenate | bytes 13631488 | tf_op jit(solution)/shard_map/concatenate | solution.py:923
  79.6 53.4 %gather5.1 = (bf16[16,128,2048]{2,1,0:T(8,128)(2,1)}, s32[16,8,128]{2,1,0:T(8,128)}) custom-call(bf16[128,2048]{1,0:T(8,128)(2,1)} %bitcast.238, s32[8,128]{1,0:T(8,128)} %pad_bitcast_fusion.refs_1_, bf16[16,128,2048]{2,1,0:T(8,128)(2,1)} %bitcast.239, s32[16,8,128]{2,1,0:T(8,128)} %get-tuple-element.83.refs_3_), custom_call_target="tpu_custom_call", output_to_operand_aliasing={{0}: (2, {}), {1}: (3, {})} | custom-call | tf_op jit(solution)/shard_map/gather5/pallas_call | solution.py:263
  133.1 144.5 %gather4.1 = (bf16[4,2048,768]{2,1,0:T(8,128)(2,1)}, bf16[4,512,1024]{2,1,0:T(8,128)(2,1)}, bf16[4,512,2048]{2,1,0:T(8,128)(2,1)}) custom-call(bf16[2048,768]{1,0:T(8,128)(2,1)} %bitcast.274, bf16[512,1024]{1,0:T(8,128)(2,1)} %bitcast.283, bf16[512,2048]{1,0:T(8,128)(2,1)} %bitcast.278), custom_call_target="tpu_custom_call" | custom-call | tf_op jit(solution)/shard_map/gather4/pallas_call | solution.py:263
  327.1 52.1 %gather6.1 = bf16[16,128,2048]{2,1,0:T(8,128)(2,1)} custom-call(bf16[128,2048]{1,0:T(8,128)(2,1)} %multiply_convert_fusion.refs_0_, bf16[16,128,2048]{2,1,0:T(8,128)(2,1)} %get-tuple-element.82.refs_1_), custom_call_target="tpu_custom_call", output_to_operand_aliasing={{}: (1, {})} | custom-call | tf_op jit(solution)/shard_map/gather6/pallas_call | solution.py:263
  382.1 31.6 %experts.3 = (bf16[2304,1536]{1,0:T(8,128)(2,1)}, bf16[2304,768]{1,0:T(8,128)(2,1)}, f32[2304,16]{1,0:T(8,128)}, bf16[2,768,704]{2,1,0:T(8,128)(2,1)}) custom-call(s32[3]{0:T(128)} %get-tuple-element.192.control, bf16[2048,2048]{1,0:T(8,128)(2,1)} %bitcast.249, ...), custom_call_target="tpu_custom_call", output_to_operand_aliasing={{0}: (6, {}), {1}: (7, {}), {2}: (8, {}), {3}: (9, {})} | custom-call | flops 19327352832 | bytes 33554432 | tf_op jit(solution)/shard_map/experts/pallas_call | solution.py:686
  413.7 50.3 %experts_back.2 = (bf16[2304,1536]{1,0:T(8,128)(2,1)}, f32[2304,1]{1,0:T(8,128)}, bf16[2304,2048]{1,0:T(8,128)(2,1)}) custom-call(s32[3]{0:T(128)} %get-tuple-element.192.control, bf16[2048,2048]{1,0:T(8,128)(2,1)} %bitcast.240, bf16[2304,1536]{1,0:T(8,128)(2,1)} %get-tuple-element.101.refs_1_, f32[2304,16]{1,0:T(8,128)} %get-tuple-element.102.refs_2_, ...), custom_call_target="tpu_custom_call" | custom-call | flops 19327352832 | bytes 33554432 | tf_op jit(solution)/shard_map/experts_back/pallas_call | solution.py:686
  464.1 52.7 %scatter7.1 = f32[128,2048]{1,0:T(8,128)} custom-call(bf16[18,128,2048]{2,1,0:T(8,128)(2,1)} %bitcast.263), custom_call_target="tpu_custom_call" | custom-call | tf_op jit(solution)/shard_map/scatter7/pallas_call | solution.py:461
  526.2 11.4 %attend_back.2 = (bf16[512,768]{1,0:T(8,128)(2,1)}, bf16[512,1024]{1,0:T(8,128)(2,1)}, f32[512,64]{1,0:T(8,128)}) custom-call(bf16[512,768]{1,0:T(8,128)(2,1)} %get-tuple-element.105.q_ref, bf16[512,1024]{1,0:T(8,128)(2,1)} %bitcast.266, bf16[128,576]{1,0:T(8,128)(2,1)} %pad_maximum_fusion.2.key_ref.refs_1_, bf16[512,512]{1,0:T(8,128)(2,1)} %bitcast.292, ...), custom_call_target="tpu_custom_call" | custom-call | flops 436207616 | bytes 4194304 | tf_op jit(solution)/shard_map/attend_back/pallas_call | solution.py:590
  537.5 9.9 convolution_bitcast_fusion.6
  562.0 10.9 %collective-permute-done.1 = bf16[128,2048]{1,0:T(8,128)(2,1)S(1)} collective-permute-done((bf16[128,2048]{1,0:T(8,128)(2,1)S(1)}, bf16[128,2048]{1,0:T(8,128)(2,1)S(1)}, u32[]{:S(2)}, u32[]{:S(2)}) %collective-permute-start.1) | collective-permute-done | bytes 524320 | tf_op jit(solution)/shard_map/ppermute | solution.py:1145
  588.2 16.5 %finish.1 = bf16[2304,2048]{1,0:T(8,128)(2,1)} custom-call(s32[3]{0:T(128)} %get-tuple-element.192.control, bf16[2304,768]{1,0:T(8,128)(2,1)} %get-tuple-element.135.refs_0_, bf16[2,768,704]{2,1,0:T(8,128)(2,1)} %get-tuple-element.103.refs_5_.refs_1_, bf16[768,2048]{1,0:T(8,128)(2,1)} %bitcast.340, bf16[704,2048]{1,0:T(8,128)(2,1)} %bitcast.344), custom_call_target="tpu_custom_call" | custom-call | flops 6442450944 | bytes 33554432 | tf_op jit(solution)/shard_map/finish/pallas_call | solution.py:686
  604.6 53.5 %scatter10.1 = f32[128,2048]{1,0:T(8,128)} custom-call(bf16[18,128,2048]{2,1,0:T(8,128)(2,1)} %bitcast.264), custom_call_target="tpu_custom_call" | custom-call | tf_op jit(solution)/shard_map/scatter10/pallas_call | solution.py:461
  658.1 67.1 %gather9.1 = (bf16[16,128,2048]{2,1,0:T(8,128)(2,1)}, bf16[16,128,576]{2,1,0:T(8,128)(2,1)}) custom-call(bf16[128,2048]{1,0:T(8,128)(2,1)} %copy-done.10, bf16[128,576]{1,0:T(8,128)(2,1)} %pad_maximum_fusion.2.key_ref.refs_1_, bf16[16,128,2048]{2,1,0:T(8,128)(2,1)} %get-tuple-element.109, ...), custom_call_target="tpu_custom_call", output_to_operand_aliasing={{0}: (2, {}), {1}: (3, {})} | custom-call | tf_op jit(solution)/shard_map/gather9/pallas_call | solution.py:263
  725.3 20.6 %shared.3 = (bf16[2,2304,704]{2,1,0:T(8,128)(2,1)}, bf16[2304,704]{1,0:T(8,128)(2,1)}) custom-call(s32[3]{0:T(128)} %get-tuple-element.192.control, bf16[2048,2048]{1,0:T(8,128)(2,1)} %bitcast.250, bf16[1408,2048]{1,0:T(8,128)(2,1)} %bitcast.336, bf16[2,2304,704]{2,1,0:T(8,128)(2,1)} %get-tuple-element.140.refs_2_, ...), custom_call_target="tpu_custom_call", output_to_operand_aliasing={{0}: (3, {}), {1}: (4, {})} | custom-call | flops 11811160064 | bytes 33554432 | tf_op jit(solution)/shard_map/shared/pallas_call | solution.py:686
  745.9 30.8 %heads.3 = (bf16[2304,512]{1,0:T(8,128)(2,1)}, bf16[2304,768]{1,0:T(8,128)(2,1)}, bf16[2304,1024]{1,0:T(8,128)(2,1)}) custom-call(s32[3]{0:T(128)} %get-tuple-element.192.control, bf16[2048,2048]{1,0:T(8,128)(2,1)} %bitcast.268, bf16[2048,576]{1,0:T(8,128)(2,1)} %bitcast.258, ...), custom_call_target="tpu_custom_call", output_to_operand_aliasing={{0}: (9, {}), {1}: (10, {}), {2}: (11, {})} | custom-call | flops 12884901888 | bytes 33554432 | tf_op jit(solution)/shard_map/heads/pallas_call | solution.py:686
  777.1 11.9 %convolution_bitcast_fusion = f32[1,1,768,2048]{3,2,1,0:T(8,128)} fusion(bf16[2048,2048]{1,0:T(8,128)(2,1)} %bitcast.242, bf16[2304,768]{1,0:T(8,128)(2,1)} %get-tuple-element.135.refs_0_), kind=kOutput, calls=%fused_computation.18 | convolution fusion | flops 6442450944 | bytes 17825792 | tf_op jit(solution)/shard_map/dot_general | solution.py:35
  789.0 10.4 %convolution_bitcast_fusion.2 = f32[1,704,2048]{2,1,0:T(8,128)} fusion(bf16[2048,2048]{1,0:T(8,128)(2,1)} %bitcast.243, bf16[2304,704]{1,0:T(8,128)(2,1)S(1)} %copy-done.67), kind=kOutput, calls=%fused_computation.20 | convolution fusion | flops 5905580032 | bytes 17301504 | tf_op jit(solution)/shard_map/dot_general | solution.py:35
  799.5 12.5 %fusion.19 = (bf16[1,2048,704]{2,1,0:T(8,128)(2,1)}, bf16[1,2048,704]{2,1,0:T(8,128)(2,1)}) fusion(bf16[2,2304,704]{2,1,0:T(8,128)(2,1)} %get-tuple-element.142, bf16[2048,2048]{1,0:T(8,128)(2,1)S(1)} %bitcast.246, bf16[1,704,2048]{2,1,0:T(8,128)(2,1)S(1)} %copy-done.65), kind=kOutput, calls=%fused_computation.26 | convolution fusion | flops 5927206912 | bytes 22806528 | tf_op jit(solution)/shard_map/dot_general | solution.py:29
  812.0 18.4 %fusion.13 = f32[1,2048,2,704]{1,3,2,0:T(8,128)} fusion(bf16[2048,2048,1]{1,0,2:T(8,128)(2,1)S(1)} %bitcast.255, bf16[1,2048,704]{2,1,0:T(8,128)(2,1)} %get-tuple-element.159, bf16[1,2048,704]{2,1,0:T(8,128)(2,1)} %get-tuple-element.158), kind=kOutput, calls=%fused_computation.17 | convolution fusion | flops 11822694400 | bytes 25690112 | tf_op jit(solution)/shard_map/dot_general | solution.py:1205
  830.5 9.9 convolution_convert_fusion.1.grad_ref
  840.3 39.5 %attend_back.3 = (bf16[2048,768]{1,0:T(8,128)(2,1)}, bf16[2048,1024]{1,0:T(8,128)(2,1)}, f32[2048,64]{1,0:T(8,128)}) custom-call(bf16[2304,768]{1,0:T(8,128)(2,1)} %get-tuple-element.130.q_ref, bf16[2304,1024]{1,0:T(8,128)(2,1)} %get-tuple-element.131.lat_ref, bf16[2048,576]{1,0:T(8,128)(2,1)} %bitcast.259, ...), custom_call_target="tpu_custom_call" | custom-call | flops 1744830464 | bytes 16777216 | tf_op jit(solution)/shard_map/attend_back/pallas_call | solution.py:590
  888.6 20.0 %pair_grad.1 = f32[2048,2,768]{2,1,0:T(2,128)} custom-call(bf16[2048,2048]{1,0:T(8,128)(2,1)} %bitcast.251, bf16[2304,1536]{1,0:T(8,128)(2,1)} %get-tuple-element.144.grad_ref), custom_call_target="tpu_custom_call" | custom-call | flops 12884901888 | bytes 27262976 | tf_op jit(solution)/shard_map/pair_grad/pallas_call | solution.py:870
  941.0 23.3 %gather13.1 = (bf16[16,128,576]{2,1,0:T(8,128)(2,1)}, f32[16,8,896]{2,1,0:T(8,128)}) custom-call(bf16[128,576]{1,0:T(8,128)(2,1)} %copy-done.20, f32[8,896]{1,0:T(8,128)} %reshape.545.refs_1_), custom_call_target="tpu_custom_call" | custom-call | tf_op jit(solution)/shard_map/gather13/pallas_call | solution.py:263
  967.9 9.9 %convolution_bitcast_fusion.3 = f32[1,2048,576]{1,2,0:T(8,128)} fusion(bf16[16,128,2048]{2,1,0:T(8,128)(2,1)} %get-tuple-element.125, bf16[16,128,576]{2,1,0:T(8,128)(2,1)} %get-tuple-element.138), kind=kOutput, calls=%fused_computation.21 | convolution fusion | flops 4831838208 | bytes 15466496 | tf_op jit(solution)/shard_map/dot_general | solution.py:35
  (289 shorter events, 206.6 us)
Async XLA Ops:
  7.2 823.3 %all-gather.2.cloned.1.call-start = ((), (), s32[]{:S(2)}) async-start(), calls=%async_computation.1 | async-start | bytes 8912896 | tf_op jit(solution)/shard_map/all_gather | solution.py:1169
  133.1 145.9 %copy-start.25 = (s32[16,8,128]{2,1,0:T(8,128)S(1)}, s32[16,8,128]{2,1,0:T(8,128)}, u32[]{:S(2)}) copy-start(s32[16,8,128]{2,1,0:T(8,128)} %get-tuple-element.86) | copy-start | bytes 196612
  133.1 149.1 %copy-start.53 = (s32[128]{0:T(128)S(1)}, s32[128]{0:T(128)}, u32[]{:S(2)}) copy-start(s32[128]{0:T(128)} %get-tuple-element.155) | copy-start | bytes 1540
  133.1 155.8 %copy-start.38 = (f32[32]{0:T(128)S(1)}, f32[32]{0:T(128)}, u32[]{:S(2)}) copy-start(f32[32]{0:T(128)} %copy-done.37) | copy-start | bytes 388
  133.1 161.3 %copy-start.2 = (bf16[1,1,128,2048]{3,2,1,0:T(8,128)(2,1)S(1)}, bf16[1,1,128,2048]{3,2,1,0:T(8,128)(2,1)}, u32[]{:S(2)}) copy-start(bf16[1,1,128,2048]{3,2,1,0:T(8,128)(2,1)} %param.15) | copy-start | bytes 1572868
  277.6 16.8 %collective-permute-start = (bf16[128,2048]{1,0:T(8,128)(2,1)}, bf16[128,2048]{1,0:T(8,128)(2,1)S(1)}, u32[]{:S(2)}, u32[]{:S(2)}) collective-permute-start(bf16[128,2048]{1,0:T(8,128)(2,1)} %add_convert_fusion.1), channel_id=1, source_target_pairs={{0,16},{1,17},{2,18},{3,19},{4,20},{5,21},{6,22},{7,23},{8,24},{9,... | collective-permute-start | bytes 1572872 | tf_op jit(solution)/shard_map/ppermute | solution.py:1081
  282.1 14.3 %copy-start.30 = (s32[16,128]{1,0:T(8,128)}, s32[16,128]{1,0:T(8,128)S(1)}, u32[]{:S(2)}) copy-start(s32[16,128]{1,0:T(8,128)S(1)} %get-tuple-element.151) | copy-start | bytes 24580
  294.4 263.7 %copy-start.7 = (bf16[128,2048]{1,0:T(8,128)(2,1)}, bf16[128,2048]{1,0:T(8,128)(2,1)S(1)}, u32[]{:S(2)}) copy-start(bf16[128,2048]{1,0:T(8,128)(2,1)S(1)} %collective-permute-done) | copy-start | bytes 1572868
  295.2 262.9 %copy-start.45 = (f32[128]{0:T(128)}, f32[128]{0:T(128)S(1)}, u32[]{:S(2)}) copy-start(f32[128]{0:T(128)S(1)} %get-tuple-element.179) | copy-start | bytes 1540
  305.2 247.8 %copy-start.48 = (f32[128]{0:T(128)}, f32[128]{0:T(128)S(1)}, u32[]{:S(2)}) copy-start(f32[128]{0:T(128)S(1)} %get-tuple-element.181) | copy-start | bytes 1540
  305.2 247.8 %copy-start.59 = (f32[128]{0:T(128)}, f32[128]{0:T(128)S(1)}, u32[]{:S(2)}) copy-start(f32[128]{0:T(128)S(1)} %get-tuple-element.180) | copy-start | bytes 1540
  325.1 260.4 %copy-start.40 = (f32[128]{0:T(128)}, f32[128]{0:T(128)S(1)}, u32[]{:S(2)}) copy-start(f32[128]{0:T(128)S(1)} %get-tuple-element.183) | copy-start | bytes 1540
  325.1 260.4 %copy-start.51 = (f32[128]{0:T(128)}, f32[128]{0:T(128)S(1)}, u32[]{:S(2)}) copy-start(f32[128]{0:T(128)S(1)} %get-tuple-element.182) | copy-start | bytes 1540
  560.7 12.2 %collective-permute-start.1 = (bf16[128,2048]{1,0:T(8,128)(2,1)S(1)}, bf16[128,2048]{1,0:T(8,128)(2,1)S(1)}, u32[]{:S(2)}, u32[]{:S(2)}) collective-permute-start(bf16[128,2048]{1,0:T(8,128)(2,1)S(1)} %add_convert_fusion), channel_id=1, source_target_pairs={{16,0},{17,1},{18,2},{19,3},{20,4},{21,5},{22,6},{23,7},{24,8},{25... | collective-permute-start | bytes 1572872 | tf_op jit(solution)/shard_map/ppermute | solution.py:1145
  585.4 19.2 %copy-start.57 = (f32[128]{0:T(128)}, f32[128]{0:T(128)S(1)}, u32[]{:S(2)}) copy-start(f32[128]{0:T(128)S(1)} %broadcast_multiply_fusion.3) | copy-start | bytes 1540
  587.7 346.4 %reduce-scatter.2.cloned.1.call-start = ((), (), s32[]{:S(2)}) async-start(), calls=%async_computation.2 | async-start | bytes 3440640 | tf_op jit(solution)/shard_map/reduce_scatter | solution.py:1174
  745.9 30.8 %copy-start.23 = (f32[2304,1]{1,0:T(8,128)S(1)}, f32[2304,1]{1,0:T(8,128)}, u32[]{:S(2)}) copy-start(f32[2304,1]{1,0:T(8,128)} %get-tuple-element.136) | copy-start | bytes 27652
  777.1 22.4 %slice-start = ((s8[8388608]{0:T(1024)(128)(4,1)}), s8[4194304]{0:T(1024)(128)(4,1)S(1)}, s32[]{:S(2)}) async-start(s8[8388608]{0:T(1024)(128)(4,1)} %bitcast.244), calls=%async_computation.3 | async-start | bytes 8388608
  789.0 23.0 %slice-start.2 = ((s8[8388608]{0:T(1024)(128)(4,1)}), s8[4194304]{0:T(1024)(128)(4,1)S(1)}, s32[]{:S(2)}) async-start(s8[8388608]{0:T(1024)(128)(4,1)} %bitcast.253), calls=%async_computation.5 | async-start | bytes 8388608
  840.3 40.5 %copy-start.22 = (bf16[1,512,1024]{2,1,0:T(8,128)(2,1)S(1)}, bf16[1,512,1024]{2,1,0:T(8,128)(2,1)}, u32[]{:S(2)}) copy-start(bf16[1,512,1024]{2,1,0:T(8,128)(2,1)} %param.22) | copy-start | bytes 3145732
  908.6 16.4 %slice-start.4 = ((s8[8388608]{0:T(1024)(128)(4,1)}), s8[4194304]{0:T(1024)(128)(4,1)S(1)}, s32[]{:S(2)}) async-start(s8[8388608]{0:T(1024)(128)(4,1)} %bitcast.269), calls=%async_computation.7 | async-start | bytes 8388608
  925.1 12.9 %copy-start.3 = (bf16[1,1,128,2048]{3,2,1,0:T(8,128)(2,1)S(1)}, bf16[1,1,128,2048]{3,2,1,0:T(8,128)(2,1)}, u32[]{:S(2)}) copy-start(bf16[1,1,128,2048]{3,2,1,0:T(8,128)(2,1)} %param.15) | copy-start | bytes 1572868
  925.1 12.9 %copy-start.8 = (bf16[128,2048]{1,0:T(8,128)(2,1)S(1)}, bf16[128,2048]{1,0:T(8,128)(2,1)}, u32[]{:S(2)}) copy-start(bf16[128,2048]{1,0:T(8,128)(2,1)} %copy-done.7) | copy-start | bytes 1572868
  925.1 12.9 %copy-start.29 = (f32[1,2048]{1,0:T(1,128)S(1)}, f32[1,2048]{1,0:T(1,128)}, u32[]{:S(2)}) copy-start(f32[1,2048]{1,0:T(1,128)} %param.18) | copy-start | bytes 24580
  (54 other events, 366.8 us)
Sparse Core Ops, SparseCore 0:
  587.8 219.9 all-gather.1
  888.7 33.8 reduce-scatter.1

commit v5 on v4

--- a/solution.py
+++ b/solution.py
@@ -284,6 +284,109 @@
     return [out.reshape(-1, out.shape[2]) for out in outs]
 
 
+def spread_kernel(cuts, active, *refs):
+    arrays = len(cuts)
+    x_refs, o_refs = refs[:arrays], refs[arrays : 2 * arrays]
+    own_sem, over_out, over_in, side_out, side_in, pair_out, pair_in = refs[2 * arrays :]
+    units = [
+        (a, pl.ds(part * (x_refs[a].shape[0] // parts), x_refs[a].shape[0] // parts))
+        for a, parts in enumerate(cuts)
+        for part in range(parts)
+    ]
+
+    def run():
+        member, spot = lax.axis_index(MEMBERS), lax.axis_index(PACKS)
+        chip, core, odd = member // 2, lax.rem(member, 2), lax.rem(spot, 2)
+        beside = {PACKS: spot + 1 - 2 * odd}
+        barrier = pltpu.get_barrier_semaphore()
+        for target in (to_partner(chip, core), to_other(chip, core), beside):
+            pl.semaphore_signal(barrier, inc=1, device_id=target, device_id_type=MESH)
+        pl.semaphore_wait(barrier, 3)
+
+        def piece(unit, c):
+            array, cut = units[unit]
+            return o_refs[array].at[c * 2 + core, cut]
+
+        def first(unit):
+            array, cut = units[unit]
+            return x_refs[array].at[cut]
+
+        def over(unit):
+            return remote(first(unit), piece(unit, chip), to_other(chip, core), over_out.at[unit], over_in.at[unit])
+
+        def side(unit):
+            source = piece(unit, 1 - chip)
+            return remote(source, source, beside, side_out.at[unit], side_in.at[unit])
+
+        def pair(source, unit, c, index):
+            return remote(
+                source, piece(unit, c), to_partner(chip, core), pair_out.at[index, unit], pair_in.at[index, unit]
+            )
+
+        for unit in range(len(units)):
+            pl.when(odd == unit % 2)(lambda: over(unit).start())
+        for unit in range(len(units)):
+            pair(first(unit), unit, chip, 0).start()
+        own = [
+            pltpu.make_async_copy(x_refs[a], o_refs[a].at[member], own_sem.at[a]) for a in range(arrays)
+        ]
+        for copy in own:
+            copy.start()
+        for unit in range(len(units)):
+
+            def taken(unit=unit):
+                over(unit).wait_recv()
+                side(unit).start()
+                pair(piece(unit, 1 - chip), unit, 1 - chip, 1).start()
+
+            pl.when(odd == unit % 2)(taken)
+        for unit in range(len(units)):
+
+            def handed(unit=unit):
+                side(unit).wait_recv()
+                pair(piece(unit, 1 - chip), unit, 1 - chip, 1).start()
+
+            pl.when(odd != unit % 2)(handed)
+        for copy in own:
+            copy.wait()
+        for unit in range(len(units)):
+
+            def sent(unit=unit):
+                over(unit).wait_send()
+                side(unit).wait_send()
+
+            pl.when(odd == unit % 2)(sent)
+            pair(first(unit), unit, chip, 0).wait()
+            pair(first(unit), unit, 1 - chip, 1).wait()
+
+    pl.when(lax.axis_index(SECTION) == active)(run)
+
+
+def spread_blocks(values, number, active, parts=8):
+    if lax.axis_size(MEMBERS) != 4 or lax.axis_size(PACKS) % 2:
+        return gather_blocks(values, False, number, active)
+    units = parts * len(values)
+    dma = pltpu.SemaphoreType.DMA
+    outs = pl.pallas_call(
+        functools.partial(spread_kernel, [parts] * len(values), active),
+        out_shape=[jax.ShapeDtypeStruct((4, *value.shape), value.dtype) for value in values],
+        in_specs=[pl.BlockSpec(memory_space=pltpu.VMEM)] * len(values),
+        out_specs=[pl.BlockSpec(memory_space=pl.ANY)] * len(values),
+        scratch_shapes=[
+            dma((len(values),)),
+            dma((units,)),
+            dma((units,)),
+            dma((units,)),
+            dma((units,)),
+            dma((2, units)),
+            dma((2, units)),
+        ],
+        compiler_params=pltpu.CompilerParams(collective_id=number, has_side_effects=True),
+        name=f"spread{number}",
+    )(*values)
+    return [out.reshape(-1, out.shape[2]) for out in outs]
+
+
 def add_into(target, sources, rows, step=16):
     def some(index, carry):
         at = pl.ds(pl.multiple_of(index * step, step), step)
@@ -712,7 +815,7 @@
 
         def run():
             pl.when(pl.program_id(0) == 0)(lambda: load(stored, weights, sems))
-            body(control, sources, weights, results, scratch)
+            body(inside_pack(control), [sources[0][...], *sources[1:]], weights, results, scratch)
 
         pl.when(control[2] == 1)(run)
 
@@ -729,12 +832,11 @@
     return dot_t(x, shared_in[:half]), dot_t(x, shared_in[half:])
 
 
-def experts_body(control, sources, weights, results, scratch):
-    x_ref, routed_ref, own_ref = sources
+def experts_body(inside, sources, weights, results, scratch):
+    x, own_ref, routed_ref = sources
     in_ref, shared_in_ref = weights[:2]
     pre_ref, gated_ref, prob_ref, shared_pre_ref = results[:4]
     units = gated_ref.shape[1]
-    x = x_ref[...]
     pre = dot(x, in_ref[...])
     logits = pre[:, 2 * units : 2 * units + own_ref.shape[1]]
     powers = jnp.exp(logits - jnp.max(logits, axis=1, keepdims=True))
@@ -752,7 +854,7 @@
         return left, right
 
     if len(weights) == 2:
-        pl.when(inside_pack(control))(lambda: shared() and None)
+        pl.when(inside)(lambda: shared() and None)
         return
     out_ref, shared_out_ref = weights[2:]
     partial_ref = results[4]
@@ -764,33 +866,32 @@
     def without():
         partial_ref[...] = bf16(dot(gated, out_ref[...]))
 
-    pl.when(inside_pack(control))(with_shared)
-    pl.when(jnp.logical_not(inside_pack(control)))(without)
-
-
-def finish_body(control, sources, weights, results, scratch):
-    gated_ref, shared_pre_ref = sources
+    pl.when(inside)(with_shared)
+    pl.when(jnp.logical_not(inside))(without)
+
+
+def finish_body(inside, sources, weights, results, scratch):
+    gated, shared_pre_ref = sources
     out_ref, shared_out_ref = weights
     (partial_ref,) = results
 
     def with_shared():
         hidden = bf16(gated_hidden(shared_pre_ref[0].astype(jnp.float32), shared_pre_ref[1].astype(jnp.float32)))
-        partial_ref[...] = bf16(dot(gated_ref[...], out_ref[...]) + dot(hidden, shared_out_ref[...]))
+        partial_ref[...] = bf16(dot(gated, out_ref[...]) + dot(hidden, shared_out_ref[...]))
 
     def without():
-        partial_ref[...] = bf16(dot(gated_ref[...], out_ref[...]))
-
-    pl.when(inside_pack(control))(with_shared)
-    pl.when(jnp.logical_not(inside_pack(control)))(without)
-
-
-def experts_back_body(control, sources, weights, results, scratch):
-    grad_ref, pre_ref, prob_ref, routed_ref, own_ref, shared_pre_ref = sources
+        partial_ref[...] = bf16(dot(gated, out_ref[...]))
+
+    pl.when(inside)(with_shared)
+    pl.when(jnp.logical_not(inside))(without)
+
+
+def experts_back_body(inside, sources, weights, results, scratch):
+    grad, own_ref, pre_ref, prob_ref, routed_ref, shared_pre_ref = sources
     in_ref, shared_in_ref, out_ref, shared_out_ref = weights
     grad_pre_ref, moved_ref, partial_ref = results
     (joined_ref,) = scratch
     units = out_ref.shape[0]
-    grad = grad_ref[...]
     prob = prob_ref[...]
     own_prob = jnp.sum(prob * own_ref[...], axis=1, keepdims=True) * routed_ref[...]
     gate, up = pre_ref[:, :units].astype(jnp.float32), pre_ref[:, units:].astype(jnp.float32)
@@ -818,27 +919,27 @@
     def without():
         partial_ref[...] = bf16(base)
 
-    pl.when(inside_pack(control))(with_shared)
-    pl.when(jnp.logical_not(inside_pack(control)))(without)
-
-
-def shared_body(control, sources, weights, results, scratch):
+    pl.when(inside)(with_shared)
+    pl.when(jnp.logical_not(inside))(without)
+
+
+def shared_body(inside, sources, weights, results, scratch):
     pre_ref, hid_ref = results
-    left, right = shared_units(sources[0][...], weights[0])
+    left, right = shared_units(sources[0], weights[0])
     pre_ref[0] = bf16(left)
     pre_ref[1] = bf16(right)
     hid_ref[...] = bf16(gated_hidden(left, right))
 
 
-def heads_body(block, control, sources, weights, results, scratch):
-    x_ref, key_ref, cos_ref, sin_ref, col_ref, row_ref = sources
+def heads_body(block, inside, sources, weights, results, scratch):
+    x, key_ref, cos_ref, sin_ref, col_ref, row_ref = sources
     query_w_ref, expand_ref = weights
     out_ref, rot_ref, lat_ref = results
     (q_ref,) = scratch
     heads = q_ref.shape[1] // QK
-    q_ref[...] = dot(x_ref[...], query_w_ref[...])
+    q_ref[...] = dot(x, query_w_ref[...])
     lat_ref[...] = bf16(dot(key_ref[:, :LAT], expand_ref[...]))
-    for start in range(0, x_ref.shape[0], block):
+    for start in range(0, x.shape[0], block):
         at = pl.ds(start, block)
         attend_kernel(
             heads,
@@ -883,6 +984,32 @@
     )(x, grad)
 
 
+def join_kernel(in_ref, router_ref, out_ref):
+    units, routes_width = in_ref.shape[2], router_ref.shape[1]
+    both = in_ref[...].astype(jnp.float32)
+    out_ref[:, :units] = bf16(both[:, 0])
+    out_ref[:, units : 2 * units] = bf16(both[:, 1])
+    out_ref[:, 2 * units :] = jnp.zeros_like(out_ref[:, 2 * units :])
+    out_ref[:, 2 * units : 2 * units + routes_width] = router_ref[...]
+
+
+def join(expert_in, router):
+    width, _, units = expert_in.shape
+    total = 2 * units + router.shape[1] + -router.shape[1] % 128
+    tile = 256
+    return pl.pallas_call(
+        join_kernel,
+        grid=(width // tile,),
+        in_specs=[
+            pl.BlockSpec((tile, 2, units), lambda i: (i, 0, 0)),
+            pl.BlockSpec((tile, router.shape[1]), lambda i: (i, 0)),
+        ],
+        out_specs=pl.BlockSpec((tile, total), lambda i: (i, 0)),
+        out_shape=jax.ShapeDtypeStruct((width, total), expert_in.dtype),
+        name="join",
+    )(expert_in, router)
+
+
 def blank(shape, dtype):
     return pl.pallas_call(
         lambda out_ref: None,
@@ -891,6 +1018,280 @@
         compiler_params=pltpu.CompilerParams(has_side_effects=True),
         name="blank",
     )()
+
+
+def arrival_order(spots):
+    tiles = [(rank + 1.1 * over, rank, over) for rank in range(spots) for over in (0, 1)]
+    return [(rank, over == 1) for _, rank, over in sorted(tiles)]
+
+
+def ranked_spots(spots, spot):
+    ranks = []
+    for rank in range(spots):
+        value = 0
+        for own in range(spots):
+            nearest = sorted(range(spots), key=lambda other: (abs(other - own), other))
+            value = value + jnp.where(spot == own, nearest[rank], 0)
+        ranks.append(value)
+    return ranks
+
+
+def pick(index, values):
+    total = 0
+    for position, value in enumerate(values):
+        total = total + jnp.where(index == position, value, 0)
+    return total
+
+
+def fused_kernel(spots, parts, active, body, pack_kinds, n_weights, n_into, *refs):
+    source_kinds, result_kinds = pack_kinds
+    n_sources, n_results = len(source_kinds), len(result_kinds)
+    x_ref, small_ref, refs = refs[0], refs[1], refs[2:]
+    sources, refs = refs[:n_sources], refs[n_sources:]
+    stored, refs = refs[:n_weights], refs[n_weights + n_into :]
+    o_ref, refs = refs[0], refs[1:]
+    results, refs = refs[:n_results], refs[n_results:]
+    x_tile, refs = refs[0], refs[1:]
+    source_tiles, refs = refs[:n_sources], refs[n_sources:]
+    result_tiles, refs = refs[:n_results], refs[n_results:]
+    weights, refs = refs[:n_weights], refs[n_weights:]
+    sems, scratch = refs[:12], refs[12:]
+    own_sem, weight_sem, tile_sem, out_sem = sems[:4]
+    up_out, up_in, down_out, down_in, over_out, over_in, pair_out, pair_in = sems[4:]
+    block = x_ref.shape[0]
+    rows = block // parts
+    tile = 2 * block
+
+    def run():
+        loads = [
+            pltpu.make_async_copy(source, target, weight_sem.at[index])
+            for index, (source, target) in enumerate(zip(stored, weights))
+        ]
+        for copy in loads:
+            copy.start()
+        spot, chip, core = places(spots)
+        greet(spots, spot, chip, core)
+        piece = lambda index, part: o_ref.at[index, pl.ds(part * rows, rows)]
+        first = lambda part: x_ref.at[pl.ds(part * rows, rows)]
+
+        def up(source, at, part, reach):
+            return remote(
+                source, piece(slot(at, chip, core), part), {PACKS: spot + 1}, up_out.at[reach, part], up_in.at[reach, part]
+            )
+
+        def down(source, at, part, reach):
+            return remote(
+                source,
+                piece(slot(at, chip, core), part),
+                {PACKS: spot - 1},
+                down_out.at[reach, part],
+                down_in.at[reach, part],
+            )
+
+        def over(source, at, part):
+            return remote(
+                source, piece(slot(at, chip, core), part), to_other(chip, core), over_out.at[at, part], over_in.at[at, part]
+            )
+
+        def pair(source, at, c, part):
+            return remote(
+                source,
+                piece(slot(at, c, core), part),
+                to_partner(chip, core),
+                pair_out.at[c, at, part],
+                pair_in.at[c, at, part],
+            )
+
+        mine = slot(spot, chip, core)
+        for part in range(parts):
+            source = first(part)
+            pair(source, spot, chip, part).start()
+            over(source, spot, part).start()
+            pl.when(spot < spots - 1)(lambda: up(source, spot, part, 0).start())
+            pl.when(spot > 0)(lambda: down(source, spot, part, 0).start())
+        own = pltpu.make_async_copy(x_ref, o_ref.at[mine], own_sem.at[0])
+        own.start()
+        own.wait()
+        ranks = ranked_spots(spots, spot)
+        order = arrival_order(spots)
+
+        def arrive(rank, across):
+            at = ranks[rank]
+            if across:
+                for part in range(parts):
+                    source = piece(slot(at, 1 - chip, core), part)
+                    over(source, at, part).wait_recv()
+                    pair(source, at, 1 - chip, part).start()
+                for part in range(parts):
+                    pair(first(part), at, 1 - chip, part).wait_recv()
+                return
+            if rank > 0:
+                for reach in range(1, spots):
+                    for part in range(parts):
+
+                        def below(reach=reach, part=part):
+                            source = piece(slot(at, chip, core), part)
+                            up(source, at, part, reach - 1).wait_recv()
+                            pl.when(spot < spots - 1)(lambda: up(source, at, part, reach).start())
+                            over(source, at, part).start()
+                            pair(source, at, chip, part).start()
+
+                        def above(reach=reach, part=part):
+                            source = piece(slot(at, chip, core), part)
+                            down(source, at, part, reach - 1).wait_recv()
+                            pl.when(spot > 0)(lambda: down(source, at, part, reach).start())
+                            over(source, at, part).start()
+                            pair(source, at, chip, part).start()
+
+                        pl.when(spot - at == reach)(below)
+                        pl.when(at - spot == reach)(above)
+            for part in range(parts):
+                pair(first(part), at, chip, part).wait_recv()
+
+        def window(ref, kind, at, c):
+            if kind:
+                return ref.at[:, pl.ds(pl.multiple_of(c * tile, tile), tile)]
+            return ref.at[pl.ds(pl.multiple_of((at * 2 + c) * tile, tile), tile)]
+
+        def outward(index, which, at, c):
+            return pltpu.make_async_copy(
+                result_tiles[index].at[which], window(results[index], result_kinds[index], at, c), out_sem.at[which, index]
+            )
+
+        def step(number, carry):
+            for position, (rank, across) in enumerate(order):
+                pl.when(number == position)(functools.partial(arrive, rank, across))
+            at = pick(number, [ranks[rank] for rank, _ in order])
+            c = pick(number, [1 - chip if across else chip for _, across in order])
+            inside = at == spot
+            inputs = [pltpu.make_async_copy(o_ref.at[pl.ds(slot(at, c, 0), 2)], x_tile, tile_sem.at[0])]
+            for index, kind in enumerate(source_kinds):
+                if not kind:
+                    inputs.append(
+                        pltpu.make_async_copy(
+                            window(sources[index], kind, at, c), source_tiles[index], tile_sem.at[1 + index]
+                        )
+                    )
+            for copy in inputs:
+                copy.start()
+            for index, kind in enumerate(source_kinds):
+                if kind:
+
+                    def fetch(index=index, kind=kind):
+                        copy = pltpu.make_async_copy(
+                            window(sources[index], kind, at, c), source_tiles[index], tile_sem.at[1 + index]
+                        )
+                        copy.start()
+                        copy.wait()
+
+                    pl.when(inside)(fetch)
+
+            @pl.when(number == 0)
+            def _():
+                for copy in loads:
+                    copy.wait()
+
+            which = lax.rem(number, 2)
+
+            @pl.when(number >= 2)
+            def _():
+                for index, kind in enumerate(result_kinds):
+                    if not kind:
+                        outward(index, which, at, c).wait()
+
+            for copy in inputs:
+                copy.wait()
+            body(
+                inside,
+                [x_tile[...].reshape(tile, x_tile.shape[2]), small_ref, *source_tiles],
+                weights,
+                [target.at[which] for target in result_tiles],
+                scratch,
+            )
+            for index, kind in enumerate(result_kinds):
+                if kind:
+
+                    def put(index=index):
+                        copy = outward(index, which, at, c)
+                        copy.start()
+                        copy.wait()
+
+                    pl.when(inside)(put)
+                else:
+                    outward(index, which, at, c).start()
+            return carry
+
+        lax.fori_loop(0, 2 * spots, step, 0)
+        for which in range(2):
+            for index, kind in enumerate(result_kinds):
+                if not kind:
+                    outward(index, which, spot, chip).wait()
+        for part in range(parts):
+            for at in range(spots):
+                over(first(part), at, part).wait_send()
+                for c in range(2):
+                    pair(first(part), at, c, part).wait_send()
+            for reach in range(spots - 1):
+                pl.when((spot >= reach) & (spot < spots - 1))(lambda: up(first(part), spot, part, reach).wait_send())
+                pl.when((spot + reach < spots) & (spot > 0))(lambda: down(first(part), spot, part, reach).wait_send())
+
+    pl.when(lax.axis_index(SECTION) == active)(run)
+
+
+def fused_call(tiles, rows_in, number, active, body, small, sources, weights, results, gathered, into, scratch=(), parts=4):
+    spots = lax.axis_size(PACKS)
+    block, width = rows_in.shape
+    tile = 2 * block
+    dma = pltpu.SemaphoreType.DMA
+    hops = max(spots - 1, 1)
+    anywhere = pl.BlockSpec(memory_space=pl.ANY)
+    inside = pl.BlockSpec(memory_space=pltpu.VMEM)
+    shapes = [jax.ShapeDtypeStruct((spots * 4, block, width), rows_in.dtype), *(shape for shape, _ in results)]
+    held = [gathered.reshape(shapes[0].shape), *into]
+    first = 2 + len(sources) + len(weights)
+
+    def hold(array, kind, *lead):
+        shape = (2, tile, array.shape[2]) if kind else (tile, array.shape[1])
+        return pltpu.VMEM((*lead, *shape), array.dtype)
+
+    outs = pl.pallas_call(
+        functools.partial(
+            fused_kernel,
+            spots,
+            parts,
+            active,
+            body,
+            ([kind for _, kind in sources], [kind for _, kind in results]),
+            len(weights),
+            len(held),
+        ),
+        out_shape=shapes,
+        in_specs=[inside, inside, *([anywhere] * (len(sources) + len(weights) + len(held)))],
+        out_specs=[anywhere] * len(shapes),
+        input_output_aliases={first + index: index for index in range(len(held))},
+        scratch_shapes=[
+            pltpu.VMEM((2, block, width), rows_in.dtype),
+            *(hold(array, kind) for array, kind in sources),
+            *(hold(shape, kind, 2) for shape, kind in results),
+            *(pltpu.VMEM(weight.shape, weight.dtype) for weight in weights),
+            dma((1,)),
+            dma((len(weights),)),
+            dma((1 + len(sources),)),
+            dma((2, len(results))),
+            dma((hops, parts)),
+            dma((hops, parts)),
+            dma((hops, parts)),
+            dma((hops, parts)),
+            dma((spots, parts)),
+            dma((spots, parts)),
+            dma((2, spots, parts)),
+            dma((2, spots, parts)),
+            *scratch,
+        ],
+        compiler_params=pltpu.CompilerParams(collective_id=number, has_side_effects=True),
+        name=f"fused{number}",
+    )(rows_in, small, *(array for array, _ in sources), *weights, *held)
+    return outs[0].reshape(-1, width), list(outs[1:])
 
 
 def body(
@@ -920,14 +1321,7 @@
     units = expert_out.shape[0]
     experts_count = router_weight.shape[1]
     shared_in_t = jnp.transpose(shared_in[0], (1, 2, 0)).reshape(2 * half, width)
-    joined_in = jnp.concatenate(
-        [
-            expert_in.reshape(width, 2 * units),
-            router_weight,
-            jnp.zeros((width, -experts_count % 128), jnp.bfloat16),
-        ],
-        axis=1,
-    )
+    joined_in = join(expert_in[0, 0], router_weight)
 
     packs, members = lax.axis_size(PACKS), lax.axis_size(MEMBERS)
     count = packs * members
@@ -939,31 +1333,48 @@
     heads = output_weight.shape[0] // VD
     top = routes.shape[3]
     tiles = [Tiles(all_rows, pack_rows, pack, active) for active in range(2)]
+    fusing = members == 4 and tiles[0].tile == 2 * rows
 
     def own_pack(value):
         size = value.shape[0] // packs
         return lax.dynamic_slice_in_dim(value, pack * size, size, 0)
 
+    freqs = rope_base ** (-jnp.arange(HALF, dtype=jnp.float32) / HALF)
+    angles = jnp.arange(rows, dtype=jnp.float32)[:, None] * freqs[None, :]
+    turns = jnp.concatenate([jnp.cos(angles), jnp.sin(angles)], axis=1)
+
     def tables_of(block_lengths):
         segment, position = block_layout(block_lengths, rows)
         blocks = segment.shape[0]
-        freqs = rope_base ** (-jnp.arange(HALF, dtype=jnp.float32) / HALF)
-        angles = position.reshape(-1).astype(jnp.float32)[:, None] * freqs[None, :]
+        chosen = position.reshape(-1)[:, None] == jnp.arange(rows, dtype=jnp.int32)[None, :]
+        found = jnp.dot(
+            chosen.astype(jnp.float32),
+            turns,
+            precision=lax.Precision.HIGHEST,
+            preferred_element_type=jnp.float32,
+        )
         return (
-            jnp.cos(angles),
-            jnp.sin(angles),
+            found[:, :HALF],
+            found[:, HALF:],
             segment.reshape(blocks * rows, 1),
             segment.reshape(blocks, 1, rows),
         )
 
     own_lengths = lax.dynamic_index_in_dim(lengths[0, 0], member, 0, keepdims=False)
-    layout = jnp.concatenate([routes.reshape(rows * top), own_lengths])
-    layout = jnp.pad(layout, (0, -layout.shape[0] % 1024)).reshape(8, -1)
-
-    def routed_of(layout_all):
-        routes_all = layout_all.reshape(count, -1)[:, : rows * top].reshape(all_rows, top)
-        return jnp.any(routes_all == me, axis=1, keepdims=True).astype(jnp.float32)
-
+    layout = jnp.concatenate(
+        [
+            jnp.transpose(routes[0, 0]),
+            jnp.pad(own_lengths, (0, rows - own_lengths.shape[0]))[None],
+            jnp.zeros((-(top + 1) % 8, rows), jnp.int32),
+        ],
+        axis=0,
+    )
+
+    layout_all = lax.all_gather(layout.astype(jnp.float32), BOTH, axis=0, tiled=True)
+    layout_all = layout_all.astype(jnp.int32).reshape(count, -1, rows)
+    routed = jnp.any(layout_all[:, :top] == me, axis=1).astype(jnp.float32).reshape(all_rows, 1)
+
+    tables_all = tables_of(layout_all[:, top, : lengths.shape[3]])
     tables_pack = tables_of(lengths[0, 0])
     tables_own = tables_of(own_lengths[None])
     own_cos, own_sin = tables_own[:2]
@@ -979,7 +1390,7 @@
         )
         return normed, keyed, (compressed, scale_attn, scale_latent)
 
-    def run_experts(section, x, routed, into, full):
+    def run_experts(section, x, routed, gathered, into, number, full):
         at = tiles[section]
         results = [
             at.result(2 * units),
@@ -991,34 +1402,51 @@
         if full:
             results.append(at.result(width))
             weights += [expert_out, shared_out]
-        return at.call(
+        if fusing:
+            shapes = [(shape, index == 3) for index, (shape, _) in enumerate(results)]
+            return fused_call(
+                at, x, number, section, experts_body, own_column, [(routed, False)], weights, shapes, gathered, into
+            )
+        (x_all,) = gather_blocks([x], True, number, section, [gathered])
+        return x_all, at.call(
             tiled(experts_body),
             "experts",
-            [(x, at.source(width)), (routed, at.source(1)), (own_column, at.small(own_column))],
+            [(x_all, at.source(width)), (own_column, at.small(own_column)), (routed, at.source(1))],
+            weights,
+            results,
+            into[:4],
+        )
+
+    def run_experts_back(section, grad, routed, stored, gathered, into, number):
+        at = tiles[section]
+        pre, _, prob, shared_pre = stored
+        weights = [joined_in, shared_in_t, expert_out, shared_out]
+        results = [at.result(2 * units), at.result(1, jnp.float32), at.result(width)]
+        scratch = [pltpu.VMEM((at.tile, joined_in.shape[1]), jnp.bfloat16)]
+        if fusing and number is not None:
+            shapes = [(shape, False) for shape, _ in results]
+            sources = [(pre, False), (prob, False), (routed, False), (shared_pre, True)]
+            return fused_call(
+                at, grad, number, section, experts_back_body, own_column, sources, weights, shapes, gathered, into, scratch
+            )
+        grad_all = gathered
+        if number is not None:
+            (grad_all,) = gather_blocks([grad], True, number, section, [gathered])
+        return grad_all, at.call(
+            tiled(experts_back_body),
+            "experts_back",
+            [
+                (grad_all, at.source(width)),
+                (own_column, at.small(own_column)),
+                (pre, at.source(2 * units)),
+                (prob, at.source(experts_count)),
+                (routed, at.source(1)),
+                (shared_pre, at.pack_source(half)),
+            ],
             weights,
             results,
             into,
-            flops=6 * all_rows * width * units,
-        )
-
-    def run_experts_back(section, grad, routed, stored, into):
-        at = tiles[section]
-        pre, _, prob, shared_pre = stored
-        return at.call(
-            tiled(experts_back_body),
-            "experts_back",
-            [
-                (grad, at.source(width)),
-                (pre, at.source(2 * units)),
-                (prob, at.source(experts_count)),
-                (routed, at.source(1)),
-                (own_column, at.small(own_column)),
-                (shared_pre, at.pack_source(half)),
-            ],
-            [joined_in, shared_in_t, expert_out, shared_out],
-            [at.result(2 * units), at.result(1, jnp.float32), at.result(width)],
-            into,
-            [pltpu.VMEM((at.tile, joined_in.shape[1]), jnp.bfloat16)],
+            scratch,
             flops=6 * all_rows * width * units,
         )
 
@@ -1066,21 +1494,26 @@
         tables_pack,
     )
     mixed_first = fresh + scatter_blocks(bf16(dot(attended, output_weight)), rows, False, 1, 0)
-    ffn_all, layout_all = gather_blocks(
-        [bf16(rms_forward(mixed_first, ffn_gain)[0]), layout], True, 2, 0
-    )
-    *stored, partial = run_experts(0, ffn_all, routed_of(layout_all), (), True)
+    empty = [
+        blank((all_rows, width), jnp.bfloat16),
+        *(
+            blank(shape, dtype)
+            for shape, dtype in (
+                ((all_rows + tiles[0].tile, 2 * units), jnp.bfloat16),
+                ((all_rows + tiles[0].tile, units), jnp.bfloat16),
+                ((all_rows + tiles[0].tile, experts_count), jnp.float32),
+                ((2, pack_rows + tiles[0].tile, half), jnp.bfloat16),
+            )
+        ),
+    ]
+    ffn_all, (*stored, partial) = run_experts(
+        0, bf16(rms_forward(mixed_first, ffn_gain)[0]), routed, empty[0], empty[1:], 2, True
+    )
     result_first = mixed_first + scatter_blocks(partial, rows, True, 3, 0)
-    heads_weights = gather_blocks([query_weight, expand_weight, output_weight], False, 4, 1, parts=8)
-    target_all, layout_all = gather_blocks(
-        [boundary[0, 0], layout], True, 5, 1, [blank(ffn_all.shape, jnp.bfloat16), layout_all]
-    )
-    sent, target_all, layout_all, heads_weights = lax.optimization_barrier(
-        (bf16(result_first), target_all, layout_all, heads_weights)
-    )
+    heads_weights = spread_blocks([query_weight, expand_weight, output_weight], 4, 1)
+    (target_all,) = gather_blocks([boundary[0, 0]], True, 5, 1, [blank((all_rows, width), jnp.bfloat16)])
+    sent, target_all, heads_weights = lax.optimization_barrier((bf16(result_first), target_all, heads_weights))
     inbound = lax.ppermute(sent, SECTION, [(0, 1)])
-    routed = routed_of(layout_all)
-    tables_all = tables_of(layout_all.reshape(count, -1)[:, rows * top : rows * top + lengths.shape[3]])
     query_heads, expand_heads, output_heads = (
         value.reshape(members, -1, value.shape[1]) for value in heads_weights
     )
@@ -1096,8 +1529,7 @@
     )
     mixed = jnp.where(is_first, mixed_first, mixed)
     ffn32, scale_ffn = rms_forward(mixed, ffn_gain)
-    (ffn_all,) = gather_blocks([bf16(ffn32)], True, 6, 1, [ffn_all])
-    stored = run_experts(1, ffn_all, routed, stored, False)
+    ffn_all, stored = run_experts(1, bf16(ffn32), routed, ffn_all, stored, 6, False)
 
     def latent_back(own):
         grad_latent, grad_latent_gain = rms_backward(
@@ -1110,7 +1542,7 @@
         grad_hidden_norm, grad_attn_gain = rms_backward(hidden, scale_attn, attn_gain, grad_normed)
         return grad_compressed, grad_hidden_norm, grad_attn_gain, grad_latent_gain
 
-    *grad_units, partial = run_experts_back(1, target_all, routed, stored, ())
+    _, (*grad_units, partial) = run_experts_back(1, None, routed, stored, target_all, (), None)
     grad_ffn_second = scatter_blocks(partial, rows, True, 7, 1)
     grad_mixed = fresh + rms_backward(mixed, scale_ffn, ffn_gain, grad_ffn_second)[0]
     grad_attended = jnp.einsum(
@@ -1145,12 +1577,8 @@
     downbound = lax.ppermute(grad_second, SECTION, [(1, 0)]).astype(jnp.float32)
 
     normed_late, keyed_late, gated_late, _ = lax.optimization_barrier((normed, keyed, stored[1], grad_second))
-    normed_all, keyed_all = gather_blocks([normed_late, keyed_late], True, 9, 1, all_inputs)
-    prepared = prepare(1, normed_all, keyed_all, ffn_all, tables_all, prepared)
-    attended_all, query_all, latent_all, shared_pre, shared_hid = prepared
-    attended_all, shared_hid = attended_all[:all_rows], shared_hid[:all_rows]
     at = tiles[1]
-    (partial,) = at.call(
+    finished = at.call(
         tiled(finish_body),
         "finish",
         [(gated_late, at.source(units)), (stored[3], at.pack_source(half))],
@@ -1158,12 +1586,18 @@
         [at.result(width)],
         flops=2 * all_rows * width * units,
     )
-    result = mixed + scatter_blocks(partial, rows, True, 10, 1)
-
     upstream = jnp.where(is_first, downbound, fresh)
-    (upstream_all,) = gather_blocks([bf16(upstream)], True, 11, 0, [target_all])
-    grad_pre, moved, partial = run_experts_back(0, upstream_all, routed, stored, grad_units)
-    grad_ffn = jnp.where(is_first, scatter_blocks(partial, rows, True, 12, 0), grad_ffn_second)
+    upstream_all, (grad_pre, moved, partial) = run_experts_back(
+        0, bf16(upstream), routed, stored, target_all, [*grad_units, *finished], 11
+    )
+    summed = scatter_blocks(partial, rows, True, 12)
+    result = mixed + summed
+    grad_ffn = jnp.where(is_first, summed, grad_ffn_second)
+    normed_late, keyed_late, _ = lax.optimization_barrier((normed_late, keyed_late, summed))
+    normed_all, keyed_all = gather_blocks([normed_late, keyed_late], True, 9, 1, all_inputs)
+    prepared = prepare(1, normed_all, keyed_all, ffn_all, tables_all, prepared)
+    attended_all, query_all, latent_all, shared_pre, shared_hid = prepared
+    attended_all, shared_hid = attended_all[:all_rows], shared_hid[:all_rows]
     grad_mixed_norm, grad_ffn_gain = rms_backward(mixed, scale_ffn, ffn_gain, grad_ffn)
     grad_mixed = upstream + grad_mixed_norm
     grad_mixed_all = lax.all_gather(bf16(grad_mixed), BOTH, axis=0, tiled=True)

time: 1000 us -> 971 us (0.971)
  Pallas kernels: 715 us -> 661 us
  blocking collectives: 0 us -> 22.3 us
  local copies, waits for them, and re-layouts: 40.3 us -> 26.9 us
  matrix products: 165 us -> 175 us
    pallas_call x9 -> x5, Pallas kernels: 352 us -> 148 us  [gather_blocks(): pl.pallas_call(functools.partial(gather_kernel, spots, cuts, active), out...]
    pallas_call x0 -> x5, Pallas kernels: none -> 193 us  [the longest x3 88.4 us: fused_call(): pl.pallas_call(functools.partial(fused_kernel, spots, parts, active, body...]
    pallas_call x9 -> x6, Pallas kernels: 164 us -> 125 us  [call(): pl.pallas_call(functools.partial(kernel, len(arrays), len(weights), len(i...]
    all_gather x0 -> x1, blocking collectives: none -> 22.3 us  [body(): lax.all_gather(layout.astype(jnp.float32), BOTH, axis=0, tiled=True)]
    ppermute x1, waiting for transfers between devices: 0.01 us -> 17.9 us  [body(): inbound = lax.ppermute(sent, SECTION, [(0, 1)])]
    concatenate x1, local copies, waits for them, and re-layouts: 11 us -> 0.07 us  [body(): jnp.concatenate([jnp.transpose(routes[0, 0]), jnp.pad(own_lengths, (0, ro...]
    ppermute x1, waiting for transfers between devices: 10.9 us -> 0.01 us  [body(): downbound = lax.ppermute(grad_second, SECTION, [(1, 0)]).astype(jnp.float32)]
    pallas_call x5 -> x4, Pallas kernels: 113 us -> 107 us  [scatter_blocks(): pl.pallas_call(functools.partial(scatter_kernel, spots, parts, active), o...]
  transfers between devices with their start and end apart: 4 -> 4, of which waited for: 1 -> 1; matrix products, arithmetic and copies ran while one was open for 10% -> 10% of each run, Pallas kernels for 21% -> 16%
where the time goes in v5:
time: 971 us; the launch traced here: 961 us
  Pallas kernels  661 us (68%)
  matrix products  175 us (18%)
  other arithmetic  39.8 us (4%)
  local copies, waits for them, and re-layouts  26.9 us (3%)
  blocking collectives  22.3 us (2%)
  waiting for transfers between devices  18 us (2%)
  between operations  15.7 us (2%)
    pallas_call x5, Pallas kernels, gather_blocks(): pl.pallas_call(functools.partial(gather_kernel, spots, cuts, active), out...  148 us
    pallas_call x6, Pallas kernels, call(): pl.pallas_call(functools.partial(kernel, len(arrays), len(weights), len(i...  125 us
    pallas_call x4, Pallas kernels, scatter_blocks(): pl.pallas_call(functools.partial(scatter_kernel, spots, parts, active), o...  107 us
    pallas_call x3, Pallas kernels, fused_call(): pl.pallas_call(functools.partial(fused_kernel, spots, parts, active, body...  88.4 us
    pallas_call x1, Pallas kernels, spread_blocks(): pl.pallas_call(functools.partial(spread_kernel, [parts] * len(values), ac...  86.2 us
    dot_general x7, matrix products, t_dot(): lax.dot_general(left, right, (((0,), (0,)), ((), ())), preferred_element_...  63.1 us
    pallas_call x2, Pallas kernels, attend_back(): pl.pallas_call(functools.partial(attend_back_kernel, heads), grid=(count,...  51.4 us
    dot_general x6, matrix products, dot_t(): lax.dot_general(left, right, (((1,), (1,)), ((), ())), preferred_element_...  36.3 us
  transfers between devices with their start and end apart: 4, of which 1 were waited for; matrix products, arithmetic and copies ran while one was open for 10% of the time, Pallas kernels for 16%

profile of v5, /device:TPU:3, one launch (start us, length us, event | category | flops | bytes accessed | tf_op | source)
XLA Modules:
  0.0 960.9 jit_solution(5489174044865029282)
XLA Ops:
  44.6 22.3 %all_gather.6 = f32[128,128]{1,0:T(8,128)S(1)} all-gather(f32[8,128]{1,0:T(8,128)S(1)} %add_convert_fusion.6), channel_id=1, replica_groups=mesh['section'=2,'dp'=4,'expert'=4] {'dp','expert'}, dimensions={0}, use_global_device_ids=true | all-gather | bytes 69632 | tf_op jit(solution)/shard_map/all_gather | solution.py:1373
  72.0 18.5 %join.1.refs_3_.refs_6_ = bf16[2048,1664]{1,0:T(8,128)(2,1)} custom-call(bf16[2048,2,768]{2,1,0:T(2,128)(2,1)} %bitcast.276, bf16[2048,16]{1,0:T(8,128)(2,1)} %bitcast.282), custom_call_target="tpu_custom_call" | custom-call | tf_op jit(solution)/shard_map/join/pallas_call | solution.py:1000
  90.5 11.5 %fused2.1 = (bf16[16,128,2048]{2,1,0:T(8,128)(2,1)}, bf16[2304,1536]{1,0:T(8,128)(2,1)}, bf16[2304,768]{1,0:T(8,128)(2,1)}, f32[2304,16]{1,0:T(8,128)}, bf16[2,7...) custom-call(bf16[128,2048]{1,0:T(8,128)(2,1)} %multiply_convert_fusi, ...), custom_call_target="tpu_custom_call", output_to_operand_aliasing={{0}: (7, {}), {1}: (8, {}), {2}: (9, {}), {3}: (10, {}), {4... | custom-call | tf_op jit(solution)/shard_map/fused2/pallas_call | solution.py:1257
  107.0 51.7 %gather5.1 = bf16[16,128,2048]{2,1,0:T(8,128)(2,1)} custom-call(bf16[128,2048]{1,0:T(8,128)(2,1)} %bitcast.241, bf16[16,128,2048]{2,1,0:T(8,128)(2,1)} %bitcast.242), custom_call_target="tpu_custom_call", output_to_operand_aliasing={{}: (1, {})} | custom-call | tf_op jit(solution)/shard_map/gather5/pallas_call | solution.py:263
  158.7 86.2 %spread4.1 = (bf16[4,2048,768]{2,1,0:T(8,128)(2,1)}, bf16[4,512,1024]{2,1,0:T(8,128)(2,1)}, bf16[4,512,2048]{2,1,0:T(8,128)(2,1)}) custom-call(bf16[2048,768]{1,0:T(8,128)(2,1)} %bitcast.277, bf16[512,1024]{1,0:T(8,128)(2,1)} %bitcast.286, bf16[512,2048]{1,0:T(8,128)(2,1)} %bitcast.280), custom_call_target="tpu_custom_call" | custom-call | tf_op jit(solution)/shard_map/spread4/pallas_call | solution.py:370
  261.6 17.9 %collective-permute-done = bf16[128,2048]{1,0:T(8,128)(2,1)S(1)} collective-permute-done((bf16[128,2048]{1,0:T(8,128)(2,1)}, bf16[128,2048]{1,0:T(8,128)(2,1)S(1)}, u32[]{:S(2)}, u32[]{:S(2)}) %collective-permute-start) | collective-permute-done | bytes 524320 | tf_op jit(solution)/shard_map/ppermute | solution.py:1516
  315.9 74.4 %fused6.1 = (bf16[16,128,2048]{2,1,0:T(8,128)(2,1)}, bf16[2304,1536]{1,0:T(8,128)(2,1)}, bf16[2304,768]{1,0:T(8,128)(2,1)}, f32[2304,16]{1,0:T(8,128)}, bf16[2,768,704]{2,1,0:T(8,128)(2,1)}) custom-call(bf16[128,2048]{1,0:T(8,128)(2,1)} %multiply_convert_fusion.refs_0_, ...), custom_call_target="tpu_custom_call", output_to_operand_aliasing={{0}: (5, {}), {1}: (6, {}), {2}: (7, {}), {3}: (8, {}), {4}... | custom-call | tf_op jit(solution)/shard_map/fused6/pallas_call | solution.py:1257
  390.3 50.3 %experts_back.1 = (bf16[2304,1536]{1,0:T(8,128)(2,1)}, f32[2304,1]{1,0:T(8,128)}, bf16[2304,2048]{1,0:T(8,128)(2,1)}) custom-call(s32[3]{0:T(128)} %get-tuple-element.193.control, bf16[2048,2048]{1,0:T(8,128)(2,1)} %bitcast.243, f32[1,16]{1,0:T(1,128)} %compare_convert_fusion.1.refs_1_, bf16[2304,1536]{1,0:T(8,128)(2,1)} %get-tuple-element.97.refs_2_, ...), custom_call_target="tpu_custom_call" | custom-call | flops 19327352832 | bytes 33554432 | tf_op jit(solution)/shard_map/experts_back/pallas_call | solution.py:789
  440.7 50.7 %scatter7.1 = f32[128,2048]{1,0:T(8,128)} custom-call(bf16[18,128,2048]{2,1,0:T(8,128)(2,1)} %bitcast.267), custom_call_target="tpu_custom_call" | custom-call | tf_op jit(solution)/shard_map/scatter7/pallas_call | solution.py:564
  500.8 11.8 %attend_back.2 = (bf16[512,768]{1,0:T(8,128)(2,1)}, bf16[512,1024]{1,0:T(8,128)(2,1)}, f32[512,64]{1,0:T(8,128)}) custom-call(bf16[512,768]{1,0:T(8,128)(2,1)} %get-tuple-element.101.q_ref, bf16[512,1024]{1,0:T(8,128)(2,1)} %bitcast.269, bf16[128,576]{1,0:T(8,128)(2,1)} %pad_maximum_fusion.2.key_ref.refs_1_, bf16[512,512]{1,0:T(8,128)(2,1)} %bitcast.293, ...), custom_call_target="tpu_custom_call" | custom-call | flops 436207616 | bytes 4194304 | tf_op jit(solution)/shard_map/attend_back/pallas_call | solution.py:693
  543.6 16.8 %finish.1.refs_13_ = bf16[2304,2048]{1,0:T(8,128)(2,1)} custom-call(s32[3]{0:T(128)} %get-tuple-element.193.control, bf16[2304,768]{1,0:T(8,128)(2,1)} %get-tuple-element.117.refs_0_, bf16[2,768,704]{2,1,0:T(8,128)(2,1)} %get-tuple-element.99.refs_5_.refs_1_, bf16[768,2048]{1,0:T(8,128)(2,1)} %bitcast.256, bf16[704,2048]{1,0:T(8,128)(2,1)} %bitcast.260), custom_call_target="tpu_custom_call" | custom-call | flops 6442450944 | bytes 33554432 | tf_op jit(solution)/shard_map/finish/pallas_call | solution.py:789
  563.9 52.5 %scatter12.1 = f32[128,2048]{1,0:T(8,128)} custom-call(bf16[18,128,2048]{2,1,0:T(8,128)(2,1)} %bitcast.253), custom_call_target="tpu_custom_call" | custom-call | tf_op jit(solution)/shard_map/scatter12/pallas_call | solution.py:564
  621.3 20.6 %shared.3 = (bf16[2,2304,704]{2,1,0:T(8,128)(2,1)}, bf16[2304,704]{1,0:T(8,128)(2,1)}) custom-call(s32[3]{0:T(128)} %get-tuple-element.193.control, bf16[2048,2048]{1,0:T(8,128)(2,1)} %bitcast.235, bf16[1408,2048]{1,0:T(8,128)(2,1)} %bitcast.252, bf16[2,2304,704]{2,1,0:T(8,128)(2,1)} %get-tuple-element.140.refs_2_, ...), custom_call_target="tpu_custom_call", output_to_operand_aliasing={{0}: (3, {}), {1}: (4, {})} | custom-call | flops 11811160064 | bytes 33554432 | tf_op jit(solution)/shard_map/shared/pallas_call | solution.py:789
  641.9 67.5 %gather9.1 = (bf16[16,128,2048]{2,1,0:T(8,128)(2,1)}, bf16[16,128,576]{2,1,0:T(8,128)(2,1)}) custom-call(bf16[128,2048]{1,0:T(8,128)(2,1)} %copy-done.9, bf16[128,576]{1,0:T(8,128)(2,1)} %pad_maximum_fusion.2.key_ref.refs_1_, bf16[16,128,2048]{2,1,0:T(8,128)(2,1)} %get-tuple-element.105, ...), custom_call_target="tpu_custom_call", output_to_operand_aliasing={{0}: (2, {}), {1}: (3, {})} | custom-call | tf_op jit(solution)/shard_map/gather9/pallas_call | solution.py:263
  711.7 31.0 %heads.3 = (bf16[2304,512]{1,0:T(8,128)(2,1)}, bf16[2304,768]{1,0:T(8,128)(2,1)}, bf16[2304,1024]{1,0:T(8,128)(2,1)}) custom-call(s32[3]{0:T(128)} %get-tuple-element.193.control, bf16[2048,2048]{1,0:T(8,128)(2,1)} %bitcast.271, bf16[2048,576]{1,0:T(8,128)(2,1)} %bitcast.263, ...), custom_call_target="tpu_custom_call", output_to_operand_aliasing={{0}: (9, {}), {1}: (10, {}), {2}: (11, {})} | custom-call | flops 12884901888 | bytes 33554432 | tf_op jit(solution)/shard_map/heads/pallas_call | solution.py:789
  742.8 12.0 %convolution_bitcast_fusion = f32[1,1,768,2048]{3,2,1,0:T(8,128)} fusion(bf16[2048,2048]{1,0:T(8,128)(2,1)} %bitcast.244, bf16[2304,768]{1,0:T(8,128)(2,1)} %get-tuple-element.117.refs_0_), kind=kOutput, calls=%fused_computation.18 | convolution fusion | flops 6442450944 | bytes 17825792 | tf_op jit(solution)/shard_map/dot_general | solution.py:35
  754.8 10.4 %convolution_bitcast_fusion.2 = f32[1,704,2048]{2,1,0:T(8,128)} fusion(bf16[2048,2048]{1,0:T(8,128)(2,1)} %bitcast.245, bf16[2304,704]{1,0:T(8,128)(2,1)S(1)} %copy-done.64), kind=kOutput, calls=%fused_computation.20 | convolution fusion | flops 5905580032 | bytes 17301504 | tf_op jit(solution)/shard_map/dot_general | solution.py:35
  765.2 15.2 %fusion.19 = (bf16[1,2048,704]{2,1,0:T(8,128)(2,1)}, bf16[1,2048,704]{2,1,0:T(8,128)(2,1)}) fusion(bf16[2,2304,704]{2,1,0:T(8,128)(2,1)} %get-tuple-element.142, bf16[2048,2048]{1,0:T(8,128)(2,1)} %bitcast.246, bf16[1,704,2048]{2,1,0:T(8,128)(2,1)S(1)} %copy-done.12), kind=kOutput, calls=%fused_computation.26 | convolution fusion | flops 5927206912 | bytes 22806528 | tf_op jit(solution)/shard_map/dot_general | solution.py:29
  780.4 18.2 %fusion.13 = f32[1,2048,2,704]{1,3,2,0:T(8,128)} fusion(bf16[2048,2048,1]{1,0,2:T(8,128)(2,1)S(1)} %bitcast.240, bf16[1,2048,704]{2,1,0:T(8,128)(2,1)} %get-tuple-element.159, bf16[1,2048,704]{2,1,0:T(8,128)(2,1)} %get-tuple-element.158), kind=kOutput, calls=%fused_computation.17 | convolution fusion | flops 11822694400 | bytes 25690112 | tf_op jit(solution)/shard_map/dot_general | solution.py:1639
  798.6 9.9 %convolution_convert_fusion.1.grad_ref = bf16[2048,512]{1,0:T(8,128)(2,1)} fusion(bf16[2048,2048]{1,0:T(8,128)(2,1)} %all-gather.2.cloned.1.call-done, bf16[1,512,2048]{2,1,0:T(8,128)(2,1)} %param.23), kind=kOutput, calls=%fused_computation.28 | convolution fusion | flops 4296015872 | bytes 12582912 | tf_op jit(solution)/shard_map/dot_general | solution.py:29
  808.5 39.6 %attend_back.3 = (bf16[2048,768]{1,0:T(8,128)(2,1)}, bf16[2048,1024]{1,0:T(8,128)(2,1)}, f32[2048,64]{1,0:T(8,128)}) custom-call(bf16[2304,768]{1,0:T(8,128)(2,1)} %get-tuple-element.130.q_ref, bf16[2304,1024]{1,0:T(8,128)(2,1)} %get-tuple-element.131.lat_ref, bf16[2048,576]{1,0:T(8,128)(2,1)} %bitcast.264, ...), custom_call_target="tpu_custom_call" | custom-call | flops 1744830464 | bytes 16777216 | tf_op jit(solution)/shard_map/attend_back/pallas_call | solution.py:693
  856.9 20.0 %pair_grad.1 = f32[2048,2,768]{2,1,0:T(2,128)} custom-call(bf16[2048,2048]{1,0:T(8,128)(2,1)} %bitcast.236, bf16[2304,1536]{1,0:T(8,128)(2,1)} %get-tuple-element.144.grad_ref), custom_call_target="tpu_custom_call" | custom-call | flops 12884901888 | bytes 27262976 | tf_op jit(solution)/shard_map/pair_grad/pallas_call | solution.py:971
  909.0 23.3 %gather13.1 = (bf16[16,128,576]{2,1,0:T(8,128)(2,1)}, f32[16,8,896]{2,1,0:T(8,128)}) custom-call(bf16[128,576]{1,0:T(8,128)(2,1)} %copy-done.23, f32[8,896]{1,0:T(8,128)} %reshape.502.refs_1_), custom_call_target="tpu_custom_call" | custom-call | tf_op jit(solution)/shard_map/gather13/pallas_call | solution.py:263
  936.0 9.9 %convolution_bitcast_fusion.3 = f32[1,2048,576]{1,2,0:T(8,128)} fusion(bf16[16,128,2048]{2,1,0:T(8,128)(2,1)} %get-tuple-element.125, bf16[16,128,576]{2,1,0:T(8,128)(2,1)} %get-tuple-element.137), kind=kOutput, calls=%fused_computation.21 | convolution fusion | flops 4831838208 | bytes 15466496 | tf_op jit(solution)/shard_map/dot_general | solution.py:35
  (274 shorter events, 202.9 us)
Async XLA Ops:
  7.2 791.4 %all-gather.2.cloned.1.call-start = ((), (), s32[]{:S(2)}) async-start(), calls=%async_computation.1 | async-start | bytes 8912896 | tf_op jit(solution)/shard_map/all_gather | solution.py:1603
  12.6 516.0 %copy-start.16 = (f32[128,64]{1,0:T(8,128)}, f32[128,64]{1,0:T(8,128)S(1)}, u32[]{:S(2)}) copy-start(f32[128,64]{1,0:T(8,128)S(1)} %fusion.66) | copy-start | bytes 98308
  14.2 14.7 %copy-start.39 = (s32[4,128]{1,0:T(4,128)}, s32[4,128]{1,0:T(4,128)S(1)}, u32[]{:S(2)}) copy-start(s32[4,128]{1,0:T(4,128)S(1)} %get-tuple-element.153) | copy-start | bytes 6148
  41.5 27.3 %copy-start.32 = (bf16[1,2048,16]{1,2,0:T(8,128)(2,1)S(1)}, bf16[1,2048,16]{1,2,0:T(8,128)(2,1)}, u32[]{:S(2)}) copy-start(bf16[1,2048,16]{1,2,0:T(8,128)(2,1)} %param.25) | copy-start | bytes 196612
  41.5 28.3 %copy-start.27 = (f32[1,2048]{1,0:T(1,128)S(1)}, f32[1,2048]{1,0:T(1,128)}, u32[]{:S(2)}) copy-start(f32[1,2048]{1,0:T(1,128)} %param.24) | copy-start | bytes 24580
  66.9 23.7 %copy-start.29 = (s32[16,8,128]{2,1,0:T(8,128)}, s32[16,8,128]{2,1,0:T(8,128)S(1)}, u32[]{:S(2)}) copy-start(s32[16,8,128]{2,1,0:T(8,128)S(1)} %convert_bitcast_fusion) | copy-start | bytes 196612
  244.8 34.7 %copy-start.2 = (bf16[1,1,128,2048]{3,2,1,0:T(8,128)(2,1)S(1)}, bf16[1,1,128,2048]{3,2,1,0:T(8,128)(2,1)}, u32[]{:S(2)}) copy-start(bf16[1,1,128,2048]{3,2,1,0:T(8,128)(2,1)} %param.15) | copy-start | bytes 1572868
  244.9 34.7 %collective-permute-start = (bf16[128,2048]{1,0:T(8,128)(2,1)}, bf16[128,2048]{1,0:T(8,128)(2,1)S(1)}, u32[]{:S(2)}, u32[]{:S(2)}) collective-permute-start(bf16[128,2048]{1,0:T(8,128)(2,1)} %add_convert_fusion.1), channel_id=1, source_target_pairs={{0,16},{1,17},{2,18},{3,19},{4,20},{5,21},{6,22},{7,23},{8,24},{9,... | collective-permute-start | bytes 1572872 | tf_op jit(solution)/shard_map/ppermute | solution.py:1516
  261.6 21.5 %copy-start.34 = (f32[1,512]{1,0:T(1,128)S(1)}, f32[1,512]{1,0:T(1,128)}, u32[]{:S(2)}) copy-start(f32[1,512]{1,0:T(1,128)} %param.21) | copy-start | bytes 6148
  279.5 259.4 %copy-start.7 = (bf16[128,2048]{1,0:T(8,128)(2,1)}, bf16[128,2048]{1,0:T(8,128)(2,1)S(1)}, u32[]{:S(2)}) copy-start(bf16[128,2048]{1,0:T(8,128)(2,1)S(1)} %collective-permute-done) | copy-start | bytes 1572868
  313.9 179.2 %copy-start.40 = (f32[128]{0:T(128)}, f32[128]{0:T(128)S(1)}, u32[]{:S(2)}) copy-start(f32[128]{0:T(128)S(1)} %get-tuple-element.183) | copy-start | bytes 1540
  314.0 179.2 %copy-start.50 = (f32[128]{0:T(128)}, f32[128]{0:T(128)S(1)}, u32[]{:S(2)}) copy-start(f32[128]{0:T(128)S(1)} %get-tuple-element.182) | copy-start | bytes 1540
  493.2 19.4 %copy-start.35 = (f32[1,512]{1,0:T(1,128)S(1)}, f32[1,512]{1,0:T(1,128)}, u32[]{:S(2)}) copy-start(f32[1,512]{1,0:T(1,128)} %param.21) | copy-start | bytes 6148
  542.3 18.2 %collective-permute-start.1 = (bf16[128,2048]{1,0:T(8,128)(2,1)}, bf16[128,2048]{1,0:T(8,128)(2,1)S(1)}, u32[]{:S(2)}, u32[]{:S(2)}) collective-permute-start(bf16[128,2048]{1,0:T(8,128)(2,1)} %add_convert_fusion), channel_id=1, source_target_pairs={{16,0},{17,1},{18,2},{19,3},{20,4},{21,5},{22,6},{23,7},{24,8},{25... | collective-permute-start | bytes 1572872 | tf_op jit(solution)/shard_map/ppermute | solution.py:1577
  560.4 58.5 %copy-start.18 = (bf16[128,2048]{1,0:T(8,128)(2,1)}, bf16[128,2048]{1,0:T(8,128)(2,1)S(1)}, u32[]{:S(2)}) copy-start(bf16[128,2048]{1,0:T(8,128)(2,1)S(1)} %collective-permute-done.1) | copy-start | bytes 1572868
  619.0 22.9 %copy-start.56 = (f32[128]{0:T(128)}, f32[128]{0:T(128)S(1)}, u32[]{:S(2)}) copy-start(f32[128]{0:T(128)S(1)} %broadcast_multiply_fusion.3) | copy-start | bytes 1540
  621.2 281.0 %reduce-scatter.2.cloned.1.call-start = ((), (), s32[]{:S(2)}) async-start(), calls=%async_computation.2 | async-start | bytes 3440640 | tf_op jit(solution)/shard_map/reduce_scatter | solution.py:1608
  742.8 12.0 %copy-start.64 = (bf16[2304,704]{1,0:T(8,128)(2,1)S(1)}, bf16[2304,704]{1,0:T(8,128)(2,1)}, u32[]{:S(2)}) copy-start(bf16[2304,704]{1,0:T(8,128)(2,1)} %get-tuple-element.143) | copy-start | bytes 9732100
  754.8 25.7 %slice-start = ((s8[8388608]{0:T(1024)(128)(4,1)}), s8[4194304]{0:T(1024)(128)(4,1)S(1)}, s32[]{:S(2)}) async-start(s8[8388608]{0:T(1024)(128)(4,1)} %bitcast.238), calls=%async_computation.3 | async-start | bytes 8388608
  765.2 15.2 %slice-start.1 = ((s8[8388608]{0:T(1024)(128)(4,1)}), s8[4194304]{0:T(1024)(128)(4,1)S(1)}, s32[]{:S(2)}) async-start(s8[8388608]{0:T(1024)(128)(4,1)} %bitcast.238), calls=%async_computation.4 | async-start | bytes 8388608
  876.9 16.3 %slice-start.2 = ((s8[8388608]{0:T(1024)(128)(4,1)}), s8[4194304]{0:T(1024)(128)(4,1)S(1)}, s32[]{:S(2)}) async-start(s8[8388608]{0:T(1024)(128)(4,1)} %bitcast.272), calls=%async_computation.5 | async-start | bytes 8388608
  893.2 11.4 %copy-start.17 = (f32[128,64]{1,0:T(8,128)S(1)}, f32[128,64]{1,0:T(8,128)}, u32[]{:S(2)}) copy-start(f32[128,64]{1,0:T(8,128)} %copy-done.16) | copy-start | bytes 98308
  893.2 12.7 %copy-start.31 = (f32[1,2048]{1,0:T(1,128)S(1)}, f32[1,2048]{1,0:T(1,128)}, u32[]{:S(2)}) copy-start(f32[1,2048]{1,0:T(1,128)} %param.18) | copy-start | bytes 24580
  893.2 12.7 %copy-start.45 = (f32[128]{0:T(128)S(1)}, f32[128]{0:T(128)}, u32[]{:S(2)}) copy-start(f32[128]{0:T(128)} %copy-done.43) | copy-start | bytes 1540
  (49 other events, 248.1 us)
Sparse Core Ops, SparseCore 0:
  621.4 154.6 all-gather.1
  857.1 33.8 reduce-scatter.1

commit v6 on v5

--- a/solution.py
+++ b/solution.py
@@ -132,7 +132,7 @@
     return spot * 4 + chip * 2 + core
 
 
-def gather_kernel(spots, cuts, active, *refs):
+def gather_kernel(spots, cuts, wide, active, *refs):
     arrays = len(cuts)
     x_refs, o_refs, sems = refs[:arrays], refs[-9 - arrays : -9], refs[-9:]
     own_sem, up_out, up_in, down_out, down_in, over_out, over_in, pair_out, pair_in = sems
@@ -154,6 +154,12 @@
             array, cut = units[unit]
             return x_refs[array].at[cut]
 
+        def lane(unit):
+            return wide[units[unit][0]]
+
+        def spread(unit):
+            return range(spots) if lane(unit) else [0]
+
         def up(source, at, unit, reach):
             return remote(
                 source, piece(unit, slot(at, chip, core)), {PACKS: spot + 1}, up_out.at[reach, unit], up_in.at[reach, unit]
@@ -182,19 +188,26 @@
                 pair_in.at[c, at, unit],
             )
 
-        mine = slot(spot, chip, core)
+        home = lambda unit: spot if lane(unit) else 0
         for unit in range(len(units)):
             source = first(unit)
-            over(source, spot, unit).start()
-            if spots > 1:
+            over(source, home(unit), unit).start()
+            if spots > 1 and lane(unit):
                 pl.when(spot < spots - 1)(lambda: up(source, spot, unit, 0).start())
                 pl.when(spot > 0)(lambda: down(source, spot, unit, 0).start())
-            pair(source, spot, chip, unit).start()
-        own = [pltpu.make_async_copy(x_refs[a], o_refs[a].at[mine], own_sem.at[a]) for a in range(arrays)]
+            pair(source, home(unit), chip, unit).start()
+        own = [
+            pltpu.make_async_copy(
+                x_refs[a], o_refs[a].at[slot(spot if wide[a] else 0, chip, core)], own_sem.at[a]
+            )
+            for a in range(arrays)
+        ]
         for copy in own:
             copy.start()
         for reach in range(1, spots):
             for unit in range(len(units)):
+                if not lane(unit):
+                    continue
 
                 def below(reach=reach, unit=unit):
                     at = spot - reach
@@ -219,7 +232,10 @@
             if reach > 0:
                 sides = [(spot >= reach, spot - reach), (spot + reach < spots, spot + reach)]
             for unit in range(len(units)):
+                if not lane(unit) and reach > 0:
+                    continue
                 for there, at in sides:
+                    at = at if lane(unit) else 0
 
                     def hand_on(at=at, unit=unit):
                         source = piece(unit, slot(at, 1 - chip, core))
@@ -230,12 +246,12 @@
         for copy in own:
             copy.wait()
         for unit in range(len(units)):
-            source = piece(unit, mine)
-            for at in range(spots):
+            source = first(unit)
+            for at in spread(unit):
                 over(source, at, unit).wait_send()
                 for c in range(2):
                     pair(source, at, c, unit).wait()
-            for reach in range(spots - 1):
+            for reach in range(spots - 1 if lane(unit) else 0):
                 pl.when((spot >= reach) & (spot < spots - 1))(lambda: up(source, spot, unit, reach).wait_send())
                 pl.when((spot + reach < spots) & (spot > 0))(lambda: down(source, spot, unit, reach).wait_send())
 
@@ -245,10 +261,12 @@
         pl.when(lax.axis_index(SECTION) == active)(run)
 
 
-def gather_blocks(values, across, number, active=None, into=None, parts=4):
-    axes = BOTH if across else MEMBERS
+def gather_blocks(values, across, number, active=None, into=None, parts=4, wide=None):
+    wide = [across] * len(values) if wide is None else wide
     if lax.axis_size(MEMBERS) != 4:
-        found = [lax.all_gather(value, axes, axis=0, tiled=True) for value in values]
+        found = [
+            lax.all_gather(value, BOTH if far else MEMBERS, axis=0, tiled=True) for value, far in zip(values, wide)
+        ]
         if into is None:
             return found
         chosen = lax.axis_index(SECTION) == active
@@ -258,10 +276,13 @@
     units = sum(cuts)
     dma = pltpu.SemaphoreType.DMA
     hops = max(spots - 1, 1)
-    shapes = [jax.ShapeDtypeStruct((spots * 4, *value.shape), value.dtype) for value in values]
+    shapes = [
+        jax.ShapeDtypeStruct(((spots if far else 1) * 4, *value.shape), value.dtype)
+        for value, far in zip(values, wide)
+    ]
     held = [] if into is None else [old.reshape(shape.shape) for old, shape in zip(into, shapes)]
     outs = pl.pallas_call(
-        functools.partial(gather_kernel, spots, cuts, active),
+        functools.partial(gather_kernel, spots, cuts, wide, active),
         out_shape=shapes,
         in_specs=[pl.BlockSpec(memory_space=pltpu.VMEM)] * len(values)
         + [pl.BlockSpec(memory_space=pl.ANY)] * len(held),
@@ -727,11 +748,29 @@
     return bf16(grad_hidden * up * slope), bf16(grad_hidden * act)
 
 
-def load(sources, targets, sems):
-    copies = [
-        pltpu.make_async_copy(source, target, sems.at[index])
-        for index, (source, target) in enumerate(zip(sources, targets))
-    ]
+def columns(pieces):
+    start = 0
+    for piece in pieces:
+        yield start, piece.shape[1]
+        start += piece.shape[1]
+
+
+def hold_weight(pieces):
+    return pltpu.VMEM((pieces[0].shape[0], sum(piece.shape[1] for piece in pieces)), pieces[0].dtype)
+
+
+def loads_of(counts, sources, targets, sems):
+    copies = []
+    for pieces, target in zip(counts, targets):
+        group, sources = sources[:pieces], sources[pieces:]
+        for source, (start, size) in zip(group, columns(group)):
+            place = target if pieces == 1 else target.at[:, pl.ds(start, size)]
+            copies.append(pltpu.make_async_copy(source, place, sems.at[len(copies)]))
+    return copies
+
+
+def load(*args):
+    copies = loads_of(*args)
     for copy in copies:
         copy.start()
     for copy in copies:
@@ -785,17 +824,19 @@
         arrays, specs = zip(*sources)
         shapes, out_specs = zip(*results)
         anywhere = pl.BlockSpec(memory_space=pl.ANY)
-        first = 1 + len(arrays) + len(weights)
+        pieces = [piece for weight in weights for piece in weight]
+        counts = [len(weight) for weight in weights]
+        first = 1 + len(arrays) + len(pieces)
         return pl.pallas_call(
-            functools.partial(kernel, len(arrays), len(weights), len(into), len(results)),
+            functools.partial(kernel, len(arrays), counts, len(into), len(results)),
             grid_spec=pltpu.PrefetchScalarGridSpec(
                 num_scalar_prefetch=1,
                 grid=(self.count,),
-                in_specs=[*specs, *([anywhere] * (len(weights) + len(into)))],
+                in_specs=[*specs, *([anywhere] * (len(pieces) + len(into)))],
                 out_specs=list(out_specs),
                 scratch_shapes=[
-                    *[pltpu.VMEM(weight.shape, weight.dtype) for weight in weights],
-                    pltpu.SemaphoreType.DMA((len(weights),)),
+                    *[hold_weight(weight) for weight in weights],
+                    pltpu.SemaphoreType.DMA((len(pieces),)),
                     *scratch,
                 ],
             ),
@@ -803,18 +844,19 @@
             input_output_aliases={first + index: index for index in range(len(into))},
             name=name,
             cost_estimate=pl.CostEstimate(flops=flops, bytes_accessed=self.rows * 16384, transcendentals=0),
-        )(self.control, *arrays, *weights, *into)
+        )(self.control, *arrays, *pieces, *into)
 
 
 def tiled(body):
-    def kernel(n_sources, n_weights, n_into, n_results, control, *refs):
+    def kernel(n_sources, counts, n_into, n_results, control, *refs):
+        n_weights, n_pieces = len(counts), sum(counts)
         sources, refs = refs[:n_sources], refs[n_sources:]
-        stored, refs = refs[:n_weights], refs[n_weights + n_into :]
+        stored, refs = refs[:n_pieces], refs[n_pieces + n_into :]
         results, refs = refs[:n_results], refs[n_results:]
         weights, sems, scratch = refs[:n_weights], refs[n_weights], refs[n_weights + 1 :]
 
         def run():
-            pl.when(pl.program_id(0) == 0)(lambda: load(stored, weights, sems))
+            pl.when(pl.program_id(0) == 0)(lambda: load(counts, stored, weights, sems))
             body(inside_pack(control), [sources[0][...], *sources[1:]], weights, results, scratch)
 
         pl.when(control[2] == 1)(run)
@@ -984,32 +1026,6 @@
     )(x, grad)
 
 
-def join_kernel(in_ref, router_ref, out_ref):
-    units, routes_width = in_ref.shape[2], router_ref.shape[1]
-    both = in_ref[...].astype(jnp.float32)
-    out_ref[:, :units] = bf16(both[:, 0])
-    out_ref[:, units : 2 * units] = bf16(both[:, 1])
-    out_ref[:, 2 * units :] = jnp.zeros_like(out_ref[:, 2 * units :])
-    out_ref[:, 2 * units : 2 * units + routes_width] = router_ref[...]
-
-
-def join(expert_in, router):
-    width, _, units = expert_in.shape
-    total = 2 * units + router.shape[1] + -router.shape[1] % 128
-    tile = 256
-    return pl.pallas_call(
-        join_kernel,
-        grid=(width // tile,),
-        in_specs=[
-            pl.BlockSpec((tile, 2, units), lambda i: (i, 0, 0)),
-            pl.BlockSpec((tile, router.shape[1]), lambda i: (i, 0)),
-        ],
-        out_specs=pl.BlockSpec((tile, total), lambda i: (i, 0)),
-        out_shape=jax.ShapeDtypeStruct((width, total), expert_in.dtype),
-        name="join",
-    )(expert_in, router)
-
-
 def blank(shape, dtype):
     return pl.pallas_call(
         lambda out_ref: None,
@@ -1043,12 +1059,13 @@
     return total
 
 
-def fused_kernel(spots, parts, active, body, pack_kinds, n_weights, n_into, *refs):
+def fused_kernel(spots, parts, active, body, pack_kinds, counts, n_into, *refs):
     source_kinds, result_kinds = pack_kinds
     n_sources, n_results = len(source_kinds), len(result_kinds)
+    n_weights, n_pieces = len(counts), sum(counts)
     x_ref, small_ref, refs = refs[0], refs[1], refs[2:]
     sources, refs = refs[:n_sources], refs[n_sources:]
-    stored, refs = refs[:n_weights], refs[n_weights + n_into :]
+    stored, refs = refs[:n_pieces], refs[n_pieces + n_into :]
     o_ref, refs = refs[0], refs[1:]
     results, refs = refs[:n_results], refs[n_results:]
     x_tile, refs = refs[0], refs[1:]
@@ -1063,10 +1080,7 @@
     tile = 2 * block
 
     def run():
-        loads = [
-            pltpu.make_async_copy(source, target, weight_sem.at[index])
-            for index, (source, target) in enumerate(zip(stored, weights))
-        ]
+        loads = loads_of(counts, stored, weights, weight_sem)
         for copy in loads:
             copy.start()
         spot, chip, core = places(spots)
@@ -1115,6 +1129,28 @@
         ranks = ranked_spots(spots, spot)
         order = arrival_order(spots)
 
+        def hand_on(reach):
+            for part in range(parts):
+
+                def below(part=part):
+                    at = spot - reach
+                    source = piece(slot(at, chip, core), part)
+                    up(source, at, part, reach - 1).wait_recv()
+                    pl.when(spot < spots - 1)(lambda: up(source, at, part, reach).start())
+                    over(source, at, part).start()
+                    pair(source, at, chip, part).start()
+
+                def above(part=part):
+                    at = spot + reach
+                    source = piece(slot(at, chip, core), part)
+                    down(source, at, part, reach - 1).wait_recv()
+                    pl.when(spot > 0)(lambda: down(source, at, part, reach).start())
+                    over(source, at, part).start()
+                    pair(source, at, chip, part).start()
+
+                pl.when(spot >= reach)(below)
+                pl.when(spot + reach < spots)(above)
+
         def arrive(rank, across):
             at = ranks[rank]
             if across:
@@ -1126,25 +1162,7 @@
                     pair(first(part), at, 1 - chip, part).wait_recv()
                 return
             if rank > 0:
-                for reach in range(1, spots):
-                    for part in range(parts):
-
-                        def below(reach=reach, part=part):
-                            source = piece(slot(at, chip, core), part)
-                            up(source, at, part, reach - 1).wait_recv()
-                            pl.when(spot < spots - 1)(lambda: up(source, at, part, reach).start())
-                            over(source, at, part).start()
-                            pair(source, at, chip, part).start()
-
-                        def above(reach=reach, part=part):
-                            source = piece(slot(at, chip, core), part)
-                            down(source, at, part, reach - 1).wait_recv()
-                            pl.when(spot > 0)(lambda: down(source, at, part, reach).start())
-                            over(source, at, part).start()
-                            pair(source, at, chip, part).start()
-
-                        pl.when(spot - at == reach)(below)
-                        pl.when(at - spot == reach)(above)
+                hand_on(rank)
             for part in range(parts):
                 pair(first(part), at, chip, part).wait_recv()
 
@@ -1248,7 +1266,8 @@
     inside = pl.BlockSpec(memory_space=pltpu.VMEM)
     shapes = [jax.ShapeDtypeStruct((spots * 4, block, width), rows_in.dtype), *(shape for shape, _ in results)]
     held = [gathered.reshape(shapes[0].shape), *into]
-    first = 2 + len(sources) + len(weights)
+    pieces = [piece for weight in weights for piece in weight]
+    first = 2 + len(sources) + len(pieces)
 
     def hold(array, kind, *lead):
         shape = (2, tile, array.shape[2]) if kind else (tile, array.shape[1])
@@ -1262,20 +1281,20 @@
             active,
             body,
             ([kind for _, kind in sources], [kind for _, kind in results]),
-            len(weights),
+            [len(weight) for weight in weights],
             len(held),
         ),
         out_shape=shapes,
-        in_specs=[inside, inside, *([anywhere] * (len(sources) + len(weights) + len(held)))],
+        in_specs=[inside, inside, *([anywhere] * (len(sources) + len(pieces) + len(held)))],
         out_specs=[anywhere] * len(shapes),
         input_output_aliases={first + index: index for index in range(len(held))},
         scratch_shapes=[
             pltpu.VMEM((2, block, width), rows_in.dtype),
             *(hold(array, kind) for array, kind in sources),
             *(hold(shape, kind, 2) for shape, kind in results),
-            *(pltpu.VMEM(weight.shape, weight.dtype) for weight in weights),
+            *(hold_weight(weight) for weight in weights),
             dma((1,)),
-            dma((len(weights),)),
+            dma((len(pieces),)),
             dma((1 + len(sources),)),
             dma((2, len(results))),
             dma((hops, parts)),
@@ -1290,7 +1309,7 @@
         ],
         compiler_params=pltpu.CompilerParams(collective_id=number, has_side_effects=True),
         name=f"fused{number}",
-    )(rows_in, small, *(array for array, _ in sources), *weights, *held)
+    )(rows_in, small, *(array for array, _ in sources), *pieces, *held)
     return outs[0].reshape(-1, width), list(outs[1:])
 
 
@@ -1321,7 +1340,11 @@
     units = expert_out.shape[0]
     experts_count = router_weight.shape[1]
     shared_in_t = jnp.transpose(shared_in[0], (1, 2, 0)).reshape(2 * half, width)
-    joined_in = join(expert_in[0, 0], router_weight)
+    joined_in = (
+        expert_in.reshape(width, 2 * units),
+        jnp.pad(router_weight, ((0, 0), (0, -experts_count % 128))),
+    )
+    joined_width = sum(piece.shape[1] for piece in joined_in)
 
     packs, members = lax.axis_size(PACKS), lax.axis_size(MEMBERS)
     count = packs * members
@@ -1370,11 +1393,11 @@
         axis=0,
     )
 
-    layout_all = lax.all_gather(layout.astype(jnp.float32), BOTH, axis=0, tiled=True)
-    layout_all = layout_all.astype(jnp.int32).reshape(count, -1, rows)
-    routed = jnp.any(layout_all[:, :top] == me, axis=1).astype(jnp.float32).reshape(all_rows, 1)
-
-    tables_all = tables_of(layout_all[:, top, : lengths.shape[3]])
+
+    def routed_of(layout_all):
+        named = layout_all.reshape(count, -1, rows)[:, :top] == me
+        return jnp.any(named, axis=1).astype(jnp.float32).reshape(all_rows, 1)
+
     tables_pack = tables_of(lengths[0, 0])
     tables_own = tables_of(own_lengths[None])
     own_cos, own_sin = tables_own[:2]
@@ -1398,10 +1421,10 @@
             at.result(experts_count, jnp.float32),
             at.pack_result(half),
         ]
-        weights = [joined_in, shared_in_t]
+        weights = [joined_in, (shared_in_t,)]
         if full:
             results.append(at.result(width))
-            weights += [expert_out, shared_out]
+            weights += [(expert_out,), (shared_out,)]
         if fusing:
             shapes = [(shape, index == 3) for index, (shape, _) in enumerate(results)]
             return fused_call(
@@ -1420,9 +1443,9 @@
     def run_experts_back(section, grad, routed, stored, gathered, into, number):
         at = tiles[section]
         pre, _, prob, shared_pre = stored
-        weights = [joined_in, shared_in_t, expert_out, shared_out]
+        weights = [joined_in, (shared_in_t,), (expert_out,), (shared_out,)]
         results = [at.result(2 * units), at.result(1, jnp.float32), at.result(width)]
-        scratch = [pltpu.VMEM((at.tile, joined_in.shape[1]), jnp.bfloat16)]
+        scratch = [pltpu.VMEM((at.tile, joined_width), jnp.bfloat16)]
         if fusing and number is not None:
             shapes = [(shape, False) for shape, _ in results]
             sources = [(pre, False), (prob, False), (routed, False), (shared_pre, True)]
@@ -1466,7 +1489,7 @@
                 (seg_col, at.source(1)),
                 (seg_row, row_spec),
             ],
-            [query_weight, expand_weight],
+            [(query_weight,), (expand_weight,)],
             [at.result(heads * VD), at.result(heads * QK), at.result(heads * KV)],
             into[:3],
             [pltpu.VMEM((at.tile, heads * QK), jnp.float32)],
@@ -1476,7 +1499,7 @@
             tiled(shared_body),
             "shared",
             [(ffn_all, at.source(width))],
-            [shared_in_t],
+            [(shared_in_t,)],
             [at.pair_result(half), at.result(half)],
             into[3:],
             flops=4 * all_rows * width * half,
@@ -1486,7 +1509,9 @@
     fresh = boundary[0, 0].astype(jnp.float32)
 
     normed, keyed, _ = inputs_of(fresh)
-    normed_pack, keyed_pack = gather_blocks([normed, keyed], False, 0, 0)
+    normed_pack, keyed_pack, layout_all = gather_blocks(
+        [normed, keyed, layout], True, 0, 0, wide=[False, False, True]
+    )
     attended, _ = attend(
         dot(normed_pack, query_weight),
         bf16(dot(keyed_pack[:, :LAT], expand_weight)),
@@ -1507,13 +1532,19 @@
         ),
     ]
     ffn_all, (*stored, partial) = run_experts(
-        0, bf16(rms_forward(mixed_first, ffn_gain)[0]), routed, empty[0], empty[1:], 2, True
+        0, bf16(rms_forward(mixed_first, ffn_gain)[0]), routed_of(layout_all), empty[0], empty[1:], 2, True
     )
     result_first = mixed_first + scatter_blocks(partial, rows, True, 3, 0)
     heads_weights = spread_blocks([query_weight, expand_weight, output_weight], 4, 1)
-    (target_all,) = gather_blocks([boundary[0, 0]], True, 5, 1, [blank((all_rows, width), jnp.bfloat16)])
-    sent, target_all, heads_weights = lax.optimization_barrier((bf16(result_first), target_all, heads_weights))
+    target_all, layout_all = gather_blocks(
+        [boundary[0, 0], layout], True, 5, 1, [blank((all_rows, width), jnp.bfloat16), layout_all]
+    )
+    sent, target_all, layout_all, heads_weights = lax.optimization_barrier(
+        (bf16(result_first), target_all, layout_all, heads_weights)
+    )
     inbound = lax.ppermute(sent, SECTION, [(0, 1)])
+    routed = routed_of(layout_all)
+    tables_all = tables_of(layout_all.reshape(count, -1, rows)[:, top, : lengths.shape[3]])
     query_heads, expand_heads, output_heads = (
         value.reshape(members, -1, value.shape[1]) for value in heads_weights
     )
@@ -1582,7 +1613,7 @@
         tiled(finish_body),
         "finish",
         [(gated_late, at.source(units)), (stored[3], at.pack_source(half))],
-        [expert_out, shared_out],
+        [(expert_out,), (shared_out,)],
         [at.result(width)],
         flops=2 * all_rows * width * units,
     )

time: 971 us -> 933 us (0.961)
  blocking collectives: 22.3 us -> 0 us
  Pallas kernels: 661 us -> 641 us
  waiting for transfers between devices: 18 us -> 0.04 us
  other arithmetic: 39.8 us -> 52 us
  local copies, waits for them, and re-layouts: 26.9 us -> 37.1 us
    all_gather x1 -> x0, blocking collectives: 22.3 us -> none  [body(): lax.all_gather(layout.astype(jnp.float32), BOTH, axis=0, tiled=True)]
    ppermute x1, waiting for transfers between devices: 17.9 us -> 0.01 us  [body(): inbound = lax.ppermute(sent, SECTION, [(0, 1)])]
    pallas_call x3, Pallas kernels: 88.4 us -> 76.5 us  [fused_call(): pl.pallas_call(functools.partial(fused_kernel, spots, parts, active, body...]
    pallas_call x12 -> x11, Pallas kernels: 292 us -> 282 us  [the longest x5 157 us: gather_blocks(): pl.pallas_call(functools.partial(gather_kernel, spots, cuts, wide, active...]
  transfers between devices with their start and end apart: 4 -> 4, of which waited for: 1 -> 0; matrix products, arithmetic and copies ran while one was open for 10% -> 12% of each run, Pallas kernels for 16% -> 17%
where the time goes in v6:
time: 933 us; the launch traced here: 923 us
  Pallas kernels  641 us (69%)
  matrix products  175 us (19%)
  other arithmetic  52 us (6%)
  local copies, waits for them, and re-layouts  37.1 us (4%)
  between operations  15.7 us (2%)
    pallas_call x5, Pallas kernels, gather_blocks(): pl.pallas_call(functools.partial(gather_kernel, spots, cuts, wide, active...  157 us
    pallas_call x6, Pallas kernels, call(): pl.pallas_call(functools.partial(kernel, len(arrays), counts, len(into),...  125 us
    pallas_call x4, Pallas kernels, scatter_blocks(): pl.pallas_call(functools.partial(scatter_kernel, spots, parts, active), o...  107 us
    pallas_call x1, Pallas kernels, spread_blocks(): pl.pallas_call(functools.partial(spread_kernel, [parts] * len(values), ac...  87.3 us
    pallas_call x3, Pallas kernels, fused_call(): pl.pallas_call(functools.partial(fused_kernel, spots, parts, active, body...  76.5 us
    dot_general x7, matrix products, t_dot(): lax.dot_general(left, right, (((0,), (0,)), ((), ())), preferred_element_...  63.5 us
    pallas_call x2, Pallas kernels, attend_back(): pl.pallas_call(functools.partial(attend_back_kernel, heads), grid=(count,...  51.4 us
    dot_general x6, matrix products, dot_t(): lax.dot_general(left, right, (((1,), (1,)), ((), ())), preferred_element_...  36.1 us
  transfers between devices with their start and end apart: 4, of which 0 were waited for; matrix products, arithmetic and copies ran while one was open for 12% of the time, Pallas kernels for 17%

profile of v6, /device:TPU:3, one launch (start us, length us, event | category | flops | bytes accessed | tf_op | source)
XLA Modules:
  0.0 923.2 jit_solution(391155065740110793)
XLA Ops:
  62.8 11.9 %fused2.1 = (bf16[16,128,2048]{2,1,0:T(8,128)(2,1)}, bf16[2304,1536]{1,0:T(8,128)(2,1)}, bf16[2304,768]{1,0:T(8,128)(2,1)}, f32[2304,16]{1,0:T(8,128)}, bf16[2,7...) custom-call(bf16[128,2048]{1,0:T(8,128)(2,1)} %multiply_convert_fusi, ...), custom_call_target="tpu_custom_call", output_to_operand_aliasing={{0}: (8, {}), {1}: (9, {}), {2}: (10, {}), {3}: (11, {}), {... | custom-call | tf_op jit(solution)/shard_map/fused2/pallas_call | solution.py:1276
  79.7 53.4 %gather5.1 = (bf16[16,128,2048]{2,1,0:T(8,128)(2,1)}, s32[16,8,128]{2,1,0:T(8,128)}) custom-call(bf16[128,2048]{1,0:T(8,128)(2,1)} %bitcast.243, s32[8,128]{1,0:T(8,128)} %add_add_fusion.refs_2_.refs_1_, bf16[16,128,2048]{2,1,0:T(8,128)(2,1)} %bitcast.248, s32[16,8,128]{2,1,0:T(8,128)} %get-tuple-element.86.refs_3_), custom_call_target="tpu_custom_call", output_to_operand_aliasing={{0}: (2, {}), {1}: (3, {})} | custom-call | tf_op jit(solution)/shard_map/gather5/pallas_call | solution.py:284
  133.1 87.3 %spread4.1 = (bf16[4,2048,768]{2,1,0:T(8,128)(2,1)}, bf16[4,512,1024]{2,1,0:T(8,128)(2,1)}, bf16[4,512,2048]{2,1,0:T(8,128)(2,1)}) custom-call(bf16[2048,768]{1,0:T(8,128)(2,1)} %bitcast.283, bf16[512,1024]{1,0:T(8,128)(2,1)} %bitcast.292, bf16[512,2048]{1,0:T(8,128)(2,1)} %bitcast.286), custom_call_target="tpu_custom_call" | custom-call | tf_op jit(solution)/shard_map/spread4/pallas_call | solution.py:391
  285.2 62.1 %fused6.1 = (bf16[16,128,2048]{2,1,0:T(8,128)(2,1)}, bf16[2304,1536]{1,0:T(8,128)(2,1)}, bf16[2304,768]{1,0:T(8,128)(2,1)}, f32[2304,16]{1,0:T(8,128)}, bf16[2,768,704]{2,1,0:T(8,128)(2,1)}) custom-call(bf16[128,2048]{1,0:T(8,128)(2,1)} %multiply_convert_fusion.refs_0_, ...), custom_call_target="tpu_custom_call", output_to_operand_aliasing={{0}: (6, {}), {1}: (7, {}), {2}: (8, {}), {3}: (9, {}), {4}... | custom-call | tf_op jit(solution)/shard_map/fused6/pallas_call | solution.py:1276
  347.3 50.4 %experts_back.1 = (bf16[2304,1536]{1,0:T(8,128)(2,1)}, f32[2304,1]{1,0:T(8,128)}, bf16[2304,2048]{1,0:T(8,128)(2,1)}) custom-call(s32[3]{0:T(128)} %get-tuple-element.201.control, bf16[2048,2048]{1,0:T(8,128)(2,1)} %bitcast.249, f32[1,16]{1,0:T(1,128)} %compare_convert_fusion.1.refs_1_, bf16[2304,1536]{1,0:T(8,128)(2,1)} %get-tuple-element.105.refs_2_, ...), custom_call_target="tpu_custom_call" | custom-call | flops 19327352832 | bytes 33554432 | tf_op jit(solution)/shard_map/experts_back/pallas_call | solution.py:830
  397.7 51.1 %scatter7.1 = f32[128,2048]{1,0:T(8,128)} custom-call(bf16[18,128,2048]{2,1,0:T(8,128)(2,1)} %bitcast.273), custom_call_target="tpu_custom_call" | custom-call | tf_op jit(solution)/shard_map/scatter7/pallas_call | solution.py:585
  458.2 11.8 %attend_back.2 = (bf16[512,768]{1,0:T(8,128)(2,1)}, bf16[512,1024]{1,0:T(8,128)(2,1)}, f32[512,64]{1,0:T(8,128)}) custom-call(bf16[512,768]{1,0:T(8,128)(2,1)} %get-tuple-element.109.q_ref, bf16[512,1024]{1,0:T(8,128)(2,1)} %bitcast.275, bf16[128,576]{1,0:T(8,128)(2,1)} %pad_maximum_fusion.2.key_ref.refs_1_, bf16[512,512]{1,0:T(8,128)(2,1)} %bitcast.299, ...), custom_call_target="tpu_custom_call" | custom-call | flops 436207616 | bytes 4194304 | tf_op jit(solution)/shard_map/attend_back/pallas_call | solution.py:714
  475.3 9.6 %convolution_bitcast_fusion.6 = f32[128,2048]{1,0:T(8,128)} fusion(bf16[4,128,768]{2,1,0:T(8,128)(2,1)S(1)} %bitcast.289, bf16[4,2048,768]{2,1,0:T(8,128)(2,1)} %get-tuple-element.90), kind=kOutput, calls=%fused_computation.35 | convolution fusion | flops 1610612736 | bytes 14417920 | tf_op jit(solution)/shard_map/mrc,mdc->rd/dot_general | solution.py:1587
  501.0 16.8 %finish.1.refs_14_ = bf16[2304,2048]{1,0:T(8,128)(2,1)} custom-call(s32[3]{0:T(128)} %get-tuple-element.201.control, bf16[2304,768]{1,0:T(8,128)(2,1)} %get-tuple-element.125.refs_0_, bf16[2,768,704]{2,1,0:T(8,128)(2,1)} %get-tuple-element.107.refs_5_.refs_1_, bf16[768,2048]{1,0:T(8,128)(2,1)} %bitcast.262, bf16[704,2048]{1,0:T(8,128)(2,1)} %bitcast.266), custom_call_target="tpu_custom_call" | custom-call | flops 6442450944 | bytes 33554432 | tf_op jit(solution)/shard_map/finish/pallas_call | solution.py:830
  521.2 52.3 %scatter12.1 = f32[128,2048]{1,0:T(8,128)} custom-call(bf16[18,128,2048]{2,1,0:T(8,128)(2,1)} %bitcast.259), custom_call_target="tpu_custom_call" | custom-call | tf_op jit(solution)/shard_map/scatter12/pallas_call | solution.py:585
  578.4 20.6 %shared.3 = (bf16[2,2304,704]{2,1,0:T(8,128)(2,1)}, bf16[2304,704]{1,0:T(8,128)(2,1)}) custom-call(s32[3]{0:T(128)} %get-tuple-element.201.control, bf16[2048,2048]{1,0:T(8,128)(2,1)} %bitcast.237, bf16[1408,2048]{1,0:T(8,128)(2,1)} %bitcast.258, bf16[2,2304,704]{2,1,0:T(8,128)(2,1)} %get-tuple-element.148.refs_2_, ...), custom_call_target="tpu_custom_call", output_to_operand_aliasing={{0}: (3, {}), {1}: (4, {})} | custom-call | flops 11811160064 | bytes 33554432 | tf_op jit(solution)/shard_map/shared/pallas_call | solution.py:830
  599.0 72.6 %gather9.1 = (bf16[16,128,2048]{2,1,0:T(8,128)(2,1)}, bf16[16,128,576]{2,1,0:T(8,128)(2,1)}) custom-call(bf16[128,2048]{1,0:T(8,128)(2,1)} %copy-done.9, bf16[128,576]{1,0:T(8,128)(2,1)} %pad_maximum_fusion.2.key_ref.refs_1_, bf16[16,128,2048]{2,1,0:T(8,128)(2,1)} %get-tuple-element.113, ...), custom_call_target="tpu_custom_call", output_to_operand_aliasing={{0}: (2, {}), {1}: (3, {})} | custom-call | tf_op jit(solution)/shard_map/gather9/pallas_call | solution.py:284
  673.8 31.0 %heads.3 = (bf16[2304,512]{1,0:T(8,128)(2,1)}, bf16[2304,768]{1,0:T(8,128)(2,1)}, bf16[2304,1024]{1,0:T(8,128)(2,1)}) custom-call(s32[3]{0:T(128)} %get-tuple-element.201.control, bf16[2048,2048]{1,0:T(8,128)(2,1)} %bitcast.277, bf16[2048,576]{1,0:T(8,128)(2,1)} %bitcast.269, ...), custom_call_target="tpu_custom_call", output_to_operand_aliasing={{0}: (9, {}), {1}: (10, {}), {2}: (11, {})} | custom-call | flops 12884901888 | bytes 33554432 | tf_op jit(solution)/shard_map/heads/pallas_call | solution.py:830
  704.8 12.3 %convolution_bitcast_fusion = f32[1,1,768,2048]{3,2,1,0:T(8,128)} fusion(bf16[2048,2048]{1,0:T(8,128)(2,1)} %bitcast.250, bf16[2304,768]{1,0:T(8,128)(2,1)} %get-tuple-element.125.refs_0_), kind=kOutput, calls=%fused_computation.18 | convolution fusion | flops 6442450944 | bytes 17825792 | tf_op jit(solution)/shard_map/dot_general | solution.py:35
  717.1 10.4 %convolution_bitcast_fusion.2 = f32[1,704,2048]{2,1,0:T(8,128)} fusion(bf16[2048,2048]{1,0:T(8,128)(2,1)} %bitcast.251, bf16[2304,704]{1,0:T(8,128)(2,1)S(1)} %copy-done.62), kind=kOutput, calls=%fused_computation.20 | convolution fusion | flops 5905580032 | bytes 17301504 | tf_op jit(solution)/shard_map/dot_general | solution.py:35
  727.6 15.1 %fusion.19 = (bf16[1,2048,704]{2,1,0:T(8,128)(2,1)}, bf16[1,2048,704]{2,1,0:T(8,128)(2,1)}) fusion(bf16[2,2304,704]{2,1,0:T(8,128)(2,1)} %get-tuple-element.150, bf16[2048,2048]{1,0:T(8,128)(2,1)} %bitcast.252, bf16[1,704,2048]{2,1,0:T(8,128)(2,1)S(1)} %copy-done.12), kind=kOutput, calls=%fused_computation.26 | convolution fusion | flops 5927206912 | bytes 22806528 | tf_op jit(solution)/shard_map/dot_general | solution.py:29
  742.7 18.2 %fusion.13 = f32[1,2048,2,704]{1,3,2,0:T(8,128)} fusion(bf16[2048,2048,1]{1,0,2:T(8,128)(2,1)S(1)} %bitcast.242, bf16[1,2048,704]{2,1,0:T(8,128)(2,1)} %get-tuple-element.167, bf16[1,2048,704]{2,1,0:T(8,128)(2,1)} %get-tuple-element.166), kind=kOutput, calls=%fused_computation.17 | convolution fusion | flops 11822694400 | bytes 25690112 | tf_op jit(solution)/shard_map/dot_general | solution.py:1670
  760.9 9.9 %convolution_convert_fusion.1.grad_ref = bf16[2048,512]{1,0:T(8,128)(2,1)} fusion(bf16[2048,2048]{1,0:T(8,128)(2,1)} %all-gather.2.cloned.1.call-done, bf16[1,512,2048]{2,1,0:T(8,128)(2,1)} %param.23), kind=kOutput, calls=%fused_computation.28 | convolution fusion | flops 4296015872 | bytes 12582912 | tf_op jit(solution)/shard_map/dot_general | solution.py:29
  770.7 39.7 %attend_back.3 = (bf16[2048,768]{1,0:T(8,128)(2,1)}, bf16[2048,1024]{1,0:T(8,128)(2,1)}, f32[2048,64]{1,0:T(8,128)}) custom-call(bf16[2304,768]{1,0:T(8,128)(2,1)} %get-tuple-element.138.q_ref, bf16[2304,1024]{1,0:T(8,128)(2,1)} %get-tuple-element.139.lat_ref, bf16[2048,576]{1,0:T(8,128)(2,1)} %bitcast.270, ...), custom_call_target="tpu_custom_call" | custom-call | flops 1744830464 | bytes 16777216 | tf_op jit(solution)/shard_map/attend_back/pallas_call | solution.py:714
  819.2 20.0 %pair_grad.1 = f32[2048,2,768]{2,1,0:T(2,128)} custom-call(bf16[2048,2048]{1,0:T(8,128)(2,1)} %bitcast.238, bf16[2304,1536]{1,0:T(8,128)(2,1)} %get-tuple-element.152.grad_ref), custom_call_target="tpu_custom_call" | custom-call | flops 12884901888 | bytes 27262976 | tf_op jit(solution)/shard_map/pair_grad/pallas_call | solution.py:1013
  845.9 9.7 %convolution_bitcast_fusion.4 = f32[1,512,2048]{2,1,0:T(8,128)} fusion(bf16[2048,2048]{1,0:T(8,128)(2,1)} %all-gather.2.cloned.1.call-done, bf16[2304,512]{1,0:T(8,128)(2,1)S(1)} %copy-done.61), kind=kOutput, calls=%fused_computation.22 | convolution fusion | flops 4294967296 | bytes 14680064 | tf_op jit(solution)/shard_map/dot_general | solution.py:35
  855.6 9.0 convolution_bitcast_fusion.1
  871.3 23.3 %gather13.1 = (bf16[16,128,576]{2,1,0:T(8,128)(2,1)}, f32[16,8,896]{2,1,0:T(8,128)}) custom-call(bf16[128,576]{1,0:T(8,128)(2,1)} %copy-done.23, f32[8,896]{1,0:T(8,128)} %reshape.524.refs_1_), custom_call_target="tpu_custom_call" | custom-call | tf_op jit(solution)/shard_map/gather13/pallas_call | solution.py:284
  898.4 9.9 %convolution_bitcast_fusion.3 = f32[1,2048,576]{1,2,0:T(8,128)} fusion(bf16[16,128,2048]{2,1,0:T(8,128)(2,1)} %get-tuple-element.133, bf16[16,128,576]{2,1,0:T(8,128)(2,1)} %get-tuple-element.145), kind=kOutput, calls=%fused_computation.21 | convolution fusion | flops 4831838208 | bytes 15466496 | tf_op jit(solution)/shard_map/dot_general | solution.py:35
  (272 shorter events, 199.3 us)
Async XLA Ops:
  7.2 753.7 %all-gather.2.cloned.1.call-start = ((), (), s32[]{:S(2)}) async-start(), calls=%async_computation.1 | async-start | bytes 8912896 | tf_op jit(solution)/shard_map/all_gather | solution.py:1634
  10.1 15.2 %copy-start.25 = (f32[128,32]{1,0:T(8,128)}, f32[128,32]{1,0:T(8,128)S(1)}, u32[]{:S(2)}) copy-start(f32[128,32]{1,0:T(8,128)S(1)} %get-tuple-element.193) | copy-start | bytes 49156
  12.6 473.3 %copy-start.16 = (f32[128,64]{1,0:T(8,128)}, f32[128,64]{1,0:T(8,128)S(1)}, u32[]{:S(2)}) copy-start(f32[128,64]{1,0:T(8,128)S(1)} %fusion.66) | copy-start | bytes 98308
  15.5 18.3 %copy-start.38 = (s32[4,128]{1,0:T(4,128)}, s32[4,128]{1,0:T(4,128)S(1)}, u32[]{:S(2)}) copy-start(s32[4,128]{1,0:T(4,128)S(1)} %get-tuple-element.161) | copy-start | bytes 6148
  220.4 28.4 %copy-start.2 = (bf16[1,1,128,2048]{3,2,1,0:T(8,128)(2,1)S(1)}, bf16[1,1,128,2048]{3,2,1,0:T(8,128)(2,1)}, u32[]{:S(2)}) copy-start(bf16[1,1,128,2048]{3,2,1,0:T(8,128)(2,1)} %param.15) | copy-start | bytes 1572868
  220.4 28.4 %collective-permute-start = (bf16[128,2048]{1,0:T(8,128)(2,1)}, bf16[128,2048]{1,0:T(8,128)(2,1)S(1)}, u32[]{:S(2)}, u32[]{:S(2)}) collective-permute-start(bf16[128,2048]{1,0:T(8,128)(2,1)} %add_convert_fusion.1), channel_id=1, source_target_pairs={{0,16},{1,17},{2,18},{3,19},{4,20},{5,21},{6,22},{7,23},{8,24},{9,... | collective-permute-start | bytes 1572872 | tf_op jit(solution)/shard_map/ppermute | solution.py:1545
  248.8 247.5 %copy-start.7 = (bf16[128,2048]{1,0:T(8,128)(2,1)}, bf16[128,2048]{1,0:T(8,128)(2,1)S(1)}, u32[]{:S(2)}) copy-start(bf16[128,2048]{1,0:T(8,128)(2,1)S(1)} %collective-permute-done) | copy-start | bytes 1572868
  283.2 167.3 %copy-start.39 = (f32[128]{0:T(128)}, f32[128]{0:T(128)S(1)}, u32[]{:S(2)}) copy-start(f32[128]{0:T(128)S(1)} %get-tuple-element.191) | copy-start | bytes 1540
  283.2 167.3 %copy-start.49 = (f32[128]{0:T(128)}, f32[128]{0:T(128)S(1)}, u32[]{:S(2)}) copy-start(f32[128]{0:T(128)S(1)} %get-tuple-element.190) | copy-start | bytes 1540
  450.5 19.4 %copy-start.34 = (f32[1,512]{1,0:T(1,128)S(1)}, f32[1,512]{1,0:T(1,128)}, u32[]{:S(2)}) copy-start(f32[1,512]{1,0:T(1,128)} %param.21) | copy-start | bytes 6148
  499.6 18.1 %collective-permute-start.1 = (bf16[128,2048]{1,0:T(8,128)(2,1)}, bf16[128,2048]{1,0:T(8,128)(2,1)S(1)}, u32[]{:S(2)}, u32[]{:S(2)}) collective-permute-start(bf16[128,2048]{1,0:T(8,128)(2,1)} %add_convert_fusion), channel_id=1, source_target_pairs={{16,0},{17,1},{18,2},{19,3},{20,4},{21,5},{22,6},{23,7},{24,8},{25... | collective-permute-start | bytes 1572872 | tf_op jit(solution)/shard_map/ppermute | solution.py:1608
  517.8 58.3 %copy-start.18 = (bf16[128,2048]{1,0:T(8,128)(2,1)}, bf16[128,2048]{1,0:T(8,128)(2,1)S(1)}, u32[]{:S(2)}) copy-start(bf16[128,2048]{1,0:T(8,128)(2,1)S(1)} %collective-permute-done.1) | copy-start | bytes 1572868
  576.1 22.9 %copy-start.55 = (f32[128]{0:T(128)}, f32[128]{0:T(128)S(1)}, u32[]{:S(2)}) copy-start(f32[128]{0:T(128)S(1)} %broadcast_multiply_fusion.3) | copy-start | bytes 1540
  578.4 286.3 %reduce-scatter.2.cloned.1.call-start = ((), (), s32[]{:S(2)}) async-start(), calls=%async_computation.2 | async-start | bytes 3440640 | tf_op jit(solution)/shard_map/reduce_scatter | solution.py:1639
  704.8 12.3 %copy-start.62 = (bf16[2304,704]{1,0:T(8,128)(2,1)S(1)}, bf16[2304,704]{1,0:T(8,128)(2,1)}, u32[]{:S(2)}) copy-start(bf16[2304,704]{1,0:T(8,128)(2,1)} %get-tuple-element.151) | copy-start | bytes 9732100
  717.1 10.4 %copy-start.12 = (bf16[1,704,2048]{2,1,0:T(8,128)(2,1)S(1)}, bf16[1,704,2048]{2,1,0:T(8,128)(2,1)}, u32[]{:S(2)}) copy-start(bf16[1,704,2048]{2,1,0:T(8,128)(2,1)} %param.27) | copy-start | bytes 8650756
  717.1 25.5 %slice-start = ((s8[8388608]{0:T(1024)(128)(4,1)}), s8[4194304]{0:T(1024)(128)(4,1)S(1)}, s32[]{:S(2)}) async-start(s8[8388608]{0:T(1024)(128)(4,1)} %bitcast.240), calls=%async_computation.3 | async-start | bytes 8388608
  727.6 15.1 %slice-start.1 = ((s8[8388608]{0:T(1024)(128)(4,1)}), s8[4194304]{0:T(1024)(128)(4,1)S(1)}, s32[]{:S(2)}) async-start(s8[8388608]{0:T(1024)(128)(4,1)} %bitcast.240), calls=%async_computation.4 | async-start | bytes 8388608
  839.2 16.4 %slice-start.2 = ((s8[8388608]{0:T(1024)(128)(4,1)}), s8[4194304]{0:T(1024)(128)(4,1)S(1)}, s32[]{:S(2)}) async-start(s8[8388608]{0:T(1024)(128)(4,1)} %bitcast.278), calls=%async_computation.5 | async-start | bytes 8388608
  855.6 10.3 %copy-start.35 = (f32[1,512]{1,0:T(1,128)S(1)}, f32[1,512]{1,0:T(1,128)}, u32[]{:S(2)}) copy-start(f32[1,512]{1,0:T(1,128)} %param.21) | copy-start | bytes 6148
  855.6 10.3 %copy-start.47 = (f32[128]{0:T(128)S(1)}, f32[128]{0:T(128)}, u32[]{:S(2)}) copy-start(f32[128]{0:T(128)} %copy-done.46) | copy-start | bytes 1540
  855.6 11.4 %copy-start.17 = (f32[128,64]{1,0:T(8,128)S(1)}, f32[128,64]{1,0:T(8,128)}, u32[]{:S(2)}) copy-start(f32[128,64]{1,0:T(8,128)} %copy-done.16) | copy-start | bytes 98308
  855.6 12.7 %copy-start.31 = (f32[1,2048]{1,0:T(1,128)S(1)}, f32[1,2048]{1,0:T(1,128)}, u32[]{:S(2)}) copy-start(f32[1,2048]{1,0:T(1,128)} %param.18) | copy-start | bytes 24580
  855.6 12.7 %copy-start.44 = (f32[128]{0:T(128)S(1)}, f32[128]{0:T(128)}, u32[]{:S(2)}) copy-start(f32[128]{0:T(128)} %copy-done.42) | copy-start | bytes 1540
  (47 other events, 224.5 us)
Sparse Core Ops, SparseCore 0:
  578.5 143.9 all-gather.1
  819.3 32.8 reduce-scatter.1

commit v7 on v6

--- a/solution.py
+++ b/solution.py
@@ -71,12 +71,14 @@
 
 
 def block_layout(block_lengths, rows):
-    starts = jnp.cumsum(block_lengths, axis=1) - block_lengths
-    index = jnp.arange(rows, dtype=jnp.int32)
-    begun = index[None, :, None] >= starts[:, None, :]
-    segment = jnp.sum(begun.astype(jnp.int32), axis=2)
-    opening = jnp.max(jnp.where(begun, starts[:, None, :], 0), axis=2)
-    return segment, index[None, :] - opening
+    index = lax.broadcasted_iota(jnp.int32, (block_lengths.shape[0], rows), 1)
+    start, segment, opening = 0, 0, 0
+    for sequence in range(block_lengths.shape[1]):
+        begun = index >= start
+        segment = segment + begun.astype(jnp.int32)
+        opening = jnp.where(begun, start, opening)
+        start = start + block_lengths[:, sequence : sequence + 1]
+    return segment, index - opening
 
 
 def places(spots):
@@ -913,7 +915,7 @@
 
 
 def finish_body(inside, sources, weights, results, scratch):
-    gated, shared_pre_ref = sources
+    gated, _, shared_pre_ref = sources
     out_ref, shared_out_ref = weights
     (partial_ref,) = results
 
@@ -1313,6 +1315,305 @@
     return outs[0].reshape(-1, width), list(outs[1:])
 
 
+def sum_kernel(spots, parts, active, body, pack_kinds, counts, n_into, *refs):
+    source_kinds, result_kinds = pack_kinds
+    n_sources, n_results = len(source_kinds), len(result_kinds)
+    n_weights, n_pieces = len(counts), sum(counts)
+    small_ref, refs = refs[0], refs[1:]
+    sources, refs = refs[:n_sources], refs[n_sources:]
+    stored, refs = refs[:n_pieces], refs[n_pieces + n_into :]
+    o_ref, refs = refs[0], refs[1:]
+    results, refs = refs[:n_results], refs[n_results:]
+    source_tiles, refs = refs[:n_sources], refs[n_sources:]
+    result_tiles, refs = refs[:n_results], refs[n_results:]
+    weights, refs = refs[:n_weights], refs[n_weights:]
+    x_buf, pair_buf, over_src, over_buf, line_src, up_buf, down_buf = refs[:7]
+    weight_sem, tile_sem, out_sem, pair_out, pair_in, over_out, over_in, line_out, up_in, down_in = refs[7:17]
+    scratch = refs[17:]
+    block = o_ref.shape[0]
+    rows = block // parts
+    tile = 2 * block
+    cut = lambda part: pl.ds(part * rows, rows)
+
+    def run():
+        loads = loads_of(counts, stored, weights, weight_sem)
+        for copy in loads:
+            copy.start()
+        spot, chip, core = places(spots)
+
+        def order(step):
+            if step == spots - 1:
+                return spot
+            fall = spots - 1 - step
+            fall = jnp.where(fall <= spot, fall - 1, fall)
+            rise = jnp.where(step >= spot, step + 1, step)
+            return jnp.where(2 * spot < spots - 1, fall, rise)
+
+        def place(number):
+            at = pick(number // 2, [order(step) for step in range(spots)])
+            return at, jnp.where(number % 2 == 0, 1 - chip, chip)
+
+        def window(ref, kind, at, c):
+            if kind:
+                return ref.at[:, pl.ds(pl.multiple_of(c * tile, tile), tile)]
+            return ref.at[pl.ds(pl.multiple_of((at * 2 + c) * tile, tile), tile)]
+
+        def inputs(number):
+            at, c = place(number)
+            which = lax.rem(number, 2)
+            return [
+                pltpu.make_async_copy(
+                    window(sources[index], kind, at, c), source_tiles[index].at[which], tile_sem.at[which, index]
+                )
+                for index, kind in enumerate(source_kinds)
+                if not kind
+            ]
+
+        for copy in inputs(0):
+            copy.start()
+        greet(spots, spot, chip, core)
+
+        def mine(at, c, k, part):
+            return x_buf.at[at * 2 + c, pl.ds(pl.multiple_of(k * block + part * rows, rows), rows)]
+
+        def pair(at, c, part):
+            return remote(
+                mine(at, c, 1 - core, part),
+                pair_buf.at[at, c, cut(part)],
+                to_partner(chip, core),
+                pair_out.at[at, c, part],
+                pair_in.at[at, c, part],
+            )
+
+        def over(at, part):
+            return remote(
+                over_src.at[at, cut(part)],
+                over_buf.at[at, cut(part)],
+                to_other(chip, core),
+                over_out.at[at, part],
+                over_in.at[at, part],
+            )
+
+        def up(at, part):
+            return remote(
+                line_src.at[at, cut(part)],
+                up_buf.at[at, cut(part)],
+                {PACKS: spot + 1},
+                line_out.at[at, part],
+                up_in.at[at, part],
+            )
+
+        def down(at, part):
+            return remote(
+                line_src.at[at, cut(part)],
+                down_buf.at[at, cut(part)],
+                {PACKS: spot - 1},
+                line_out.at[at, part],
+                down_in.at[at, part],
+            )
+
+        def across(step):
+            at = order(step)
+            for part in range(parts):
+                pair(at, 1 - chip, part).wait_recv()
+                add_into(
+                    over_src.at[at, cut(part)],
+                    [mine(at, 1 - chip, core, part), pair_buf.at[at, 1 - chip, cut(part)]],
+                    rows,
+                )
+                over(at, part).start()
+
+        def along(step):
+            at = order(step)
+            for part in range(parts):
+                pair(at, chip, part).wait_recv()
+                over(at, part).wait_recv()
+                base = [mine(at, chip, core, part), pair_buf.at[at, chip, cut(part)], over_buf.at[at, cut(part)]]
+                ups, downs = up_buf.at[at, cut(part)], down_buf.at[at, cut(part)]
+                if step < spots - 1:
+                    target = line_src.at[at, cut(part)]
+
+                    def rising(first):
+                        if not first:
+                            up(at, part).wait_recv()
+                        add_into(target, base if first else base + [ups], rows)
+                        up(at, part).start()
+
+                    def falling(first):
+                        if not first:
+                            down(at, part).wait_recv()
+                        add_into(target, base if first else base + [downs], rows)
+                        down(at, part).start()
+
+                    pl.when((at > spot) & (spot == 0))(lambda: rising(True))
+                    pl.when((at > spot) & (spot > 0))(lambda: rising(False))
+                    pl.when((at < spot) & (spot == spots - 1))(lambda: falling(True))
+                    pl.when((at < spot) & (spot < spots - 1))(lambda: falling(False))
+                elif spots == 1:
+                    add_into(o_ref.at[cut(part)], base, rows)
+                else:
+
+                    def finish(ends):
+                        if ends < 1:
+                            up(at, part).wait_recv()
+                        if ends > -1:
+                            down(at, part).wait_recv()
+                        extra = ([ups] if ends < 1 else []) + ([downs] if ends > -1 else [])
+                        add_into(o_ref.at[cut(part)], base + extra, rows)
+
+                    pl.when(spot == 0)(lambda: finish(1))
+                    pl.when(spot == spots - 1)(lambda: finish(-1))
+                    pl.when((spot > 0) & (spot < spots - 1))(lambda: finish(0))
+
+        late = 4 + jnp.where((spot > 0) & (spot < spots - 1), 1, 0)
+
+        def outward(index, which, at, c):
+            return pltpu.make_async_copy(
+                result_tiles[index].at[which], window(results[index], result_kinds[index], at, c), out_sem.at[which, index]
+            )
+
+        def step(number, carry):
+            at, c = place(number)
+            inside = at == spot
+            which = lax.rem(number, 2)
+            for copy in inputs(number):
+                copy.wait()
+
+            @pl.when(number + 1 < 2 * spots)
+            def _():
+                for copy in inputs(number + 1):
+                    copy.start()
+
+            for index, kind in enumerate(source_kinds):
+                if kind:
+
+                    def fetch(index=index, kind=kind):
+                        copy = pltpu.make_async_copy(
+                            window(sources[index], kind, at, c), source_tiles[index], tile_sem.at[0, index]
+                        )
+                        copy.start()
+                        copy.wait()
+
+                    pl.when(inside)(fetch)
+
+            @pl.when(number == 0)
+            def _():
+                for copy in loads:
+                    copy.wait()
+
+            @pl.when(number >= 2)
+            def _():
+                for index, kind in enumerate(result_kinds):
+                    if not kind:
+                        outward(index, which, at, c).wait()
+
+            tiles = [
+                target if kind else target.at[which] for target, kind in zip(source_tiles, source_kinds)
+            ]
+            body(
+                inside,
+                [tiles[0][...], small_ref, *tiles[1:]],
+                weights,
+                [*(target.at[which] for target in result_tiles), x_buf.at[at * 2 + c]],
+                scratch,
+            )
+            for part in range(parts):
+                pair(at, c, part).start()
+            for index, kind in enumerate(result_kinds):
+                if kind:
+
+                    def put(index=index):
+                        copy = outward(index, which, at, c)
+                        copy.start()
+                        copy.wait()
+
+                    pl.when(inside)(put)
+                else:
+                    outward(index, which, at, c).start()
+            for number_of in range(spots):
+                pl.when(number == 2 * number_of + 1)(functools.partial(across, number_of))
+                pl.when(number == 2 * number_of + late)(functools.partial(along, number_of))
+            return carry
+
+        lax.fori_loop(0, 2 * spots, step, 0)
+        for number_of in range(spots):
+            pl.when(2 * number_of + late >= 2 * spots)(functools.partial(along, number_of))
+        for which in range(2):
+            for index, kind in enumerate(result_kinds):
+                if not kind:
+                    outward(index, which, spot, chip).wait()
+        for part in range(parts):
+            for number_of in range(spots):
+                at = order(number_of)
+                pair(at, 0, part).wait_send()
+                pair(at, 1, part).wait_send()
+                over(at, part).wait_send()
+                if number_of < spots - 1:
+                    up(at, part).wait_send()
+
+    pl.when(lax.axis_index(SECTION) == active)(run)
+
+
+def sum_call(rows, number, active, body, small, sources, weights, results, into, scratch=(), parts=4):
+    spots = lax.axis_size(PACKS)
+    width = weights[-1][0].shape[1]
+    tile = 2 * rows
+    dma = pltpu.SemaphoreType.DMA
+    anywhere = pl.BlockSpec(memory_space=pl.ANY)
+    inside = pl.BlockSpec(memory_space=pltpu.VMEM)
+    pieces = [piece for weight in weights for piece in weight]
+    first = 1 + len(sources) + len(pieces)
+    held = lambda *lead: pltpu.VMEM((*lead, rows, width), jnp.bfloat16)
+
+    def hold(array, kind, *lead):
+        if kind:
+            return pltpu.VMEM((*lead, 2, tile, array.shape[2]), array.dtype)
+        return pltpu.VMEM((2, tile, array.shape[1]), array.dtype)
+
+    outs = pl.pallas_call(
+        functools.partial(
+            sum_kernel,
+            spots,
+            parts,
+            active,
+            body,
+            ([kind for _, kind in sources], [kind for _, kind in results]),
+            [len(weight) for weight in weights],
+            len(into),
+        ),
+        out_shape=[jax.ShapeDtypeStruct((rows, width), jnp.float32), *(shape for shape, _ in results)],
+        in_specs=[inside, *([anywhere] * (len(sources) + len(pieces) + len(into)))],
+        out_specs=[inside, *([anywhere] * len(results))],
+        input_output_aliases={first + index: 1 + index for index in range(len(into))},
+        scratch_shapes=[
+            *(hold(array, kind) for array, kind in sources),
+            *(hold(shape, kind, 2) for shape, kind in results),
+            *(hold_weight(weight) for weight in weights),
+            pltpu.VMEM((2 * spots, tile, width), jnp.bfloat16),
+            held(spots, 2),
+            held(spots),
+            held(spots),
+            held(spots),
+            held(spots),
+            held(spots),
+            dma((len(pieces),)),
+            dma((2, len(sources))),
+            dma((2, max(len(results), 1))),
+            dma((spots, 2, parts)),
+            dma((spots, 2, parts)),
+            dma((spots, parts)),
+            dma((spots, parts)),
+            dma((spots, parts)),
+            dma((spots, parts)),
+            dma((spots, parts)),
+            *scratch,
+        ],
+        compiler_params=pltpu.CompilerParams(collective_id=number, has_side_effects=True),
+        name=f"sum{number}",
+    )(small, *(array for array, _ in sources), *pieces, *into)
+    return outs[0], list(outs[1:])
+
+
 def body(
     boundary,
     lengths,
@@ -1440,37 +1741,31 @@
             into[:4],
         )
 
-    def run_experts_back(section, grad, routed, stored, gathered, into, number):
+    def summed_over(section, number, body_of, name, sources, weights, results, into, scratch=()):
+        at = tiles[section]
+        if fusing:
+            shapes = [(shape, shape.ndim == 3) for shape, _ in results]
+            return sum_call(rows, number, section, body_of, own_column, sources, weights, shapes, into, scratch)
+        specs = [(array, at.pack_source(half) if kind else at.source(array.shape[1])) for array, kind in sources]
+        specs.insert(1, (own_column, at.small(own_column)))
+        *found, partial = at.call(
+            tiled(body_of), name, specs, weights, [*results, at.result(width)], into, scratch
+        )
+        return scatter_blocks(partial, rows, True, number, section), found
+
+    def run_experts_back(section, number, grad_all, routed, stored, into):
         at = tiles[section]
         pre, _, prob, shared_pre = stored
-        weights = [joined_in, (shared_in_t,), (expert_out,), (shared_out,)]
-        results = [at.result(2 * units), at.result(1, jnp.float32), at.result(width)]
-        scratch = [pltpu.VMEM((at.tile, joined_width), jnp.bfloat16)]
-        if fusing and number is not None:
-            shapes = [(shape, False) for shape, _ in results]
-            sources = [(pre, False), (prob, False), (routed, False), (shared_pre, True)]
-            return fused_call(
-                at, grad, number, section, experts_back_body, own_column, sources, weights, shapes, gathered, into, scratch
-            )
-        grad_all = gathered
-        if number is not None:
-            (grad_all,) = gather_blocks([grad], True, number, section, [gathered])
-        return grad_all, at.call(
-            tiled(experts_back_body),
+        return summed_over(
+            section,
+            number,
+            experts_back_body,
             "experts_back",
-            [
-                (grad_all, at.source(width)),
-                (own_column, at.small(own_column)),
-                (pre, at.source(2 * units)),
-                (prob, at.source(experts_count)),
-                (routed, at.source(1)),
-                (shared_pre, at.pack_source(half)),
-            ],
-            weights,
-            results,
+            [(grad_all, False), (pre, False), (prob, False), (routed, False), (shared_pre, True)],
+            [joined_in, (shared_in_t,), (expert_out,), (shared_out,)],
+            [at.result(2 * units), at.result(1, jnp.float32)],
             into,
-            scratch,
-            flops=6 * all_rows * width * units,
+            [pltpu.VMEM((at.tile, joined_width), jnp.bfloat16)],
         )
 
     def prepare(section, normed_all, keyed_all, ffn_all, tables, into):
@@ -1573,8 +1868,7 @@
         grad_hidden_norm, grad_attn_gain = rms_backward(hidden, scale_attn, attn_gain, grad_normed)
         return grad_compressed, grad_hidden_norm, grad_attn_gain, grad_latent_gain
 
-    _, (*grad_units, partial) = run_experts_back(1, None, routed, stored, target_all, (), None)
-    grad_ffn_second = scatter_blocks(partial, rows, True, 7, 1)
+    grad_ffn_second, grad_units = run_experts_back(1, 7, target_all, routed, stored, ())
     grad_mixed = fresh + rms_backward(mixed, scale_ffn, ffn_gain, grad_ffn_second)[0]
     grad_attended = jnp.einsum(
         "rd,mcd->mrc", bf16(grad_mixed), output_heads, preferred_element_type=jnp.float32
@@ -1608,23 +1902,22 @@
     downbound = lax.ppermute(grad_second, SECTION, [(1, 0)]).astype(jnp.float32)
 
     normed_late, keyed_late, gated_late, _ = lax.optimization_barrier((normed, keyed, stored[1], grad_second))
-    at = tiles[1]
-    finished = at.call(
-        tiled(finish_body),
+    finished, _ = summed_over(
+        1,
+        10,
+        finish_body,
         "finish",
-        [(gated_late, at.source(units)), (stored[3], at.pack_source(half))],
+        [(gated_late, False), (stored[3], True)],
         [(expert_out,), (shared_out,)],
-        [at.result(width)],
-        flops=2 * all_rows * width * units,
-    )
+        [],
+        (),
+    )
+    result = mixed + finished
     upstream = jnp.where(is_first, downbound, fresh)
-    upstream_all, (grad_pre, moved, partial) = run_experts_back(
-        0, bf16(upstream), routed, stored, target_all, [*grad_units, *finished], 11
-    )
-    summed = scatter_blocks(partial, rows, True, 12)
-    result = mixed + summed
-    grad_ffn = jnp.where(is_first, summed, grad_ffn_second)
-    normed_late, keyed_late, _ = lax.optimization_barrier((normed_late, keyed_late, summed))
+    (upstream_all,) = gather_blocks([bf16(upstream)], True, 11, 0, [target_all])
+    grad_ffn, (grad_pre, moved) = run_experts_back(0, 12, upstream_all, routed, stored, grad_units)
+    grad_ffn = jnp.where(is_first, grad_ffn, grad_ffn_second)
+    normed_late, keyed_late, _ = lax.optimization_barrier((normed_late, keyed_late, finished))
     normed_all, keyed_all = gather_blocks([normed_late, keyed_late], True, 9, 1, all_inputs)
     prepared = prepare(1, normed_all, keyed_all, ffn_all, tables_all, prepared)
     attended_all, query_all, latent_all, shared_pre, shared_hid = prepared

time: 933 us -> 889 us (0.953)
  Pallas kernels: 641 us -> 599 us
  waiting for transfers between devices: 0.04 us -> 12.2 us
    pallas_call x0 -> x3, Pallas kernels: none -> 136 us  [sum_call(): pl.pallas_call(functools.partial(sum_kernel, spots, parts, active, body,...]
    pallas_call x4 -> x2, Pallas kernels: 107 us -> 3.77 us  [scatter_blocks(): pl.pallas_call(functools.partial(scatter_kernel, spots, parts, active), o...]
    pallas_call x6 -> x4, Pallas kernels: 125 us -> 57.3 us  [call(): pl.pallas_call(functools.partial(kernel, len(arrays), counts, len(into),...]
    ppermute x1, waiting for transfers between devices: 0.01 us -> 10.3 us  [body(): downbound = lax.ppermute(grad_second, SECTION, [(1, 0)]).astype(jnp.float32)]
    pallas_call x3 -> x2, Pallas kernels: 76.5 us -> 72.4 us  [fused_call(): pl.pallas_call(functools.partial(fused_kernel, spots, parts, active, body...]
    pallas_call x5 -> x6, Pallas kernels: 157 us -> 155 us  [gather_blocks(): pl.pallas_call(functools.partial(gather_kernel, spots, cuts, wide, active...]
  transfers between devices with their start and end apart: 4 -> 4, of which waited for: 0 -> 2; matrix products, arithmetic and copies ran while one was open for 12% -> 12% of each run, Pallas kernels for 17% -> 22%
where the time goes in v7:
time: 889 us; the launch traced here: 880 us
  Pallas kernels  599 us (67%)
  matrix products  168 us (19%)
  other arithmetic  46 us (5%)
  local copies, waits for them, and re-layouts  35.6 us (4%)
  between operations  16.7 us (2%)
  waiting for transfers between devices  12.2 us (1%)
    pallas_call x6, Pallas kernels, gather_blocks(): pl.pallas_call(functools.partial(gather_kernel, spots, cuts, wide, active...  155 us
    pallas_call x3, Pallas kernels, sum_call(): pl.pallas_call(functools.partial(sum_kernel, spots, parts, active, body,...  136 us
    pallas_call x1, Pallas kernels, spread_blocks(): pl.pallas_call(functools.partial(spread_kernel, [parts] * len(values), ac...  87.3 us
    pallas_call x2, Pallas kernels, fused_call(): pl.pallas_call(functools.partial(fused_kernel, spots, parts, active, body...  72.4 us
    dot_general x7, matrix products, t_dot(): lax.dot_general(left, right, (((0,), (0,)), ((), ())), preferred_element_...  63.4 us
    pallas_call x4, Pallas kernels, call(): pl.pallas_call(functools.partial(kernel, len(arrays), counts, len(into),...  57.3 us
    pallas_call x2, Pallas kernels, attend_back(): pl.pallas_call(functools.partial(attend_back_kernel, heads), grid=(count,...  50.8 us
    dot_general x6, matrix products, dot_t(): lax.dot_general(left, right, (((1,), (1,)), ((), ())), preferred_element_...  34.7 us
  transfers between devices with their start and end apart: 4, of which 2 were waited for; matrix products, arithmetic and copies ran while one was open for 12% of the time, Pallas kernels for 22%

profile of v7, /device:TPU:3, one launch (start us, length us, event | category | flops | bytes accessed | tf_op | source)
XLA Modules:
  0.0 880.0 jit_solution(14828839987498213606)
XLA Ops:
  37.8 8.2 attend.2
  62.0 8.7 fused2.1
  75.7 53.4 %gather5.1 = (bf16[16,128,2048]{2,1,0:T(8,128)(2,1)}, s32[16,8,128]{2,1,0:T(8,128)}) custom-call(bf16[128,2048]{1,0:T(8,128)(2,1)} %bitcast.265, s32[8,128]{1,0:T(8,128)} %add_add_fusion.refs_2_.refs_1_, bf16[16,128,2048]{2,1,0:T(8,128)(2,1)} %bitcast.245, s32[16,8,128]{2,1,0:T(8,128)} %get-tuple-element.85.refs_3_), custom_call_target="tpu_custom_call", output_to_operand_aliasing={{0}: (2, {}), {1}: (3, {})} | custom-call | tf_op jit(solution)/shard_map/gather5/pallas_call | solution.py:286
  129.1 87.3 %spread4.1 = (bf16[4,2048,768]{2,1,0:T(8,128)(2,1)}, bf16[4,512,1024]{2,1,0:T(8,128)(2,1)}, bf16[4,512,2048]{2,1,0:T(8,128)(2,1)}) custom-call(bf16[2048,768]{1,0:T(8,128)(2,1)} %bitcast.294, bf16[512,1024]{1,0:T(8,128)(2,1)} %bitcast.303, bf16[512,2048]{1,0:T(8,128)(2,1)} %bitcast.297), custom_call_target="tpu_custom_call" | custom-call | tf_op jit(solution)/shard_map/spread4/pallas_call | solution.py:393
  273.9 63.7 %fused6.1 = (bf16[16,128,2048]{2,1,0:T(8,128)(2,1)}, bf16[2304,1536]{1,0:T(8,128)(2,1)}, bf16[2304,768]{1,0:T(8,128)(2,1)}, f32[2304,16]{1,0:T(8,128)}, bf16[2,768,704]{2,1,0:T(8,128)(2,1)}) custom-call(bf16[128,2048]{1,0:T(8,128)(2,1)} %multiply_convert_fusion.refs_0_, ...), custom_call_target="tpu_custom_call", output_to_operand_aliasing={{0}: (6, {}), {1}: (7, {}), {2}: (8, {}), {3}: (9, {}), {4}... | custom-call | tf_op jit(solution)/shard_map/fused6/pallas_call | solution.py:1278
  337.6 75.9 %sum7.1 = (f32[128,2048]{1,0:T(8,128)}, bf16[2304,1536]{1,0:T(8,128)(2,1)}, f32[2304,1]{1,0:T(8,128)}) custom-call(f32[1,16]{1,0:T(1,128)} %compare_convert_fusion.6.refs_1_.refs_0_, bf16[2048,2048]{1,0:T(8,128)(2,1)} %bitcast.246, bf16[2304,1536]{1,0:T(8,128)(2,1)} %get-tuple-element.104.refs_2_, f32[2304,16]{1,0:T(8,128)} %get-tuple-element.105.refs_3_, ...), custom_call_target="tpu_custom_call" | custom-call | tf_op jit(solution)/shard_map/sum7/pallas_call | solution.py:1573
  423.0 11.4 %attend_back.2 = (bf16[512,768]{1,0:T(8,128)(2,1)}, bf16[512,1024]{1,0:T(8,128)(2,1)}, f32[512,64]{1,0:T(8,128)}) custom-call(bf16[512,768]{1,0:T(8,128)(2,1)} %get-tuple-element.108.q_ref, bf16[512,1024]{1,0:T(8,128)(2,1)} %bitcast.286, bf16[128,576]{1,0:T(8,128)(2,1)} %pad_maximum_fusion.2.key_ref.refs_1_, bf16[512,512]{1,0:T(8,128)(2,1)} %bitcast.310, ...), custom_call_target="tpu_custom_call" | custom-call | flops 436207616 | bytes 4194304 | tf_op jit(solution)/shard_map/attend_back/pallas_call | solution.py:716
  434.3 10.0 %convolution_bitcast_fusion.6 = f32[128,2048]{1,0:T(8,128)} fusion(bf16[4,128,768]{2,1,0:T(8,128)(2,1)} %bitcast.300, bf16[4,2048,768]{2,1,0:T(8,128)(2,1)} %get-tuple-element.89), kind=kOutput, calls=%fused_computation.35 | convolution fusion | flops 1610612736 | bytes 14417920 | tf_op jit(solution)/shard_map/mrc,mdc->rd/dot_general | solution.py:1881
  462.4 10.3 %collective-permute-done.1 = bf16[128,2048]{1,0:T(8,128)(2,1)S(1)} collective-permute-done((bf16[128,2048]{1,0:T(8,128)(2,1)S(1)}, bf16[128,2048]{1,0:T(8,128)(2,1)S(1)}, u32[]{:S(2)}, u32[]{:S(2)}) %collective-permute-start.1) | collective-permute-done | bytes 524320 | tf_op jit(solution)/shard_map/ppermute | solution.py:1902
  484.4 56.2 %sum10.1 = f32[128,2048]{1,0:T(8,128)} custom-call(f32[1,16]{1,0:T(1,128)} %compare_convert_fusion.6.refs_1_.refs_0_, bf16[2304,768]{1,0:T(8,128)(2,1)} %get-tuple-element.127.refs_1_, bf16[2,768,704]{2,1,0:T(8,128)(2,1)} %get-tuple-element.106.refs_5_.refs_2_, bf16[768,2048]{1,0:T(8,128)(2,1)} %bitcast.275, bf16[704,2048]{1,0:T(8,128)(2,1)} %bitcast.279), custom_call_target="tpu_custom_call" | custom-call | tf_op jit(solution)/shard_map/sum10/pallas_call | solution.py:1573
  540.5 67.7 %gather9.1 = (bf16[16,128,2048]{2,1,0:T(8,128)(2,1)}, bf16[16,128,576]{2,1,0:T(8,128)(2,1)}) custom-call(bf16[128,2048]{1,0:T(8,128)(2,1)} %copy-done.12, bf16[128,576]{1,0:T(8,128)(2,1)} %pad_maximum_fusion.2.key_ref.refs_1_, bf16[16,128,2048]{2,1,0:T(8,128)(2,1)} %get-tuple-element.112, ...), custom_call_target="tpu_custom_call", output_to_operand_aliasing={{0}: (2, {}), {1}: (3, {})} | custom-call | tf_op jit(solution)/shard_map/gather9/pallas_call | solution.py:286
  608.3 20.6 %shared.3 = (bf16[2,2304,704]{2,1,0:T(8,128)(2,1)}, bf16[2304,704]{1,0:T(8,128)(2,1)}) custom-call(s32[3]{0:T(128)} %get-tuple-element.200.control, bf16[2048,2048]{1,0:T(8,128)(2,1)} %bitcast.259, bf16[1408,2048]{1,0:T(8,128)(2,1)} %bitcast.271, bf16[2,2304,704]{2,1,0:T(8,128)(2,1)} %get-tuple-element.146.refs_2_, ...), custom_call_target="tpu_custom_call", output_to_operand_aliasing={{0}: (3, {}), {1}: (4, {})} | custom-call | flops 11811160064 | bytes 33554432 | tf_op jit(solution)/shard_map/shared/pallas_call | solution.py:832
  628.9 30.7 %heads.3 = (bf16[2304,512]{1,0:T(8,128)(2,1)}, bf16[2304,768]{1,0:T(8,128)(2,1)}, bf16[2304,1024]{1,0:T(8,128)(2,1)}) custom-call(s32[3]{0:T(128)} %get-tuple-element.200.control, bf16[2048,2048]{1,0:T(8,128)(2,1)} %bitcast.288, bf16[2048,576]{1,0:T(8,128)(2,1)} %bitcast.281, ...), custom_call_target="tpu_custom_call", output_to_operand_aliasing={{0}: (9, {}), {1}: (10, {}), {2}: (11, {})} | custom-call | flops 12884901888 | bytes 33554432 | tf_op jit(solution)/shard_map/heads/pallas_call | solution.py:832
  661.7 12.0 %convolution_bitcast_fusion = f32[1,1,768,2048]{3,2,1,0:T(8,128)} fusion(bf16[2048,2048]{1,0:T(8,128)(2,1)} %bitcast.248, bf16[2304,768]{1,0:T(8,128)(2,1)} %get-tuple-element.127.refs_1_), kind=kOutput, calls=%fused_computation.18 | convolution fusion | flops 6442450944 | bytes 17825792 | tf_op jit(solution)/shard_map/dot_general | solution.py:35
  673.8 10.4 %convolution_bitcast_fusion.2 = f32[1,704,2048]{2,1,0:T(8,128)} fusion(bf16[2048,2048]{1,0:T(8,128)(2,1)} %bitcast.249, bf16[2304,704]{1,0:T(8,128)(2,1)S(1)} %copy-done.63), kind=kOutput, calls=%fused_computation.20 | convolution fusion | flops 5905580032 | bytes 17301504 | tf_op jit(solution)/shard_map/dot_general | solution.py:35
  684.2 13.4 %fusion.19 = (bf16[1,2048,704]{2,1,0:T(8,128)(2,1)}, bf16[1,2048,704]{2,1,0:T(8,128)(2,1)}) fusion(bf16[2,2304,704]{2,1,0:T(8,128)(2,1)} %get-tuple-element.148, bf16[2048,2048]{1,0:T(8,128)(2,1)S(1)} %bitcast.252, bf16[1,704,2048]{2,1,0:T(8,128)(2,1)} %param.27), kind=kOutput, calls=%fused_computation.26 | convolution fusion | flops 5927206912 | bytes 22806528 | tf_op jit(solution)/shard_map/dot_general | solution.py:29
  697.6 18.4 %fusion.13 = f32[1,2048,2,704]{1,3,2,0:T(8,128)} fusion(bf16[2048,2048,1]{1,0,2:T(8,128)(2,1)S(1)} %bitcast.264, bf16[1,2048,704]{2,1,0:T(8,128)(2,1)} %get-tuple-element.161, bf16[1,2048,704]{2,1,0:T(8,128)(2,1)} %get-tuple-element.160), kind=kOutput, calls=%fused_computation.17 | convolution fusion | flops 11822694400 | bytes 25690112 | tf_op jit(solution)/shard_map/dot_general | solution.py:1963
  716.0 9.9 %convolution_convert_fusion.1.grad_ref = bf16[2048,512]{1,0:T(8,128)(2,1)} fusion(bf16[2048,2048]{1,0:T(8,128)(2,1)} %all-gather.2.cloned.1.call-done, bf16[1,512,2048]{2,1,0:T(8,128)(2,1)} %param.23), kind=kOutput, calls=%fused_computation.28 | convolution fusion | flops 4296015872 | bytes 12582912 | tf_op jit(solution)/shard_map/dot_general | solution.py:29
  725.9 39.5 %attend_back.3 = (bf16[2048,768]{1,0:T(8,128)(2,1)}, bf16[2048,1024]{1,0:T(8,128)(2,1)}, f32[2048,64]{1,0:T(8,128)}) custom-call(bf16[2304,768]{1,0:T(8,128)(2,1)} %get-tuple-element.137.q_ref, bf16[2304,1024]{1,0:T(8,128)(2,1)} %get-tuple-element.138.lat_ref, bf16[2048,576]{1,0:T(8,128)(2,1)} %bitcast.282, ...), custom_call_target="tpu_custom_call" | custom-call | flops 1744830464 | bytes 16777216 | tf_op jit(solution)/shard_map/attend_back/pallas_call | solution.py:716
  774.4 20.0 %pair_grad.1 = f32[2048,2,768]{2,1,0:T(2,128)} custom-call(bf16[2048,2048]{1,0:T(8,128)(2,1)} %bitcast.260, bf16[2304,1536]{1,0:T(8,128)(2,1)} %get-tuple-element.150.grad_ref), custom_call_target="tpu_custom_call" | custom-call | flops 12884901888 | bytes 27262976 | tf_op jit(solution)/shard_map/pair_grad/pallas_call | solution.py:1015
  801.1 9.8 %convolution_bitcast_fusion.4 = f32[1,512,2048]{2,1,0:T(8,128)} fusion(bf16[2048,2048]{1,0:T(8,128)(2,1)} %all-gather.2.cloned.1.call-done, bf16[2304,512]{1,0:T(8,128)(2,1)S(1)} %copy-done.62), kind=kOutput, calls=%fused_computation.22 | convolution fusion | flops 4294967296 | bytes 14680064 | tf_op jit(solution)/shard_map/dot_general | solution.py:35
  810.9 9.0 %convolution_bitcast_fusion.1 = f32[1,2048,768]{2,1,0:T(8,128)} fusion(bf16[2048,2048]{1,0:T(8,128)(2,1)S(1)} %bitcast.291, bf16[2048,768]{1,0:T(8,128)(2,1)S(1)} %copy-done.61), kind=kOutput, calls=%fused_computation.19 | convolution fusion | flops 6442450944 | bytes 17825792 | tf_op jit(solution)/shard_map/dot_general | solution.py:35
  826.6 23.7 %gather13.1 = (bf16[16,128,576]{2,1,0:T(8,128)(2,1)}, f32[16,8,896]{2,1,0:T(8,128)}) custom-call(bf16[128,576]{1,0:T(8,128)(2,1)} %copy-done.25, f32[8,896]{1,0:T(8,128)} %reshape.756.refs_1_), custom_call_target="tpu_custom_call" | custom-call | tf_op jit(solution)/shard_map/gather13/pallas_call | solution.py:286
  855.2 10.0 %convolution_bitcast_fusion.3 = f32[1,2048,576]{1,2,0:T(8,128)} fusion(bf16[16,128,2048]{2,1,0:T(8,128)(2,1)} %get-tuple-element.132, bf16[16,128,576]{2,1,0:T(8,128)(2,1)} %get-tuple-element.144), kind=kOutput, calls=%fused_computation.21 | convolution fusion | flops 4831838208 | bytes 15466496 | tf_op jit(solution)/shard_map/dot_general | solution.py:35
  (277 shorter events, 183.2 us)
Async XLA Ops:
  7.2 10.9 %copy-start = (bf16[1,2048,576]{1,2,0:T(8,128)(2,1)S(1)}, bf16[1,2048,576]{1,2,0:T(8,128)(2,1)}, u32[]{:S(2)}) copy-start(bf16[1,2048,576]{1,2,0:T(8,128)(2,1)} %param.20) | copy-start | bytes 7077892
  7.2 708.8 %all-gather.2.cloned.1.call-start = ((), (), s32[]{:S(2)}) async-start(), calls=%async_computation.1 | async-start | bytes 8912896 | tf_op jit(solution)/shard_map/all_gather | solution.py:1927
  8.6 11.8 %copy-start.34 = (bf16[1,2048,16]{1,2,0:T(8,128)(2,1)S(1)}, bf16[1,2048,16]{1,2,0:T(8,128)(2,1)}, u32[]{:S(2)}) copy-start(bf16[1,2048,16]{1,2,0:T(8,128)(2,1)} %param.25) | copy-start | bytes 196612
  8.6 12.8 %copy-start.35 = (f32[1,512]{1,0:T(1,128)S(1)}, f32[1,512]{1,0:T(1,128)}, u32[]{:S(2)}) copy-start(f32[1,512]{1,0:T(1,128)} %param.21) | copy-start | bytes 6148
  15.0 433.2 %copy-start.17 = (f32[128,64]{1,0:T(8,128)}, f32[128,64]{1,0:T(8,128)S(1)}, u32[]{:S(2)}) copy-start(f32[128,64]{1,0:T(8,128)S(1)} %fusion.66) | copy-start | bytes 98308
  216.4 24.9 %copy-start.2 = (bf16[1,1,128,2048]{3,2,1,0:T(8,128)(2,1)S(1)}, bf16[1,1,128,2048]{3,2,1,0:T(8,128)(2,1)}, u32[]{:S(2)}) copy-start(bf16[1,1,128,2048]{3,2,1,0:T(8,128)(2,1)} %param.15) | copy-start | bytes 1572868
  216.4 24.9 %collective-permute-start = (bf16[128,2048]{1,0:T(8,128)(2,1)}, bf16[128,2048]{1,0:T(8,128)(2,1)S(1)}, u32[]{:S(2)}, u32[]{:S(2)}) collective-permute-start(bf16[128,2048]{1,0:T(8,128)(2,1)} %add_convert_fusion.1), channel_id=1, source_target_pairs={{0,16},{1,17},{2,18},{3,19},{4,20},{5,21},{6,22},{7,23},{8,24},{9,... | collective-permute-start | bytes 1572872 | tf_op jit(solution)/shard_map/ppermute | solution.py:1840
  241.3 217.1 %copy-start.8 = (bf16[128,2048]{1,0:T(8,128)(2,1)}, bf16[128,2048]{1,0:T(8,128)(2,1)S(1)}, u32[]{:S(2)}) copy-start(bf16[128,2048]{1,0:T(8,128)(2,1)S(1)} %collective-permute-done) | copy-start | bytes 1572868
  272.0 143.3 %copy-start.41 = (f32[128]{0:T(128)}, f32[128]{0:T(128)S(1)}, u32[]{:S(2)}) copy-start(f32[128]{0:T(128)S(1)} %get-tuple-element.187) | copy-start | bytes 1540
  272.0 143.3 %copy-start.50 = (f32[128]{0:T(128)}, f32[128]{0:T(128)S(1)}, u32[]{:S(2)}) copy-start(f32[128]{0:T(128)S(1)} %get-tuple-element.186) | copy-start | bytes 1540
  461.0 11.7 %collective-permute-start.1 = (bf16[128,2048]{1,0:T(8,128)(2,1)S(1)}, bf16[128,2048]{1,0:T(8,128)(2,1)S(1)}, u32[]{:S(2)}, u32[]{:S(2)}) collective-permute-start(bf16[128,2048]{1,0:T(8,128)(2,1)S(1)} %add_convert_fusion), channel_id=1, source_target_pairs={{16,0},{17,1},{18,2},{19,3},{20,4},{21,5},{22,6},{23,7},{24,8},{25... | collective-permute-start | bytes 1572872 | tf_op jit(solution)/shard_map/ppermute | solution.py:1902
  482.0 58.5 %copy-start.56 = (f32[128]{0:T(128)}, f32[128]{0:T(128)S(1)}, u32[]{:S(2)}) copy-start(f32[128]{0:T(128)S(1)} %broadcast_multiply_fusion.3) | copy-start | bytes 1540
  484.3 335.6 %reduce-scatter.2.cloned.1.call-start = ((), (), s32[]{:S(2)}) async-start(), calls=%async_computation.2 | async-start | bytes 3440640 | tf_op jit(solution)/shard_map/reduce_scatter | solution.py:1932
  661.7 12.0 %copy-start.63 = (bf16[2304,704]{1,0:T(8,128)(2,1)S(1)}, bf16[2304,704]{1,0:T(8,128)(2,1)}, u32[]{:S(2)}) copy-start(bf16[2304,704]{1,0:T(8,128)(2,1)} %get-tuple-element.149) | copy-start | bytes 9732100
  661.7 22.4 %slice-start = ((s8[8388608]{0:T(1024)(128)(4,1)}), s8[4194304]{0:T(1024)(128)(4,1)S(1)}, s32[]{:S(2)}) async-start(s8[8388608]{0:T(1024)(128)(4,1)} %bitcast.250), calls=%async_computation.3 | async-start | bytes 8388608
  673.7 10.4 %slice-start.1 = ((s8[8388608]{0:T(1024)(128)(4,1)}), s8[4194304]{0:T(1024)(128)(4,1)S(1)}, s32[]{:S(2)}) async-start(s8[8388608]{0:T(1024)(128)(4,1)} %bitcast.250), calls=%async_computation.4 | async-start | bytes 8388608
  673.8 23.8 %slice-start.2 = ((s8[8388608]{0:T(1024)(128)(4,1)}), s8[4194304]{0:T(1024)(128)(4,1)S(1)}, s32[]{:S(2)}) async-start(s8[8388608]{0:T(1024)(128)(4,1)} %bitcast.262), calls=%async_computation.5 | async-start | bytes 8388608
  684.2 13.4 %slice-start.3 = ((s8[8388608]{0:T(1024)(128)(4,1)}), s8[4194304]{0:T(1024)(128)(4,1)S(1)}, s32[]{:S(2)}) async-start(s8[8388608]{0:T(1024)(128)(4,1)} %bitcast.262), calls=%async_computation.6 | async-start | bytes 8388608
  794.4 16.4 %slice-start.4 = ((s8[8388608]{0:T(1024)(128)(4,1)}), s8[4194304]{0:T(1024)(128)(4,1)S(1)}, s32[]{:S(2)}) async-start(s8[8388608]{0:T(1024)(128)(4,1)} %bitcast.289), calls=%async_computation.7 | async-start | bytes 8388608
  810.9 10.3 %copy-start.18 = (f32[128,64]{1,0:T(8,128)S(1)}, f32[128,64]{1,0:T(8,128)}, u32[]{:S(2)}) copy-start(f32[128,64]{1,0:T(8,128)} %copy-done.17) | copy-start | bytes 98308
  810.9 10.4 %copy-start.38 = (f32[1,512]{1,0:T(1,128)S(1)}, f32[1,512]{1,0:T(1,128)}, u32[]{:S(2)}) copy-start(f32[1,512]{1,0:T(1,128)} %param.21) | copy-start | bytes 6148
  810.9 12.7 %copy-start.33 = (f32[1,2048]{1,0:T(1,128)S(1)}, f32[1,2048]{1,0:T(1,128)}, u32[]{:S(2)}) copy-start(f32[1,2048]{1,0:T(1,128)} %param.18) | copy-start | bytes 24580
  810.9 12.7 %copy-start.46 = (f32[128]{0:T(128)S(1)}, f32[128]{0:T(128)}, u32[]{:S(2)}) copy-start(f32[128]{0:T(128)} %copy-done.44) | copy-start | bytes 1540
  855.2 10.1 %copy-start.21 = (f32[16,2048]{0,1:T(8,128)S(1)}, f32[16,2048]{0,1:T(8,128)}, u32[]{:S(2)}) copy-start(f32[16,2048]{0,1:T(8,128)} %copy.141) | copy-start | bytes 393220
  (50 other events, 277.1 us)
Sparse Core Ops, SparseCore 0:
  484.4 199.6 all-gather.1
  774.5 34.2 reduce-scatter.1

commit v8 on v7

--- a/solution.py
+++ b/solution.py
@@ -309,8 +309,8 @@
 
 def spread_kernel(cuts, active, *refs):
     arrays = len(cuts)
-    x_refs, o_refs = refs[:arrays], refs[arrays : 2 * arrays]
-    own_sem, over_out, over_in, side_out, side_in, pair_out, pair_in = refs[2 * arrays :]
+    sources, o_refs, x_refs = refs[:arrays], refs[arrays : 2 * arrays], refs[2 * arrays : 3 * arrays]
+    own_sem, over_out, over_in, side_out, side_in, pair_out, pair_in = refs[3 * arrays :]
     units = [
         (a, pl.ds(part * (x_refs[a].shape[0] // parts), x_refs[a].shape[0] // parts))
         for a, parts in enumerate(cuts)
@@ -318,6 +318,11 @@
     ]
 
     def run():
+        taken_in = [pltpu.make_async_copy(sources[a], x_refs[a], own_sem.at[a]) for a in range(arrays)]
+        for copy in taken_in:
+            copy.start()
+        for copy in taken_in:
+            copy.wait()
         member, spot = lax.axis_index(MEMBERS), lax.axis_index(PACKS)
         chip, core, odd = member // 2, lax.rem(member, 2), lax.rem(spot, 2)
         beside = {PACKS: spot + 1 - 2 * odd}
@@ -393,9 +398,10 @@
     outs = pl.pallas_call(
         functools.partial(spread_kernel, [parts] * len(values), active),
         out_shape=[jax.ShapeDtypeStruct((4, *value.shape), value.dtype) for value in values],
-        in_specs=[pl.BlockSpec(memory_space=pltpu.VMEM)] * len(values),
+        in_specs=[pl.BlockSpec(memory_space=pl.ANY)] * len(values),
         out_specs=[pl.BlockSpec(memory_space=pl.ANY)] * len(values),
         scratch_shapes=[
+            *(pltpu.VMEM(value.shape, value.dtype) for value in values),
             dma((len(values),)),
             dma((units,)),
             dma((units,)),
@@ -1349,9 +1355,14 @@
             rise = jnp.where(step >= spot, step + 1, step)
             return jnp.where(2 * spot < spots - 1, fall, rise)
 
+        turns = [(0, True)]
+        for ahead in range(1, spots):
+            turns += [(ahead, True), (ahead - 1, False)]
+        turns.append((spots - 1, False))
+
         def place(number):
-            at = pick(number // 2, [order(step) for step in range(spots)])
-            return at, jnp.where(number % 2 == 0, 1 - chip, chip)
+            at = pick(number, [order(turn) for turn, _ in turns])
+            return at, pick(number, [1 - chip if far else chip for _, far in turns])
 
         def window(ref, kind, at, c):
             if kind:
@@ -1465,7 +1476,7 @@
                     pl.when(spot == spots - 1)(lambda: finish(-1))
                     pl.when((spot > 0) & (spot < spots - 1))(lambda: finish(0))
 
-        late = 4 + jnp.where((spot > 0) & (spot < spots - 1), 1, 0)
+        late = 3 + jnp.where((spot > 0) & (spot < spots - 1), 2, 0)
 
         def outward(index, which, at, c):
             return pltpu.make_async_copy(
@@ -1531,7 +1542,7 @@
                 else:
                     outward(index, which, at, c).start()
             for number_of in range(spots):
-                pl.when(number == 2 * number_of + 1)(functools.partial(across, number_of))
+                pl.when(number == 2 * number_of)(functools.partial(across, number_of))
                 pl.when(number == 2 * number_of + late)(functools.partial(along, number_of))
             return carry
 
@@ -1947,12 +1958,16 @@
     grad_compressed, grad_hidden_norm, grad_attn_gain, grad_latent_gain = latent_back(own)
     grad_hidden = grad_mixed + grad_hidden_norm
 
-    small = jnp.concatenate([grad_attn_gain, grad_latent_gain, grad_ffn_gain, moved[:all_rows, 0]])
-    small = jnp.pad(small, (0, -small.shape[0] % 1024)).reshape(8, -1)
-    grad_compressed_all, small_all = gather_blocks([grad_compressed, small], True, 13)
-    small_all = small_all.reshape(count, -1)
-    gains = jnp.sum(small_all[:, : 2 * width + LAT], axis=0)
-    moved_all = small_all[:, 2 * width + LAT : 2 * width + LAT + all_rows].T
+    gains = jnp.concatenate([grad_attn_gain, grad_latent_gain, grad_ffn_gain])
+    rounded = lax.reduce_precision(gains, 8, 7)
+    small = jnp.concatenate([bf16(rounded), bf16(gains - rounded), bf16(moved[:all_rows, 0])])
+    small = jnp.pad(small, (0, -small.shape[0] % rows)).reshape(rows, -1)
+    last = lax.all_gather(jnp.concatenate([grad_compressed, small], axis=1), BOTH, axis=0, tiled=True)
+    grad_compressed_all = last[:, : LAT + ROPE]
+    small_all = last[:, LAT + ROPE :].reshape(count, -1).astype(jnp.float32)
+    many = 2 * width + LAT
+    gains = jnp.sum(small_all[:, :many] + small_all[:, many : 2 * many], axis=0)
+    moved_all = small_all[:, 2 * many : 2 * many + all_rows].T
     prob = stored[2][:all_rows]
     grad_logits = bf16(moved_all - prob * jnp.sum(moved_all, axis=1, keepdims=True))
     left, right = gated_back(

time: 889 us -> 876 us (0.985)
  Pallas kernels: 599 us -> 565 us
    pallas_call x6 -> x5, Pallas kernels: 155 us -> 131 us  [gather_blocks(): pl.pallas_call(functools.partial(gather_kernel, spots, cuts, wide, active...]
    pallas_call x3, Pallas kernels: 136 us -> 126 us  [sum_call(): pl.pallas_call(functools.partial(sum_kernel, spots, parts, active, body,...]
  transfers between devices with their start and end apart: 4 -> 5, of which waited for: 2 -> 2; matrix products, arithmetic and copies ran while one was open for 12% -> 12% of each run, Pallas kernels for 22% -> 23%
where the time goes in v8:
time: 876 us; the launch traced here: 865 us
  Pallas kernels  565 us (64%)
  matrix products  167 us (19%)
  other arithmetic  51.5 us (6%)
  local copies, waits for them, and re-layouts  38.7 us (4%)
  between operations  16.3 us (2%)
  waiting for transfers between devices  14.7 us (2%)
  starting transfers between devices  11.7 us (1%)
    pallas_call x5, Pallas kernels, gather_blocks(): pl.pallas_call(functools.partial(gather_kernel, spots, cuts, wide, active...  131 us
    pallas_call x3, Pallas kernels, sum_call(): pl.pallas_call(functools.partial(sum_kernel, spots, parts, active, body,...  126 us
    pallas_call x1, Pallas kernels, spread_blocks(): pl.pallas_call(functools.partial(spread_kernel, [parts] * len(values), ac...  87.3 us
    pallas_call x2, Pallas kernels, fused_call(): pl.pallas_call(functools.partial(fused_kernel, spots, parts, active, body...  71.5 us
    dot_general x7, matrix products, t_dot(): lax.dot_general(left, right, (((0,), (0,)), ((), ())), preferred_element_...  62.9 us
    pallas_call x4, Pallas kernels, call(): pl.pallas_call(functools.partial(kernel, len(arrays), counts, len(into),...  57.7 us
    pallas_call x2, Pallas kernels, attend_back(): pl.pallas_call(functools.partial(attend_back_kernel, heads), grid=(count,...  50.8 us
    dot_general x6, matrix products, dot_t(): lax.dot_general(left, right, (((1,), (1,)), ((), ())), preferred_element_...  35.4 us
  transfers between devices with their start and end apart: 5, of which 2 were waited for; matrix products, arithmetic and copies ran while one was open for 12% of the time, Pallas kernels for 23%

profile of v8, /device:TPU:3, one launch (start us, length us, event | category | flops | bytes accessed | tf_op | source)
XLA Modules:
  0.0 865.0 jit_solution(1698021699596782531)
XLA Ops:
  37.9 8.2 attend.2
  62.2 8.7 %fused2.1 = (bf16[16,128,2048]{2,1,0:T(8,128)(2,1)}, bf16[2304,1536]{1,0:T(8,128)(2,1)}, bf16[2304,768]{1,0:T(8,128)(2,1)}, f32[2304,16]{1,0:T(8,128)}, bf16[2,7...) custom-call(bf16[128,2048]{1,0:T(8,128)(2,1)} %multiply_convert_fusi, ...), custom_call_target="tpu_custom_call", output_to_operand_aliasing={{0}: (8, {}), {1}: (9, {}), {2}: (10, {}), {3}: (11, {}), {... | custom-call | tf_op jit(solution)/shard_map/fused2/pallas_call | solution.py:1284
  75.8 53.4 %gather5.1 = (bf16[16,128,2048]{2,1,0:T(8,128)(2,1)}, s32[16,8,128]{2,1,0:T(8,128)}) custom-call(bf16[128,2048]{1,0:T(8,128)(2,1)} %bitcast.256, s32[8,128]{1,0:T(8,128)} %add_add_fusion.refs_2_.refs_1_, bf16[16,128,2048]{2,1,0:T(8,128)(2,1)} %bitcast.240, s32[16,8,128]{2,1,0:T(8,128)} %get-tuple-element.83.refs_3_), custom_call_target="tpu_custom_call", output_to_operand_aliasing={{0}: (2, {}), {1}: (3, {})} | custom-call | tf_op jit(solution)/shard_map/gather5/pallas_call | solution.py:286
  129.3 87.3 %spread4.1 = (bf16[4,2048,768]{2,1,0:T(8,128)(2,1)}, bf16[4,512,1024]{2,1,0:T(8,128)(2,1)}, bf16[4,512,2048]{2,1,0:T(8,128)(2,1)}) custom-call(bf16[2048,768]{1,0:T(8,128)(2,1)} %bitcast.286, bf16[512,1024]{1,0:T(8,128)(2,1)} %bitcast.293, bf16[512,2048]{1,0:T(8,128)(2,1)} %bitcast.289), custom_call_target="tpu_custom_call" | custom-call | tf_op jit(solution)/shard_map/spread4/pallas_call | solution.py:398
  272.2 62.8 %fused6.1 = (bf16[16,128,2048]{2,1,0:T(8,128)(2,1)}, bf16[2304,1536]{1,0:T(8,128)(2,1)}, bf16[2304,768]{1,0:T(8,128)(2,1)}, f32[2304,16]{1,0:T(8,128)}, bf16[2,768,704]{2,1,0:T(8,128)(2,1)}) custom-call(bf16[128,2048]{1,0:T(8,128)(2,1)} %multiply_convert_fusion.refs_0_, ...), custom_call_target="tpu_custom_call", output_to_operand_aliasing={{0}: (6, {}), {1}: (7, {}), {2}: (8, {}), {3}: (9, {}), {4}... | custom-call | tf_op jit(solution)/shard_map/fused6/pallas_call | solution.py:1284
  335.0 67.3 %sum7.1 = (f32[128,2048]{1,0:T(8,128)}, bf16[2304,1536]{1,0:T(8,128)(2,1)}, f32[2304,1]{1,0:T(8,128)}) custom-call(f32[1,16]{1,0:T(1,128)} %compare_convert_fusion.6.refs_1_.refs_0_, bf16[2048,2048]{1,0:T(8,128)(2,1)} %bitcast.241, bf16[2304,1536]{1,0:T(8,128)(2,1)} %get-tuple-element.102.refs_2_, f32[2304,16]{1,0:T(8,128)} %get-tuple-element.103.refs_3_, ...), custom_call_target="tpu_custom_call" | custom-call | tf_op jit(solution)/shard_map/sum7/pallas_call | solution.py:1584
  411.7 11.4 %attend_back.2 = (bf16[512,768]{1,0:T(8,128)(2,1)}, bf16[512,1024]{1,0:T(8,128)(2,1)}, f32[512,64]{1,0:T(8,128)}) custom-call(bf16[512,768]{1,0:T(8,128)(2,1)} %get-tuple-element.106.q_ref, bf16[512,1024]{1,0:T(8,128)(2,1)} %bitcast.277, bf16[128,576]{1,0:T(8,128)(2,1)} %pad_maximum_fusion.3.key_ref.refs_1_, bf16[512,512]{1,0:T(8,128)(2,1)} %bitcast.300, ...), custom_call_target="tpu_custom_call" | custom-call | flops 436207616 | bytes 4194304 | tf_op jit(solution)/shard_map/attend_back/pallas_call | solution.py:722
  423.1 10.0 %convolution_bitcast_fusion.6 = f32[128,2048]{1,0:T(8,128)} fusion(bf16[4,128,768]{2,1,0:T(8,128)(2,1)} %bitcast.292, bf16[4,2048,768]{2,1,0:T(8,128)(2,1)} %get-tuple-element.87), kind=kOutput, calls=%fused_computation.36 | convolution fusion | flops 1610612736 | bytes 14417920 | tf_op jit(solution)/shard_map/mrc,mdc->rd/dot_general | solution.py:1892
  449.7 10.0 %collective-permute-start.1 = (bf16[128,2048]{1,0:T(8,128)(2,1)S(1)}, bf16[128,2048]{1,0:T(8,128)(2,1)S(1)}, u32[]{:S(2)}, u32[]{:S(2)}) collective-permute-start(bf16[128,2048]{1,0:T(8,128)(2,1)S(1)} %add_convert_fusion), channel_id=1, source_target_pairs={{16,0},{17,1},{18,2},{19,3},{20,4},{21,5},{22,6},{23,7},{24,8},{25... | collective-permute-start | bytes 1572872 | tf_op jit(solution)/shard_map/ppermute | solution.py:1913
  459.7 11.1 %collective-permute-done.1 = bf16[128,2048]{1,0:T(8,128)(2,1)S(1)} collective-permute-done((bf16[128,2048]{1,0:T(8,128)(2,1)S(1)}, bf16[128,2048]{1,0:T(8,128)(2,1)S(1)}, u32[]{:S(2)}, u32[]{:S(2)}) %collective-permute-start.1) | collective-permute-done | bytes 524320 | tf_op jit(solution)/shard_map/ppermute | solution.py:1913
  483.3 55.5 %sum10.1 = f32[128,2048]{1,0:T(8,128)} custom-call(f32[1,16]{1,0:T(1,128)} %compare_convert_fusion.6.refs_1_.refs_0_, bf16[2304,768]{1,0:T(8,128)(2,1)} %get-tuple-element.125.refs_1_, bf16[2,768,704]{2,1,0:T(8,128)(2,1)} %get-tuple-element.104.refs_5_.refs_2_, bf16[768,2048]{1,0:T(8,128)(2,1)} %bitcast.266, bf16[704,2048]{1,0:T(8,128)(2,1)} %bitcast.270), custom_call_target="tpu_custom_call" | custom-call | tf_op jit(solution)/shard_map/sum10/pallas_call | solution.py:1584
  538.8 67.7 %gather9.1 = (bf16[16,128,2048]{2,1,0:T(8,128)(2,1)}, bf16[16,128,576]{2,1,0:T(8,128)(2,1)}) custom-call(bf16[128,2048]{1,0:T(8,128)(2,1)} %copy-done.9, bf16[128,576]{1,0:T(8,128)(2,1)} %pad_maximum_fusion.3.key_ref.refs_1_, bf16[16,128,2048]{2,1,0:T(8,128)(2,1)} %get-tuple-element.110, ...), custom_call_target="tpu_custom_call", output_to_operand_aliasing={{0}: (2, {}), {1}: (3, {})} | custom-call | tf_op jit(solution)/shard_map/gather9/pallas_call | solution.py:286
  606.5 21.0 %shared.3 = (bf16[2,2304,704]{2,1,0:T(8,128)(2,1)}, bf16[2304,704]{1,0:T(8,128)(2,1)}) custom-call(s32[3]{0:T(128)} %get-tuple-element.198.control, bf16[2048,2048]{1,0:T(8,128)(2,1)} %bitcast.252, bf16[1408,2048]{1,0:T(8,128)(2,1)} %bitcast.262, bf16[2,2304,704]{2,1,0:T(8,128)(2,1)} %get-tuple-element.142.refs_2_, ...), custom_call_target="tpu_custom_call", output_to_operand_aliasing={{0}: (3, {}), {1}: (4, {})} | custom-call | flops 11811160064 | bytes 33554432 | tf_op jit(solution)/shard_map/shared/pallas_call | solution.py:838
  627.4 30.6 %heads.3 = (bf16[2304,512]{1,0:T(8,128)(2,1)}, bf16[2304,768]{1,0:T(8,128)(2,1)}, bf16[2304,1024]{1,0:T(8,128)(2,1)}) custom-call(s32[3]{0:T(128)} %get-tuple-element.198.control, bf16[2048,2048]{1,0:T(8,128)(2,1)} %bitcast.279, bf16[2048,576]{1,0:T(8,128)(2,1)} %bitcast.272, ...), custom_call_target="tpu_custom_call", output_to_operand_aliasing={{0}: (9, {}), {1}: (10, {}), {2}: (11, {})} | custom-call | flops 12884901888 | bytes 33554432 | tf_op jit(solution)/shard_map/heads/pallas_call | solution.py:838
  660.2 11.9 %convolution_bitcast_fusion = f32[1,1,768,2048]{3,2,1,0:T(8,128)} fusion(bf16[2048,2048]{1,0:T(8,128)(2,1)} %bitcast.243, bf16[2304,768]{1,0:T(8,128)(2,1)} %get-tuple-element.125.refs_1_), kind=kOutput, calls=%fused_computation.18 | convolution fusion | flops 6442450944 | bytes 17825792 | tf_op jit(solution)/shard_map/dot_general | solution.py:35
  672.2 10.4 %convolution_bitcast_fusion.2 = f32[1,704,2048]{2,1,0:T(8,128)} fusion(bf16[2048,2048]{1,0:T(8,128)(2,1)} %bitcast.244, bf16[2304,704]{1,0:T(8,128)(2,1)S(1)} %copy-done.61), kind=kOutput, calls=%fused_computation.20 | convolution fusion | flops 5905580032 | bytes 17301504 | tf_op jit(solution)/shard_map/dot_general | solution.py:35
  682.7 9.9 %convolution_convert_fusion.1.grad_ref = bf16[2048,512]{1,0:T(8,128)(2,1)} fusion(bf16[2048,2048]{1,0:T(8,128)(2,1)} %all-gather.3.cloned.1.call-done, bf16[1,512,2048]{2,1,0:T(8,128)(2,1)} %param.23), kind=kOutput, calls=%fused_computation.28 | convolution fusion | flops 4296015872 | bytes 12582912 | tf_op jit(solution)/shard_map/dot_general | solution.py:29
  692.5 39.5 %attend_back.3 = (bf16[2048,768]{1,0:T(8,128)(2,1)}, bf16[2048,1024]{1,0:T(8,128)(2,1)}, f32[2048,64]{1,0:T(8,128)}) custom-call(bf16[2304,768]{1,0:T(8,128)(2,1)} %get-tuple-element.135.q_ref, bf16[2304,1024]{1,0:T(8,128)(2,1)} %get-tuple-element.136.lat_ref, bf16[2048,576]{1,0:T(8,128)(2,1)} %bitcast.273, ...), custom_call_target="tpu_custom_call" | custom-call | flops 1744830464 | bytes 16777216 | tf_op jit(solution)/shard_map/attend_back/pallas_call | solution.py:722
  741.1 13.4 %fusion.19 = (bf16[1,2048,704]{2,1,0:T(8,128)(2,1)S(1)}, bf16[1,2048,704]{2,1,0:T(8,128)(2,1)S(1)}) fusion(bf16[2,2304,704]{2,1,0:T(8,128)(2,1)} %get-tuple-element.144, bf16[2048,2048]{1,0:T(8,128)(2,1)} %bitcast.245, bf16[1,704,2048]{2,1,0:T(8,128)(2,1)} %param.27), kind=kOutput, calls=%fused_computation.26 | convolution fusion | flops 5927206912 | bytes 22806528 | tf_op jit(solution)/shard_map/dot_general | solution.py:29
  754.6 17.3 %fusion.13 = f32[1,2048,2,704]{1,3,2,0:T(8,128)} fusion(bf16[2048,2048,1]{1,0,2:T(8,128)(2,1)} %bitcast.253, bf16[1,2048,704]{2,1,0:T(8,128)(2,1)S(1)} %get-tuple-element.157, bf16[1,2048,704]{2,1,0:T(8,128)(2,1)S(1)} %get-tuple-element.156), kind=kOutput, calls=%fused_computation.17 | convolution fusion | flops 11822694400 | bytes 25690112 | tf_op jit(solution)/shard_map/dot_general | solution.py:1978
  785.8 20.2 %pair_grad.1 = f32[2048,2,768]{2,1,0:T(2,128)} custom-call(bf16[2048,2048]{1,0:T(8,128)(2,1)} %bitcast.254, bf16[2304,1536]{1,0:T(8,128)(2,1)} %get-tuple-element.146.grad_ref), custom_call_target="tpu_custom_call" | custom-call | flops 12884901888 | bytes 27262976 | tf_op jit(solution)/shard_map/pair_grad/pallas_call | solution.py:1021
  812.6 9.6 %convolution_bitcast_fusion.4 = f32[1,512,2048]{2,1,0:T(8,128)} fusion(bf16[2048,2048]{1,0:T(8,128)(2,1)} %all-gather.3.cloned.1.call-done, bf16[2304,512]{1,0:T(8,128)(2,1)S(1)} %copy-done.60), kind=kOutput, calls=%fused_computation.22 | convolution fusion | flops 4294967296 | bytes 14680064 | tf_op jit(solution)/shard_map/dot_general | solution.py:35
  822.3 9.0 %convolution_bitcast_fusion.1 = f32[1,2048,768]{2,1,0:T(8,128)} fusion(bf16[2048,2048]{1,0:T(8,128)(2,1)S(1)} %bitcast.283, bf16[2048,768]{1,0:T(8,128)(2,1)S(1)} %copy-done.59), kind=kOutput, calls=%fused_computation.19 | convolution fusion | flops 6442450944 | bytes 17825792 | tf_op jit(solution)/shard_map/dot_general | solution.py:35
  849.0 9.2 %convolution_bitcast_fusion.3 = f32[1,2048,576]{1,2,0:T(8,128)} fusion(bf16[2048,2048]{1,0:T(8,128)(2,1)} %bitcast.280, bf16[2048,664]{1,0:T(8,128)(2,1)S(1)} %copy-done.31), kind=kOutput, calls=%fused_computation.21 | convolution fusion | flops 4831838208 | bytes 15728640 | tf_op jit(solution)/shard_map/dot_general | solution.py:35
  (267 shorter events, 193.4 us)
Async XLA Ops:
  7.2 11.0 %copy-start = (bf16[1,2048,576]{1,2,0:T(8,128)(2,1)S(1)}, bf16[1,2048,576]{1,2,0:T(8,128)(2,1)}, u32[]{:S(2)}) copy-start(bf16[1,2048,576]{1,2,0:T(8,128)(2,1)} %param.20) | copy-start | bytes 7077892
  7.2 675.5 %all-gather.3.cloned.1.call-start = ((), (), s32[]{:S(2)}) async-start(), calls=%async_computation.1 | async-start | bytes 8912896 | tf_op jit(solution)/shard_map/all_gather | solution.py:1938
  8.6 11.9 %copy-start.32 = (bf16[1,2048,16]{1,2,0:T(8,128)(2,1)S(1)}, bf16[1,2048,16]{1,2,0:T(8,128)(2,1)}, u32[]{:S(2)}) copy-start(bf16[1,2048,16]{1,2,0:T(8,128)(2,1)} %param.25) | copy-start | bytes 196612
  8.6 12.9 %copy-start.33 = (f32[1,512]{1,0:T(1,128)S(1)}, f32[1,512]{1,0:T(1,128)}, u32[]{:S(2)}) copy-start(f32[1,512]{1,0:T(1,128)} %param.21) | copy-start | bytes 6148
  15.1 421.8 %copy-start.14 = (f32[128,64]{1,0:T(8,128)}, f32[128,64]{1,0:T(8,128)S(1)}, u32[]{:S(2)}) copy-start(f32[128,64]{1,0:T(8,128)S(1)} %fusion.74) | copy-start | bytes 98308
  216.6 22.9 %copy-start.2 = (bf16[1,1,128,2048]{3,2,1,0:T(8,128)(2,1)S(1)}, bf16[1,1,128,2048]{3,2,1,0:T(8,128)(2,1)}, u32[]{:S(2)}) copy-start(bf16[1,1,128,2048]{3,2,1,0:T(8,128)(2,1)} %param.15) | copy-start | bytes 1572868
  216.6 22.9 %collective-permute-start = (bf16[128,2048]{1,0:T(8,128)(2,1)}, bf16[128,2048]{1,0:T(8,128)(2,1)S(1)}, u32[]{:S(2)}, u32[]{:S(2)}) collective-permute-start(bf16[128,2048]{1,0:T(8,128)(2,1)} %add_convert_fusion.1), channel_id=1, source_target_pairs={{0,16},{1,17},{2,18},{3,19},{4,20},{5,21},{6,22},{7,23},{8,24},{9,... | collective-permute-start | bytes 1572872 | tf_op jit(solution)/shard_map/ppermute | solution.py:1851
  240.5 10.0 %copy-start.9 = (bf16[128,2048]{1,0:T(8,128)(2,1)}, bf16[128,2048]{1,0:T(8,128)(2,1)S(1)}, u32[]{:S(2)}) copy-start(bf16[128,2048]{1,0:T(8,128)(2,1)S(1)} %multiply_convert_fusion.1.refs_0_) | copy-start | bytes 1572868
  270.2 133.8 %copy-start.39 = (f32[128]{0:T(128)}, f32[128]{0:T(128)S(1)}, u32[]{:S(2)}) copy-start(f32[128]{0:T(128)S(1)} %get-tuple-element.185) | copy-start | bytes 1540
  270.2 133.8 %copy-start.48 = (f32[128]{0:T(128)}, f32[128]{0:T(128)S(1)}, u32[]{:S(2)}) copy-start(f32[128]{0:T(128)S(1)} %get-tuple-element.184) | copy-start | bytes 1540
  423.0 10.1 %copy-start.8 = (bf16[4,512,1024]{2,1,0:T(8,128)(2,1)S(1)}, bf16[4,512,1024]{2,1,0:T(8,128)(2,1)}, u32[]{:S(2)}) copy-start(bf16[4,512,1024]{2,1,0:T(8,128)(2,1)} %get-tuple-element.88) | copy-start | bytes 12582916
  423.1 10.0 %copy-start.11 = (f32[128,576]{1,0:T(8,128)S(1)}, f32[128,576]{1,0:T(8,128)}, u32[]{:S(2)}) copy-start(f32[128,576]{1,0:T(8,128)} %copy-done.10) | copy-start | bytes 884740
  423.1 10.0 %copy-start.24 = (bf16[512,1024]{1,0:T(8,128)(2,1)S(1)}, bf16[512,1024]{1,0:T(8,128)(2,1)}, u32[]{:S(2)}) copy-start(bf16[512,1024]{1,0:T(8,128)(2,1)} %get-tuple-element.108) | copy-start | bytes 3145732
  423.1 10.0 %copy-start.35 = (f32[1,512]{1,0:T(1,128)S(1)}, f32[1,512]{1,0:T(1,128)}, u32[]{:S(2)}) copy-start(f32[1,512]{1,0:T(1,128)} %param.21) | copy-start | bytes 6148
  449.7 21.0 %collective-permute-start.1 = (bf16[128,2048]{1,0:T(8,128)(2,1)S(1)}, bf16[128,2048]{1,0:T(8,128)(2,1)S(1)}, u32[]{:S(2)}, u32[]{:S(2)}) collective-permute-start(bf16[128,2048]{1,0:T(8,128)(2,1)S(1)} %add_convert_fusion), channel_id=1, source_target_pairs={{16,0},{17,1},{18,2},{19,3},{20,4},{21,5},{22,6},{23,7},{24,8},{25... | collective-permute-start | bytes 1572872 | tf_op jit(solution)/shard_map/ppermute | solution.py:1913
  481.0 57.8 %copy-start.54 = (f32[128]{0:T(128)}, f32[128]{0:T(128)S(1)}, u32[]{:S(2)}) copy-start(f32[128]{0:T(128)S(1)} %broadcast_multiply_fusion.3) | copy-start | bytes 1540
  483.3 292.2 %reduce-scatter.2.cloned.1.call-start = ((), (), s32[]{:S(2)}) async-start(), calls=%async_computation.2 | async-start | bytes 3440640 | tf_op jit(solution)/shard_map/reduce_scatter | solution.py:1943
  660.2 11.9 %copy-start.61 = (bf16[2304,704]{1,0:T(8,128)(2,1)S(1)}, bf16[2304,704]{1,0:T(8,128)(2,1)}, u32[]{:S(2)}) copy-start(bf16[2304,704]{1,0:T(8,128)(2,1)} %get-tuple-element.145) | copy-start | bytes 9732100
  741.0 92.4 %all-gather.5.cloned.1.call-start = ((), (), s32[]{:S(2)}) async-start(), calls=%async_computation.3 | async-start | bytes 3342336 | tf_op jit(solution)/shard_map/all_gather | solution.py:1965
  754.5 22.2 %copy-start.15 = (f32[128,64]{1,0:T(8,128)S(1)}, f32[128,64]{1,0:T(8,128)}, u32[]{:S(2)}) copy-start(f32[128,64]{1,0:T(8,128)} %copy-done.14) | copy-start | bytes 98308
  754.5 22.3 %copy-start.36 = (f32[1,512]{1,0:T(1,128)S(1)}, f32[1,512]{1,0:T(1,128)}, u32[]{:S(2)}) copy-start(f32[1,512]{1,0:T(1,128)} %param.21) | copy-start | bytes 6148
  754.5 22.3 %copy-start.46 = (f32[128]{0:T(128)S(1)}, f32[128]{0:T(128)}, u32[]{:S(2)}) copy-start(f32[128]{0:T(128)} %copy-done.45) | copy-start | bytes 1540
  754.5 24.5 %copy-start.28 = (f32[1,2048]{1,0:T(1,128)S(1)}, f32[1,2048]{1,0:T(1,128)}, u32[]{:S(2)}) copy-start(f32[1,2048]{1,0:T(1,128)} %param.18) | copy-start | bytes 24580
  805.9 16.3 %slice-start = ((s8[8388608]{0:T(1024)(128)(4,1)}), s8[4194304]{0:T(1024)(128)(4,1)S(1)}, s32[]{:S(2)}) async-start(s8[8388608]{0:T(1024)(128)(4,1)} %bitcast.281), calls=%async_computation.4 | async-start | bytes 8388608
  (45 other events, 256.3 us)
Sparse Core Ops, SparseCore 0:
  483.4 191.6 all-gather.2
  741.1 34.2 reduce-scatter.1
  785.9 46.0 all-gather.4

commit v9 on v8

--- a/solution.py
+++ b/solution.py
@@ -800,11 +800,8 @@
     def small(self, array):
         return pl.BlockSpec(array.shape, lambda i, control: (0,) * array.ndim)
 
-    def pack_source(self, width):
-        def index(i, control):
-            return (0, jnp.clip(i - control[0], 0, control[1] - control[0] - 1), 0)
-
-        return pl.BlockSpec((2, self.tile, width), index)
+    def pair_source(self, width):
+        return pl.BlockSpec((2, self.tile, width), lambda i, control: (0, i * control[2], 0))
 
     def result(self, width, dtype=jnp.bfloat16):
         def index(i, control):
@@ -818,14 +815,6 @@
             return (0, jnp.where(control[2] == 1, i, self.count), 0)
 
         shape = jax.ShapeDtypeStruct((2, self.rows + self.tile, width), jnp.bfloat16)
-        return shape, pl.BlockSpec((2, self.tile, width), index)
-
-    def pack_result(self, width):
-        def index(i, control):
-            spot = jnp.clip(i - control[0], 0, control[1] - control[0] - 1)
-            return (0, jnp.where(control[2] == 1, spot, control[1] - control[0]), 0)
-
-        shape = jax.ShapeDtypeStruct((2, self.pack_rows + self.tile, width), jnp.bfloat16)
         return shape, pl.BlockSpec((2, self.tile, width), index)
 
     def call(self, kernel, name, sources, weights, results, into=(), scratch=(), flops=0):
@@ -885,7 +874,7 @@
 def experts_body(inside, sources, weights, results, scratch):
     x, own_ref, routed_ref = sources
     in_ref, shared_in_ref = weights[:2]
-    pre_ref, gated_ref, prob_ref, shared_pre_ref = results[:4]
+    pre_ref, gated_ref, prob_ref, shared_pre_ref, hid_ref = results[:5]
     units = gated_ref.shape[1]
     pre = dot(x, in_ref[...])
     logits = pre[:, 2 * units : 2 * units + own_ref.shape[1]]
@@ -899,18 +888,20 @@
 
     def shared():
         left, right = shared_units(x, shared_in_ref)
+        hidden = bf16(gated_hidden(left, right))
         shared_pre_ref[0] = bf16(left)
         shared_pre_ref[1] = bf16(right)
-        return left, right
+        hid_ref[...] = hidden
+        return hidden
 
     if len(weights) == 2:
-        pl.when(inside)(lambda: shared() and None)
+        shared()
         return
     out_ref, shared_out_ref = weights[2:]
-    partial_ref = results[4]
+    partial_ref = results[5]
 
     def with_shared():
-        hidden = bf16(gated_hidden(*shared()))
+        hidden = shared()
         partial_ref[...] = bf16(dot(gated, out_ref[...]) + dot(hidden, shared_out_ref[...]))
 
     def without():
@@ -1176,7 +1167,7 @@
 
         def window(ref, kind, at, c):
             if kind:
-                return ref.at[:, pl.ds(pl.multiple_of(c * tile, tile), tile)]
+                return ref.at[:, pl.ds(pl.multiple_of((at * 2 + c) * tile, tile), tile)]
             return ref.at[pl.ds(pl.multiple_of((at * 2 + c) * tile, tile), tile)]
 
         def outward(index, which, at, c):
@@ -1221,9 +1212,8 @@
 
             @pl.when(number >= 2)
             def _():
-                for index, kind in enumerate(result_kinds):
-                    if not kind:
-                        outward(index, which, at, c).wait()
+                for index in range(n_results):
+                    outward(index, which, at, c).wait()
 
             for copy in inputs:
                 copy.wait()
@@ -1234,24 +1224,14 @@
                 [target.at[which] for target in result_tiles],
                 scratch,
             )
-            for index, kind in enumerate(result_kinds):
-                if kind:
-
-                    def put(index=index):
-                        copy = outward(index, which, at, c)
-                        copy.start()
-                        copy.wait()
-
-                    pl.when(inside)(put)
-                else:
-                    outward(index, which, at, c).start()
+            for index in range(n_results):
+                outward(index, which, at, c).start()
             return carry
 
         lax.fori_loop(0, 2 * spots, step, 0)
         for which in range(2):
-            for index, kind in enumerate(result_kinds):
-                if not kind:
-                    outward(index, which, spot, chip).wait()
+            for index in range(n_results):
+                outward(index, which, spot, chip).wait()
         for part in range(parts):
             for at in range(spots):
                 over(first(part), at, part).wait_send()
@@ -1366,7 +1346,7 @@
 
         def window(ref, kind, at, c):
             if kind:
-                return ref.at[:, pl.ds(pl.multiple_of(c * tile, tile), tile)]
+                return ref.at[:, pl.ds(pl.multiple_of((at * 2 + c) * tile, tile), tile)]
             return ref.at[pl.ds(pl.multiple_of((at * 2 + c) * tile, tile), tile)]
 
         def inputs(number):
@@ -1731,7 +1711,8 @@
             at.result(2 * units),
             at.result(units),
             at.result(experts_count, jnp.float32),
-            at.pack_result(half),
+            at.pair_result(half),
+            at.result(half),
         ]
         weights = [joined_in, (shared_in_t,)]
         if full:
@@ -1749,7 +1730,7 @@
             [(x_all, at.source(width)), (own_column, at.small(own_column)), (routed, at.source(1))],
             weights,
             results,
-            into[:4],
+            into[:5],
         )
 
     def summed_over(section, number, body_of, name, sources, weights, results, into, scratch=()):
@@ -1757,7 +1738,7 @@
         if fusing:
             shapes = [(shape, shape.ndim == 3) for shape, _ in results]
             return sum_call(rows, number, section, body_of, own_column, sources, weights, shapes, into, scratch)
-        specs = [(array, at.pack_source(half) if kind else at.source(array.shape[1])) for array, kind in sources]
+        specs = [(array, at.pair_source(half) if kind else at.source(array.shape[1])) for array, kind in sources]
         specs.insert(1, (own_column, at.small(own_column)))
         *found, partial = at.call(
             tiled(body_of), name, specs, weights, [*results, at.result(width)], into, scratch
@@ -1766,7 +1747,7 @@
 
     def run_experts_back(section, number, grad_all, routed, stored, into):
         at = tiles[section]
-        pre, _, prob, shared_pre = stored
+        pre, _, prob, shared_pre, _ = stored
         return summed_over(
             section,
             number,
@@ -1779,12 +1760,12 @@
             [pltpu.VMEM((at.tile, joined_width), jnp.bfloat16)],
         )
 
-    def prepare(section, normed_all, keyed_all, ffn_all, tables, into):
+    def run_heads(section, normed_all, keyed_all, tables, into):
         at = tiles[section]
         cosine, sine, seg_col, seg_row = tables
         blocks = at.tile // rows
         row_spec = pl.BlockSpec((blocks, 1, rows), lambda i, control: (i * control[2], 0, 0))
-        found = at.call(
+        return at.call(
             tiled(functools.partial(heads_body, rows)),
             "heads",
             [
@@ -1797,20 +1778,22 @@
             ],
             [(query_weight,), (expand_weight,)],
             [at.result(heads * VD), at.result(heads * QK), at.result(heads * KV)],
-            into[:3],
+            into,
             [pltpu.VMEM((at.tile, heads * QK), jnp.float32)],
             flops=4 * all_rows * width * heads * QK,
         )
-        shared = at.call(
+
+    def run_shared(section, ffn_all, into):
+        at = tiles[section]
+        return at.call(
             tiled(shared_body),
             "shared",
             [(ffn_all, at.source(width))],
             [(shared_in_t,)],
             [at.pair_result(half), at.result(half)],
-            into[3:],
+            into,
             flops=4 * all_rows * width * half,
         )
-        return [*found, *shared]
 
     fresh = boundary[0, 0].astype(jnp.float32)
 
@@ -1833,7 +1816,8 @@
                 ((all_rows + tiles[0].tile, 2 * units), jnp.bfloat16),
                 ((all_rows + tiles[0].tile, units), jnp.bfloat16),
                 ((all_rows + tiles[0].tile, experts_count), jnp.float32),
-                ((2, pack_rows + tiles[0].tile, half), jnp.bfloat16),
+                ((2, all_rows + tiles[0].tile, half), jnp.bfloat16),
+                ((all_rows + tiles[0].tile, half), jnp.bfloat16),
             )
         ),
     ]
@@ -1851,6 +1835,12 @@
     inbound = lax.ppermute(sent, SECTION, [(0, 1)])
     routed = routed_of(layout_all)
     tables_all = tables_of(layout_all.reshape(count, -1, rows)[:, top, : lengths.shape[3]])
+
+    normed, keyed, ffn_all, _ = lax.optimization_barrier((normed, keyed, ffn_all, sent))
+    all_inputs = gather_blocks([normed, keyed], True, 8, 0)
+    prepared = run_heads(0, *all_inputs, tables_all, ())
+    stored[3:] = run_shared(0, ffn_all, stored[3:])
+    inbound, prepared, all_inputs, stored = lax.optimization_barrier((inbound, prepared, all_inputs, stored))
     query_heads, expand_heads, output_heads = (
         value.reshape(members, -1, value.shape[1]) for value in heads_weights
     )
@@ -1907,9 +1897,6 @@
     )
     grad_second = bf16(grad_mixed + latent_back(own_second)[1])
 
-    all_inputs = gather_blocks([normed, keyed], True, 8, 0)
-    prepared = prepare(0, *all_inputs, ffn_all, tables_all, ())
-    grad_second, prepared, all_inputs = lax.optimization_barrier((grad_second, prepared, all_inputs))
     downbound = lax.ppermute(grad_second, SECTION, [(1, 0)]).astype(jnp.float32)
 
     normed_late, keyed_late, gated_late, _ = lax.optimization_barrier((normed, keyed, stored[1], grad_second))
@@ -1930,8 +1917,8 @@
     grad_ffn = jnp.where(is_first, grad_ffn, grad_ffn_second)
     normed_late, keyed_late, _ = lax.optimization_barrier((normed_late, keyed_late, finished))
     normed_all, keyed_all = gather_blocks([normed_late, keyed_late], True, 9, 1, all_inputs)
-    prepared = prepare(1, normed_all, keyed_all, ffn_all, tables_all, prepared)
-    attended_all, query_all, latent_all, shared_pre, shared_hid = prepared
+    attended_all, query_all, latent_all = run_heads(1, normed_all, keyed_all, tables_all, prepared)
+    shared_pre, shared_hid = stored[3:]
     attended_all, shared_hid = attended_all[:all_rows], shared_hid[:all_rows]
     grad_mixed_norm, grad_ffn_gain = rms_backward(mixed, scale_ffn, ffn_gain, grad_ffn)
     grad_mixed = upstream + grad_mixed_norm

time: 876 us -> 855 us (0.976)
  Pallas kernels: 565 us -> 552 us
  waiting for transfers between devices: 14.7 us -> 25.3 us
    pallas_call x4 -> x3, Pallas kernels: 57.7 us -> 37.2 us  [call(): pl.pallas_call(functools.partial(kernel, len(arrays), counts, len(into),...]
    all_gather x1, waiting for transfers between devices: 0.02 us -> 13.6 us  [body(): grad_mixed_all = lax.all_gather(bf16(grad_mixed), BOTH, axis=0, tiled=True)]
  transfers between devices with their start and end apart: 5 -> 5, of which waited for: 2 -> 3; matrix products, arithmetic and copies ran while one was open for 12% -> 11% of each run, Pallas kernels for 23% -> 22%
where the time goes in v9:
time: 855 us; the launch traced here: 844 us
  Pallas kernels  552 us (65%)
  matrix products  165 us (19%)
  other arithmetic  46 us (5%)
  local copies, waits for them, and re-layouts  36.3 us (4%)
  waiting for transfers between devices  25.3 us (3%)
  between operations  16.4 us (2%)
    pallas_call x5, Pallas kernels, gather_blocks(): pl.pallas_call(functools.partial(gather_kernel, spots, cuts, wide, active...  132 us
    pallas_call x3, Pallas kernels, sum_call(): pl.pallas_call(functools.partial(sum_kernel, spots, parts, active, body,...  125 us
    pallas_call x1, Pallas kernels, spread_blocks(): pl.pallas_call(functools.partial(spread_kernel, [parts] * len(values), ac...  87.3 us
    pallas_call x2, Pallas kernels, fused_call(): pl.pallas_call(functools.partial(fused_kernel, spots, parts, active, body...  79.3 us
    dot_general x7, matrix products, t_dot(): lax.dot_general(left, right, (((0,), (0,)), ((), ())), preferred_element_...  62.6 us
    pallas_call x2, Pallas kernels, attend_back(): pl.pallas_call(functools.partial(attend_back_kernel, heads), grid=(count,...  50.9 us
    pallas_call x3, Pallas kernels, call(): pl.pallas_call(functools.partial(kernel, len(arrays), counts, len(into),...  37.2 us
    dot_general x6, matrix products, dot_t(): lax.dot_general(left, right, (((1,), (1,)), ((), ())), preferred_element_...  34.9 us
  transfers between devices with their start and end apart: 5, of which 3 were waited for; matrix products, arithmetic and copies ran while one was open for 11% of the time, Pallas kernels for 22%

profile of v9, /device:TPU:3, one launch (start us, length us, event | category | flops | bytes accessed | tf_op | source)
XLA Modules:
  0.0 843.9 jit_solution(12487313878282069954)
XLA Ops:
  37.8 8.2 attend.2
  62.0 11.0 %fused2.1 = (bf16[16,128,2048]{2,1,0:T(8,128)(2,1)}, bf16[2304,1536]{1,0:T(8,128)(2,1)}, bf16[2304,768]{1,0:T(8,128)(2,1)}, f32[2304,16]{1,0:T(8,128)}, bf16[2,2...) custom-call(bf16[128,2048]{1,0:T(8,128)(2,1)} %multiply_convert_fusi, ...), custom_call_target="tpu_custom_call", output_to_operand_aliasing={{0}: (8, {}), {1}: (9, {}), {2}: (10, {}), {3}: (11, {}), {... | custom-call | tf_op jit(solution)/shard_map/fused2/pallas_call | solution.py:1264
  77.9 53.4 %gather5.1 = (bf16[16,128,2048]{2,1,0:T(8,128)(2,1)}, s32[16,8,128]{2,1,0:T(8,128)}) custom-call(bf16[128,2048]{1,0:T(8,128)(2,1)} %bitcast.257, s32[8,128]{1,0:T(8,128)} %add_add_fusion.refs_2_.refs_1_, bf16[16,128,2048]{2,1,0:T(8,128)(2,1)} %bitcast.242, s32[16,8,128]{2,1,0:T(8,128)} %get-tuple-element.89.refs_3_), custom_call_target="tpu_custom_call", output_to_operand_aliasing={{0}: (2, {}), {1}: (3, {})} | custom-call | tf_op jit(solution)/shard_map/gather5/pallas_call | solution.py:286
  131.4 87.3 %spread4.1 = (bf16[4,2048,768]{2,1,0:T(8,128)(2,1)}, bf16[4,512,1024]{2,1,0:T(8,128)(2,1)}, bf16[4,512,2048]{2,1,0:T(8,128)(2,1)}) custom-call(bf16[2048,768]{1,0:T(8,128)(2,1)} %bitcast.286, bf16[512,1024]{1,0:T(8,128)(2,1)} %bitcast.293, bf16[512,2048]{1,0:T(8,128)(2,1)} %bitcast.289), custom_call_target="tpu_custom_call" | custom-call | tf_op jit(solution)/shard_map/spread4/pallas_call | solution.py:398
  256.1 8.2 attend.3
  271.6 68.3 %fused6.1 = (bf16[16,128,2048]{2,1,0:T(8,128)(2,1)}, bf16[2304,1536]{1,0:T(8,128)(2,1)}, bf16[2304,768]{1,0:T(8,128)(2,1)}, f32[2304,16]{1,0:T(8,128)}, bf16[2,2...) custom-call(bf16[128,2048]{1,0:T(8,128)(2,1)} %multiply_convert_fusi, ...), custom_call_target="tpu_custom_call", output_to_operand_aliasing={{0}: (6, {}), {1}: (7, {}), {2}: (8, {}), {3}: (9, {}), {4}... | custom-call | tf_op jit(solution)/shard_map/fused6/pallas_call | solution.py:1264
  339.9 64.7 %sum7.1 = (f32[128,2048]{1,0:T(8,128)}, bf16[2304,1536]{1,0:T(8,128)(2,1)}, f32[2304,1]{1,0:T(8,128)}) custom-call(f32[1,16]{1,0:T(1,128)} %compare_convert_fusion.6.refs_1_.refs_0_, bf16[2048,2048]{1,0:T(8,128)(2,1)} %bitcast.243, bf16[2304,1536]{1,0:T(8,128)(2,1)} %get-tuple-element.125.refs_2_, f32[2304,16]{1,0:T(8,128)} %get-tuple-element.126.refs_3_, ...), custom_call_target="tpu_custom_call" | custom-call | tf_op jit(solution)/shard_map/sum7/pallas_call | solution.py:1564
  414.1 11.4 %attend_back.2 = (bf16[512,768]{1,0:T(8,128)(2,1)}, bf16[512,1024]{1,0:T(8,128)(2,1)}, f32[512,64]{1,0:T(8,128)}) custom-call(bf16[512,768]{1,0:T(8,128)(2,1)} %get-tuple-element.129.q_ref, bf16[512,1024]{1,0:T(8,128)(2,1)} %bitcast.277, bf16[128,576]{1,0:T(8,128)(2,1)} %pad_maximum_fusion.3.key_ref.refs_1_, bf16[512,512]{1,0:T(8,128)(2,1)} %bitcast.300, ...), custom_call_target="tpu_custom_call" | custom-call | flops 436207616 | bytes 4194304 | tf_op jit(solution)/shard_map/attend_back/pallas_call | solution.py:722
  425.5 10.0 %convolution_bitcast_fusion.6 = f32[128,2048]{1,0:T(8,128)} fusion(bf16[4,128,768]{2,1,0:T(8,128)(2,1)} %bitcast.292, bf16[4,2048,768]{2,1,0:T(8,128)(2,1)} %get-tuple-element.93), kind=kOutput, calls=%fused_computation.36 | convolution fusion | flops 1610612736 | bytes 14417920 | tf_op jit(solution)/shard_map/mrc,mdc->rd/dot_general | solution.py:1882
  445.2 9.4 %collective-permute-done.1 = bf16[128,2048]{1,0:T(8,128)(2,1)S(1)} collective-permute-done((bf16[128,2048]{1,0:T(8,128)(2,1)S(1)}, bf16[128,2048]{1,0:T(8,128)(2,1)S(1)}, u32[]{:S(2)}, u32[]{:S(2)}) %collective-permute-start.1) | collective-permute-done | bytes 524320 | tf_op jit(solution)/shard_map/ppermute | solution.py:1900
  467.1 56.8 %sum10.1 = f32[128,2048]{1,0:T(8,128)} custom-call(f32[1,16]{1,0:T(1,128)} %compare_convert_fusion.6.refs_1_.refs_0_, bf16[2304,768]{1,0:T(8,128)(2,1)} %get-tuple-element.139.refs_1_, bf16[2,2304,704]{2,1,0:T(8,128)(2,1)} %get-tuple-element.127.refs_5_.refs_2_, bf16[768,2048]{1,0:T(8,128)(2,1)} %bitcast.266, bf16[704,2048]{1,0:T(8,128)(2,1)} %bitcast.270), custom_call_target="tpu_custom_call" | custom-call | tf_op jit(solution)/shard_map/sum10/pallas_call | solution.py:1564
  523.8 68.3 %gather9.1 = (bf16[16,128,2048]{2,1,0:T(8,128)(2,1)}, bf16[16,128,576]{2,1,0:T(8,128)(2,1)}) custom-call(bf16[128,2048]{1,0:T(8,128)(2,1)} %copy-done.17, bf16[128,576]{1,0:T(8,128)(2,1)} %pad_maximum_fusion.3.key_ref.refs_1_, bf16[16,128,2048]{2,1,0:T(8,128)(2,1)} %get-tuple-element.100, ...), custom_call_target="tpu_custom_call", output_to_operand_aliasing={{0}: (2, {}), {1}: (3, {})} | custom-call | tf_op jit(solution)/shard_map/gather9/pallas_call | solution.py:286
  592.2 30.9 %heads.3 = (bf16[2304,512]{1,0:T(8,128)(2,1)}, bf16[2304,768]{1,0:T(8,128)(2,1)}, bf16[2304,1024]{1,0:T(8,128)(2,1)}) custom-call(s32[3]{0:T(128)} %get-tuple-element.210.control, bf16[2048,2048]{1,0:T(8,128)(2,1)} %bitcast.279, bf16[2048,576]{1,0:T(8,128)(2,1)} %bitcast.272, ...), custom_call_target="tpu_custom_call", output_to_operand_aliasing={{0}: (9, {}), {1}: (10, {}), {2}: (11, {})} | custom-call | flops 12884901888 | bytes 33554432 | tf_op jit(solution)/shard_map/heads/pallas_call | solution.py:827
  625.2 12.0 %convolution_bitcast_fusion = f32[1,1,768,2048]{3,2,1,0:T(8,128)} fusion(bf16[2048,2048]{1,0:T(8,128)(2,1)} %bitcast.245, bf16[2304,768]{1,0:T(8,128)(2,1)} %get-tuple-element.139.refs_1_), kind=kOutput, calls=%fused_computation.18 | convolution fusion | flops 6442450944 | bytes 17825792 | tf_op jit(solution)/shard_map/dot_general | solution.py:35
  637.2 10.4 %convolution_bitcast_fusion.2 = f32[1,704,2048]{2,1,0:T(8,128)} fusion(bf16[2048,2048]{1,0:T(8,128)(2,1)} %bitcast.246, bf16[2304,704]{1,0:T(8,128)(2,1)S(1)} %copy-done.8), kind=kOutput, calls=%fused_computation.20 | convolution fusion | flops 5905580032 | bytes 17301504 | tf_op jit(solution)/shard_map/dot_general | solution.py:35
  647.7 13.6 %all-gather.3.cloned.1.call-done = bf16[2048,2048]{1,0:T(8,128)(2,1)} async-done(((bf16[128,2048]{1,0:T(8,128)(2,1)}), bf16[2048,2048]{1,0:T(8,128)(2,1)}) %all-gather.3.cloned.1.call-update) | async-done | bytes 8388624 | tf_op jit(solution)/shard_map/all_gather | solution.py:1925
  661.3 9.9 %convolution_convert_fusion.1.grad_ref = bf16[2048,512]{1,0:T(8,128)(2,1)} fusion(bf16[2048,2048]{1,0:T(8,128)(2,1)} %all-gather.3.cloned.1.call-done, bf16[1,512,2048]{2,1,0:T(8,128)(2,1)} %param.23), kind=kOutput, calls=%fused_computation.28 | convolution fusion | flops 4296015872 | bytes 12582912 | tf_op jit(solution)/shard_map/dot_general | solution.py:29
  671.1 39.5 %attend_back.3 = (bf16[2048,768]{1,0:T(8,128)(2,1)}, bf16[2048,1024]{1,0:T(8,128)(2,1)}, f32[2048,64]{1,0:T(8,128)}) custom-call(bf16[2304,768]{1,0:T(8,128)(2,1)} %get-tuple-element.149.q_ref, bf16[2304,1024]{1,0:T(8,128)(2,1)} %get-tuple-element.150.lat_ref, bf16[2048,576]{1,0:T(8,128)(2,1)} %bitcast.273, ...), custom_call_target="tpu_custom_call" | custom-call | flops 1744830464 | bytes 16777216 | tf_op jit(solution)/shard_map/attend_back/pallas_call | solution.py:722
  719.7 13.9 %fusion.19 = (bf16[1,2048,704]{2,1,0:T(8,128)(2,1)S(1)}, bf16[1,2048,704]{2,1,0:T(8,128)(2,1)S(1)}) fusion(bf16[2,2304,704]{2,1,0:T(8,128)(2,1)} %get-tuple-element.127.refs_5_.refs_2_, bf16[2048,2048]{1,0:T(8,128)(2,1)} %bitcast.247, bf16[1,704,2048]{2,1,0:T(8,128)(2,1)} %param.27), kind=kOutput, calls=%fused_computation.26 | convolution fusion | flops 5927206912 | bytes 22806528 | tf_op jit(solution)/shard_map/dot_general | solution.py:29
  733.6 17.3 %fusion.13 = f32[1,2048,2,704]{1,3,2,0:T(8,128)} fusion(bf16[2048,2048,1]{1,0,2:T(8,128)(2,1)} %bitcast.254, bf16[1,2048,704]{2,1,0:T(8,128)(2,1)S(1)} %get-tuple-element.169, bf16[1,2048,704]{2,1,0:T(8,128)(2,1)S(1)} %get-tuple-element.168), kind=kOutput, calls=%fused_computation.17 | convolution fusion | flops 11822694400 | bytes 25690112 | tf_op jit(solution)/shard_map/dot_general | solution.py:1965
  763.3 20.2 %pair_grad.1 = f32[2048,2,768]{2,1,0:T(2,128)} custom-call(bf16[2048,2048]{1,0:T(8,128)(2,1)} %bitcast.255, bf16[2304,1536]{1,0:T(8,128)(2,1)} %get-tuple-element.158.grad_ref), custom_call_target="tpu_custom_call" | custom-call | flops 12884901888 | bytes 27262976 | tf_op jit(solution)/shard_map/pair_grad/pallas_call | solution.py:1012
  790.1 9.6 %convolution_bitcast_fusion.4 = f32[1,512,2048]{2,1,0:T(8,128)} fusion(bf16[2048,2048]{1,0:T(8,128)(2,1)} %all-gather.3.cloned.1.call-done, bf16[2304,512]{1,0:T(8,128)(2,1)S(1)} %copy-done.65), kind=kOutput, calls=%fused_computation.22 | convolution fusion | flops 4294967296 | bytes 14680064 | tf_op jit(solution)/shard_map/dot_general | solution.py:35
  799.9 9.0 %convolution_bitcast_fusion.1 = f32[1,2048,768]{2,1,0:T(8,128)} fusion(bf16[2048,2048]{1,0:T(8,128)(2,1)S(1)} %bitcast.283, bf16[2048,768]{1,0:T(8,128)(2,1)S(1)} %copy-done.64), kind=kOutput, calls=%fused_computation.19 | convolution fusion | flops 6442450944 | bytes 17825792 | tf_op jit(solution)/shard_map/dot_general | solution.py:35
  827.9 9.2 %convolution_bitcast_fusion.3 = f32[1,2048,576]{1,2,0:T(8,128)} fusion(bf16[2048,2048]{1,0:T(8,128)(2,1)} %bitcast.280, bf16[2048,664]{1,0:T(8,128)(2,1)S(1)} %copy-done.34), kind=kOutput, calls=%fused_computation.21 | convolution fusion | flops 4831838208 | bytes 15728640 | tf_op jit(solution)/shard_map/dot_general | solution.py:35
  (275 shorter events, 175.2 us)
Async XLA Ops:
  7.2 10.9 %copy-start = (bf16[1,2048,576]{1,2,0:T(8,128)(2,1)S(1)}, bf16[1,2048,576]{1,2,0:T(8,128)(2,1)}, u32[]{:S(2)}) copy-start(bf16[1,2048,576]{1,2,0:T(8,128)(2,1)} %param.20) | copy-start | bytes 7077892
  7.2 654.1 %all-gather.3.cloned.1.call-start = ((), (), s32[]{:S(2)}) async-start(), calls=%async_computation.1 | async-start | bytes 8912896 | tf_op jit(solution)/shard_map/all_gather | solution.py:1925
  8.6 11.8 %copy-start.35 = (bf16[1,2048,16]{1,2,0:T(8,128)(2,1)S(1)}, bf16[1,2048,16]{1,2,0:T(8,128)(2,1)}, u32[]{:S(2)}) copy-start(bf16[1,2048,16]{1,2,0:T(8,128)(2,1)} %param.25) | copy-start | bytes 196612
  8.6 12.8 %copy-start.36 = (f32[1,512]{1,0:T(1,128)S(1)}, f32[1,512]{1,0:T(1,128)}, u32[]{:S(2)}) copy-start(f32[1,512]{1,0:T(1,128)} %param.21) | copy-start | bytes 6148
  131.4 90.4 %copy-start.25 = (f32[128,32]{1,0:T(8,128)S(1)}, f32[128,32]{1,0:T(8,128)}, u32[]{:S(2)}) copy-start(f32[128,32]{1,0:T(8,128)} %copy-done.24) | copy-start | bytes 49156
  218.7 24.0 %collective-permute-start = (bf16[128,2048]{1,0:T(8,128)(2,1)}, bf16[128,2048]{1,0:T(8,128)(2,1)S(1)}, u32[]{:S(2)}, u32[]{:S(2)}) collective-permute-start(bf16[128,2048]{1,0:T(8,128)(2,1)} %add_convert_fusion.1), channel_id=1, source_target_pairs={{0,16},{1,17},{2,18},{3,19},{4,20},{5,21},{6,22},{7,23},{8,24},{9,... | collective-permute-start | bytes 1572872 | tf_op jit(solution)/shard_map/ppermute | solution.py:1835
  243.7 9.9 %copy-start.17 = (bf16[128,2048]{1,0:T(8,128)(2,1)}, bf16[128,2048]{1,0:T(8,128)(2,1)S(1)}, u32[]{:S(2)}) copy-start(bf16[128,2048]{1,0:T(8,128)(2,1)S(1)} %multiply_convert_fusion.1.refs_0_) | copy-start | bytes 1572868
  269.7 136.7 %copy-start.42 = (f32[128]{0:T(128)}, f32[128]{0:T(128)S(1)}, u32[]{:S(2)}) copy-start(f32[128]{0:T(128)S(1)} %get-tuple-element.197) | copy-start | bytes 1540
  269.7 136.7 %copy-start.52 = (f32[128]{0:T(128)}, f32[128]{0:T(128)S(1)}, u32[]{:S(2)}) copy-start(f32[128]{0:T(128)S(1)} %get-tuple-element.196) | copy-start | bytes 1540
  425.4 10.0 %copy-start.11 = (bf16[4,512,1024]{2,1,0:T(8,128)(2,1)S(1)}, bf16[4,512,1024]{2,1,0:T(8,128)(2,1)}, u32[]{:S(2)}) copy-start(bf16[4,512,1024]{2,1,0:T(8,128)(2,1)} %get-tuple-element.94) | copy-start | bytes 12582916
  425.4 10.0 %copy-start.13 = (f32[128,576]{1,0:T(8,128)S(1)}, f32[128,576]{1,0:T(8,128)}, u32[]{:S(2)}) copy-start(f32[128,576]{1,0:T(8,128)} %copy-done.12) | copy-start | bytes 884740
  425.5 10.0 %copy-start.27 = (bf16[512,1024]{1,0:T(8,128)(2,1)S(1)}, bf16[512,1024]{1,0:T(8,128)(2,1)}, u32[]{:S(2)}) copy-start(bf16[512,1024]{1,0:T(8,128)(2,1)} %get-tuple-element.131) | copy-start | bytes 3145732
  425.5 10.0 %copy-start.38 = (f32[1,512]{1,0:T(1,128)S(1)}, f32[1,512]{1,0:T(1,128)}, u32[]{:S(2)}) copy-start(f32[1,512]{1,0:T(1,128)} %param.21) | copy-start | bytes 6148
  443.6 10.9 %collective-permute-start.1 = (bf16[128,2048]{1,0:T(8,128)(2,1)S(1)}, bf16[128,2048]{1,0:T(8,128)(2,1)S(1)}, u32[]{:S(2)}, u32[]{:S(2)}) collective-permute-start(bf16[128,2048]{1,0:T(8,128)(2,1)S(1)} %add_convert_fusion), channel_id=1, source_target_pairs={{16,0},{17,1},{18,2},{19,3},{20,4},{21,5},{22,6},{23,7},{24,8},{25... | collective-permute-start | bytes 1572872 | tf_op jit(solution)/shard_map/ppermute | solution.py:1900
  464.8 59.1 %copy-start.59 = (f32[128]{0:T(128)}, f32[128]{0:T(128)S(1)}, u32[]{:S(2)}) copy-start(f32[128]{0:T(128)S(1)} %broadcast_multiply_fusion.3) | copy-start | bytes 1540
  467.0 286.1 %reduce-scatter.2.cloned.1.call-start = ((), (), s32[]{:S(2)}) async-start(), calls=%async_computation.2 | async-start | bytes 3440640 | tf_op jit(solution)/shard_map/reduce_scatter | solution.py:1930
  625.2 12.0 %copy-start.8 = (bf16[2304,704]{1,0:T(8,128)(2,1)S(1)}, bf16[2304,704]{1,0:T(8,128)(2,1)}, u32[]{:S(2)}) copy-start(bf16[2304,704]{1,0:T(8,128)(2,1)} %get-tuple-element.157) | copy-start | bytes 9732100
  719.6 91.3 %all-gather.5.cloned.1.call-start = ((), (), s32[]{:S(2)}) async-start(), calls=%async_computation.3 | async-start | bytes 3342336 | tf_op jit(solution)/shard_map/all_gather | solution.py:1952
  733.6 20.9 %copy-start.39 = (f32[1,512]{1,0:T(1,128)S(1)}, f32[1,512]{1,0:T(1,128)}, u32[]{:S(2)}) copy-start(f32[1,512]{1,0:T(1,128)} %param.21) | copy-start | bytes 6148
  733.6 20.9 %copy-start.50 = (f32[128]{0:T(128)S(1)}, f32[128]{0:T(128)}, u32[]{:S(2)}) copy-start(f32[128]{0:T(128)} %copy-done.49) | copy-start | bytes 1540
  783.5 16.3 %slice-start = ((s8[8388608]{0:T(1024)(128)(4,1)}), s8[4194304]{0:T(1024)(128)(4,1)S(1)}, s32[]{:S(2)}) async-start(s8[8388608]{0:T(1024)(128)(4,1)} %bitcast.281), calls=%async_computation.4 | async-start | bytes 8388608
  790.1 9.6 %slice-start.1 = ((s8[8388608]{0:T(1024)(128)(4,1)}), s8[4194304]{0:T(1024)(128)(4,1)S(1)}, s32[]{:S(2)}) async-start(s8[8388608]{0:T(1024)(128)(4,1)} %bitcast.281), calls=%async_computation.5 | async-start | bytes 8388608
  790.1 9.6 %copy-start.64 = (bf16[2048,768]{1,0:T(8,128)(2,1)S(1)}, bf16[2048,768]{1,0:T(8,128)(2,1)}, u32[]{:S(2)}) copy-start(bf16[2048,768]{1,0:T(8,128)(2,1)} %get-tuple-element.151) | copy-start | bytes 9437188
  810.9 11.3 %copy-start.7 = (f32[2304,16]{1,0:T(8,128)S(1)}, f32[2304,16]{1,0:T(8,128)}, u32[]{:S(2)}) copy-start(f32[2304,16]{1,0:T(8,128)} %get-tuple-element.126.refs_3_) | copy-start | bytes 442372
  (49 other events, 263.6 us)
Sparse Core Ops, SparseCore 0:
  467.1 194.0 all-gather.2
  719.8 33.3 reduce-scatter.1
  763.4 45.9 all-gather.4

commit v10 on v9

--- a/solution.py
+++ b/solution.py
@@ -640,7 +640,7 @@
         scores = jnp.where(allowed, dot_t(query, key) * factor, masked_score)
         top = jnp.max(scores, axis=1, keepdims=True)
         powers = jnp.exp(scores - top)
-        probs = powers / jnp.sum(powers, axis=1, keepdims=True)
+        probs = powers * (1.0 / jnp.sum(powers, axis=1, keepdims=True))
         out_ref[:, head * VD : (head + 1) * VD] = bf16(dot(bf16(probs), value))
 
 
@@ -693,7 +693,7 @@
         scores = jnp.where(allowed, dot_t(query, key) * factor, masked_score)
         top = jnp.max(scores, axis=1, keepdims=True)
         powers = jnp.exp(scores - top)
-        probs = powers / jnp.sum(powers, axis=1, keepdims=True)
+        probs = powers * (1.0 / jnp.sum(powers, axis=1, keepdims=True))
         grad_value = t_dot(bf16(probs), grad)
         grad_probs = dot_t(grad, value)
         centre = jnp.sum(probs * grad_probs, axis=1, keepdims=True)
@@ -1301,7 +1301,7 @@
     return outs[0].reshape(-1, width), list(outs[1:])
 
 
-def sum_kernel(spots, parts, active, body, pack_kinds, counts, n_into, *refs):
+def sum_kernel(spots, parts, active, body, pack_kinds, counts, later, n_into, *refs):
     source_kinds, result_kinds = pack_kinds
     n_sources, n_results = len(source_kinds), len(result_kinds)
     n_weights, n_pieces = len(counts), sum(counts)
@@ -1323,7 +1323,8 @@
 
     def run():
         loads = loads_of(counts, stored, weights, weight_sem)
-        for copy in loads:
+        early = [copy for index, copy in enumerate(loads) if index not in later]
+        for copy in early:
             copy.start()
         spot, chip, core = places(spots)
 
@@ -1489,8 +1490,15 @@
 
             @pl.when(number == 0)
             def _():
-                for copy in loads:
+                for copy in early:
                     copy.wait()
+                for index in later:
+                    loads[index].start()
+
+            @pl.when(number == min(1, spots - 1))
+            def _():
+                for index in later:
+                    loads[index].wait()
 
             @pl.when(number >= 2)
             def _():
@@ -1545,7 +1553,7 @@
     pl.when(lax.axis_index(SECTION) == active)(run)
 
 
-def sum_call(rows, number, active, body, small, sources, weights, results, into, scratch=(), parts=4):
+def sum_call(rows, number, active, body, small, sources, weights, later, results, into, scratch=(), parts=4):
     spots = lax.axis_size(PACKS)
     width = weights[-1][0].shape[1]
     tile = 2 * rows
@@ -1570,6 +1578,7 @@
             body,
             ([kind for _, kind in sources], [kind for _, kind in results]),
             [len(weight) for weight in weights],
+            later,
             len(into),
         ),
         out_shape=[jax.ShapeDtypeStruct((rows, width), jnp.float32), *(shape for shape, _ in results)],
@@ -1733,11 +1742,11 @@
             into[:5],
         )
 
-    def summed_over(section, number, body_of, name, sources, weights, results, into, scratch=()):
+    def summed_over(section, number, body_of, name, sources, weights, later, results, into, scratch=()):
         at = tiles[section]
         if fusing:
             shapes = [(shape, shape.ndim == 3) for shape, _ in results]
-            return sum_call(rows, number, section, body_of, own_column, sources, weights, shapes, into, scratch)
+            return sum_call(rows, number, section, body_of, own_column, sources, weights, later, shapes, into, scratch)
         specs = [(array, at.pair_source(half) if kind else at.source(array.shape[1])) for array, kind in sources]
         specs.insert(1, (own_column, at.small(own_column)))
         *found, partial = at.call(
@@ -1755,6 +1764,7 @@
             "experts_back",
             [(grad_all, False), (pre, False), (prob, False), (routed, False), (shared_pre, True)],
             [joined_in, (shared_in_t,), (expert_out,), (shared_out,)],
+            [2, 4],
             [at.result(2 * units), at.result(1, jnp.float32)],
             into,
             [pltpu.VMEM((at.tile, joined_width), jnp.bfloat16)],
@@ -1907,6 +1917,7 @@
         "finish",
         [(gated_late, False), (stored[3], True)],
         [(expert_out,), (shared_out,)],
+        [1],
         [],
         (),
     )

time: 855 us -> 851 us (level)
  no operation moved by 1% of the time
where the time goes in v10:
time: 851 us; the launch traced here: 840 us
  Pallas kernels  546 us (64%)
  matrix products  165 us (19%)
  other arithmetic  46 us (5%)
  local copies, waits for them, and re-layouts  36.3 us (4%)
  waiting for transfers between devices  24.6 us (3%)
  between operations  16.4 us (2%)
    pallas_call x5, Pallas kernels, gather_blocks(): pl.pallas_call(functools.partial(gather_kernel, spots, cuts, wide, active...  131 us
    pallas_call x3, Pallas kernels, sum_call(): pl.pallas_call(functools.partial(sum_kernel, spots, parts, active, body,...  120 us
    pallas_call x1, Pallas kernels, spread_blocks(): pl.pallas_call(functools.partial(spread_kernel, [parts] * len(values), ac...  87.3 us
    pallas_call x2, Pallas kernels, fused_call(): pl.pallas_call(functools.partial(fused_kernel, spots, parts, active, body...  79.3 us
    dot_general x7, matrix products, t_dot(): lax.dot_general(left, right, (((0,), (0,)), ((), ())), preferred_element_...  62.7 us
    pallas_call x2, Pallas kernels, attend_back(): pl.pallas_call(functools.partial(attend_back_kernel, heads), grid=(count,...  50.9 us
    pallas_call x3, Pallas kernels, call(): pl.pallas_call(functools.partial(kernel, len(arrays), counts, len(into),...  36.9 us
    dot_general x6, matrix products, dot_t(): lax.dot_general(left, right, (((1,), (1,)), ((), ())), preferred_element_...  34.9 us
  transfers between devices with their start and end apart: 5, of which 3 were waited for; matrix products, arithmetic and copies ran while one was open for 11% of the time, Pallas kernels for 22%

profile of v10, /device:TPU:3, one launch (start us, length us, event | category | flops | bytes accessed | tf_op | source)
XLA Modules:
  0.0 839.7 jit_solution(3840229771109526230)
XLA Ops:
  37.8 8.2 attend.2
  62.0 11.0 %fused2.1 = (bf16[16,128,2048]{2,1,0:T(8,128)(2,1)}, bf16[2304,1536]{1,0:T(8,128)(2,1)}, bf16[2304,768]{1,0:T(8,128)(2,1)}, f32[2304,16]{1,0:T(8,128)}, bf16[2,2...) custom-call(bf16[128,2048]{1,0:T(8,128)(2,1)} %multiply_convert_fusi, ...), custom_call_target="tpu_custom_call", output_to_operand_aliasing={{0}: (8, {}), {1}: (9, {}), {2}: (10, {}), {3}: (11, {}), {... | custom-call | tf_op jit(solution)/shard_map/fused2/pallas_call | solution.py:1264
  77.9 53.4 %gather5.1 = (bf16[16,128,2048]{2,1,0:T(8,128)(2,1)}, s32[16,8,128]{2,1,0:T(8,128)}) custom-call(bf16[128,2048]{1,0:T(8,128)(2,1)} %bitcast.257, s32[8,128]{1,0:T(8,128)} %add_add_fusion.refs_2_.refs_1_, bf16[16,128,2048]{2,1,0:T(8,128)(2,1)} %bitcast.242, s32[16,8,128]{2,1,0:T(8,128)} %get-tuple-element.89.refs_3_), custom_call_target="tpu_custom_call", output_to_operand_aliasing={{0}: (2, {}), {1}: (3, {})} | custom-call | tf_op jit(solution)/shard_map/gather5/pallas_call | solution.py:286
  131.4 87.3 %spread4.1 = (bf16[4,2048,768]{2,1,0:T(8,128)(2,1)}, bf16[4,512,1024]{2,1,0:T(8,128)(2,1)}, bf16[4,512,2048]{2,1,0:T(8,128)(2,1)}) custom-call(bf16[2048,768]{1,0:T(8,128)(2,1)} %bitcast.286, bf16[512,1024]{1,0:T(8,128)(2,1)} %bitcast.293, bf16[512,2048]{1,0:T(8,128)(2,1)} %bitcast.289), custom_call_target="tpu_custom_call" | custom-call | tf_op jit(solution)/shard_map/spread4/pallas_call | solution.py:398
  256.1 8.2 attend.3
  271.6 68.3 %fused6.1 = (bf16[16,128,2048]{2,1,0:T(8,128)(2,1)}, bf16[2304,1536]{1,0:T(8,128)(2,1)}, bf16[2304,768]{1,0:T(8,128)(2,1)}, f32[2304,16]{1,0:T(8,128)}, bf16[2,2...) custom-call(bf16[128,2048]{1,0:T(8,128)(2,1)} %multiply_convert_fusi, ...), custom_call_target="tpu_custom_call", output_to_operand_aliasing={{0}: (6, {}), {1}: (7, {}), {2}: (8, {}), {3}: (9, {}), {4}... | custom-call | tf_op jit(solution)/shard_map/fused6/pallas_call | solution.py:1264
  339.9 62.3 %sum7.1 = (f32[128,2048]{1,0:T(8,128)}, bf16[2304,1536]{1,0:T(8,128)(2,1)}, f32[2304,1]{1,0:T(8,128)}) custom-call(f32[1,16]{1,0:T(1,128)} %compare_convert_fusion.6.refs_1_.refs_0_, bf16[2048,2048]{1,0:T(8,128)(2,1)} %bitcast.243, bf16[2304,1536]{1,0:T(8,128)(2,1)} %get-tuple-element.125.refs_2_, f32[2304,16]{1,0:T(8,128)} %get-tuple-element.126.refs_3_, ...), custom_call_target="tpu_custom_call" | custom-call | tf_op jit(solution)/shard_map/sum7/pallas_call | solution.py:1572
  411.7 11.4 %attend_back.2 = (bf16[512,768]{1,0:T(8,128)(2,1)}, bf16[512,1024]{1,0:T(8,128)(2,1)}, f32[512,64]{1,0:T(8,128)}) custom-call(bf16[512,768]{1,0:T(8,128)(2,1)} %get-tuple-element.129.q_ref, bf16[512,1024]{1,0:T(8,128)(2,1)} %bitcast.277, bf16[128,576]{1,0:T(8,128)(2,1)} %pad_maximum_fusion.3.key_ref.refs_1_, bf16[512,512]{1,0:T(8,128)(2,1)} %bitcast.300, ...), custom_call_target="tpu_custom_call" | custom-call | flops 436207616 | bytes 4194304 | tf_op jit(solution)/shard_map/attend_back/pallas_call | solution.py:722
  423.1 10.0 %convolution_bitcast_fusion.6 = f32[128,2048]{1,0:T(8,128)} fusion(bf16[4,128,768]{2,1,0:T(8,128)(2,1)} %bitcast.292, bf16[4,2048,768]{2,1,0:T(8,128)(2,1)} %get-tuple-element.93), kind=kOutput, calls=%fused_computation.36 | convolution fusion | flops 1610612736 | bytes 14417920 | tf_op jit(solution)/shard_map/mrc,mdc->rd/dot_general | solution.py:1892
  445.2 11.1 %collective-permute-done.1 = bf16[128,2048]{1,0:T(8,128)(2,1)S(1)} collective-permute-done((bf16[128,2048]{1,0:T(8,128)(2,1)S(1)}, bf16[128,2048]{1,0:T(8,128)(2,1)S(1)}, u32[]{:S(2)}, u32[]{:S(2)}) %collective-permute-start.1) | collective-permute-done | bytes 524320 | tf_op jit(solution)/shard_map/ppermute | solution.py:1910
  468.8 54.5 %sum10.1 = f32[128,2048]{1,0:T(8,128)} custom-call(f32[1,16]{1,0:T(1,128)} %compare_convert_fusion.6.refs_1_.refs_0_, bf16[2304,768]{1,0:T(8,128)(2,1)} %get-tuple-element.139.refs_1_, bf16[2,2304,704]{2,1,0:T(8,128)(2,1)} %get-tuple-element.127.refs_5_.refs_2_, bf16[768,2048]{1,0:T(8,128)(2,1)} %bitcast.266, bf16[704,2048]{1,0:T(8,128)(2,1)} %bitcast.270), custom_call_target="tpu_custom_call" | custom-call | tf_op jit(solution)/shard_map/sum10/pallas_call | solution.py:1572
  523.3 67.1 %gather9.1 = (bf16[16,128,2048]{2,1,0:T(8,128)(2,1)}, bf16[16,128,576]{2,1,0:T(8,128)(2,1)}) custom-call(bf16[128,2048]{1,0:T(8,128)(2,1)} %copy-done.17, bf16[128,576]{1,0:T(8,128)(2,1)} %pad_maximum_fusion.3.key_ref.refs_1_, bf16[16,128,2048]{2,1,0:T(8,128)(2,1)} %get-tuple-element.100, ...), custom_call_target="tpu_custom_call", output_to_operand_aliasing={{0}: (2, {}), {1}: (3, {})} | custom-call | tf_op jit(solution)/shard_map/gather9/pallas_call | solution.py:286
  590.4 30.7 %heads.3 = (bf16[2304,512]{1,0:T(8,128)(2,1)}, bf16[2304,768]{1,0:T(8,128)(2,1)}, bf16[2304,1024]{1,0:T(8,128)(2,1)}) custom-call(s32[3]{0:T(128)} %get-tuple-element.210.control, bf16[2048,2048]{1,0:T(8,128)(2,1)} %bitcast.279, bf16[2048,576]{1,0:T(8,128)(2,1)} %bitcast.272, ...), custom_call_target="tpu_custom_call", output_to_operand_aliasing={{0}: (9, {}), {1}: (10, {}), {2}: (11, {})} | custom-call | flops 12884901888 | bytes 33554432 | tf_op jit(solution)/shard_map/heads/pallas_call | solution.py:827
  623.3 12.0 %convolution_bitcast_fusion = f32[1,1,768,2048]{3,2,1,0:T(8,128)} fusion(bf16[2048,2048]{1,0:T(8,128)(2,1)} %bitcast.245, bf16[2304,768]{1,0:T(8,128)(2,1)} %get-tuple-element.139.refs_1_), kind=kOutput, calls=%fused_computation.18 | convolution fusion | flops 6442450944 | bytes 17825792 | tf_op jit(solution)/shard_map/dot_general | solution.py:35
  635.3 10.5 %convolution_bitcast_fusion.2 = f32[1,704,2048]{2,1,0:T(8,128)} fusion(bf16[2048,2048]{1,0:T(8,128)(2,1)} %bitcast.246, bf16[2304,704]{1,0:T(8,128)(2,1)S(1)} %copy-done.8), kind=kOutput, calls=%fused_computation.20 | convolution fusion | flops 5905580032 | bytes 17301504 | tf_op jit(solution)/shard_map/dot_general | solution.py:35
  645.8 11.4 %all-gather.3.cloned.1.call-done = bf16[2048,2048]{1,0:T(8,128)(2,1)} async-done(((bf16[128,2048]{1,0:T(8,128)(2,1)}), bf16[2048,2048]{1,0:T(8,128)(2,1)}) %all-gather.3.cloned.1.call-update) | async-done | bytes 8388624 | tf_op jit(solution)/shard_map/all_gather | solution.py:1936
  657.2 9.9 %convolution_convert_fusion.1.grad_ref = bf16[2048,512]{1,0:T(8,128)(2,1)} fusion(bf16[2048,2048]{1,0:T(8,128)(2,1)} %all-gather.3.cloned.1.call-done, bf16[1,512,2048]{2,1,0:T(8,128)(2,1)} %param.23), kind=kOutput, calls=%fused_computation.28 | convolution fusion | flops 4296015872 | bytes 12582912 | tf_op jit(solution)/shard_map/dot_general | solution.py:29
  667.1 39.5 %attend_back.3 = (bf16[2048,768]{1,0:T(8,128)(2,1)}, bf16[2048,1024]{1,0:T(8,128)(2,1)}, f32[2048,64]{1,0:T(8,128)}) custom-call(bf16[2304,768]{1,0:T(8,128)(2,1)} %get-tuple-element.149.q_ref, bf16[2304,1024]{1,0:T(8,128)(2,1)} %get-tuple-element.150.lat_ref, bf16[2048,576]{1,0:T(8,128)(2,1)} %bitcast.273, ...), custom_call_target="tpu_custom_call" | custom-call | flops 1744830464 | bytes 16777216 | tf_op jit(solution)/shard_map/attend_back/pallas_call | solution.py:722
  715.6 13.9 %fusion.19 = (bf16[1,2048,704]{2,1,0:T(8,128)(2,1)S(1)}, bf16[1,2048,704]{2,1,0:T(8,128)(2,1)S(1)}) fusion(bf16[2,2304,704]{2,1,0:T(8,128)(2,1)} %get-tuple-element.127.refs_5_.refs_2_, bf16[2048,2048]{1,0:T(8,128)(2,1)} %bitcast.247, bf16[1,704,2048]{2,1,0:T(8,128)(2,1)} %param.27), kind=kOutput, calls=%fused_computation.26 | convolution fusion | flops 5927206912 | bytes 22806528 | tf_op jit(solution)/shard_map/dot_general | solution.py:29
  729.6 17.4 %fusion.13 = f32[1,2048,2,704]{1,3,2,0:T(8,128)} fusion(bf16[2048,2048,1]{1,0,2:T(8,128)(2,1)} %bitcast.254, bf16[1,2048,704]{2,1,0:T(8,128)(2,1)S(1)} %get-tuple-element.169, bf16[1,2048,704]{2,1,0:T(8,128)(2,1)S(1)} %get-tuple-element.168), kind=kOutput, calls=%fused_computation.17 | convolution fusion | flops 11822694400 | bytes 25690112 | tf_op jit(solution)/shard_map/dot_general | solution.py:1976
  759.2 20.2 %pair_grad.1 = f32[2048,2,768]{2,1,0:T(2,128)} custom-call(bf16[2048,2048]{1,0:T(8,128)(2,1)} %bitcast.255, bf16[2304,1536]{1,0:T(8,128)(2,1)} %get-tuple-element.158.grad_ref), custom_call_target="tpu_custom_call" | custom-call | flops 12884901888 | bytes 27262976 | tf_op jit(solution)/shard_map/pair_grad/pallas_call | solution.py:1012
  786.0 9.6 %convolution_bitcast_fusion.4 = f32[1,512,2048]{2,1,0:T(8,128)} fusion(bf16[2048,2048]{1,0:T(8,128)(2,1)} %all-gather.3.cloned.1.call-done, bf16[2304,512]{1,0:T(8,128)(2,1)S(1)} %copy-done.65), kind=kOutput, calls=%fused_computation.22 | convolution fusion | flops 4294967296 | bytes 14680064 | tf_op jit(solution)/shard_map/dot_general | solution.py:35
  795.8 9.0 %convolution_bitcast_fusion.1 = f32[1,2048,768]{2,1,0:T(8,128)} fusion(bf16[2048,2048]{1,0:T(8,128)(2,1)S(1)} %bitcast.283, bf16[2048,768]{1,0:T(8,128)(2,1)S(1)} %copy-done.64), kind=kOutput, calls=%fused_computation.19 | convolution fusion | flops 6442450944 | bytes 17825792 | tf_op jit(solution)/shard_map/dot_general | solution.py:35
  823.8 9.2 %convolution_bitcast_fusion.3 = f32[1,2048,576]{1,2,0:T(8,128)} fusion(bf16[2048,2048]{1,0:T(8,128)(2,1)} %bitcast.280, bf16[2048,664]{1,0:T(8,128)(2,1)S(1)} %copy-done.34), kind=kOutput, calls=%fused_computation.21 | convolution fusion | flops 4831838208 | bytes 15728640 | tf_op jit(solution)/shard_map/dot_general | solution.py:35
  (275 shorter events, 177.5 us)
Async XLA Ops:
  7.2 10.9 %copy-start = (bf16[1,2048,576]{1,2,0:T(8,128)(2,1)S(1)}, bf16[1,2048,576]{1,2,0:T(8,128)(2,1)}, u32[]{:S(2)}) copy-start(bf16[1,2048,576]{1,2,0:T(8,128)(2,1)} %param.20) | copy-start | bytes 7077892
  7.2 650.0 %all-gather.3.cloned.1.call-start = ((), (), s32[]{:S(2)}) async-start(), calls=%async_computation.1 | async-start | bytes 8912896 | tf_op jit(solution)/shard_map/all_gather | solution.py:1936
  8.6 11.8 %copy-start.35 = (bf16[1,2048,16]{1,2,0:T(8,128)(2,1)S(1)}, bf16[1,2048,16]{1,2,0:T(8,128)(2,1)}, u32[]{:S(2)}) copy-start(bf16[1,2048,16]{1,2,0:T(8,128)(2,1)} %param.25) | copy-start | bytes 196612
  8.6 12.8 %copy-start.36 = (f32[1,512]{1,0:T(1,128)S(1)}, f32[1,512]{1,0:T(1,128)}, u32[]{:S(2)}) copy-start(f32[1,512]{1,0:T(1,128)} %param.21) | copy-start | bytes 6148
  131.4 90.4 %copy-start.25 = (f32[128,32]{1,0:T(8,128)S(1)}, f32[128,32]{1,0:T(8,128)}, u32[]{:S(2)}) copy-start(f32[128,32]{1,0:T(8,128)} %copy-done.24) | copy-start | bytes 49156
  218.7 24.0 %collective-permute-start = (bf16[128,2048]{1,0:T(8,128)(2,1)}, bf16[128,2048]{1,0:T(8,128)(2,1)S(1)}, u32[]{:S(2)}, u32[]{:S(2)}) collective-permute-start(bf16[128,2048]{1,0:T(8,128)(2,1)} %add_convert_fusion.1), channel_id=1, source_target_pairs={{0,16},{1,17},{2,18},{3,19},{4,20},{5,21},{6,22},{7,23},{8,24},{9,... | collective-permute-start | bytes 1572872 | tf_op jit(solution)/shard_map/ppermute | solution.py:1845
  243.7 9.9 %copy-start.17 = (bf16[128,2048]{1,0:T(8,128)(2,1)}, bf16[128,2048]{1,0:T(8,128)(2,1)S(1)}, u32[]{:S(2)}) copy-start(bf16[128,2048]{1,0:T(8,128)(2,1)S(1)} %multiply_convert_fusion.1.refs_0_) | copy-start | bytes 1572868
  269.7 134.3 %copy-start.42 = (f32[128]{0:T(128)}, f32[128]{0:T(128)S(1)}, u32[]{:S(2)}) copy-start(f32[128]{0:T(128)S(1)} %get-tuple-element.197) | copy-start | bytes 1540
  269.7 134.3 %copy-start.52 = (f32[128]{0:T(128)}, f32[128]{0:T(128)S(1)}, u32[]{:S(2)}) copy-start(f32[128]{0:T(128)S(1)} %get-tuple-element.196) | copy-start | bytes 1540
  423.1 10.0 %copy-start.11 = (bf16[4,512,1024]{2,1,0:T(8,128)(2,1)S(1)}, bf16[4,512,1024]{2,1,0:T(8,128)(2,1)}, u32[]{:S(2)}) copy-start(bf16[4,512,1024]{2,1,0:T(8,128)(2,1)} %get-tuple-element.94) | copy-start | bytes 12582916
  423.1 10.0 %copy-start.13 = (f32[128,576]{1,0:T(8,128)S(1)}, f32[128,576]{1,0:T(8,128)}, u32[]{:S(2)}) copy-start(f32[128,576]{1,0:T(8,128)} %copy-done.12) | copy-start | bytes 884740
  423.1 10.0 %copy-start.27 = (bf16[512,1024]{1,0:T(8,128)(2,1)S(1)}, bf16[512,1024]{1,0:T(8,128)(2,1)}, u32[]{:S(2)}) copy-start(bf16[512,1024]{1,0:T(8,128)(2,1)} %get-tuple-element.131) | copy-start | bytes 3145732
  423.1 10.0 %copy-start.38 = (f32[1,512]{1,0:T(1,128)S(1)}, f32[1,512]{1,0:T(1,128)}, u32[]{:S(2)}) copy-start(f32[1,512]{1,0:T(1,128)} %param.21) | copy-start | bytes 6148
  441.3 15.0 %collective-permute-start.1 = (bf16[128,2048]{1,0:T(8,128)(2,1)S(1)}, bf16[128,2048]{1,0:T(8,128)(2,1)S(1)}, u32[]{:S(2)}, u32[]{:S(2)}) collective-permute-start(bf16[128,2048]{1,0:T(8,128)(2,1)S(1)} %add_convert_fusion), channel_id=1, source_target_pairs={{16,0},{17,1},{18,2},{19,3},{20,4},{21,5},{22,6},{23,7},{24,8},{25... | collective-permute-start | bytes 1572872 | tf_op jit(solution)/shard_map/ppermute | solution.py:1910
  466.5 56.8 %copy-start.59 = (f32[128]{0:T(128)}, f32[128]{0:T(128)S(1)}, u32[]{:S(2)}) copy-start(f32[128]{0:T(128)S(1)} %broadcast_multiply_fusion.3) | copy-start | bytes 1540
  468.7 280.3 %reduce-scatter.2.cloned.1.call-start = ((), (), s32[]{:S(2)}) async-start(), calls=%async_computation.2 | async-start | bytes 3440640 | tf_op jit(solution)/shard_map/reduce_scatter | solution.py:1941
  623.3 12.0 %copy-start.8 = (bf16[2304,704]{1,0:T(8,128)(2,1)S(1)}, bf16[2304,704]{1,0:T(8,128)(2,1)}, u32[]{:S(2)}) copy-start(bf16[2304,704]{1,0:T(8,128)(2,1)} %get-tuple-element.157) | copy-start | bytes 9732100
  715.6 91.2 %all-gather.5.cloned.1.call-start = ((), (), s32[]{:S(2)}) async-start(), calls=%async_computation.3 | async-start | bytes 3342336 | tf_op jit(solution)/shard_map/all_gather | solution.py:1963
  729.5 20.8 %copy-start.39 = (f32[1,512]{1,0:T(1,128)S(1)}, f32[1,512]{1,0:T(1,128)}, u32[]{:S(2)}) copy-start(f32[1,512]{1,0:T(1,128)} %param.21) | copy-start | bytes 6148
  729.5 20.8 %copy-start.50 = (f32[128]{0:T(128)S(1)}, f32[128]{0:T(128)}, u32[]{:S(2)}) copy-start(f32[128]{0:T(128)} %copy-done.49) | copy-start | bytes 1540
  779.4 16.3 %slice-start = ((s8[8388608]{0:T(1024)(128)(4,1)}), s8[4194304]{0:T(1024)(128)(4,1)S(1)}, s32[]{:S(2)}) async-start(s8[8388608]{0:T(1024)(128)(4,1)} %bitcast.281), calls=%async_computation.4 | async-start | bytes 8388608
  786.0 9.6 %slice-start.1 = ((s8[8388608]{0:T(1024)(128)(4,1)}), s8[4194304]{0:T(1024)(128)(4,1)S(1)}, s32[]{:S(2)}) async-start(s8[8388608]{0:T(1024)(128)(4,1)} %bitcast.281), calls=%async_computation.5 | async-start | bytes 8388608
  786.0 9.6 %copy-start.64 = (bf16[2048,768]{1,0:T(8,128)(2,1)S(1)}, bf16[2048,768]{1,0:T(8,128)(2,1)}, u32[]{:S(2)}) copy-start(bf16[2048,768]{1,0:T(8,128)(2,1)} %get-tuple-element.151) | copy-start | bytes 9437188
  806.8 11.3 %copy-start.7 = (f32[2304,16]{1,0:T(8,128)S(1)}, f32[2304,16]{1,0:T(8,128)}, u32[]{:S(2)}) copy-start(f32[2304,16]{1,0:T(8,128)} %get-tuple-element.126.refs_3_) | copy-start | bytes 442372
  (49 other events, 263.6 us)
Sparse Core Ops, SparseCore 0:
  468.8 188.3 all-gather.2
  715.7 33.2 reduce-scatter.1
  759.3 45.9 all-gather.4
